TPU v7x, 256 devices: a whole 4x4x8 slice. The times are simulated.
256 devices in a mesh: wide: 128 (over y_lo, z, x, core), narrow: 2 (over y_hi).
Axes of the slice: x: 4, y: 4 (y_hi: 2, y_lo: 2; y = y_hi * 2 + y_lo), z: 8, core: 2. Of those that a mesh axis runs over, the one named last changes fastest.
Arguments:
- points: bfloat16 [4096, 3, 512], P('wide'), may hold values from -6 to 6
- vectors: bfloat16 [4096, 16, 512], P('wide', None, 'narrow'), may hold values from -6 to 6
- counts: int32 [128], P('wide'), may hold values from 8 to 32, as said below
- src_basis: bfloat16 [4096, 64, 512], P('wide', None, 'narrow'), may hold values from -0.25 to 0.25
- tgt_basis: bfloat16 [4096, 64, 512], P('wide'), may hold values from -0.75 to 0.75
- adm_src: int32 [4096, 8], P('wide'), may hold values from 0 to 4095, as said below
- couplings: bfloat16 [4096, 64, 512], P('wide'), may hold values from -0.25 to 0.25
Outputs:
- field: bfloat16 [4096, 16, 512], P('wide', None, 'narrow')
Inputs may be any that keep to these rules, and one draw needn't show every extreme that they name: `counts`: some index of wide holds exactly 32 live slots. `adm_src`: every entry is a live slot: d * 32 + s with s < counts[d].
All inputs are finite; a program needn't handle non-finite values.
Results may differ from a plain program's by a relative error of at most 0.005.
Values may be sent and summed in bfloat16 or wider, within the bound.
No kernel may reach another device: no remote copies, remote signals or barrier semaphores. Data moves between devices by JAX's collectives and lax.ppermute only.
A program may use at most 64 MiB of HBM per device.

v0:
```python
import math

import jax
import jax.numpy as jnp
from jax import lax
from jax.sharding import Mesh
from jax.sharding import PartitionSpec as P

WIDE = ("wide_0", "wide_1", "wide_2", "wide_3")


inverse_four_pi = 1.0 / (4.0 * math.pi)
soften_sq = 0.0025


def shifted(array, axis, by):
    devices = lax.axis_size(axis)
    return lax.ppermute(array, axis, [(i, (i + by) % devices) for i in range(devices)])


def sent_to_all(array, axis):
    copies = jnp.broadcast_to(array, (lax.axis_size(axis), *array.shape))
    return lax.all_to_all(copies, axis, split_axis=0, concat_axis=0, tiled=True)


def of_everyone(array, axis):
    return sent_to_all(array, axis).sum(axis=0)


def joined_along(blocks, dim):
    blocks = jnp.moveaxis(blocks, 0, dim)
    shape = blocks.shape
    return blocks.reshape(*shape[:dim], shape[dim] * shape[dim + 1], *shape[dim + 2 :])


def gathered_by_axis(array, axes, dim):
    far, near = axes
    blocks = sent_to_all(sent_to_all(array, far), near)
    return joined_along(blocks.swapaxes(0, 1).reshape(-1, *array.shape), dim)


def cut_along(array, dim, devices):
    shape = array.shape
    blocks = array.reshape(*shape[:dim], devices, shape[dim] // devices, *shape[dim + 1 :])
    return jnp.moveaxis(blocks, dim, 0)


def summed_on_arrival(array, axis, dim):
    devices = lax.axis_size(axis)
    blocks = lax.all_to_all(cut_along(array, dim, devices), axis, 0, 0, tiled=True)
    return jnp.sum(blocks, axis=0)


def kernel_block(targets, sources):
    target_f = targets.astype(jnp.float32)
    source_f = sources.astype(jnp.float32)
    squared = jnp.zeros((targets.shape[1], sources.shape[1]), jnp.float32)
    for axis_index in range(3):
        differ = target_f[axis_index][:, None] - source_f[axis_index][None, :]
        squared = squared + differ * differ
    return (inverse_four_pi / jnp.sqrt(squared + soften_sq)).astype(jnp.bfloat16)


def near_leaf(targets, sources, source_vals):
    kernel = kernel_block(targets, sources)
    return jnp.einsum("pq,rq->rp", kernel, source_vals, preferred_element_type=jnp.float32)


def near_block_sum(points, source_points, source_vals, group_size):
    leaves = points.shape[0]
    shaped = (
        points.reshape((leaves // group_size, group_size) + points.shape[1:]),
        source_points.reshape((leaves // group_size, group_size) + source_points.shape[1:]),
        source_vals.reshape((leaves // group_size, group_size) + source_vals.shape[1:]),
    )

    def run_group(blocks):
        return jax.vmap(near_leaf)(blocks[0], blocks[1], blocks[2])

    result = lax.map(run_group, shaped)
    return result.reshape((leaves,) + result.shape[2:])


def local(points, vectors, counts, src_basis, tgt_basis, adm_src, couplings):
    leaf_dev = vectors.shape[0]
    half_width = vectors.shape[2]
    narrow_rank = lax.axis_index("narrow")
    narrow_size = lax.axis_size("narrow")
    live_count = counts[0]
    slot_ids = jnp.arange(leaf_dev, dtype=jnp.int32)
    is_live = slot_ids < live_count
    values = jnp.where(is_live[:, None, None], vectors, jnp.zeros_like(vectors))
    own_points = lax.dynamic_slice_in_dim(points, narrow_rank * half_width, half_width, 2)
    last_vals = lax.dynamic_index_in_dim(values, live_count - 1, 0, keepdims=False)
    last_points = lax.dynamic_index_in_dim(own_points, live_count - 1, 0, keepdims=False)
    left_vals, left_points = shifted((last_vals, last_points), WIDE, 1)
    right_vals, right_points = shifted((values[0], own_points[0]), WIDE, -1)
    at_end = (slot_ids == live_count - 1)[:, None, None]
    prev_vals = jnp.concatenate([left_vals[None], values[:-1]], 0)
    prev_points = jnp.concatenate([left_points[None], own_points[:-1]], 0)
    next_vals = jnp.where(at_end, right_vals[None], jnp.concatenate([values[1:], values[:1]], 0))
    next_points = jnp.where(
        at_end, right_points[None], jnp.concatenate([own_points[1:], own_points[:1]], 0)
    )
    source_points = jnp.concatenate([prev_points, own_points, next_points], 2)
    source_vals = jnp.concatenate([prev_vals, values, next_vals], 2)
    near_part = near_block_sum(points, source_points, source_vals, 4)
    partial_value = jnp.einsum(
        "lrp,lap->lra", values, src_basis, preferred_element_type=jnp.float32
    )
    coeffs = of_everyone(partial_value, "narrow").astype(jnp.bfloat16)
    wanted = adm_src.reshape(-1)
    adm_count = adm_src.shape[1]
    rank_width = coeffs.shape[2]
    rhs_rows = coeffs.shape[1] // narrow_size
    coef_table = lax.dynamic_slice_in_dim(coeffs, narrow_rank * rhs_rows, rhs_rows, 1).reshape(
        leaf_dev, rhs_rows * rank_width
    )
    shard_rows = gathered_by_axis(coef_table, (("wide_0", "wide_1", "wide_2"), "wide_3"), 0)
    piece_ids = jnp.arange(shard_rows.shape[0], dtype=jnp.int32)
    one_hot = (wanted[:, None] == piece_ids[None, :]).astype(jnp.bfloat16)
    selected = jnp.dot(one_hot, shard_rows, preferred_element_type=jnp.float32)
    selected = selected.astype(jnp.bfloat16).reshape(leaf_dev, adm_count, rhs_rows, rank_width)
    selected = selected.transpose(0, 2, 1, 3).reshape(leaf_dev, rhs_rows, adm_count * rank_width)
    target_coeffs = jnp.einsum(
        "lrk,lak->lra", selected, couplings, preferred_element_type=jnp.float32
    ).astype(jnp.bfloat16)
    far_rows = jnp.einsum(
        "lra,lap->lrp", target_coeffs, tgt_basis, preferred_element_type=jnp.float32
    )
    summand = near_part + lax.dynamic_update_slice_in_dim(
        jnp.zeros_like(near_part), far_rows, narrow_rank * rhs_rows, 1
    )
    summed = summed_on_arrival(summand, "narrow", 2)
    return jnp.where(is_live[:, None, None], summed, jnp.zeros_like(summed)).astype(jnp.bfloat16)


def solution(mesh):
    split = Mesh(
        mesh.devices.reshape(2, 8, 4, 2, mesh.shape["narrow"]),
        ("wide_0", "wide_1", "wide_2", "wide_3", "narrow"),
    )
    in_specs = (
        P(WIDE, None, None),
        P(WIDE, None, "narrow"),
        P(WIDE),
        P(WIDE, None, "narrow"),
        P(WIDE, None, None),
        P(WIDE, None),
        P(WIDE, None, None),
    )
    out_specs = P(WIDE, None, "narrow")
    return jax.shard_map(local, mesh=split, in_specs=in_specs, out_specs=out_specs, check_vma=False)
```

profile of v0, /device:TPU:6, one launch (start us, length us, event | category | flops | bytes accessed | tf_op | source)
XLA Modules:
  0.0 140.2 jit_solution(2564424050931970838)
XLA Ops:
  3.3 1.1 broadcast_select_fusion
  5.0 1.5 %collective-permute-start.1 = (bf16[16,256]{1,0:T(8,128)(2,1)}, bf16[16,256]{1,0:T(8,128)(2,1)}, u32[]{:S(2)}, u32[]{:S(2)}) collective-permute-start(bf16[16,256]{1,0:T(8,128)(2,1)} %get-tuple-element.65), channel_id=1, source_target_pairs={{0,254},{2,0},{4,2},{6,4},{8,6},{10,8},{12,10},{14,12},{16,14},{18... | collective-permute-start | bytes 24584 | tf_op jit(solution)/shard_map/ppermute | solution.py:18
  6.5 1.7 %collective-permute-start = (bf16[16,256]{1,0:T(8,128)(2,1)}, bf16[16,256]{1,0:T(8,128)(2,1)}, u32[]{:S(2)}, u32[]{:S(2)}) collective-permute-start(bf16[16,256]{1,0:T(8,128)(2,1)} %get-tuple-element.64), channel_id=1, source_target_pairs={{0,2},{2,4},{4,6},{6,8},{8,10},{10,12},{12,14},{14,16},{16,18},{18... | collective-permute-start | bytes 24584 | tf_op jit(solution)/shard_map/ppermute | solution.py:18
  8.2 1.6 %fusion.13 = f32[32,16,64]{2,1,0:T(8,128)S(1)} fusion(bf16[32,16,256]{2,1,0:T(8,128)(2,1)S(1)} %broadcast_select_fusion, bf16[32,64,256]{2,1,0:T(8,128)(2,1)} %param.12), kind=kOutput, calls=%fused_computation.45 | convolution fusion | flops 16777216 | bytes 1441792 | tf_op jit(solution)/shard_map/lrp,lap->lra/dot_general | solution.py:108
  9.8 1.0 reshape.56
  10.9 4.5 %all-to-all-start = ((f32[2,1,32768]{2,1,0:T(1,128)}), f32[2,1,32768]{2,1,0:T(1,128)}, u32[]{:S(2)}, u32[]{:S(2)}) async-start(f32[2,1,32768]{2,1,0:T(1,128)} %reshape.56), calls=%async_computation | async-start | bytes 524288 | tf_op jit(solution)/shard_map/all_to_all | solution.py:23
  21.5 0.8 pad_maximum_fusion.1
  23.1 1.1 maximum_select_fusion
  24.2 1.9 %pad_maximum_fusion = bf16[32,16,768]{2,1,0:T(8,128)(2,1)} fusion(bf16[32,16,256]{2,1,0:T(8,128)(2,1)S(1)} %maximum_select_fusion, bf16[32,16,256]{2,1,0:T(8,128)(2,1)S(1)} %broadcast_select_fusion, bf16[31,16,256]{2,1,0:T(8,128)(2,1)} %get-tuple-element.67, bf16[1,16,256]{2,1,0:T(8,128)(2,1)} %bitcast.14), kind=kLoop, calls=%fused_computation.25 | loop fusion | flops 3145728 | bytes 1572864 | tf_op jit(solution)/shard_map/concatenate | solution.py:106
  26.6 2.4 %reduce = f32[2,32768]{1,0:T(2,128)S(1)} reduce(f32[2,1,32768]{2,1,0:T(1,128)} %all-to-all-done, f32[]{:T(128)} %broadcast.28), dimensions={1}, to_apply=%all_to_all.12.reduce_sub_computation | reduce | bytes 524292 | tf_op jit(solution)/shard_map/all_to_all | solution.py:23
  29.0 1.2 reshape.57
  30.1 1.1 reduce_sum.18
  31.3 1.6 %broadcast_in_dim.91 = bf16[64,32,512]{2,1,0:T(8,128)(2,1)} broadcast(bf16[32,512]{1,0:T(8,128)(2,1)S(1)} %reshape.49), dimensions={1,2} | broadcast | bytes 2129920 | tf_op jit(solution)/shard_map/broadcast_in_dim | solution.py:22
  32.9 15.9 %all-to-all-start.1 = ((bf16[64,32,512]{2,1,0:T(8,128)(2,1)}), bf16[64,32,512]{2,1,0:T(8,128)(2,1)}, u32[]{:S(2)}, u32[]{:S(2)}) async-start(bf16[64,32,512]{2,1,0:T(8,128)(2,1)} %broadcast_in_dim.91), calls=%async_computation.1 | async-start | bytes 4194304 | tf_op jit(solution)/shard_map/all_to_all | solution.py:23
  48.8 43.1 %while.10 = (s32[]{:T(128)}, f32[8,4,16,512]{3,2,1,0:T(8,128)S(1)}, bf16[8,4,16,768]{3,2,1,0:T(8,128)(2,1)}, bf16[8,4,3,512]{3,1,0,2:T(4,128)(2,1)}, bf16[8,4,3,768]{3,1,0,2:T(4,128)(2,1)}, /*index=5*/s32[]{:T(128)}) while((s32[]{:T(128)}, f32[8,4,16,512]{3,2,1,0:T(8,128)S(1)}, bf16[8,4,16,768]{3,2,1,0:T(8,128)(2,1)}, ...), condition=%wide.region_1.2_spmd, body=%wide.region_0.1_spmd.sunk | while | flops 67648512 | bytes 506957 | solution.py:80
  50.3 3.9 %fusion.23 = f32[8,4,16,512]{3,2,1,0:T(8,128)S(1)} fusion(f32[8,4,16,512]{3,2,1,0:T(8,128)S(1)} %get-tuple-element.123, s32[]{:T(128)} %get-tuple-element.122, f32[4,768]{1,0:T(4,128)S(1)} %get-tuple-element.110, f32[4,512]{1,0:T(4,128)S(1)} %get-tuple-element.111, f32[4,768]{1,0:T(4,128)S(1)} %get-tuple-element.112, ...), kind=kOutput, calls=%fused_computation.3.clone.1 | convolution fusion | flops 67633152 | bytes 291840 | tf_op jit(solution)/shard_map/while/body/eval_jaxpr/vmap(pq,rq->rp)/dot_general | solution.py:66
  55.7 3.9 %fusion.23 = f32[8,4,16,512]{3,2,1,0:T(8,128)S(1)} fusion(f32[8,4,16,512]{3,2,1,0:T(8,128)S(1)} %get-tuple-element.123, s32[]{:T(128)} %get-tuple-element.122, f32[4,768]{1,0:T(4,128)S(1)} %get-tuple-element.110, f32[4,512]{1,0:T(4,128)S(1)} %get-tuple-element.111, f32[4,768]{1,0:T(4,128)S(1)} %get-tuple-element.112, ...), kind=kOutput, calls=%fused_computation.3.clone.1 | convolution fusion | flops 67633152 | bytes 291840 | tf_op jit(solution)/shard_map/while/body/eval_jaxpr/vmap(pq,rq->rp)/dot_general | solution.py:66
  61.1 3.9 %fusion.23 = f32[8,4,16,512]{3,2,1,0:T(8,128)S(1)} fusion(f32[8,4,16,512]{3,2,1,0:T(8,128)S(1)} %get-tuple-element.123, s32[]{:T(128)} %get-tuple-element.122, f32[4,768]{1,0:T(4,128)S(1)} %get-tuple-element.110, f32[4,512]{1,0:T(4,128)S(1)} %get-tuple-element.111, f32[4,768]{1,0:T(4,128)S(1)} %get-tuple-element.112, ...), kind=kOutput, calls=%fused_computation.3.clone.1 | convolution fusion | flops 67633152 | bytes 291840 | tf_op jit(solution)/shard_map/while/body/eval_jaxpr/vmap(pq,rq->rp)/dot_general | solution.py:66
  66.5 3.9 %fusion.23 = f32[8,4,16,512]{3,2,1,0:T(8,128)S(1)} fusion(f32[8,4,16,512]{3,2,1,0:T(8,128)S(1)} %get-tuple-element.123, s32[]{:T(128)} %get-tuple-element.122, f32[4,768]{1,0:T(4,128)S(1)} %get-tuple-element.110, f32[4,512]{1,0:T(4,128)S(1)} %get-tuple-element.111, f32[4,768]{1,0:T(4,128)S(1)} %get-tuple-element.112, ...), kind=kOutput, calls=%fused_computation.3.clone.1 | convolution fusion | flops 67633152 | bytes 291840 | tf_op jit(solution)/shard_map/while/body/eval_jaxpr/vmap(pq,rq->rp)/dot_general | solution.py:66
  71.8 3.9 %fusion.23 = f32[8,4,16,512]{3,2,1,0:T(8,128)S(1)} fusion(f32[8,4,16,512]{3,2,1,0:T(8,128)S(1)} %get-tuple-element.123, s32[]{:T(128)} %get-tuple-element.122, f32[4,768]{1,0:T(4,128)S(1)} %get-tuple-element.110, f32[4,512]{1,0:T(4,128)S(1)} %get-tuple-element.111, f32[4,768]{1,0:T(4,128)S(1)} %get-tuple-element.112, ...), kind=kOutput, calls=%fused_computation.3.clone.1 | convolution fusion | flops 67633152 | bytes 291840 | tf_op jit(solution)/shard_map/while/body/eval_jaxpr/vmap(pq,rq->rp)/dot_general | solution.py:66
  77.2 3.9 %fusion.23 = f32[8,4,16,512]{3,2,1,0:T(8,128)S(1)} fusion(f32[8,4,16,512]{3,2,1,0:T(8,128)S(1)} %get-tuple-element.123, s32[]{:T(128)} %get-tuple-element.122, f32[4,768]{1,0:T(4,128)S(1)} %get-tuple-element.110, f32[4,512]{1,0:T(4,128)S(1)} %get-tuple-element.111, f32[4,768]{1,0:T(4,128)S(1)} %get-tuple-element.112, ...), kind=kOutput, calls=%fused_computation.3.clone.1 | convolution fusion | flops 67633152 | bytes 291840 | tf_op jit(solution)/shard_map/while/body/eval_jaxpr/vmap(pq,rq->rp)/dot_general | solution.py:66
  82.6 3.9 %fusion.23 = f32[8,4,16,512]{3,2,1,0:T(8,128)S(1)} fusion(f32[8,4,16,512]{3,2,1,0:T(8,128)S(1)} %get-tuple-element.123, s32[]{:T(128)} %get-tuple-element.122, f32[4,768]{1,0:T(4,128)S(1)} %get-tuple-element.110, f32[4,512]{1,0:T(4,128)S(1)} %get-tuple-element.111, f32[4,768]{1,0:T(4,128)S(1)} %get-tuple-element.112, ...), kind=kOutput, calls=%fused_computation.3.clone.1 | convolution fusion | flops 67633152 | bytes 291840 | tf_op jit(solution)/shard_map/while/body/eval_jaxpr/vmap(pq,rq->rp)/dot_general | solution.py:66
  88.0 3.9 %fusion.23 = f32[8,4,16,512]{3,2,1,0:T(8,128)S(1)} fusion(f32[8,4,16,512]{3,2,1,0:T(8,128)S(1)} %get-tuple-element.123, s32[]{:T(128)} %get-tuple-element.122, f32[4,768]{1,0:T(4,128)S(1)} %get-tuple-element.110, f32[4,512]{1,0:T(4,128)S(1)} %get-tuple-element.111, f32[4,768]{1,0:T(4,128)S(1)} %get-tuple-element.112, ...), kind=kOutput, calls=%fused_computation.3.clone.1 | convolution fusion | flops 67633152 | bytes 291840 | tf_op jit(solution)/shard_map/while/body/eval_jaxpr/vmap(pq,rq->rp)/dot_general | solution.py:66
  91.9 7.3 %all-to-all-done.1 = bf16[64,32,512]{2,1,0:T(8,128)(2,1)} async-done(((bf16[64,32,512]{2,1,0:T(8,128)(2,1)}), bf16[64,32,512]{2,1,0:T(8,128)(2,1)}, u32[]{:S(2)}, u32[]{:S(2)}) %all-to-all-start.1) | async-done | bytes 2097184 | tf_op jit(solution)/shard_map/all_to_all | solution.py:23
  99.2 2.1 %broadcast_in_dim.92 = bf16[2,64,32,512]{3,2,1,0:T(8,128)(2,1)S(1)} broadcast(bf16[64,32,512]{2,1,0:T(8,128)(2,1)} %all-to-all-done.1), dimensions={1,2,3} | broadcast | bytes 6291456 | tf_op jit(solution)/shard_map/broadcast_in_dim | solution.py:22
  101.3 8.8 %all_to_all.20 = bf16[2,64,32,512]{3,2,1,0:T(8,128)(2,1)S(1)} all-to-all(bf16[2,64,32,512]{3,2,1,0:T(8,128)(2,1)S(1)} %broadcast_in_dim.92), channel_id=1, replica_groups=mesh['wide_0'=2,'wide_1'=8,'wide_2'=4,'wide_3'=2,'narrow'=2] {'wide_3'}, dimensions={0} | all-to-all | bytes 8388608 | tf_op jit(solution)/shard_map/all_to_all | solution.py:23
  110.8 1.3 fusion.11
  112.1 1.1 reshape.50
  113.2 1.9 %copy.37 = bf16[32,8,8,64]{3,1,2,0:T(8,128)(2,1)} copy(bf16[32,8,8,64]{3,2,1,0:T(8,128)(2,1)} %reshape.50) | data formatting | bytes 524288 | tf_op jit(solution)/shard_map/reshape | solution.py:123
  115.2 1.4 reshape.51
  116.6 2.5 %fusion.10 = f32[32,16,512]{2,1,0:T(8,128)S(1)} fusion(f32[32,16,512]{2,1,0:T(8,128)S(1)} %bitcast.86, s32[]{:T(128)S(6)} %select_n.40, bf16[32,64,512]{2,1,0:T(8,128)(2,1)S(1)} %copy-done, bf16[32,8,512]{2,1,0:T(8,128)(2,1)S(1)} %reshape.51, bf16[32,64,512]{2,1,0:T(8,128)(2,1)} %param.15), kind=kOutput, calls=%fused_computation.21 | convolution fusion | flops 33701888 | bytes 5505028 | tf_op jit(solution)/shard_map/lra,lap->lrp/dot_general | solution.py:128
  119.2 20.0 %all_to_all.21 = f32[2,32,16,256]{3,2,1,0:T(8,128)S(1)} all-to-all(f32[2,32,16,256]{3,2,1,0:T(8,128)S(1)} %bitcast.85), channel_id=1, replica_groups=mesh['wide_0'=2,'wide_1'=8,'wide_2'=4,'wide_3'=2,'narrow'=2] {'narrow'}, dimensions={0} | all-to-all | bytes 2097152 | tf_op jit(solution)/shard_map/all_to_all | solution.py:50
  (75 shorter events, 24.1 us)
Async XLA Ops:
  0.0 116.5 %copy-start = (bf16[32,64,512]{2,1,0:T(8,128)(2,1)S(1)}, bf16[32,64,512]{2,1,0:T(8,128)(2,1)}, u32[]{:S(2)}) copy-start(bf16[32,64,512]{2,1,0:T(8,128)(2,1)} %param.13) | copy-start | bytes 6291460
  0.0 15.3 %copy-start.1 = (bf16[32,3,512]{2,0,1:T(8,128)(2,1)S(1)}, bf16[32,3,512]{2,0,1:T(8,128)(2,1)}, u32[]{:S(2)}) copy-start(bf16[32,3,512]{2,0,1:T(8,128)(2,1)} %param.9) | copy-start | bytes 294916
  1.6 6.5 %copy-start.2 = (bf16[1,3,256]{2,0,1:T(2,128)(2,1)}, bf16[1,3,256]{2,0,1:T(2,128)(2,1)S(1)}, u32[]{:S(2)}) copy-start(bf16[1,3,256]{2,0,1:T(2,128)(2,1)S(1)} %get-tuple-element.70) | copy-start | bytes 4612
  2.2 18.6 %collective-permute-start.3 = (bf16[3,256]{1,0:T(4,128)(2,1)}, bf16[3,256]{1,0:T(4,128)(2,1)}, u32[]{:S(2)}, u32[]{:S(2)}) collective-permute-start(bf16[3,256]{1,0:T(4,128)(2,1)} %bitcast.67), channel_id=1, source_target_pairs={{0,254},{2,0},{4,2},{6,4},{8,6},{10,8},{12,10},{14,12},{16,14},{18... | collective-permute-start | bytes 4616 | tf_op jit(solution)/shard_map/ppermute | solution.py:18
  3.1 17.0 %collective-permute-start.2 = (bf16[3,256]{1,0:T(4,128)(2,1)}, bf16[3,256]{1,0:T(4,128)(2,1)}, u32[]{:S(2)}, u32[]{:S(2)}) collective-permute-start(bf16[3,256]{1,0:T(4,128)(2,1)} %bitcast.68), channel_id=1, source_target_pairs={{0,2},{2,4},{4,6},{6,8},{8,10},{10,12},{12,14},{14,16},{16,18},{18... | collective-permute-start | bytes 4616 | tf_op jit(solution)/shard_map/ppermute | solution.py:18
  3.3 4.9 %copy-start.3 = (pred[32]{0:T(512)(128)(4,1)}, pred[32]{0:T(512)(128)(4,1)S(1)}, u32[]{:S(2)}) copy-start(pred[32]{0:T(512)(128)(4,1)S(1)} %iota_compare_fusion.5) | copy-start | bytes 100
  5.0 18.1 %collective-permute-start.1 = (bf16[16,256]{1,0:T(8,128)(2,1)}, bf16[16,256]{1,0:T(8,128)(2,1)}, u32[]{:S(2)}, u32[]{:S(2)}) collective-permute-start(bf16[16,256]{1,0:T(8,128)(2,1)} %get-tuple-element.65), channel_id=1, source_target_pairs={{0,254},{2,0},{4,2},{6,4},{8,6},{10,8},{12,10},{14,12},{16,14},{18... | collective-permute-start | bytes 24584 | tf_op jit(solution)/shard_map/ppermute | solution.py:18
  6.5 17.7 %collective-permute-start = (bf16[16,256]{1,0:T(8,128)(2,1)}, bf16[16,256]{1,0:T(8,128)(2,1)}, u32[]{:S(2)}, u32[]{:S(2)}) collective-permute-start(bf16[16,256]{1,0:T(8,128)(2,1)} %get-tuple-element.64), channel_id=1, source_target_pairs={{0,2},{2,4},{4,6},{6,8},{8,10},{10,12},{12,14},{14,16},{16,18},{18... | collective-permute-start | bytes 24584 | tf_op jit(solution)/shard_map/ppermute | solution.py:18
  10.9 15.2 %all-to-all-start = ((f32[2,1,32768]{2,1,0:T(1,128)}), f32[2,1,32768]{2,1,0:T(1,128)}, u32[]{:S(2)}, u32[]{:S(2)}) async-start(f32[2,1,32768]{2,1,0:T(1,128)} %reshape.56), calls=%async_computation | async-start | bytes 524288 | tf_op jit(solution)/shard_map/all_to_all | solution.py:23
  32.9 66.3 %all-to-all-start.1 = ((bf16[64,32,512]{2,1,0:T(8,128)(2,1)}), bf16[64,32,512]{2,1,0:T(8,128)(2,1)}, u32[]{:S(2)}, u32[]{:S(2)}) async-start(bf16[64,32,512]{2,1,0:T(8,128)(2,1)} %broadcast_in_dim.91), calls=%async_computation.1 | async-start | bytes 4194304 | tf_op jit(solution)/shard_map/all_to_all | solution.py:23
  110.2 0.7 copy-start.5
  116.6 22.8 %copy-start.4 = (pred[32]{0:T(512)(128)(4,1)S(1)}, pred[32]{0:T(512)(128)(4,1)}, u32[]{:S(2)}) copy-start(pred[32]{0:T(512)(128)(4,1)} %copy-done.3) | copy-start | bytes 100
where the time goes:
time: 142 us; the launch traced here: 140 us
  matrix products  36.8 us (26%)
  blocking collectives  28.8 us (20%)
  starting transfers between devices  24.1 us (17%)
  other arithmetic  22.1 us (16%)
  local copies, waits for them, and re-layouts  20 us (14%)
  waiting for transfers between devices  7.3 us (5%)
    dot_general x8, matrix products, near_leaf(): jnp.einsum('pq,rq->rp', kernel, source_vals, preferred_element_type=jnp.f...  31.4 us
    all_to_all x2, starting transfers between devices, sent_to_all(): return lax.all_to_all(copies, axis, split_axis=0, concat_axis=0, tiled=True)  20.4 us
    all_to_all x1, blocking collectives, summed_on_arrival(): lax.all_to_all(cut_along(array, dim, devices), axis, 0, 0, tiled=True)  20 us
    all_to_all x1, blocking collectives, sent_to_all(): return lax.all_to_all(copies, axis, split_axis=0, concat_axis=0, tiled=True)  8.84 us
    all_to_all x2, waiting for transfers between devices, sent_to_all(): return lax.all_to_all(copies, axis, split_axis=0, concat_axis=0, tiled=True)  7.29 us
    convert_element_type x8, other arithmetic, kernel_block(): source_f = sources.astype(jnp.float32)  5.87 us
    convert_element_type x8, other arithmetic, kernel_block(): target_f = targets.astype(jnp.float32)  5.69 us
    unnamed x17, local copies, waits for them, and re-layouts  4.2 us
  transfers between devices with their start and end apart: 6, of which 1 were waited for; matrix products, arithmetic and copies ran while one was open for 42% of the time, Pallas kernels for 0%

commit v1 on v0

v1 whole, which is shorter than its diff:
```python
import math

import jax
import jax.numpy as jnp
from jax import lax
from jax.experimental import pallas as pl
from jax.experimental.pallas import tpu as pltpu
from jax.sharding import Mesh
from jax.sharding import PartitionSpec as P

WIDE = ("y", "z", "x", "c")
PEERS = ("y", "x", "c")

inverse_four_pi = 1.0 / (4.0 * math.pi)
soften_sq = 0.0025

T, R, A, J, HALF, LEAF = 32, 16, 64, 8, 256, 512
RH = R // 2
N_Z, N_PEER = 8, 16
CAP = 48
ENTRIES = T * J
COLUMN = N_Z * T
bf16, f32, i32 = jnp.bfloat16, jnp.float32, jnp.int32

VMEM = pl.BlockSpec(memory_space=pltpu.VMEM)
SMEM = pl.BlockSpec(memory_space=pltpu.SMEM)


def nt(a, b):
    return lax.dot_general(a, b, (((1,), (1,)), ((), ())), preferred_element_type=f32)


def nn(a, b):
    return lax.dot_general(a, b, (((1,), (0,)), ((), ())), preferred_element_type=f32)


def iota(shape, dim):
    return lax.broadcasted_iota(i32, shape, dim)


def folded(wide):
    two = wide[:, :128] + wide[:, 128:]
    return two[:, :64] + two[:, 64:]


def index_kernel(count_ref, adm_ref, sel_ref, req_ref):
    count = count_ref[0]
    adm = jnp.concatenate([adm_ref[...].astype(f32), jnp.zeros((8, 96), f32)], 1).T
    leaf = jnp.concatenate(
        [jnp.broadcast_to(adm[:T, j : j + 1], (T, 128)) for j in range(J)], 0
    ).astype(i32)
    live = (iota((ENTRIES, 128), 0) & (T - 1)) < count
    column = (leaf >> 11) * 8 + ((leaf >> 5) & 7)
    row = ((leaf >> 8) & 7) * T + (leaf & (T - 1))
    member = jnp.where((column == iota((ENTRIES, 128), 1)) & live, 1.0, 0.0)
    below = jnp.where(iota((ENTRIES, ENTRIES), 0) > iota((ENTRIES, ENTRIES), 1), 1.0, 0.0)
    rank = nn(below.astype(bf16), member.astype(bf16))
    place = jnp.sum(member * rank, axis=1, keepdims=True)
    over = jnp.max(place) > CAP - 0.5
    place = jnp.broadcast_to(place, (ENTRIES, 128))
    fits = live & (place < CAP - 0.5)
    sel = jnp.where(fits, column * CAP + place.astype(i32), -1)
    sel_ref[...] = sel
    sel_row = sel.astype(f32).T[:1]
    slots = N_PEER * CAP
    pick = jnp.where(iota((slots, ENTRIES), 0) == sel_row.astype(i32), 1.0, 0.0).astype(bf16)
    wanted = nn(pick, (row + 1).astype(f32).astype(bf16))
    wanted = jnp.where(over, -1.0, wanted)
    req_ref[...] = wanted.astype(bf16).reshape(N_PEER, CAP, 128)


def index_call(counts, adm):
    return pl.pallas_call(
        index_kernel,
        out_shape=(
            jax.ShapeDtypeStruct((ENTRIES, 128), i32),
            jax.ShapeDtypeStruct((N_PEER, CAP, 128), bf16),
        ),
        in_specs=[SMEM, VMEM],
        out_specs=(VMEM, VMEM),
        name="requests",
    )(counts, adm)


def coeff_kernel(n_ref, vec_ref, basis_ref, keep_ref, send_ref, rows):
    n = n_ref[0]
    same = (iota((64, 256), 0) >> 4) == (iota((64, 256), 1) >> 6)
    for g in range(T // 4):
        lhs = vec_ref[4 * g : 4 * g + 4].reshape(64, HALF)
        rhs = basis_ref[4 * g : 4 * g + 4].reshape(4 * A, HALF)
        rows[64 * g : 64 * g + 64, :64] = folded(jnp.where(same, nt(lhs, rhs), 0.0))
    for out, first in ((send_ref, (1 - n) * RH), (keep_ref, n * RH)):
        for r in range(0, RH, 2):
            pair = [rows[pl.ds(first + r + k, T, stride=R), :][:, :64] for k in range(2)]
            out[:, r * A : (r + 2) * A] = jnp.concatenate(pair, 1)


def coeff_call(n, vectors, basis):
    shape = jax.ShapeDtypeStruct((T, RH * A), f32)
    return pl.pallas_call(
        coeff_kernel,
        out_shape=(shape, shape),
        in_specs=[SMEM, VMEM, VMEM],
        out_specs=(VMEM, VMEM),
        scratch_shapes=[pltpu.VMEM((T * R, 128), f32)],
        name="coeffs",
    )(n, vectors, basis)


def pack_kernel(req_ref, table_ref, out_ref):
    lanes = iota((CAP, 128), 1).astype(f32) + 1.0
    for r in range(0, N_PEER, 4):
        want = [req_ref[r + k].astype(f32) for k in range(4)]
        hot = [
            jnp.concatenate(
                [jnp.where(w == lanes, 1.0, 0.0), jnp.where(w == lanes + 128.0, 1.0, 0.0)], 1
            )
            for w in want
        ]
        picked = nn(jnp.concatenate(hot, 0).astype(bf16), table_ref[...])
        out_ref[r : r + 4] = picked.astype(bf16).reshape(4, CAP, RH * A)


def pack_call(req, table):
    return pl.pallas_call(
        pack_kernel,
        out_shape=jax.ShapeDtypeStruct((N_PEER, CAP, RH * A), bf16),
        in_specs=[VMEM, VMEM],
        out_specs=VMEM,
        name="pack",
    )(req, table)


def couple(picked, couple_ref, out_ref):
    lows = [picked[j * T : (j + 1) * T] for j in range(J)]
    by_rhs = []
    for r in range(RH):
        cols = [low[:, r * A : (r + 1) * A] for low in lows]
        by_rhs.append(jnp.concatenate(cols, 1).astype(bf16))
    row_t = iota((16 * RH, 256), 0) & 15
    col_t = iota((16 * RH, 256), 1) >> 6
    for h in range(2):
        lhs = jnp.concatenate([s[16 * h : 16 * h + 16] for s in by_rhs], 0)
        total = jnp.zeros((16 * RH, A), f32)
        for g in range(4):
            first = 16 * h + 4 * g
            rhs = couple_ref[first : first + 4].reshape(4 * A, J * A)
            total = total + folded(jnp.where(row_t == col_t + 4 * g, nt(lhs, rhs), 0.0))
        total = total.reshape(RH, 16, A)
        for r in range(0, RH, 2):
            pair = jnp.concatenate([total[r], total[r + 1]], 1)
            out_ref[r // 2, 16 * h : 16 * h + 16, :] = pair.astype(bf16)


def select_kernel(sel_ref, got_ref, couple_ref, out_ref):
    slots = N_PEER * CAP
    sel = sel_ref[...]
    lanes = iota((ENTRIES, 128), 1)
    hot = jnp.concatenate(
        [jnp.where(sel == lanes + 128 * k, 1.0, 0.0) for k in range(slots // 128)], 1
    )
    couple(nn(hot.astype(bf16), got_ref[...].reshape(slots, RH * A)), couple_ref, out_ref)


TC_SHAPE = jax.ShapeDtypeStruct((RH // 2, T, 2 * A), bf16)


def select_call(sel, got, couplings):
    return pl.pallas_call(
        select_kernel,
        out_shape=TC_SHAPE,
        in_specs=[VMEM, VMEM, VMEM],
        out_specs=VMEM,
        name="select",
    )(sel, got, couplings)


def couple_kernel(picked_ref, couple_ref, out_ref):
    couple(picked_ref[...], couple_ref, out_ref)


def couple_call(picked, couplings):
    return pl.pallas_call(
        couple_kernel,
        out_shape=TC_SHAPE,
        in_specs=[VMEM, VMEM],
        out_specs=VMEM,
        name="couple",
    )(picked, couplings)


def near_kernel(leaves, scalar_ref, pts_ref, vec_ref, other_ref, left_ref, right_ref, out_ref, *bufs):
    vals, pts, kern0, kern1 = bufs
    count, n = scalar_ref[0], scalar_ref[1]
    own = pl.multiple_of(n * HALF, HALF)
    other = pl.multiple_of((1 - n) * HALF, HALF)
    vals[:T, :, pl.ds(own, HALF)] = vec_ref[...]
    vals[:T, :, pl.ds(other, HALF)] = other_ref[...]
    pts[:T] = pts_ref[...]
    for k, edge in enumerate((left_ref, right_ref)):
        vals[T + k] = edge[:R]
        pts[T + k] = edge[R : R + 3]

    def sources(t):
        return jnp.where(t == 0, T, t - 1), t, jnp.where(t == count - 1, T + 1, jnp.minimum(t + 1, T - 1))

    def fill(t, kern):
        x = pts[t, :, pl.ds(own, HALF)].astype(f32)
        x = jnp.concatenate([x, jnp.zeros((5, HALF), f32)], 0).T.astype(bf16)
        for k, u in enumerate(sources(t)):
            y = pts[u]
            for p in range(0, HALF, 32):
                squared = None
                for i in range(3):
                    differ = x[p : p + 32, i : i + 1] - y[i : i + 1, :]
                    differ = differ * differ
                    squared = differ + bf16(soften_sq) if squared is None else squared + differ
                kern[p : p + 32, k * LEAF : (k + 1) * LEAF] = lax.rsqrt(squared)

    def product(t, kern):
        values = jnp.concatenate([vals[u] for u in sources(t)], 1)
        out_ref[t - leaves[0]] = nt(values, kern[...]) * inverse_four_pi

    first, last = leaves
    fill(first, kern0)

    def body(i, _):
        t = first + 2 * i
        fill(t + 1, kern1)
        product(t, kern0)
        fill(jnp.minimum(t + 2, last - 1), kern0)
        product(t + 1, kern1)
        return 0

    lax.fori_loop(0, (last - first) // 2, body, 0)


def near_call(leaves, scalars, pts, vectors, other, left, right):
    size = leaves[1] - leaves[0]
    return pl.pallas_call(
        lambda *refs: near_kernel(leaves, *refs),
        out_shape=jax.ShapeDtypeStruct((size, R, HALF), f32),
        in_specs=[SMEM] + [VMEM] * 5,
        out_specs=VMEM,
        scratch_shapes=[
            pltpu.VMEM((T + 2, R, LEAF), bf16),
            pltpu.VMEM((T + 2, 3, LEAF), bf16),
            pltpu.VMEM((HALF, 3 * LEAF), bf16),
            pltpu.VMEM((HALF, 3 * LEAF), bf16),
        ],
        cost_estimate=pl.CostEstimate(
            flops=size * 200_000_000, bytes_accessed=2_000_000, transcendentals=0
        ),
        name="near",
    )(scalars, pts, vectors, other, left, right)


def final_kernel(scalar_ref, mine_ref, theirs_ref, tgt_ref, near0_ref, near1_ref, out_ref, rows):
    count, n = scalar_ref[0], scalar_ref[1]
    for ref, first in ((mine_ref, n * RH), (theirs_ref, (1 - n) * RH)):
        for r in range(RH):
            part = ref[r // 2].astype(f32)[:, (r % 2) * A : (r % 2 + 1) * A]
            rows[pl.ds(first + r, T, stride=R), :] = jnp.concatenate([part, part], 1)
    same = (iota((64, 256), 0) >> 4) == (iota((64, 256), 1) >> 6)
    for g in range(T // 4):
        part = rows[64 * g : 64 * g + 64, :]
        lhs = jnp.where(same, jnp.concatenate([part, part], 1), 0.0).astype(bf16)
        far = nn(lhs, tgt_ref[4 * g : 4 * g + 4].reshape(4 * A, HALF)).reshape(4, R, HALF)
        near = near0_ref if g < T // 8 else near1_ref
        first = 4 * g % (T // 2)
        total = far + near[first : first + 4]
        live = (iota((4, R, HALF), 0) + 4 * g) < count
        out_ref[4 * g : 4 * g + 4] = jnp.where(live, total, 0.0).astype(bf16)


def final_call(scalars, mine, theirs, tgt, near0, near1):
    whole = lambda *shape: pl.BlockSpec(shape, lambda i, s: (0,) * len(shape))
    return pl.pallas_call(
        final_kernel,
        out_shape=jax.ShapeDtypeStruct((T, R, HALF), bf16),
        grid_spec=pltpu.PrefetchScalarGridSpec(
            num_scalar_prefetch=1,
            grid=(1,),
            in_specs=[
                whole(RH // 2, T, 2 * A),
                whole(RH // 2, T, 2 * A),
                pl.BlockSpec((T, A, HALF), lambda i, s: (0, 0, s[1])),
                whole(T // 2, R, HALF),
                whole(T // 2, R, HALF),
            ],
            out_specs=whole(T, R, HALF),
            scratch_shapes=[pltpu.VMEM((T * R, 128), f32)],
        ),
        name="final",
    )(scalars, mine, theirs, tgt, near0, near1)


def shifted(array, axis, by):
    devices = lax.axis_size(axis)
    return lax.ppermute(array, axis, [(i, (i + by) % devices) for i in range(devices)])


def to_all(array, axis):
    copies = jnp.broadcast_to(array[None], (lax.axis_size(axis), *array.shape))
    return lax.all_to_all(copies, axis, split_axis=0, concat_axis=0, tiled=True)


def local(points, vectors, counts, src_basis, tgt_basis, adm_src, couplings):
    n = lax.axis_index("n").astype(i32)
    count = counts[0]
    scalars = jnp.stack([count, n])

    keep, send = coeff_call(n[None], vectors, src_basis)
    came = shifted(send, "n", 1)
    other = shifted(vectors, "n", 1)
    sel, req = index_call(counts, adm_src.T)
    asked = lax.all_to_all(req, PEERS, split_axis=0, concat_axis=0, tiled=True)

    coeffs = (keep + came).astype(bf16)
    table = to_all(coeffs, "z").reshape(COLUMN, RH * A)

    def edge(slot):
        halves = [lax.dynamic_index_in_dim(v, slot, 0, keepdims=False) for v in (vectors, other)]
        row = jnp.where(n == 0, jnp.concatenate(halves, 1), jnp.concatenate(halves[::-1], 1))
        pts = lax.dynamic_index_in_dim(points, slot, 0, keepdims=False)
        return jnp.concatenate([row, pts, jnp.zeros((5, LEAF), bf16)], 0)

    left = shifted(edge(count - 1), WIDE, 1)
    right = shifted(edge(0), WIDE, -1)
    near_args = (scalars, points, vectors, other, left, right)
    near0 = near_call((0, T // 2), *near_args)

    def some(table):
        got = lax.all_to_all(pack_call(asked, table), PEERS, split_axis=0, concat_axis=0, tiled=True)
        return select_call(sel, got, couplings), near_call((T // 2, T), *near_args)

    def every(table):
        whole = to_all(table, PEERS).reshape(N_PEER * COLUMN, RH * A)
        leaf = adm_src.T.reshape(ENTRIES)
        place = ((leaf >> 11) * 8 + ((leaf >> 5) & 7)) * COLUMN + ((leaf >> 8) & 7) * T + (leaf & (T - 1))
        hot = (place[:, None] == jnp.arange(N_PEER * COLUMN, dtype=i32)[None, :]).astype(bf16)
        picked = jnp.dot(hot, whole, preferred_element_type=f32)
        return couple_call(picked, couplings), near_call((T // 2, T), *near_args)

    mine, near1 = lax.cond(jnp.min(asked[:, 0, 0]) >= 0, some, every, table)
    theirs = shifted(mine, "n", 1)
    return final_call(scalars, mine, theirs, tgt_basis, near0, near1)


def solution(mesh):
    split = Mesh(
        mesh.devices.reshape(2, 8, 4, 2, mesh.shape["narrow"]), ("y", "z", "x", "c", "n")
    )
    in_specs = (
        P(WIDE, None, None),
        P(WIDE, None, "n"),
        P(WIDE),
        P(WIDE, None, "n"),
        P(WIDE, None, None),
        P(WIDE, None),
        P(WIDE, None, None),
    )
    out_specs = P(WIDE, None, "n")
    return jax.shard_map(local, mesh=split, in_specs=in_specs, out_specs=out_specs, check_vma=False)
```

time: 142 us -> 83.2 us (0.59)
  the two profiles are of different devices: /device:TPU:6 before, /device:TPU:1 now
where the time goes in v1:
time: 83.2 us; the launch traced here: 82.4 us
  Pallas kernels  30.9 us (37%)
  starting transfers between devices  29.6 us (36%)
  waiting for transfers between devices  11.7 us (14%)
  local copies, waits for them, and re-layouts  7.18 us (9%)
  other arithmetic  1.66 us (2%)
  between operations  1.33 us (2%)
    pallas_call x2, Pallas kernels, near_call(): pl.pallas_call(lambda *refs: near_kernel(leaves, *refs), out_shape=jax.Sh...  19.4 us
    all_to_all x1, starting transfers between devices, to_all(): return lax.all_to_all(copies, axis, split_axis=0, concat_axis=0, tiled=True)  8.18 us
    all_to_all x1, starting transfers between devices, some(): lax.all_to_all(pack_call(asked, table), PEERS, split_axis=0, concat_axis=...  7.66 us
    ppermute x5, starting transfers between devices, shifted(): lax.ppermute(array, axis, [(i, (i + by) % devices) for i in range(devices)])  6.96 us
    all_to_all x1, starting transfers between devices, local(): asked = lax.all_to_all(req, PEERS, split_axis=0, concat_axis=0, tiled=True)  6.82 us
    ppermute x5, waiting for transfers between devices, shifted(): lax.ppermute(array, axis, [(i, (i + by) % devices) for i in range(devices)])  6.77 us
    all_to_all x1, waiting for transfers between devices, to_all(): return lax.all_to_all(copies, axis, split_axis=0, concat_axis=0, tiled=True)  3.59 us
    pallas_call x1, Pallas kernels, final_call(): pl.pallas_call(final_kernel, out_shape=jax.ShapeDtypeStruct((T, R, HALF),...  3.05 us
  transfers between devices with their start and end apart: 8, of which 4 were waited for; matrix products, arithmetic and copies ran while one was open for 9% of the time, Pallas kernels for 27%

profile of v1, /device:TPU:1, one launch (start us, length us, event | category | flops | bytes accessed | tf_op | source)
XLA Modules:
  0.0 82.4 jit_solution(1897307191441144692)
XLA Ops:
  0.7 2.1 %requests.1 = (s32[256,128]{1,0:T(8,128)S(1)}, bf16[16,48,128]{2,1,0:T(8,128)(2,1)}) custom-call(s32[1]{0:T(128)S(6)} %copy.22.count_ref, s32[8,32]{1,0:T(8,128)} %bitcast.24), custom_call_target="tpu_custom_call" | custom-call | tf_op jit(solution)/shard_map/requests/pallas_call | solution.py:73
  2.8 6.8 %all-to-all-start.2 = ((bf16[16,48,128]{2,1,0:T(8,128)(2,1)}), bf16[16,48,128]{2,1,0:T(8,128)(2,1)S(1)}, u32[]{:S(2)}, u32[]{:S(2)}) async-start(bf16[16,48,128]{2,1,0:T(8,128)(2,1)} %get-tuple-element.69), calls=%async_computation.2 | async-start | bytes 393216 | tf_op jit(solution)/shard_map/all_to_all | solution.py:317
  9.6 2.6 %collective-permute-start.1 = (bf16[32,16,256]{2,1,0:T(8,128)(2,1)}, bf16[32,16,256]{2,1,0:T(8,128)(2,1)}, u32[]{:S(2)}, u32[]{:S(2)}) collective-permute-start(bf16[32,16,256]{2,1,0:T(8,128)(2,1)} %refs_2_.1), channel_id=1, source_target_pairs={{0,1},{1,0},{2,3},{3,2},{4,5},{5,4},{6,7},{7,6},{8,9},{9,8},{10,11... | collective-permute-start | bytes 786440 | tf_op jit(solution)/shard_map/ppermute | solution.py:300
  12.2 2.6 %coeffs.1 = (f32[32,512]{1,0:T(8,128)}, f32[32,512]{1,0:T(8,128)}) custom-call(s32[1]{0:T(128)} %bitcast.4.n_ref, bf16[32,16,256]{2,1,0:T(8,128)(2,1)} %refs_2_.1, bf16[32,64,256]{2,1,0:T(8,128)(2,1)} %basis_ref.1), custom_call_target="tpu_custom_call" | custom-call | tf_op jit(solution)/shard_map/coeffs/pallas_call | solution.py:100
  14.8 0.3 collective-permute-start
  15.1 1.0 %copy.12.refs_1_ = bf16[32,3,512]{2,1,0:T(4,128)(2,1)S(1)} copy(bf16[32,3,512]{2,0,1:T(8,128)(2,1)} %param.9) | data formatting | bytes 196608 | tf_op args[0]
  16.1 0.8 constant_dynamic-slice_fusion
  16.9 0.7 slice_bitcast_fusion.1
  17.7 0.1 pad_add_fusion.refs_0_.scalar_ref
  17.8 0.1 pad.9.clone
  17.8 4.5 %collective-permute-done = f32[32,512]{1,0:T(8,128)S(1)} collective-permute-done((f32[32,512]{1,0:T(8,128)}, f32[32,512]{1,0:T(8,128)S(1)}, u32[]{:S(2)}, u32[]{:S(2)}) %collective-permute-start) | collective-permute-done | bytes 65568 | tf_op jit(solution)/shard_map/ppermute | solution.py:300
  22.3 0.9 %add_convert_fusion = bf16[32,512]{1,0:T(8,128)(2,1)S(1)} fusion(f32[32,512]{1,0:T(8,128)} %get-tuple-element.70, f32[32,512]{1,0:T(8,128)S(1)} %collective-permute-done), kind=kLoop, calls=%fused_computation.4 | loop fusion | flops 32768 | bytes 163840 | tf_op jit(solution)/shard_map/convert_element_type | solution.py:319
  23.2 0.7 broadcast_in_dim.6
  23.9 8.2 %all-to-all-start.3 = ((bf16[8,32,512]{2,1,0:T(8,128)(2,1)}), bf16[8,32,512]{2,1,0:T(8,128)(2,1)S(1)}, u32[]{:S(2)}, u32[]{:S(2)}) async-start(bf16[8,32,512]{2,1,0:T(8,128)(2,1)} %broadcast_in_dim.6), calls=%async_computation.3 | async-start | bytes 524288 | tf_op jit(solution)/shard_map/all_to_all | solution.py:305
  32.1 0.7 slice_bitcast_fusion
  32.8 0.1 maximum_maximum_fusion.1
  32.9 2.4 %collective-permute-start.2 = (bf16[24,512]{1,0:T(8,128)(2,1)S(1)}, bf16[24,512]{1,0:T(8,128)(2,1)S(1)}, u32[]{:S(2)}, u32[]{:S(2)}) collective-permute-start(bf16[24,512]{1,0:T(8,128)(2,1)S(1)} %get-tuple-element.118), channel_id=1, source_target_pairs={{0,2},{2,4},{4,6},{6,8},{8,10},{10,12},{12,14},{14,16},{16,18},{18... | collective-permute-start | bytes 73736 | tf_op jit(solution)/shard_map/ppermute | solution.py:300
  35.3 0.6 slice_reduce_fusion
  36.6 2.3 %collective-permute-done.3.refs_5_ = bf16[24,512]{1,0:T(8,128)(2,1)S(1)} collective-permute-done((bf16[24,512]{1,0:T(8,128)(2,1)S(1)}, bf16[24,512]{1,0:T(8,128)(2,1)S(1)}, u32[]{:S(2)}, u32[]{:S(2)}) %collective-permute-start.3) | collective-permute-done | bytes 24608 | tf_op jit(solution)/shard_map/ppermute | solution.py:300
  38.8 3.6 %all-to-all-done.3 = bf16[8,32,512]{2,1,0:T(8,128)(2,1)S(1)} async-done(((bf16[8,32,512]{2,1,0:T(8,128)(2,1)}), bf16[8,32,512]{2,1,0:T(8,128)(2,1)S(1)}, u32[]{:S(2)}, u32[]{:S(2)}) %all-to-all-start.3) | async-done | bytes 262176 | tf_op jit(solution)/shard_map/all_to_all | solution.py:305
  42.4 25.0 %conditional.1 = (bf16[4,32,128]{2,1,0:T(8,128)(2,1)S(1)}, f32[16,16,256]{2,1,0:T(8,128)}) conditional(s32[]{:T(128)} %convert_element_type.7, (s32[32,8]{0,1:T(8,128)}, bf16[8,32,512]{2,1,0:T(8,128)(2,1)S(1)}, bf16[32,64,512]{2,1,0:T(8,128)(2,1)}, s32[2]{0:T(128)S(1)}, bf16[32,3,512]{2,0,1:T(8,128)(2,1)}, /*index=5*/bf16[32,16,256]{2,1,0:T(8,128)(2,1)}, ...), branch_computations={%region_1.2_spmd, %region_2.3_spmd} | conditional | flops 4274793472 | bytes 33794336 | solution.py:345
  42.4 1.3 %pack.1 = bf16[16,48,512]{2,1,0:T(8,128)(2,1)} custom-call(bf16[16,48,128]{2,1,0:T(8,128)(2,1)S(1)} %get-tuple-element.54.req_ref, bf16[256,512]{1,0:T(8,128)(2,1)S(1)} %bitcast.23), custom_call_target="tpu_custom_call" | custom-call | tf_op jit(solution)/shard_map/cond/branch_1_fun/pack/pallas_call | solution.py:125
  43.7 7.7 %all-to-all-start = ((bf16[16,48,512]{2,1,0:T(8,128)(2,1)}), bf16[16,48,512]{2,1,0:T(8,128)(2,1)S(1)}, u32[]{:S(2)}, u32[]{:S(2)}) async-start(bf16[16,48,512]{2,1,0:T(8,128)(2,1)} %pack.1), calls=%async_computation | async-start | bytes 1572864 | tf_op jit(solution)/shard_map/cond/branch_1_fun/all_to_all | solution.py:334
  51.4 1.6 %copy.14.refs_1_ = bf16[32,3,512]{2,1,0:T(4,128)(2,1)} copy(bf16[32,3,512]{2,0,1:T(8,128)(2,1)} %get-tuple-element.108) | data formatting | bytes 196608 | tf_op jit(solution)/shard_map
  53.0 9.8 %near.4 = f32[16,16,256]{2,1,0:T(8,128)} custom-call(s32[2]{0:T(128)S(1)} %get-tuple-element.57.refs_0_, bf16[32,3,512]{2,1,0:T(4,128)(2,1)} %copy.14.refs_1_, bf16[32,16,256]{2,1,0:T(8,128)(2,1)} %get-tuple-element.59.refs_2_, bf16[32,16,256]{2,1,0:T(8,128)(2,1)} %get-tuple-element.60.refs_3_, bf16[24,512]{1,0:T(8,128)(2,1)S(1)} %get-tuple-element.61.refs_4_, ...), custom_call_target="tpu_custom_call" | custom-call | flops 3200000000 | bytes 2000000 | tf_op jit(solution)/shard_map/cond/branch_1_fun/near/pallas_call | solution.py:240
  62.8 1.3 %all-to-all-done.got_ref = bf16[16,48,512]{2,1,0:T(8,128)(2,1)S(1)} async-done(((bf16[16,48,512]{2,1,0:T(8,128)(2,1)}), bf16[16,48,512]{2,1,0:T(8,128)(2,1)S(1)}, u32[]{:S(2)}, u32[]{:S(2)}) %all-to-all-start) | async-done | bytes 786464 | tf_op jit(solution)/shard_map/cond/branch_1_fun/all_to_all | solution.py:334
  64.1 0.9 %copy-done.2 = bf16[16,48,512]{2,1,0:T(8,128)(2,1)} copy-done((bf16[16,48,512]{2,1,0:T(8,128)(2,1)}, bf16[16,48,512]{2,1,0:T(8,128)(2,1)S(1)}, u32[]{:S(2)}) %copy-start.2) | copy-done | bytes 786456 | tf_op jit(solution)/shard_map/cond
  65.0 2.4 %select.1 = bf16[4,32,128]{2,1,0:T(8,128)(2,1)S(1)} custom-call(s32[256,128]{1,0:T(8,128)S(1)} %get-tuple-element.53.sel_ref, bf16[16,48,512]{2,1,0:T(8,128)(2,1)} %copy-done.2, bf16[32,64,512]{2,1,0:T(8,128)(2,1)S(1)} %copy-done.1), custom_call_target="tpu_custom_call" | custom-call | tf_op jit(solution)/shard_map/cond/branch_1_fun/select/pallas_call | solution.py:169
  67.4 1.6 %collective-permute-start.4 = (bf16[4,32,128]{2,1,0:T(8,128)(2,1)S(1)}, bf16[4,32,128]{2,1,0:T(8,128)(2,1)S(1)}, u32[]{:S(2)}, u32[]{:S(2)}) collective-permute-start(bf16[4,32,128]{2,1,0:T(8,128)(2,1)S(1)} %get-tuple-element.73.mine_ref), channel_id=1, source_target_pairs={{0,1},{1,0},{2,3},{3,2},{4,5},{5,4},{6,7},{7,6},{8,9},{9,8},{10,11... | collective-permute-start | bytes 98312 | tf_op jit(solution)/shard_map/ppermute | solution.py:300
  69.1 9.6 %near.5.near0_ref = f32[16,16,256]{2,1,0:T(8,128)} custom-call(s32[2]{0:T(128)S(1)} %pad_add_fusion.refs_0_.scalar_ref, bf16[32,3,512]{2,1,0:T(4,128)(2,1)} %copy-done.5, bf16[32,16,256]{2,1,0:T(8,128)(2,1)} %refs_2_.1, bf16[32,16,256]{2,1,0:T(8,128)(2,1)} %collective-permute-done.1.refs_3_, bf16[24,512]{1,0:T(8,128)(2,1)S(1)} %collective-permute-done.2.refs_4_, ...), custom_call_target="tpu_custom_call" | custom-call | flops 3200000000 | bytes 2000000 | tf_op jit(solution)/shard_map/near/pallas_call | solution.py:240
  78.7 0.6 copy-done.6
  79.3 3.0 %final.1 = bf16[32,16,256]{2,1,0:T(8,128)(2,1)} custom-call(s32[2]{0:T(128)S(1)} %pad_add_fusion.refs_0_.scalar_ref, bf16[4,32,128]{2,1,0:T(8,128)(2,1)S(1)} %get-tuple-element.73.mine_ref, bf16[4,32,128]{2,1,0:T(8,128)(2,1)} %copy-done.6, bf16[32,64,512]{2,1,0:T(8,128)(2,1)} %tgt_ref.1, f32[16,16,256]{2,1,0:T(8,128)} %near.5.near0_ref, ...), custom_call_target="tpu_custom_call" | custom-call | tf_op jit(solution)/shard_map/final/pallas_call | solution.py:278
  (14 shorter events, 0.0 us)
Async XLA Ops:
  2.8 20.4 %all-to-all-start.2 = ((bf16[16,48,128]{2,1,0:T(8,128)(2,1)}), bf16[16,48,128]{2,1,0:T(8,128)(2,1)S(1)}, u32[]{:S(2)}, u32[]{:S(2)}) async-start(bf16[16,48,128]{2,1,0:T(8,128)(2,1)} %get-tuple-element.69), calls=%async_computation.2 | async-start | bytes 393216 | tf_op jit(solution)/shard_map/all_to_all | solution.py:317
  9.6 22.5 %collective-permute-start.1 = (bf16[32,16,256]{2,1,0:T(8,128)(2,1)}, bf16[32,16,256]{2,1,0:T(8,128)(2,1)}, u32[]{:S(2)}, u32[]{:S(2)}) collective-permute-start(bf16[32,16,256]{2,1,0:T(8,128)(2,1)} %refs_2_.1), channel_id=1, source_target_pairs={{0,1},{1,0},{2,3},{3,2},{4,5},{5,4},{6,7},{7,6},{8,9},{9,8},{10,11... | collective-permute-start | bytes 786440 | tf_op jit(solution)/shard_map/ppermute | solution.py:300
  14.8 7.5 %collective-permute-start = (f32[32,512]{1,0:T(8,128)}, f32[32,512]{1,0:T(8,128)S(1)}, u32[]{:S(2)}, u32[]{:S(2)}) collective-permute-start(f32[32,512]{1,0:T(8,128)} %get-tuple-element.71), channel_id=1, source_target_pairs={{0,1},{1,0},{2,3},{3,2},{4,5},{5,4},{6,7},{7,6},{8,9},{9,8},{10,11... | collective-permute-start | bytes 196616 | tf_op jit(solution)/shard_map/ppermute | solution.py:300
  16.1 26.3 %copy-start.5 = (bf16[32,3,512]{2,1,0:T(4,128)(2,1)}, bf16[32,3,512]{2,1,0:T(4,128)(2,1)S(1)}, u32[]{:S(2)}) copy-start(bf16[32,3,512]{2,1,0:T(4,128)(2,1)S(1)} %copy.12.refs_1_) | copy-start | bytes 294916
  23.9 18.5 %all-to-all-start.3 = ((bf16[8,32,512]{2,1,0:T(8,128)(2,1)}), bf16[8,32,512]{2,1,0:T(8,128)(2,1)S(1)}, u32[]{:S(2)}, u32[]{:S(2)}) async-start(bf16[8,32,512]{2,1,0:T(8,128)(2,1)} %broadcast_in_dim.6), calls=%async_computation.3 | async-start | bytes 524288 | tf_op jit(solution)/shard_map/all_to_all | solution.py:305
  32.9 3.7 %collective-permute-start.2 = (bf16[24,512]{1,0:T(8,128)(2,1)S(1)}, bf16[24,512]{1,0:T(8,128)(2,1)S(1)}, u32[]{:S(2)}, u32[]{:S(2)}) collective-permute-start(bf16[24,512]{1,0:T(8,128)(2,1)S(1)} %get-tuple-element.118), channel_id=1, source_target_pairs={{0,2},{2,4},{4,6},{6,8},{8,10},{10,12},{12,14},{14,16},{16,18},{18... | collective-permute-start | bytes 73736 | tf_op jit(solution)/shard_map/ppermute | solution.py:300
  35.3 3.5 %collective-permute-start.3 = (bf16[24,512]{1,0:T(8,128)(2,1)S(1)}, bf16[24,512]{1,0:T(8,128)(2,1)S(1)}, u32[]{:S(2)}, u32[]{:S(2)}) collective-permute-start(bf16[24,512]{1,0:T(8,128)(2,1)S(1)} %get-tuple-element.117), channel_id=1, source_target_pairs={{0,254},{2,0},{4,2},{6,4},{8,6},{10,8},{12,10},{14,12},{16,14},{18... | collective-permute-start | bytes 73736 | tf_op jit(solution)/shard_map/ppermute | solution.py:300
  43.7 20.4 %all-to-all-start = ((bf16[16,48,512]{2,1,0:T(8,128)(2,1)}), bf16[16,48,512]{2,1,0:T(8,128)(2,1)S(1)}, u32[]{:S(2)}, u32[]{:S(2)}) async-start(bf16[16,48,512]{2,1,0:T(8,128)(2,1)} %pack.1), calls=%async_computation | async-start | bytes 1572864 | tf_op jit(solution)/shard_map/cond/branch_1_fun/all_to_all | solution.py:334
  53.0 12.0 %copy-start.1 = (bf16[32,64,512]{2,1,0:T(8,128)(2,1)S(1)}, bf16[32,64,512]{2,1,0:T(8,128)(2,1)}, u32[]{:S(2)}) copy-start(bf16[32,64,512]{2,1,0:T(8,128)(2,1)} %get-tuple-element.56.couple_ref) | copy-start | bytes 6291460 | tf_op jit(solution)/shard_map/cond
  64.1 0.9 %copy-start.2 = (bf16[16,48,512]{2,1,0:T(8,128)(2,1)}, bf16[16,48,512]{2,1,0:T(8,128)(2,1)S(1)}, u32[]{:S(2)}) copy-start(bf16[16,48,512]{2,1,0:T(8,128)(2,1)S(1)} %all-to-all-done.got_ref) | copy-start | bytes 2359300 | tf_op jit(solution)/shard_map/cond
  67.4 11.3 %collective-permute-start.4 = (bf16[4,32,128]{2,1,0:T(8,128)(2,1)S(1)}, bf16[4,32,128]{2,1,0:T(8,128)(2,1)S(1)}, u32[]{:S(2)}, u32[]{:S(2)}) collective-permute-start(bf16[4,32,128]{2,1,0:T(8,128)(2,1)S(1)} %get-tuple-element.73.mine_ref), channel_id=1, source_target_pairs={{0,1},{1,0},{2,3},{3,2},{4,5},{5,4},{6,7},{7,6},{8,9},{9,8},{10,11... | collective-permute-start | bytes 98312 | tf_op jit(solution)/shard_map/ppermute | solution.py:300
  78.7 0.6 copy-start.6

commit v2 on v1

v2 whole, which is shorter than its diff:
```python
import math

import jax
import jax.numpy as jnp
from jax import lax
from jax.experimental import pallas as pl
from jax.experimental.pallas import tpu as pltpu
from jax.sharding import Mesh
from jax.sharding import PartitionSpec as P

WIDE = ("y", "z", "x", "c")
CHIPS = ("y", "z", "x")

inverse_four_pi = 1.0 / (4.0 * math.pi)
soften_sq = 0.0025

T, R, A, J, HALF, LEAF = 32, 16, 64, 8, 256, 512
QUARTER = R // 4
N_CHIP = 64
PAIR = 2 * T
CAP = 24
ENTRIES = PAIR * J
SLOTS = N_CHIP * CAP
ROW = QUARTER * A
bf16, f32, i32 = jnp.bfloat16, jnp.float32, jnp.int32

VMEM = pl.BlockSpec(memory_space=pltpu.VMEM)
SMEM = pl.BlockSpec(memory_space=pltpu.SMEM)


def nt(a, b):
    return lax.dot_general(a, b, (((1,), (1,)), ((), ())), preferred_element_type=f32)


def nn(a, b):
    return lax.dot_general(a, b, (((1,), (0,)), ((), ())), preferred_element_type=f32)


def iota(shape, dim):
    return lax.broadcasted_iota(i32, shape, dim)


def folded(wide):
    two = wide[:, :128] + wide[:, 128:]
    return two[:, :64] + two[:, 64:]


def index_kernel(own_ref, next_ref, sel_ref, req_ref):
    adm = jnp.concatenate([own_ref[...], next_ref[...]], 1).astype(f32)
    adm = jnp.concatenate([adm, jnp.zeros((J, 128 - PAIR), f32)], 1).T
    leaf = jnp.concatenate(
        [jnp.broadcast_to(adm[:PAIR, j : j + 1], (PAIR, 128)) for j in range(J)], 0
    ).astype(i32)
    live = leaf >= 0
    chip = leaf >> 6
    row = (leaf & (PAIR - 1)).astype(f32)
    lanes = iota((ENTRIES, 128), 1)
    member = jnp.where((chip == lanes) & live, 1.0, 0.0)
    below = jnp.where(iota((ENTRIES, ENTRIES), 0) > iota((ENTRIES, ENTRIES), 1), 1.0, 0.0)
    rank = nn(below.astype(bf16), member.astype(bf16))
    place = jnp.sum(member * rank, axis=1, keepdims=True)
    over = jnp.max(place) > CAP - 0.5
    place = jnp.broadcast_to(place, (ENTRIES, 128)).astype(i32)
    sel_ref[...] = jnp.where(live & (place < CAP), chip * CAP + place, -1)
    wanted = jnp.where(place == lanes, row + 1.0, 0.0)
    wanted = nn(member.T.astype(bf16), wanted.astype(bf16))[:N_CHIP]
    req_ref[...] = jnp.where(over, -1.0, wanted).reshape(N_CHIP, 1, 128)


def index_call(own, other):
    return pl.pallas_call(
        index_kernel,
        out_shape=(
            jax.ShapeDtypeStruct((ENTRIES, 128), i32),
            jax.ShapeDtypeStruct((N_CHIP, 1, 128), f32),
        ),
        in_specs=[VMEM, VMEM],
        out_specs=(VMEM, VMEM),
        name="requests",
    )(own, other)


def coeff_kernel(place_ref, vec_ref, basis_ref, keep_ref, c_ref, n_ref, nc_ref, rows):
    n, c = place_ref[0], place_ref[1]
    same = (iota((64, 256), 0) >> 4) == (iota((64, 256), 1) >> 6)
    for g in range(T // 4):
        lhs = vec_ref[4 * g : 4 * g + 4].reshape(64, HALF)
        rhs = basis_ref[4 * g : 4 * g + 4].reshape(4 * A, HALF)
        rows[64 * g : 64 * g + 64, :64] = folded(jnp.where(same, nt(lhs, rhs), 0.0))
    for out, to_n, to_c in (
        (c_ref, n, 1 - c),
        (n_ref, 1 - n, c),
        (nc_ref, 1 - n, 1 - c),
        (keep_ref, n, c),
    ):
        first = to_n * (R // 2) + to_c * QUARTER
        for r in range(0, QUARTER, 2):
            pair = [rows[pl.ds(first + r + k, T, stride=R), :][:, :64] for k in range(2)]
            out[:, r * A : (r + 2) * A] = jnp.concatenate(pair, 1)


def coeff_call(place, vectors, basis):
    shape = jax.ShapeDtypeStruct((T, ROW), f32)
    return pl.pallas_call(
        coeff_kernel,
        out_shape=(shape,) * 4,
        in_specs=[SMEM, VMEM, VMEM],
        out_specs=(VMEM,) * 4,
        scratch_shapes=[pltpu.VMEM((T * R, 128), f32)],
        name="coeffs",
    )(place, vectors, basis)


def pack_kernel(place_ref, req_ref, keep_ref, c_ref, n_ref, nc_ref, out_ref, table):
    c = place_ref[1]
    table[pl.ds(pl.multiple_of(c * T, T), T), :] = keep_ref[...] + n_ref[...]
    table[pl.ds(pl.multiple_of((1 - c) * T, T), T), :] = c_ref[...] + nc_ref[...]
    rows = table[...].astype(bf16)
    want = jnp.concatenate([req_ref[...].reshape(N_CHIP, 128), jnp.zeros((64, 128), f32)], 0).T
    lanes = iota((CAP, PAIR), 1).astype(f32) + 1.0
    for p in range(0, N_CHIP, 8):
        hot = [
            jnp.where(jnp.broadcast_to(want[:CAP, p + k : p + k + 1], (CAP, PAIR)) == lanes, 1.0, 0.0)
            for k in range(8)
        ]
        picked = nn(jnp.concatenate(hot, 0).astype(bf16), rows)
        out_ref[p : p + 8] = picked.astype(bf16).reshape(8, CAP, ROW)


def pack_call(place, req, keep, from_c, from_n, from_nc):
    return pl.pallas_call(
        pack_kernel,
        out_shape=jax.ShapeDtypeStruct((N_CHIP, CAP, ROW), bf16),
        in_specs=[SMEM] + [VMEM] * 5,
        out_specs=VMEM,
        scratch_shapes=[pltpu.VMEM((PAIR, ROW), f32)],
        name="pack",
    )(place, req, keep, from_c, from_n, from_nc)


def couple(picked, couple_refs, out_refs):
    lows = [picked[j * PAIR : (j + 1) * PAIR] for j in range(J)]
    by_rhs = []
    for r in range(QUARTER):
        cols = [low[:, r * A : (r + 1) * A] for low in lows]
        by_rhs.append(jnp.concatenate(cols, 1).astype(bf16))
    row_t = iota((16 * QUARTER, 256), 0) & 15
    col_t = iota((16 * QUARTER, 256), 1) >> 6
    for h in range(4):
        ref, out = couple_refs[h // 2], out_refs[h // 2]
        lhs = jnp.concatenate([s[16 * h : 16 * h + 16] for s in by_rhs], 0)
        low = 16 * (h % 2)
        total = jnp.zeros((16 * QUARTER, A), f32)
        for g in range(4):
            rhs = ref[low + 4 * g : low + 4 * g + 4].reshape(4 * A, J * A)
            total = total + folded(jnp.where(row_t == col_t + 4 * g, nt(lhs, rhs), 0.0))
        total = total.reshape(QUARTER, 16, A)
        for r in range(0, QUARTER, 2):
            pair = jnp.concatenate([total[r], total[r + 1]], 1)
            out[r // 2, low : low + 16, :] = pair.astype(bf16)


def select_kernel(sel_ref, got_ref, own_ref, next_ref, own_out, next_out):
    sel = sel_ref[...]
    lanes = iota((ENTRIES, 128), 1)
    hot = jnp.concatenate(
        [jnp.where(sel == lanes + 128 * k, 1.0, 0.0).astype(bf16) for k in range(SLOTS // 128)], 1
    )
    picked = nn(hot, got_ref[...].reshape(SLOTS, ROW))
    couple(picked, (own_ref, next_ref), (own_out, next_out))


def couple_kernel(picked_ref, own_ref, next_ref, own_out, next_out):
    couple(picked_ref[...], (own_ref, next_ref), (own_out, next_out))


TC_SHAPE = jax.ShapeDtypeStruct((QUARTER // 2, T, 2 * A), bf16)


def target_call(kernel, *args):
    return pl.pallas_call(
        kernel,
        out_shape=(TC_SHAPE, TC_SHAPE),
        in_specs=[VMEM] * len(args),
        out_specs=(VMEM, VMEM),
        name="targets",
    )(*args)


def near_kernel(leaves, scalar_ref, pts_ref, vec_ref, other_ref, left_ref, right_ref, out_ref, *bufs):
    vals, pts, *kerns = bufs
    count, n = scalar_ref[0], scalar_ref[1]
    own = pl.multiple_of(n * HALF, HALF)
    other = pl.multiple_of((1 - n) * HALF, HALF)
    vals[:T, :, pl.ds(own, HALF)] = vec_ref[...]
    vals[:T, :, pl.ds(other, HALF)] = other_ref[...]
    pts[:T] = pts_ref[...]
    for k, edge in enumerate((left_ref, right_ref)):
        vals[T + k] = edge[:R]
        pts[T + k] = edge[R : R + 3]

    def sources(t):
        return jnp.where(t == 0, T, t - 1), t, jnp.where(t == count - 1, T + 1, jnp.minimum(t + 1, T - 1))

    def fill(t, kern):
        x = pts[t, :, pl.ds(own, HALF)].astype(f32)
        x = jnp.concatenate([x, jnp.zeros((5, HALF), f32)], 0).T.astype(bf16)
        for k, u in enumerate(sources(t)):
            y = pts[u]
            for p in range(0, HALF, 32):
                squared = None
                for i in range(3):
                    differ = x[p : p + 32, i : i + 1] - y[i : i + 1, :]
                    differ = differ * differ
                    squared = differ + bf16(soften_sq) if squared is None else squared + differ
                kern[p : p + 32, k * LEAF : (k + 1) * LEAF] = lax.rsqrt(squared)

    def product(t, kern):
        values = jnp.concatenate([vals[u] for u in sources(t)], 1)
        out_ref[t - leaves[0]] = nt(values, kern[...]) * inverse_four_pi

    first, last = leaves
    fill(first, kerns[0])

    def body(i, _):
        for s in range(4):
            t = first + 4 * i + s
            fill(jnp.minimum(t + 1, last - 1), kerns[(s + 1) % 4])
            product(t, kerns[s])
        return 0

    lax.fori_loop(0, (last - first) // 4, body, 0)


def near_call(leaves, scalars, pts, vectors, other, left, right):
    size = leaves[1] - leaves[0]
    return pl.pallas_call(
        lambda *refs: near_kernel(leaves, *refs),
        out_shape=jax.ShapeDtypeStruct((size, R, HALF), f32),
        in_specs=[SMEM] + [VMEM] * 5,
        out_specs=VMEM,
        scratch_shapes=[
            pltpu.VMEM((T + 2, R, LEAF), bf16),
            pltpu.VMEM((T + 2, 3, LEAF), bf16),
        ]
        + [pltpu.VMEM((HALF, 3 * LEAF), bf16)] * 4,
        cost_estimate=pl.CostEstimate(
            flops=size * 200_000_000, bytes_accessed=2_000_000, transcendentals=0
        ),
        name="near",
    )(scalars, pts, vectors, other, left, right)


def final_kernel(scalar_ref, own_ref, c_ref, n_ref, nc_ref, tgt_ref, near_ref, out_ref, rows):
    count, n, c = scalar_ref[0], scalar_ref[1], scalar_ref[2]
    for ref, from_n, from_c in (
        (own_ref, n, c),
        (c_ref, n, 1 - c),
        (n_ref, 1 - n, c),
        (nc_ref, 1 - n, 1 - c),
    ):
        first = from_n * (R // 2) + from_c * QUARTER
        for r in range(QUARTER):
            part = ref[r // 2].astype(f32)[:, (r % 2) * A : (r % 2 + 1) * A]
            rows[pl.ds(first + r, T, stride=R), :] = jnp.concatenate([part, part], 1)
    same = (iota((64, 256), 0) >> 4) == (iota((64, 256), 1) >> 6)
    for g in range(T // 4):
        part = rows[64 * g : 64 * g + 64, :]
        lhs = jnp.where(same, jnp.concatenate([part, part], 1), 0.0).astype(bf16)
        far = nn(lhs, tgt_ref[4 * g : 4 * g + 4].reshape(4 * A, HALF)).reshape(4, R, HALF)
        total = far + near_ref[4 * g : 4 * g + 4]
        live = (iota((4, R, HALF), 0) + 4 * g) < count
        out_ref[4 * g : 4 * g + 4] = jnp.where(live, total, 0.0).astype(bf16)


def final_call(scalars, parts, tgt, near):
    whole = lambda *shape: pl.BlockSpec(shape, lambda i, s: (0,) * len(shape))
    return pl.pallas_call(
        final_kernel,
        out_shape=jax.ShapeDtypeStruct((T, R, HALF), bf16),
        grid_spec=pltpu.PrefetchScalarGridSpec(
            num_scalar_prefetch=1,
            grid=(1,),
            in_specs=[whole(QUARTER // 2, T, 2 * A)] * 4
            + [pl.BlockSpec((T, A, HALF), lambda i, s: (0, 0, s[1])), whole(T, R, HALF)],
            out_specs=whole(T, R, HALF),
            scratch_shapes=[pltpu.VMEM((T * R, 128), f32)],
        ),
        name="final",
    )(scalars, *parts, tgt, near)


def shifted(array, axis, by):
    devices = lax.axis_size(axis)
    return lax.ppermute(array, axis, [(i, (i + by) % devices) for i in range(devices)])


def crossed(array):
    return lax.ppermute(array, ("c", "n"), [(i, 3 - i) for i in range(4)])


def after(first, *arrays):
    return lax.optimization_barrier((first, *arrays))[1:]


def local(points, vectors, counts, src_basis, tgt_basis, adm_src, couplings):
    n = lax.axis_index("n").astype(i32)
    c = lax.axis_index("c").astype(i32)
    count = counts[0]
    scalars = jnp.stack([count, n, c])
    place = jnp.stack([n, c])

    live = jnp.arange(T, dtype=i32)[None, :] < count
    own_adm = jnp.where(live, adm_src.T, -1)
    next_adm = shifted(own_adm, "c", 1)

    keep, to_c, to_n, to_nc = coeff_call(place, vectors, src_basis)
    from_n = shifted(to_n, "n", 1)
    from_nc = crossed(to_nc)
    from_c = shifted(to_c, "c", 1)
    (next_adm,) = after(keep, next_adm)
    sel, req = index_call(own_adm, next_adm)
    asked = lax.all_to_all(req, CHIPS, split_axis=0, concat_axis=0, tiled=True)
    next_couplings = shifted(couplings, "c", 1)
    (sent_vectors,) = after(keep, vectors)
    other = shifted(sent_vectors, "n", 1)

    def edge(slot):
        halves = [lax.dynamic_index_in_dim(v, slot, 0, keepdims=False) for v in (vectors, other)]
        row = jnp.where(n == 0, jnp.concatenate(halves, 1), jnp.concatenate(halves[::-1], 1))
        pts = lax.dynamic_index_in_dim(points, slot, 0, keepdims=False)
        return jnp.concatenate([row, pts, jnp.zeros((5, LEAF), bf16)], 0)

    left = shifted(edge(count - 1), WIDE, 1)
    right = shifted(edge(0), WIDE, -1)
    near_args = (scalars, points, vectors, other, left, right)
    coefs = (keep, from_c, from_n, from_nc)

    def some(coefs):
        got = lax.all_to_all(
            pack_call(place, asked, *coefs), CHIPS, split_axis=0, concat_axis=0, tiled=True
        )
        return target_call(select_kernel, sel, got, couplings, next_couplings), near_call((0, T), *near_args)

    def every(coefs):
        own, other_core = coefs[0] + coefs[2], coefs[1] + coefs[3]
        pair = (own, other_core), (other_core, own)
        table = jnp.where(c == 0, jnp.concatenate(pair[0]), jnp.concatenate(pair[1])).astype(bf16)
        copies = jnp.broadcast_to(table[None], (N_CHIP, PAIR, ROW))
        whole = lax.all_to_all(copies, CHIPS, split_axis=0, concat_axis=0, tiled=True)
        leaf = jnp.concatenate([own_adm, next_adm], 1).reshape(ENTRIES)
        hot = (leaf[:, None] == jnp.arange(N_CHIP * PAIR, dtype=i32)[None, :]).astype(bf16)
        picked = jnp.dot(hot, whole.reshape(N_CHIP * PAIR, ROW), preferred_element_type=f32)
        return target_call(couple_kernel, picked, couplings, next_couplings), near_call((0, T), *near_args)

    (mine, nexts), near = lax.cond(jnp.min(asked[:, 0, 0]) >= 0, some, every, coefs)
    parts = mine, shifted(nexts, "c", 1), shifted(mine, "n", 1), crossed(nexts)
    return final_call(scalars, parts, tgt_basis, near)


def solution(mesh):
    split = Mesh(
        mesh.devices.reshape(2, 8, 4, 2, mesh.shape["narrow"]), ("y", "z", "x", "c", "n")
    )
    in_specs = (
        P(WIDE, None, None),
        P(WIDE, None, "n"),
        P(WIDE),
        P(WIDE, None, "n"),
        P(WIDE, None, None),
        P(WIDE, None),
        P(WIDE, None, None),
    )
    out_specs = P(WIDE, None, "n")
    return jax.shard_map(local, mesh=split, in_specs=in_specs, out_specs=out_specs, check_vma=False)
```

time: 83.2 us -> 87.2 us (1.048)
  waiting for transfers between devices: 11.7 us -> 18.1 us
  local copies, waits for them, and re-layouts: 7.18 us -> 3.9 us
  starting transfers between devices: 29.6 us -> 32.5 us
  Pallas kernels: 30.9 us -> 28.3 us
    all_to_all x3 -> x2, waiting for transfers between devices: 4.92 us -> 15.4 us  [the longest x1 8.08 us: some(): lax.all_to_all(pack_call(place, asked, *coefs), CHIPS, split_axis=0, conc...]
    ppermute x5 -> x9, waiting for transfers between devices: 6.77 us -> 1.39 us  [shifted(): lax.ppermute(array, axis, [(i, (i + by) % devices) for i in range(devices)])]
    pallas_call x2 -> x1, Pallas kernels: 19.4 us -> 14.4 us  [near_call(): pl.pallas_call(lambda *refs: near_kernel(leaves, *refs), out_shape=jax.Sh...]
    ppermute x5 -> x9, starting transfers between devices: 6.96 us -> 11 us  [shifted(): lax.ppermute(array, axis, [(i, (i + by) % devices) for i in range(devices)])]
    all_to_all x3 -> x2, starting transfers between devices: 22.7 us -> 19 us  [the longest x1 11.8 us: local(): asked = lax.all_to_all(req, CHIPS, split_axis=0, concat_axis=0, tiled=True)]
    pallas_call x3, Pallas kernels: 6.28 us -> 9.28 us  [the longest x1 4.68 us: target_call(): pl.pallas_call(kernel, out_shape=(TC_SHAPE, TC_SHAPE), in_specs=[VMEM] *...]
    ppermute x0 -> x2, starting transfers between devices: none -> 2.47 us  [crossed(): return lax.ppermute(array, ('c', 'n'), [(i, 3 - i) for i in range(4)])]
    ppermute x0 -> x2, waiting for transfers between devices: none -> 1.3 us  [crossed(): return lax.ppermute(array, ('c', 'n'), [(i, 3 - i) for i in range(4)])]
  transfers between devices with their start and end apart: 8 -> 13, of which waited for: 4 -> 4; matrix products, arithmetic and copies ran while one was open for 9% -> 5% of each run, Pallas kernels for 27% -> 21%
where the time goes in v2:
time: 87.2 us; the launch traced here: 86.7 us
  starting transfers between devices  32.5 us (37%)
  Pallas kernels  28.3 us (32%)
  waiting for transfers between devices  18.1 us (21%)
  local copies, waits for them, and re-layouts  3.9 us (4%)
  other arithmetic  2.26 us (3%)
  between operations  1.44 us (2%)
    pallas_call x1, Pallas kernels, near_call(): pl.pallas_call(lambda *refs: near_kernel(leaves, *refs), out_shape=jax.Sh...  14.4 us
    all_to_all x1, starting transfers between devices, local(): asked = lax.all_to_all(req, CHIPS, split_axis=0, concat_axis=0, tiled=True)  11.8 us
    ppermute x9, starting transfers between devices, shifted(): lax.ppermute(array, axis, [(i, (i + by) % devices) for i in range(devices)])  11 us
    all_to_all x1, waiting for transfers between devices, some(): lax.all_to_all(pack_call(place, asked, *coefs), CHIPS, split_axis=0, conc...  8.08 us
    all_to_all x1, waiting for transfers between devices, local(): asked = lax.all_to_all(req, CHIPS, split_axis=0, concat_axis=0, tiled=True)  7.31 us
    all_to_all x1, starting transfers between devices, some(): lax.all_to_all(pack_call(place, asked, *coefs), CHIPS, split_axis=0, conc...  7.25 us
    pallas_call x1, Pallas kernels, target_call(): pl.pallas_call(kernel, out_shape=(TC_SHAPE, TC_SHAPE), in_specs=[VMEM] *...  4.68 us
    pallas_call x1, Pallas kernels, final_call(): pl.pallas_call(final_kernel, out_shape=jax.ShapeDtypeStruct((T, R, HALF),...  3.09 us
  transfers between devices with their start and end apart: 13, of which 4 were waited for; matrix products, arithmetic and copies ran while one was open for 5% of the time, Pallas kernels for 21%

profile of v2, /device:TPU:1, one launch (start us, length us, event | category | flops | bytes accessed | tf_op | source)
XLA Modules:
  0.0 86.7 jit_solution(5494241915799391201)
XLA Ops:
  0.0 3.2 %collective-permute-start.4 = (bf16[32,64,512]{2,1,0:T(8,128)(2,1)}, bf16[32,64,512]{2,1,0:T(8,128)(2,1)S(1)}, u32[]{:S(2)}, u32[]{:S(2)}) collective-permute-start(bf16[32,64,512]{2,1,0:T(8,128)(2,1)} %param.15), channel_id=1, source_target_pairs={{0,2},{2,0},{1,3},{3,1},{4,6},{6,4},{5,7},{7,5},{8,10},{10,8},{9,1... | collective-permute-start | bytes 6291464 | tf_op jit(solution)/shard_map/ppermute | solution.py:295
  3.3 2.5 %coeffs.1 = (f32[32,256]{1,0:T(8,128)S(1)}, f32[32,256]{1,0:T(8,128)}, f32[32,256]{1,0:T(8,128)}, f32[32,256]{1,0:T(8,128)}) custom-call(s32[2]{0:T(128)S(1)} %pad_add_fusion.2.place_ref, bf16[32,16,256]{2,1,0:T(8,128)(2,1)} %vec_ref.1, bf16[32,64,256]{2,1,0:T(8,128)(2,1)} %basis_ref.1), custom_call_target="tpu_custom_call" | custom-call | tf_op jit(solution)/shard_map/coeffs/pallas_call | solution.py:104
  5.8 1.2 %collective-permute-start.5 = (bf16[32,16,256]{2,1,0:T(8,128)(2,1)}, bf16[32,16,256]{2,1,0:T(8,128)(2,1)S(1)}, u32[]{:S(2)}, u32[]{:S(2)}) collective-permute-start(bf16[32,16,256]{2,1,0:T(8,128)(2,1)} %vec_ref.1), channel_id=1, source_target_pairs={{0,1},{1,0},{2,3},{3,2},{4,5},{5,4},{6,7},{7,6},{8,9},{9,8},{10,11... | collective-permute-start | bytes 786440 | tf_op jit(solution)/shard_map/ppermute | solution.py:295
  7.7 0.7 select_bitcast_fusion.own_ref
  8.4 0.3 collective-permute-start
  8.7 1.8 %collective-permute-start.1 = (f32[32,256]{1,0:T(8,128)}, f32[32,256]{1,0:T(8,128)S(1)}, u32[]{:S(2)}, u32[]{:S(2)}) collective-permute-start(f32[32,256]{1,0:T(8,128)} %get-tuple-element.113), channel_id=1, source_target_pairs={{0,1},{1,0},{2,3},{3,2},{4,5},{5,4},{6,7},{7,6},{8,9},{9,8},{10,11... | collective-permute-start | bytes 98312 | tf_op jit(solution)/shard_map/ppermute | solution.py:295
  10.4 0.5 collective-permute-start.2
  10.9 0.7 slice_bitcast_fusion.1
  11.7 0.8 fusion.3
  12.5 0.7 pad_add_fusion.1.scalar_ref
  13.3 1.1 %collective-permute-start.3 = (f32[32,256]{1,0:T(8,128)}, f32[32,256]{1,0:T(8,128)S(1)}, u32[]{:S(2)}, u32[]{:S(2)}) collective-permute-start(f32[32,256]{1,0:T(8,128)} %get-tuple-element.115), channel_id=1, source_target_pairs={{0,3},{1,2},{2,1},{3,0},{4,7},{5,6},{6,5},{7,4},{8,11},{9,10},{10,... | collective-permute-start | bytes 98312 | tf_op jit(solution)/shard_map/ppermute | solution.py:299
  14.3 1.5 %requests.1 = (s32[512,128]{1,0:T(8,128)}, f32[64,1,128]{2,1,0:T(1,128)}) custom-call(s32[8,32]{1,0:T(8,128)S(1)} %select_bitcast_fusion.own_ref, s32[8,32]{1,0:T(8,128)S(1)} %collective-permute-done.next_ref), custom_call_target="tpu_custom_call" | custom-call | tf_op jit(solution)/shard_map/requests/pallas_call | solution.py:71
  15.8 11.8 %all-to-all-start.2 = ((f32[64,1,128]{2,1,0:T(1,128)}), f32[64,1,128]{2,1,0:T(1,128)S(1)}, u32[]{:S(2)}, u32[]{:S(2)}) async-start(f32[64,1,128]{2,1,0:T(1,128)} %get-tuple-element.112), calls=%async_computation.2 | async-start | bytes 65536 | tf_op jit(solution)/shard_map/all_to_all | solution.py:323
  27.6 0.1 maximum_maximum_fusion.1
  27.7 2.0 %collective-permute-start.6 = (bf16[24,512]{1,0:T(8,128)(2,1)S(1)}, bf16[24,512]{1,0:T(8,128)(2,1)S(1)}, u32[]{:S(2)}, u32[]{:S(2)}) collective-permute-start(bf16[24,512]{1,0:T(8,128)(2,1)S(1)} %get-tuple-element.188), channel_id=1, source_target_pairs={{0,2},{2,4},{4,6},{6,8},{8,10},{10,12},{12,14},{14,16},{16,18},{18... | collective-permute-start | bytes 73736 | tf_op jit(solution)/shard_map/ppermute | solution.py:295
  29.7 7.3 %all-to-all-done.2 = f32[64,1,128]{2,1,0:T(1,128)S(1)} async-done(((f32[64,1,128]{2,1,0:T(1,128)}), f32[64,1,128]{2,1,0:T(1,128)S(1)}, u32[]{:S(2)}, u32[]{:S(2)}) %all-to-all-start.2) | async-done | bytes 32800 | tf_op jit(solution)/shard_map/all_to_all | solution.py:323
  37.0 0.7 slice_reduce_fusion
  38.5 38.4 %conditional.1 = (bf16[2,32,128]{2,1,0:T(8,128)(2,1)S(1)}, bf16[2,32,128]{2,1,0:T(8,128)(2,1)S(1)}, f32[32,16,256]{2,1,0:T(8,128)S(1)}) conditional(s32[]{:T(128)} %convert_element_type.11, (s32[8,32]{1,0:T(8,128)S(1)}, s32[8,32]{1,0:T(8,128)S(1)}, s32[]{:T(128)}, f32[32,256]{1,0:T(8,128)S(1)}, f32[32,256]{1,0:T(8,128)S(1)}, ...), branch_computations={%region_1.2_spmd, %region_2.3_spmd} | conditional | flops 7476003328 | bytes 31698226 | solution.py:356
  38.8 2.0 %pack.1 = bf16[64,24,256]{2,1,0:T(8,128)(2,1)} custom-call(s32[2]{0:T(128)S(1)} %get-tuple-element.83.place_ref, f32[64,1,128]{2,1,0:T(1,128)S(1)} %get-tuple-element.84.req_ref, f32[32,256]{1,0:T(8,128)S(1)} %get-tuple-element.85.keep_ref, f32[32,256]{1,0:T(8,128)S(1)} %get-tuple-element.86.c_ref, f32[32,256]{1,0:T(8,128)S(1)} %get-tuple-element.87.n_ref, ...), custom_call_target="tpu_custom_call" | custom-call | tf_op jit(solution)/shard_map/cond/branch_1_fun/pack/pallas_call | solution.py:131
  40.8 7.3 %all-to-all-start = ((bf16[64,24,256]{2,1,0:T(8,128)(2,1)}), bf16[64,24,256]{2,1,0:T(8,128)(2,1)S(1)}, u32[]{:S(2)}, u32[]{:S(2)}) async-start(bf16[64,24,256]{2,1,0:T(8,128)(2,1)} %pack.1), calls=%async_computation | async-start | bytes 1572864 | tf_op jit(solution)/shard_map/cond/branch_1_fun/all_to_all | solution.py:340
  48.1 0.7 copy.13.refs_1_
  48.8 14.4 %near.3 = f32[32,16,256]{2,1,0:T(8,128)S(1)} custom-call(s32[3]{0:T(128)} %get-tuple-element.93.refs_0_, bf16[32,3,512]{2,1,0:T(4,128)(2,1)} %copy.13.refs_1_, bf16[32,16,256]{2,1,0:T(8,128)(2,1)} %get-tuple-element.95.refs_2_, bf16[32,16,256]{2,1,0:T(8,128)(2,1)} %copy-done.11, bf16[24,512]{1,0:T(8,128)(2,1)} %copy-done.12, bf16[24,512]{1,0:T(8,128)(2,1)} %copy-done.13), custom_call_target="tpu_custom_call" | custom-call | flops 6400000000 | bytes 2000000 | tf_op jit(solution)/shard_map/cond/branch_1_fun/near/pallas_call | solution.py:237
  63.3 8.1 %all-to-all-done.got_ref = bf16[64,24,256]{2,1,0:T(8,128)(2,1)S(1)} async-done(((bf16[64,24,256]{2,1,0:T(8,128)(2,1)}), bf16[64,24,256]{2,1,0:T(8,128)(2,1)S(1)}, u32[]{:S(2)}, u32[]{:S(2)}) %all-to-all-start) | async-done | bytes 786464 | tf_op jit(solution)/shard_map/cond/branch_1_fun/all_to_all | solution.py:340
  71.3 0.9 %copy-done.4 = bf16[64,24,256]{2,1,0:T(8,128)(2,1)} copy-done((bf16[64,24,256]{2,1,0:T(8,128)(2,1)}, bf16[64,24,256]{2,1,0:T(8,128)(2,1)S(1)}, u32[]{:S(2)}) %copy-start.4) | copy-done | bytes 786456 | tf_op jit(solution)/shard_map/cond
  72.2 4.7 %targets.3 = (bf16[2,32,128]{2,1,0:T(8,128)(2,1)S(1)}, bf16[2,32,128]{2,1,0:T(8,128)(2,1)S(1)}) custom-call(s32[512,128]{1,0:T(8,128)} %get-tuple-element.82.sel_ref, bf16[64,24,256]{2,1,0:T(8,128)(2,1)} %copy-done.4, bf16[32,64,512]{2,1,0:T(8,128)(2,1)S(1)} %copy-done.1, bf16[32,64,512]{2,1,0:T(8,128)(2,1)} %copy-done.3), custom_call_target="tpu_custom_call" | custom-call | tf_op jit(solution)/shard_map/cond/branch_1_fun/targets/pallas_call | solution.py:181
  76.9 1.4 %collective-permute-start.10 = (bf16[2,32,128]{2,1,0:T(8,128)(2,1)S(1)}, bf16[2,32,128]{2,1,0:T(8,128)(2,1)S(1)}, u32[]{:S(2)}, u32[]{:S(2)}) collective-permute-start(bf16[2,32,128]{2,1,0:T(8,128)(2,1)S(1)} %get-tuple-element.119), channel_id=1, source_target_pairs={{0,3},{1,2},{2,1},{3,0},{4,7},{5,6},{6,5},{7,4},{8,11},{9,10},{10,... | collective-permute-start | bytes 49160 | tf_op jit(solution)/shard_map/ppermute | solution.py:299
  78.3 0.6 collective-permute-start.8
  78.9 1.4 %collective-permute-start.9 = (bf16[2,32,128]{2,1,0:T(8,128)(2,1)S(1)}, bf16[2,32,128]{2,1,0:T(8,128)(2,1)S(1)}, u32[]{:S(2)}, u32[]{:S(2)}) collective-permute-start(bf16[2,32,128]{2,1,0:T(8,128)(2,1)S(1)} %get-tuple-element.118.own_ref), channel_id=1, source_target_pairs={{0,1},{1,0},{2,3},{3,2},{4,5},{5,4},{6,7},{7,6},{8,9},{9,8},{10,11... | collective-permute-start | bytes 49160 | tf_op jit(solution)/shard_map/ppermute | solution.py:295
  80.4 1.3 %collective-permute-done.10.nc_ref = bf16[2,32,128]{2,1,0:T(8,128)(2,1)S(1)} collective-permute-done((bf16[2,32,128]{2,1,0:T(8,128)(2,1)S(1)}, bf16[2,32,128]{2,1,0:T(8,128)(2,1)S(1)}, u32[]{:S(2)}, u32[]{:S(2)}) %collective-permute-start.10) | collective-permute-done | bytes 16416 | tf_op jit(solution)/shard_map/ppermute | solution.py:299
  81.7 1.4 %collective-permute-done.9.n_ref = bf16[2,32,128]{2,1,0:T(8,128)(2,1)S(1)} collective-permute-done((bf16[2,32,128]{2,1,0:T(8,128)(2,1)S(1)}, bf16[2,32,128]{2,1,0:T(8,128)(2,1)S(1)}, u32[]{:S(2)}, u32[]{:S(2)}) %collective-permute-start.9) | collective-permute-done | bytes 16416 | tf_op jit(solution)/shard_map/ppermute | solution.py:295
  83.0 0.6 copy-done.10
  83.6 3.1 %final.1 = bf16[32,16,256]{2,1,0:T(8,128)(2,1)} custom-call(s32[3]{0:T(128)} %pad_add_fusion.1.scalar_ref, bf16[2,32,128]{2,1,0:T(8,128)(2,1)S(1)} %get-tuple-element.118.own_ref, bf16[2,32,128]{2,1,0:T(8,128)(2,1)} %copy-done.9, bf16[2,32,128]{2,1,0:T(8,128)(2,1)} %copy-done.10, bf16[2,32,128]{2,1,0:T(8,128)(2,1)} %copy-done.8, ...), custom_call_target="tpu_custom_call" | custom-call | tf_op jit(solution)/shard_map/final/pallas_call | solution.py:278
  (35 shorter events, 0.3 us)
Async XLA Ops:
  0.0 38.5 %collective-permute-start.4 = (bf16[32,64,512]{2,1,0:T(8,128)(2,1)}, bf16[32,64,512]{2,1,0:T(8,128)(2,1)S(1)}, u32[]{:S(2)}, u32[]{:S(2)}) collective-permute-start(bf16[32,64,512]{2,1,0:T(8,128)(2,1)} %param.15), channel_id=1, source_target_pairs={{0,2},{2,0},{1,3},{3,1},{4,6},{6,4},{5,7},{7,5},{8,10},{10,8},{9,1... | collective-permute-start | bytes 6291464 | tf_op jit(solution)/shard_map/ppermute | solution.py:295
  5.8 21.8 %collective-permute-start.5 = (bf16[32,16,256]{2,1,0:T(8,128)(2,1)}, bf16[32,16,256]{2,1,0:T(8,128)(2,1)S(1)}, u32[]{:S(2)}, u32[]{:S(2)}) collective-permute-start(bf16[32,16,256]{2,1,0:T(8,128)(2,1)} %vec_ref.1), channel_id=1, source_target_pairs={{0,1},{1,0},{2,3},{3,2},{4,5},{5,4},{6,7},{7,6},{8,9},{9,8},{10,11... | collective-permute-start | bytes 786440 | tf_op jit(solution)/shard_map/ppermute | solution.py:295
  8.4 4.9 %collective-permute-start = (s32[8,32]{1,0:T(8,128)S(1)}, s32[8,32]{1,0:T(8,128)S(1)}, u32[]{:S(2)}, u32[]{:S(2)}) collective-permute-start(s32[8,32]{1,0:T(8,128)S(1)} %select_bitcast_fusion.own_ref), channel_id=1, source_target_pairs={{0,2},{2,0},{1,3},{3,1},{4,6},{6,4},{5,7},{7,5},{8,10},{10,8},{9,1... | collective-permute-start | bytes 3080 | tf_op jit(solution)/shard_map/ppermute | solution.py:295
  8.7 21.0 %collective-permute-start.1 = (f32[32,256]{1,0:T(8,128)}, f32[32,256]{1,0:T(8,128)S(1)}, u32[]{:S(2)}, u32[]{:S(2)}) collective-permute-start(f32[32,256]{1,0:T(8,128)} %get-tuple-element.113), channel_id=1, source_target_pairs={{0,1},{1,0},{2,3},{3,2},{4,5},{5,4},{6,7},{7,6},{8,9},{9,8},{10,11... | collective-permute-start | bytes 98312 | tf_op jit(solution)/shard_map/ppermute | solution.py:295
  10.4 28.0 %collective-permute-start.2 = (f32[32,256]{1,0:T(8,128)}, f32[32,256]{1,0:T(8,128)S(1)}, u32[]{:S(2)}, u32[]{:S(2)}) collective-permute-start(f32[32,256]{1,0:T(8,128)} %get-tuple-element.114), channel_id=1, source_target_pairs={{0,2},{2,0},{1,3},{3,1},{4,6},{6,4},{5,7},{7,5},{8,10},{10,8},{9,1... | collective-permute-start | bytes 98312 | tf_op jit(solution)/shard_map/ppermute | solution.py:295
  13.3 25.2 %collective-permute-start.3 = (f32[32,256]{1,0:T(8,128)}, f32[32,256]{1,0:T(8,128)S(1)}, u32[]{:S(2)}, u32[]{:S(2)}) collective-permute-start(f32[32,256]{1,0:T(8,128)} %get-tuple-element.115), channel_id=1, source_target_pairs={{0,3},{1,2},{2,1},{3,0},{4,7},{5,6},{6,5},{7,4},{8,11},{9,10},{10,... | collective-permute-start | bytes 98312 | tf_op jit(solution)/shard_map/ppermute | solution.py:299
  15.8 21.2 %all-to-all-start.2 = ((f32[64,1,128]{2,1,0:T(1,128)}), f32[64,1,128]{2,1,0:T(1,128)S(1)}, u32[]{:S(2)}, u32[]{:S(2)}) async-start(f32[64,1,128]{2,1,0:T(1,128)} %get-tuple-element.112), calls=%async_computation.2 | async-start | bytes 65536 | tf_op jit(solution)/shard_map/all_to_all | solution.py:323
  27.7 10.7 %collective-permute-start.6 = (bf16[24,512]{1,0:T(8,128)(2,1)S(1)}, bf16[24,512]{1,0:T(8,128)(2,1)S(1)}, u32[]{:S(2)}, u32[]{:S(2)}) collective-permute-start(bf16[24,512]{1,0:T(8,128)(2,1)S(1)} %get-tuple-element.188), channel_id=1, source_target_pairs={{0,2},{2,4},{4,6},{6,8},{8,10},{10,12},{12,14},{14,16},{16,18},{18... | collective-permute-start | bytes 73736 | tf_op jit(solution)/shard_map/ppermute | solution.py:295
  29.7 8.8 %collective-permute-start.7 = (bf16[24,512]{1,0:T(8,128)(2,1)S(1)}, bf16[24,512]{1,0:T(8,128)(2,1)S(1)}, u32[]{:S(2)}, u32[]{:S(2)}) collective-permute-start(bf16[24,512]{1,0:T(8,128)(2,1)S(1)} %get-tuple-element.187), channel_id=1, source_target_pairs={{0,254},{2,0},{4,2},{6,4},{8,6},{10,8},{12,10},{14,12},{16,14},{18... | collective-permute-start | bytes 73736 | tf_op jit(solution)/shard_map/ppermute | solution.py:295
  38.7 2.1 %copy-start.11 = (bf16[32,16,256]{2,1,0:T(8,128)(2,1)}, bf16[32,16,256]{2,1,0:T(8,128)(2,1)S(1)}, u32[]{:S(2)}) copy-start(bf16[32,16,256]{2,1,0:T(8,128)(2,1)S(1)} %get-tuple-element.96.refs_3_) | copy-start | bytes 786436 | tf_op jit(solution)/shard_map/cond
  38.7 2.1 %copy-start.12 = (bf16[24,512]{1,0:T(8,128)(2,1)}, bf16[24,512]{1,0:T(8,128)(2,1)S(1)}, u32[]{:S(2)}) copy-start(bf16[24,512]{1,0:T(8,128)(2,1)S(1)} %get-tuple-element.97.refs_4_) | copy-start | bytes 73732 | tf_op jit(solution)/shard_map/cond
  38.7 2.1 %copy-start.13 = (bf16[24,512]{1,0:T(8,128)(2,1)}, bf16[24,512]{1,0:T(8,128)(2,1)S(1)}, u32[]{:S(2)}) copy-start(bf16[24,512]{1,0:T(8,128)(2,1)S(1)} %get-tuple-element.98.refs_5_) | copy-start | bytes 73732 | tf_op jit(solution)/shard_map/cond
  38.7 10.1 %copy-start.3 = (bf16[32,64,512]{2,1,0:T(8,128)(2,1)}, bf16[32,64,512]{2,1,0:T(8,128)(2,1)S(1)}, u32[]{:S(2)}) copy-start(bf16[32,64,512]{2,1,0:T(8,128)(2,1)S(1)} %get-tuple-element.90.next_ref) | copy-start | bytes 6291460 | tf_op jit(solution)/shard_map/cond
  38.8 9.3 %copy-start.6 = (bf16[32,3,512]{2,0,1:T(8,128)(2,1)S(1)}, bf16[32,3,512]{2,0,1:T(8,128)(2,1)}, u32[]{:S(2)}) copy-start(bf16[32,3,512]{2,0,1:T(8,128)(2,1)} %get-tuple-element.176) | copy-start | bytes 294916 | tf_op jit(solution)/shard_map/cond
  40.8 30.5 %all-to-all-start = ((bf16[64,24,256]{2,1,0:T(8,128)(2,1)}), bf16[64,24,256]{2,1,0:T(8,128)(2,1)S(1)}, u32[]{:S(2)}, u32[]{:S(2)}) async-start(bf16[64,24,256]{2,1,0:T(8,128)(2,1)} %pack.1), calls=%async_computation | async-start | bytes 1572864 | tf_op jit(solution)/shard_map/cond/branch_1_fun/all_to_all | solution.py:340
  48.8 23.4 %copy-start.1 = (bf16[32,64,512]{2,1,0:T(8,128)(2,1)S(1)}, bf16[32,64,512]{2,1,0:T(8,128)(2,1)}, u32[]{:S(2)}) copy-start(bf16[32,64,512]{2,1,0:T(8,128)(2,1)} %get-tuple-element.89.own_ref) | copy-start | bytes 6291460 | tf_op jit(solution)/shard_map/cond
  71.3 0.9 %copy-start.4 = (bf16[64,24,256]{2,1,0:T(8,128)(2,1)}, bf16[64,24,256]{2,1,0:T(8,128)(2,1)S(1)}, u32[]{:S(2)}) copy-start(bf16[64,24,256]{2,1,0:T(8,128)(2,1)S(1)} %all-to-all-done.got_ref) | copy-start | bytes 2359300 | tf_op jit(solution)/shard_map/cond
  76.9 4.7 %collective-permute-start.10 = (bf16[2,32,128]{2,1,0:T(8,128)(2,1)S(1)}, bf16[2,32,128]{2,1,0:T(8,128)(2,1)S(1)}, u32[]{:S(2)}, u32[]{:S(2)}) collective-permute-start(bf16[2,32,128]{2,1,0:T(8,128)(2,1)S(1)} %get-tuple-element.119), channel_id=1, source_target_pairs={{0,3},{1,2},{2,1},{3,0},{4,7},{5,6},{6,5},{7,4},{8,11},{9,10},{10,... | collective-permute-start | bytes 49160 | tf_op jit(solution)/shard_map/ppermute | solution.py:299
  78.3 3.3 %collective-permute-start.8 = (bf16[2,32,128]{2,1,0:T(8,128)(2,1)S(1)}, bf16[2,32,128]{2,1,0:T(8,128)(2,1)S(1)}, u32[]{:S(2)}, u32[]{:S(2)}) collective-permute-start(bf16[2,32,128]{2,1,0:T(8,128)(2,1)S(1)} %get-tuple-element.119), channel_id=1, source_target_pairs={{0,2},{2,0},{1,3},{3,1},{4,6},{6,4},{5,7},{7,5},{8,10},{10,8},{9,1... | collective-permute-start | bytes 49160 | tf_op jit(solution)/shard_map/ppermute | solution.py:295
  78.9 4.1 %collective-permute-start.9 = (bf16[2,32,128]{2,1,0:T(8,128)(2,1)S(1)}, bf16[2,32,128]{2,1,0:T(8,128)(2,1)S(1)}, u32[]{:S(2)}, u32[]{:S(2)}) collective-permute-start(bf16[2,32,128]{2,1,0:T(8,128)(2,1)S(1)} %get-tuple-element.118.own_ref), channel_id=1, source_target_pairs={{0,1},{1,0},{2,3},{3,2},{4,5},{5,4},{6,7},{7,6},{8,9},{9,8},{10,11... | collective-permute-start | bytes 49160 | tf_op jit(solution)/shard_map/ppermute | solution.py:295
  81.7 1.4 %copy-start.8 = (bf16[2,32,128]{2,1,0:T(8,128)(2,1)}, bf16[2,32,128]{2,1,0:T(8,128)(2,1)S(1)}, u32[]{:S(2)}) copy-start(bf16[2,32,128]{2,1,0:T(8,128)(2,1)S(1)} %collective-permute-done.10.nc_ref) | copy-start | bytes 49156
  81.7 1.4 %copy-start.9 = (bf16[2,32,128]{2,1,0:T(8,128)(2,1)}, bf16[2,32,128]{2,1,0:T(8,128)(2,1)S(1)}, u32[]{:S(2)}) copy-start(bf16[2,32,128]{2,1,0:T(8,128)(2,1)S(1)} %collective-permute-done.8.c_ref) | copy-start | bytes 49156
  83.0 0.6 copy-start.10

commit v3 on v1

--- a/solution.py
+++ b/solution.py
@@ -8,6 +8,7 @@
 from jax.sharding import Mesh
 from jax.sharding import PartitionSpec as P
 
+
 WIDE = ("y", "z", "x", "c")
 PEERS = ("y", "x", "c")
 
@@ -18,12 +19,14 @@
 RH = R // 2
 N_Z, N_PEER = 8, 16
 CAP = 48
+CUT = 24
 ENTRIES = T * J
 COLUMN = N_Z * T
 bf16, f32, i32 = jnp.bfloat16, jnp.float32, jnp.int32
 
 VMEM = pl.BlockSpec(memory_space=pltpu.VMEM)
 SMEM = pl.BlockSpec(memory_space=pltpu.SMEM)
+LIMIT = pltpu.CompilerParams(vmem_limit_bytes=20 * 2**20)
 
 
 def nt(a, b):
@@ -43,7 +46,11 @@
     return two[:, :64] + two[:, 64:]
 
 
-def index_kernel(count_ref, adm_ref, sel_ref, req_ref):
+def index_kernel(count_ref, adm_ref, pts_ref, sel_ref, req_ref, rows_ref):
+    pts = pts_ref[...].astype(f32)
+    blank = jnp.zeros((5, LEAF), f32)
+    for t in range(T):
+        rows_ref[t] = jnp.concatenate([pts[i, t : t + 1] for i in range(3)] + [blank], 0).astype(bf16)
     count = count_ref[0]
     adm = jnp.concatenate([adm_ref[...].astype(f32), jnp.zeros((8, 96), f32)], 1).T
     leaf = jnp.concatenate(
@@ -69,17 +76,19 @@
     req_ref[...] = wanted.astype(bf16).reshape(N_PEER, CAP, 128)
 
 
-def index_call(counts, adm):
+def index_call(counts, adm, points):
     return pl.pallas_call(
         index_kernel,
         out_shape=(
             jax.ShapeDtypeStruct((ENTRIES, 128), i32),
             jax.ShapeDtypeStruct((N_PEER, CAP, 128), bf16),
+            jax.ShapeDtypeStruct((T, 8, LEAF), bf16),
         ),
-        in_specs=[SMEM, VMEM],
-        out_specs=(VMEM, VMEM),
+        in_specs=[SMEM, VMEM, VMEM],
+        out_specs=(VMEM, VMEM, VMEM),
         name="requests",
-    )(counts, adm)
+        compiler_params=LIMIT,
+    )(counts, adm, points)
 
 
 def coeff_kernel(n_ref, vec_ref, basis_ref, keep_ref, send_ref, rows):
@@ -104,6 +113,7 @@
         out_specs=(VMEM, VMEM),
         scratch_shapes=[pltpu.VMEM((T * R, 128), f32)],
         name="coeffs",
+        compiler_params=LIMIT,
     )(n, vectors, basis)
 
 
@@ -128,6 +138,7 @@
         in_specs=[VMEM, VMEM],
         out_specs=VMEM,
         name="pack",
+        compiler_params=LIMIT,
     )(req, table)
 
 
@@ -172,6 +183,7 @@
         in_specs=[VMEM, VMEM, VMEM],
         out_specs=VMEM,
         name="select",
+        compiler_params=LIMIT,
     )(sel, got, couplings)
 
 
@@ -186,11 +198,12 @@
         in_specs=[VMEM, VMEM],
         out_specs=VMEM,
         name="couple",
+        compiler_params=LIMIT,
     )(picked, couplings)
 
 
 def near_kernel(leaves, scalar_ref, pts_ref, vec_ref, other_ref, left_ref, right_ref, out_ref, *bufs):
-    vals, pts, kern0, kern1 = bufs
+    vals, pts, *kerns = bufs
     count, n = scalar_ref[0], scalar_ref[1]
     own = pl.multiple_of(n * HALF, HALF)
     other = pl.multiple_of((1 - n) * HALF, HALF)
@@ -199,14 +212,14 @@
     pts[:T] = pts_ref[...]
     for k, edge in enumerate((left_ref, right_ref)):
         vals[T + k] = edge[:R]
-        pts[T + k] = edge[R : R + 3]
+        pts[T + k] = edge[R : R + 8]
 
     def sources(t):
         return jnp.where(t == 0, T, t - 1), t, jnp.where(t == count - 1, T + 1, jnp.minimum(t + 1, T - 1))
 
     def fill(t, kern):
         x = pts[t, :, pl.ds(own, HALF)].astype(f32)
-        x = jnp.concatenate([x, jnp.zeros((5, HALF), f32)], 0).T.astype(bf16)
+        x = x.T.astype(bf16)
         for k, u in enumerate(sources(t)):
             y = pts[u]
             for p in range(0, HALF, 32):
@@ -222,17 +235,16 @@
         out_ref[t - leaves[0]] = nt(values, kern[...]) * inverse_four_pi
 
     first, last = leaves
-    fill(first, kern0)
+    fill(first, kerns[0])
 
     def body(i, _):
-        t = first + 2 * i
-        fill(t + 1, kern1)
-        product(t, kern0)
-        fill(jnp.minimum(t + 2, last - 1), kern0)
-        product(t + 1, kern1)
+        for s in range(4):
+            t = first + 4 * i + s
+            fill(jnp.minimum(t + 1, last - 1), kerns[(s + 1) % 4])
+            product(t, kerns[s])
         return 0
 
-    lax.fori_loop(0, (last - first) // 2, body, 0)
+    lax.fori_loop(0, (last - first) // 4, body, 0)
 
 
 def near_call(leaves, scalars, pts, vectors, other, left, right):
@@ -244,14 +256,14 @@
         out_specs=VMEM,
         scratch_shapes=[
             pltpu.VMEM((T + 2, R, LEAF), bf16),
-            pltpu.VMEM((T + 2, 3, LEAF), bf16),
-            pltpu.VMEM((HALF, 3 * LEAF), bf16),
-            pltpu.VMEM((HALF, 3 * LEAF), bf16),
-        ],
+            pltpu.VMEM((T + 2, 8, LEAF), bf16),
+        ]
+        + [pltpu.VMEM((HALF, 3 * LEAF), bf16)] * 4,
         cost_estimate=pl.CostEstimate(
             flops=size * 200_000_000, bytes_accessed=2_000_000, transcendentals=0
         ),
         name="near",
+        compiler_params=LIMIT,
     )(scalars, pts, vectors, other, left, right)
 
 
@@ -265,33 +277,23 @@
     for g in range(T // 4):
         part = rows[64 * g : 64 * g + 64, :]
         lhs = jnp.where(same, jnp.concatenate([part, part], 1), 0.0).astype(bf16)
-        far = nn(lhs, tgt_ref[4 * g : 4 * g + 4].reshape(4 * A, HALF)).reshape(4, R, HALF)
-        near = near0_ref if g < T // 8 else near1_ref
-        first = 4 * g % (T // 2)
+        tgt = tgt_ref[4 * g : 4 * g + 4, :, pl.ds(pl.multiple_of(n * HALF, HALF), HALF)]
+        far = nn(lhs, tgt.reshape(4 * A, HALF)).reshape(4, R, HALF)
+        near, first = (near0_ref, 4 * g) if 4 * g < CUT else (near1_ref, 4 * g - CUT)
         total = far + near[first : first + 4]
         live = (iota((4, R, HALF), 0) + 4 * g) < count
         out_ref[4 * g : 4 * g + 4] = jnp.where(live, total, 0.0).astype(bf16)
 
 
 def final_call(scalars, mine, theirs, tgt, near0, near1):
-    whole = lambda *shape: pl.BlockSpec(shape, lambda i, s: (0,) * len(shape))
     return pl.pallas_call(
         final_kernel,
         out_shape=jax.ShapeDtypeStruct((T, R, HALF), bf16),
-        grid_spec=pltpu.PrefetchScalarGridSpec(
-            num_scalar_prefetch=1,
-            grid=(1,),
-            in_specs=[
-                whole(RH // 2, T, 2 * A),
-                whole(RH // 2, T, 2 * A),
-                pl.BlockSpec((T, A, HALF), lambda i, s: (0, 0, s[1])),
-                whole(T // 2, R, HALF),
-                whole(T // 2, R, HALF),
-            ],
-            out_specs=whole(T, R, HALF),
-            scratch_shapes=[pltpu.VMEM((T * R, 128), f32)],
-        ),
+        in_specs=[SMEM] + [VMEM] * 5,
+        out_specs=VMEM,
+        scratch_shapes=[pltpu.VMEM((T * R, 128), f32)],
         name="final",
+        compiler_params=LIMIT,
     )(scalars, mine, theirs, tgt, near0, near1)
 
 
@@ -305,7 +307,7 @@
     return lax.all_to_all(copies, axis, split_axis=0, concat_axis=0, tiled=True)
 
 
-def local(points, vectors, counts, src_basis, tgt_basis, adm_src, couplings):
+def body(points, vectors, counts, src_basis, tgt_basis, adm_src, couplings):
     n = lax.axis_index("n").astype(i32)
     count = counts[0]
     scalars = jnp.stack([count, n])
@@ -313,7 +315,7 @@
     keep, send = coeff_call(n[None], vectors, src_basis)
     came = shifted(send, "n", 1)
     other = shifted(vectors, "n", 1)
-    sel, req = index_call(counts, adm_src.T)
+    sel, req, rows = index_call(counts, adm_src.T, points.transpose(1, 0, 2))
     asked = lax.all_to_all(req, PEERS, split_axis=0, concat_axis=0, tiled=True)
 
     coeffs = (keep + came).astype(bf16)
@@ -322,17 +324,17 @@
     def edge(slot):
         halves = [lax.dynamic_index_in_dim(v, slot, 0, keepdims=False) for v in (vectors, other)]
         row = jnp.where(n == 0, jnp.concatenate(halves, 1), jnp.concatenate(halves[::-1], 1))
-        pts = lax.dynamic_index_in_dim(points, slot, 0, keepdims=False)
-        return jnp.concatenate([row, pts, jnp.zeros((5, LEAF), bf16)], 0)
-
-    left = shifted(edge(count - 1), WIDE, 1)
-    right = shifted(edge(0), WIDE, -1)
-    near_args = (scalars, points, vectors, other, left, right)
-    near0 = near_call((0, T // 2), *near_args)
+        return jnp.concatenate([row, lax.dynamic_index_in_dim(rows, slot, 0, keepdims=False)], 0)
+
+    last, first = edge(count - 1), edge(0)
+    left = shifted(last, WIDE, 1)
+    right = shifted(first, WIDE, -1)
+    near_args = (scalars, rows, vectors, other, left, right)
+    near1 = near_call((CUT, T), *near_args)
 
     def some(table):
         got = lax.all_to_all(pack_call(asked, table), PEERS, split_axis=0, concat_axis=0, tiled=True)
-        return select_call(sel, got, couplings), near_call((T // 2, T), *near_args)
+        return select_call(sel, got, couplings), near_call((0, CUT), *near_args)
 
     def every(table):
         whole = to_all(table, PEERS).reshape(N_PEER * COLUMN, RH * A)
@@ -340,9 +342,9 @@
         place = ((leaf >> 11) * 8 + ((leaf >> 5) & 7)) * COLUMN + ((leaf >> 8) & 7) * T + (leaf & (T - 1))
         hot = (place[:, None] == jnp.arange(N_PEER * COLUMN, dtype=i32)[None, :]).astype(bf16)
         picked = jnp.dot(hot, whole, preferred_element_type=f32)
-        return couple_call(picked, couplings), near_call((T // 2, T), *near_args)
-
-    mine, near1 = lax.cond(jnp.min(asked[:, 0, 0]) >= 0, some, every, table)
+        return couple_call(picked, couplings), near_call((0, CUT), *near_args)
+
+    mine, near0 = lax.cond(jnp.min(asked[:, 0, 0]) >= 0, some, every, table)
     theirs = shifted(mine, "n", 1)
     return final_call(scalars, mine, theirs, tgt_basis, near0, near1)
 
@@ -361,4 +363,4 @@
         P(WIDE, None, None),
     )
     out_specs = P(WIDE, None, "n")
-    return jax.shard_map(local, mesh=split, in_specs=in_specs, out_specs=out_specs, check_vma=False)
+    return jax.shard_map(body, mesh=split, in_specs=in_specs, out_specs=out_specs, check_vma=False)

time: 83.2 us -> 75.7 us (0.910)
  Pallas kernels: 30.9 us -> 25.2 us
  local copies, waits for them, and re-layouts: 7.18 us -> 5 us
  other arithmetic: 1.66 us -> 0.75 us
  waiting for transfers between devices: 11.7 us -> 12.6 us
    pallas_call x2, Pallas kernels: 19.4 us -> 16.7 us  [near_call(): pl.pallas_call(lambda *refs: near_kernel(leaves, *refs), out_shape=jax.Sh...]
    another operation x2 -> x0, local copies, waits for them, and re-layouts: 1.64 us -> none
    pallas_call x1, Pallas kernels: 2.43 us -> 1.3 us  [select_call(): pl.pallas_call(select_kernel, out_shape=TC_SHAPE, in_specs=[VMEM, VMEM, V...]
    pallas_call x1, Pallas kernels: 2.56 us -> 1.57 us  [coeff_call(): pl.pallas_call(coeff_kernel, out_shape=(shape, shape), in_specs=[SMEM, VM...]
    all_to_all x1, waiting for transfers between devices: 3.59 us -> 4.54 us  [to_all(): return lax.all_to_all(copies, axis, split_axis=0, concat_axis=0, tiled=True)]
    cond x4 -> x2, local copies, waits for them, and re-layouts: 0.9 us -> 0.01 us
    pallas_call x1, Pallas kernels: 3.05 us -> 2.16 us  [final_call(): pl.pallas_call(final_kernel, out_shape=jax.ShapeDtypeStruct((T, R, HALF),...]
    convert_element_type x1, other arithmetic: 0.85 us -> 0.01 us  [body(): coeffs = (keep + came).astype(bf16)]
  transfers between devices with their start and end apart: 8 -> 8, of which waited for: 4 -> 4; matrix products, arithmetic and copies ran while one was open for 9% -> 4% of each run, Pallas kernels for 27% -> 24%
where the time goes in v3:
time: 75.7 us; the launch traced here: 75 us
  starting transfers between devices  30 us (40%)
  Pallas kernels  25.2 us (33%)
  waiting for transfers between devices  12.6 us (17%)
  local copies, waits for them, and re-layouts  5 us (7%)
  between operations  1.39 us (2%)
    pallas_call x2, Pallas kernels, near_call(): pl.pallas_call(lambda *refs: near_kernel(leaves, *refs), out_shape=jax.Sh...  16.7 us
    all_to_all x1, starting transfers between devices, to_all(): return lax.all_to_all(copies, axis, split_axis=0, concat_axis=0, tiled=True)  8.17 us
    all_to_all x1, starting transfers between devices, some(): lax.all_to_all(pack_call(asked, table), PEERS, split_axis=0, concat_axis=...  7.65 us
    ppermute x5, starting transfers between devices, shifted(): lax.ppermute(array, axis, [(i, (i + by) % devices) for i in range(devices)])  7.39 us
    ppermute x5, waiting for transfers between devices, shifted(): lax.ppermute(array, axis, [(i, (i + by) % devices) for i in range(devices)])  7.3 us
    all_to_all x1, starting transfers between devices, body(): asked = lax.all_to_all(req, PEERS, split_axis=0, concat_axis=0, tiled=True)  6.81 us
    all_to_all x1, waiting for transfers between devices, to_all(): return lax.all_to_all(copies, axis, split_axis=0, concat_axis=0, tiled=True)  4.54 us
    pallas_call x1, Pallas kernels, index_call(): pl.pallas_call(index_kernel, out_shape=(jax.ShapeDtypeStruct((ENTRIES, 12...  2.23 us
  transfers between devices with their start and end apart: 8, of which 4 were waited for; matrix products, arithmetic and copies ran while one was open for 4% of the time, Pallas kernels for 24%

profile of v3, /device:TPU:1, one launch (start us, length us, event | category | flops | bytes accessed | tf_op | source)
XLA Modules:
  0.0 75.0 jit_solution(1681223512282054050)
XLA Ops:
  0.7 0.9 %copy-done.2 = bf16[32,3,512]{2,0,1:T(8,128)(2,1)S(1)} copy-done((bf16[32,3,512]{2,0,1:T(8,128)(2,1)S(1)}, bf16[32,3,512]{2,0,1:T(8,128)(2,1)}, u32[]{:S(2)}) %copy-start.2) | copy-done | bytes 98328
  1.5 2.2 %requests.1 = (s32[256,128]{1,0:T(8,128)S(1)}, bf16[16,48,128]{2,1,0:T(8,128)(2,1)}, bf16[32,8,512]{2,1,0:T(8,128)(2,1)}) custom-call(s32[1]{0:T(128)S(6)} %copy.12.count_ref, s32[8,32]{1,0:T(8,128)} %bitcast.26, bf16[3,32,512]{2,1,0:T(8,128)(2,1)S(1)} %bitcast.23), custom_call_target="tpu_custom_call" | custom-call | tf_op jit(solution)/shard_map/requests/pallas_call | solution.py:80
  3.8 6.8 %all-to-all-start.2 = ((bf16[16,48,128]{2,1,0:T(8,128)(2,1)}), bf16[16,48,128]{2,1,0:T(8,128)(2,1)S(1)}, u32[]{:S(2)}, u32[]{:S(2)}) async-start(bf16[16,48,128]{2,1,0:T(8,128)(2,1)} %get-tuple-element.70), calls=%async_computation.2 | async-start | bytes 393216 | tf_op jit(solution)/shard_map/all_to_all | solution.py:319
  10.6 2.6 %collective-permute-start.1 = (bf16[32,16,256]{2,1,0:T(8,128)(2,1)}, bf16[32,16,256]{2,1,0:T(8,128)(2,1)}, u32[]{:S(2)}, u32[]{:S(2)}) collective-permute-start(bf16[32,16,256]{2,1,0:T(8,128)(2,1)} %refs_2_.1), channel_id=1, source_target_pairs={{0,1},{1,0},{2,3},{3,2},{4,5},{5,4},{6,7},{7,6},{8,9},{9,8},{10,11... | collective-permute-start | bytes 786440 | tf_op jit(solution)/shard_map/ppermute | solution.py:302
  13.2 1.2 %copy-done.1 = bf16[32,64,256]{2,1,0:T(8,128)(2,1)S(1)} copy-done((bf16[32,64,256]{2,1,0:T(8,128)(2,1)S(1)}, bf16[32,64,256]{2,1,0:T(8,128)(2,1)}, u32[]{:S(2)}) %copy-start.1) | copy-done | bytes 1048600
  14.4 1.6 %coeffs.1 = (f32[32,512]{1,0:T(8,128)S(1)}, f32[32,512]{1,0:T(8,128)S(1)}) custom-call(s32[1]{0:T(128)} %bitcast.4.n_ref, bf16[32,16,256]{2,1,0:T(8,128)(2,1)} %refs_2_.1, bf16[32,64,256]{2,1,0:T(8,128)(2,1)S(1)} %copy-done.1), custom_call_target="tpu_custom_call" | custom-call | tf_op jit(solution)/shard_map/coeffs/pallas_call | solution.py:109
  16.0 0.4 collective-permute-start
  16.4 0.7 slice_bitcast_fusion.2
  17.2 0.7 slice_bitcast_fusion.1
  17.9 0.1 pad_add_fusion.refs_0_.scalar_ref
  18.0 5.4 %collective-permute-done = f32[32,512]{1,0:T(8,128)S(1)} collective-permute-done((f32[32,512]{1,0:T(8,128)S(1)}, f32[32,512]{1,0:T(8,128)S(1)}, u32[]{:S(2)}, u32[]{:S(2)}) %collective-permute-start) | collective-permute-done | bytes 65568 | tf_op jit(solution)/shard_map/ppermute | solution.py:302
  23.3 0.0 collective-permute-done.1.refs_3_
  23.3 0.7 slice_bitcast_fusion
  24.1 0.0 all-to-all-done.2
  24.1 0.7 broadcast_in_dim.6
  24.8 8.2 %all-to-all-start.3 = ((bf16[8,32,512]{2,1,0:T(8,128)(2,1)}), bf16[8,32,512]{2,1,0:T(8,128)(2,1)S(1)}, u32[]{:S(2)}, u32[]{:S(2)}) async-start(bf16[8,32,512]{2,1,0:T(8,128)(2,1)} %broadcast_in_dim.6), calls=%async_computation.3 | async-start | bytes 524288 | tf_op jit(solution)/shard_map/all_to_all | solution.py:307
  33.0 2.4 %collective-permute-start.2 = (bf16[24,512]{1,0:T(8,128)(2,1)S(1)}, bf16[24,512]{1,0:T(8,128)(2,1)S(1)}, u32[]{:S(2)}, u32[]{:S(2)}) collective-permute-start(bf16[24,512]{1,0:T(8,128)(2,1)S(1)} %pad_maximum_fusion), channel_id=1, source_target_pairs={{0,2},{2,4},{4,6},{6,8},{8,10},{10,12},{12,14},{14,16},{16,18},{18... | collective-permute-start | bytes 73736 | tf_op jit(solution)/shard_map/ppermute | solution.py:302
  35.4 0.1 collective-permute-start.3
  35.5 0.6 slice_reduce_fusion
  36.8 0.0 collective-permute-done.2.refs_4_
  36.8 1.9 %collective-permute-done.3.refs_5_ = bf16[24,512]{1,0:T(8,128)(2,1)S(1)} collective-permute-done((bf16[24,512]{1,0:T(8,128)(2,1)S(1)}, bf16[24,512]{1,0:T(8,128)(2,1)S(1)}, u32[]{:S(2)}, u32[]{:S(2)}) %collective-permute-start.3) | collective-permute-done | bytes 24608 | tf_op jit(solution)/shard_map/ppermute | solution.py:302
  38.8 4.5 %all-to-all-done.3 = bf16[8,32,512]{2,1,0:T(8,128)(2,1)S(1)} async-done(((bf16[8,32,512]{2,1,0:T(8,128)(2,1)}), bf16[8,32,512]{2,1,0:T(8,128)(2,1)S(1)}, u32[]{:S(2)}, u32[]{:S(2)}) %all-to-all-start.3) | async-done | bytes 262176 | tf_op jit(solution)/shard_map/all_to_all | solution.py:307
  43.3 22.9 %conditional.1 = (bf16[4,32,128]{2,1,0:T(8,128)(2,1)S(1)}, f32[24,16,256]{2,1,0:T(8,128)}) conditional(s32[]{:T(128)} %convert_element_type.7, (s32[32,8]{0,1:T(8,128)}, bf16[8,32,512]{2,1,0:T(8,128)(2,1)S(1)}, bf16[32,64,512]{2,1,0:T(8,128)(2,1)}, s32[2]{0:T(128)S(1)}, bf16[32,8,512]{2,1,0:T(8,128)(2,1)}, /*index=5*/bf16[32,16,256]{2,1,0:T(8,128)(2,1)}, ...), branch_computations={%region_1.2_spmd, %region_2.3_spmd} | conditional | flops 5874793472 | bytes 33204484 | solution.py:347
  43.3 1.3 %pack.1 = bf16[16,48,512]{2,1,0:T(8,128)(2,1)} custom-call(bf16[16,48,128]{2,1,0:T(8,128)(2,1)S(1)} %get-tuple-element.54.req_ref, bf16[256,512]{1,0:T(8,128)(2,1)S(1)} %bitcast.25), custom_call_target="tpu_custom_call" | custom-call | tf_op jit(solution)/shard_map/cond/branch_1_fun/pack/pallas_call | solution.py:135
  44.6 7.6 %all-to-all-start = ((bf16[16,48,512]{2,1,0:T(8,128)(2,1)}), bf16[16,48,512]{2,1,0:T(8,128)(2,1)S(1)}, u32[]{:S(2)}, u32[]{:S(2)}) async-start(bf16[16,48,512]{2,1,0:T(8,128)(2,1)} %pack.1), calls=%async_computation | async-start | bytes 1572864 | tf_op jit(solution)/shard_map/cond/branch_1_fun/all_to_all | solution.py:336
  52.2 11.9 %near.4 = f32[24,16,256]{2,1,0:T(8,128)} custom-call(s32[2]{0:T(128)S(1)} %get-tuple-element.57.refs_0_, bf16[32,8,512]{2,1,0:T(8,128)(2,1)} %get-tuple-element.58.refs_1_, bf16[32,16,256]{2,1,0:T(8,128)(2,1)} %get-tuple-element.59.refs_2_, bf16[32,16,256]{2,1,0:T(8,128)(2,1)} %get-tuple-element.60.refs_3_, bf16[24,512]{1,0:T(8,128)(2,1)S(1)} %get-tuple-element.61.refs_4_, ...), custom_call_target="tpu_custom_call" | custom-call | flops 4800000000 | bytes 2000000 | tf_op jit(solution)/shard_map/cond/branch_1_fun/near/pallas_call | solution.py:252
  64.1 0.8 %all-to-all-done.got_ref = bf16[16,48,512]{2,1,0:T(8,128)(2,1)S(1)} async-done(((bf16[16,48,512]{2,1,0:T(8,128)(2,1)}), bf16[16,48,512]{2,1,0:T(8,128)(2,1)S(1)}, u32[]{:S(2)}, u32[]{:S(2)}) %all-to-all-start) | async-done | bytes 786464 | tf_op jit(solution)/shard_map/cond/branch_1_fun/all_to_all | solution.py:336
  64.9 1.3 %select.1 = bf16[4,32,128]{2,1,0:T(8,128)(2,1)S(1)} custom-call(s32[256,128]{1,0:T(8,128)S(1)} %get-tuple-element.53.sel_ref, bf16[16,48,512]{2,1,0:T(8,128)(2,1)S(1)} %all-to-all-done.got_ref, bf16[32,64,512]{2,1,0:T(8,128)(2,1)S(1)} %copy-done.4), custom_call_target="tpu_custom_call" | custom-call | tf_op jit(solution)/shard_map/cond/branch_1_fun/select/pallas_call | solution.py:180
  66.3 1.8 %collective-permute-start.4 = (bf16[4,32,128]{2,1,0:T(8,128)(2,1)S(1)}, bf16[4,32,128]{2,1,0:T(8,128)(2,1)S(1)}, u32[]{:S(2)}, u32[]{:S(2)}) collective-permute-start(bf16[4,32,128]{2,1,0:T(8,128)(2,1)S(1)} %get-tuple-element.75.mine_ref), channel_id=1, source_target_pairs={{0,1},{1,0},{2,3},{3,2},{4,5},{5,4},{6,7},{7,6},{8,9},{9,8},{10,11... | collective-permute-start | bytes 98312 | tf_op jit(solution)/shard_map/ppermute | solution.py:302
  68.1 4.8 %near.5.near1_ref = f32[8,16,256]{2,1,0:T(8,128)S(1)} custom-call(s32[2]{0:T(128)S(1)} %pad_add_fusion.refs_0_.scalar_ref, bf16[32,8,512]{2,1,0:T(8,128)(2,1)} %get-tuple-element.73.refs_1_, bf16[32,16,256]{2,1,0:T(8,128)(2,1)} %refs_2_.1, bf16[32,16,256]{2,1,0:T(8,128)(2,1)} %collective-permute-done.1.refs_3_, ...), custom_call_target="tpu_custom_call" | custom-call | flops 1600000000 | bytes 2000000 | tf_op jit(solution)/shard_map/near/pallas_call | solution.py:252
  72.8 0.0 collective-permute-done.4.theirs_ref
  72.9 2.2 %final.1 = bf16[32,16,256]{2,1,0:T(8,128)(2,1)} custom-call(s32[2]{0:T(128)S(1)} %pad_add_fusion.refs_0_.scalar_ref, bf16[4,32,128]{2,1,0:T(8,128)(2,1)S(1)} %get-tuple-element.75.mine_ref, bf16[4,32,128]{2,1,0:T(8,128)(2,1)S(1)} %collective-permute-done.4.theirs_ref, bf16[32,64,512]{2,1,0:T(8,128)(2,1)S(1)} %copy-done, ...), custom_call_target="tpu_custom_call" | custom-call | tf_op jit(solution)/shard_map/final/pallas_call | solution.py:289
  (11 shorter events, 0.0 us)
Async XLA Ops:
  0.7 0.9 %copy-start.2 = (bf16[32,3,512]{2,0,1:T(8,128)(2,1)S(1)}, bf16[32,3,512]{2,0,1:T(8,128)(2,1)}, u32[]{:S(2)}) copy-start(bf16[32,3,512]{2,0,1:T(8,128)(2,1)} %param.9) | copy-start | bytes 294916
  3.8 20.3 %all-to-all-start.2 = ((bf16[16,48,128]{2,1,0:T(8,128)(2,1)}), bf16[16,48,128]{2,1,0:T(8,128)(2,1)S(1)}, u32[]{:S(2)}, u32[]{:S(2)}) async-start(bf16[16,48,128]{2,1,0:T(8,128)(2,1)} %get-tuple-element.70), calls=%async_computation.2 | async-start | bytes 393216 | tf_op jit(solution)/shard_map/all_to_all | solution.py:319
  10.6 12.7 %collective-permute-start.1 = (bf16[32,16,256]{2,1,0:T(8,128)(2,1)}, bf16[32,16,256]{2,1,0:T(8,128)(2,1)}, u32[]{:S(2)}, u32[]{:S(2)}) collective-permute-start(bf16[32,16,256]{2,1,0:T(8,128)(2,1)} %refs_2_.1), channel_id=1, source_target_pairs={{0,1},{1,0},{2,3},{3,2},{4,5},{5,4},{6,7},{7,6},{8,9},{9,8},{10,11... | collective-permute-start | bytes 786440 | tf_op jit(solution)/shard_map/ppermute | solution.py:302
  13.2 1.2 %copy-start.1 = (bf16[32,64,256]{2,1,0:T(8,128)(2,1)S(1)}, bf16[32,64,256]{2,1,0:T(8,128)(2,1)}, u32[]{:S(2)}) copy-start(bf16[32,64,256]{2,1,0:T(8,128)(2,1)} %basis_ref.1) | copy-start | bytes 3145732
  16.0 7.3 %collective-permute-start = (f32[32,512]{1,0:T(8,128)S(1)}, f32[32,512]{1,0:T(8,128)S(1)}, u32[]{:S(2)}, u32[]{:S(2)}) collective-permute-start(f32[32,512]{1,0:T(8,128)S(1)} %get-tuple-element.72), channel_id=1, source_target_pairs={{0,1},{1,0},{2,3},{3,2},{4,5},{5,4},{6,7},{7,6},{8,9},{9,8},{10,11... | collective-permute-start | bytes 196616 | tf_op jit(solution)/shard_map/ppermute | solution.py:302
  24.8 18.5 %all-to-all-start.3 = ((bf16[8,32,512]{2,1,0:T(8,128)(2,1)}), bf16[8,32,512]{2,1,0:T(8,128)(2,1)S(1)}, u32[]{:S(2)}, u32[]{:S(2)}) async-start(bf16[8,32,512]{2,1,0:T(8,128)(2,1)} %broadcast_in_dim.6), calls=%async_computation.3 | async-start | bytes 524288 | tf_op jit(solution)/shard_map/all_to_all | solution.py:307
  33.0 3.8 %collective-permute-start.2 = (bf16[24,512]{1,0:T(8,128)(2,1)S(1)}, bf16[24,512]{1,0:T(8,128)(2,1)S(1)}, u32[]{:S(2)}, u32[]{:S(2)}) collective-permute-start(bf16[24,512]{1,0:T(8,128)(2,1)S(1)} %pad_maximum_fusion), channel_id=1, source_target_pairs={{0,2},{2,4},{4,6},{6,8},{8,10},{10,12},{12,14},{14,16},{16,18},{18... | collective-permute-start | bytes 73736 | tf_op jit(solution)/shard_map/ppermute | solution.py:302
  35.4 3.3 %collective-permute-start.3 = (bf16[24,512]{1,0:T(8,128)(2,1)S(1)}, bf16[24,512]{1,0:T(8,128)(2,1)S(1)}, u32[]{:S(2)}, u32[]{:S(2)}) collective-permute-start(bf16[24,512]{1,0:T(8,128)(2,1)S(1)} %pad_maximum_fusion.1), channel_id=1, source_target_pairs={{0,254},{2,0},{4,2},{6,4},{8,6},{10,8},{12,10},{14,12},{16,14},{18... | collective-permute-start | bytes 73736 | tf_op jit(solution)/shard_map/ppermute | solution.py:302
  44.6 20.4 %all-to-all-start = ((bf16[16,48,512]{2,1,0:T(8,128)(2,1)}), bf16[16,48,512]{2,1,0:T(8,128)(2,1)S(1)}, u32[]{:S(2)}, u32[]{:S(2)}) async-start(bf16[16,48,512]{2,1,0:T(8,128)(2,1)} %pack.1), calls=%async_computation | async-start | bytes 1572864 | tf_op jit(solution)/shard_map/cond/branch_1_fun/all_to_all | solution.py:336
  52.2 12.7 %copy-start.4 = (bf16[32,64,512]{2,1,0:T(8,128)(2,1)S(1)}, bf16[32,64,512]{2,1,0:T(8,128)(2,1)}, u32[]{:S(2)}) copy-start(bf16[32,64,512]{2,1,0:T(8,128)(2,1)} %get-tuple-element.56.couple_ref) | copy-start | bytes 6291460 | tf_op jit(solution)/shard_map/cond
  66.3 6.6 %copy-start = (bf16[32,64,512]{2,1,0:T(8,128)(2,1)S(1)}, bf16[32,64,512]{2,1,0:T(8,128)(2,1)}, u32[]{:S(2)}) copy-start(bf16[32,64,512]{2,1,0:T(8,128)(2,1)} %tgt_ref.1) | copy-start | bytes 6291460
  66.3 6.6 %collective-permute-start.4 = (bf16[4,32,128]{2,1,0:T(8,128)(2,1)S(1)}, bf16[4,32,128]{2,1,0:T(8,128)(2,1)S(1)}, u32[]{:S(2)}, u32[]{:S(2)}) collective-permute-start(bf16[4,32,128]{2,1,0:T(8,128)(2,1)S(1)} %get-tuple-element.75.mine_ref), channel_id=1, source_target_pairs={{0,1},{1,0},{2,3},{3,2},{4,5},{5,4},{6,7},{7,6},{8,9},{9,8},{10,11... | collective-permute-start | bytes 98312 | tf_op jit(solution)/shard_map/ppermute | solution.py:302

commit v4 on v3

--- a/solution.py
+++ b/solution.py
@@ -19,8 +19,8 @@
 RH = R // 2
 N_Z, N_PEER = 8, 16
 CAP = 48
-CUT = 24
 ENTRIES = T * J
+OFFSETS = (0,), (2,), (-2,), (4,), (1, 3), (-1, -3)
 COLUMN = N_Z * T
 bf16, f32, i32 = jnp.bfloat16, jnp.float32, jnp.int32
 
@@ -46,12 +46,15 @@
     return two[:, :64] + two[:, 64:]
 
 
-def index_kernel(count_ref, adm_ref, pts_ref, sel_ref, req_ref, rows_ref):
+def index_kernel(scalar_ref, adm_ref, pts_ref, vec_ref, sel_ref, req_ref, rows_ref, first_ref, last_ref):
     pts = pts_ref[...].astype(f32)
     blank = jnp.zeros((5, LEAF), f32)
     for t in range(T):
         rows_ref[t] = jnp.concatenate([pts[i, t : t + 1] for i in range(3)] + [blank], 0).astype(bf16)
-    count = count_ref[0]
+    count, own = scalar_ref[0], pl.multiple_of(scalar_ref[1] * HALF, HALF)
+    for ref, t in ((first_ref, 0), (last_ref, count - 1)):
+        ref[:R] = vec_ref[t]
+        ref[R:] = rows_ref[t, :, pl.ds(own, HALF)]
     adm = jnp.concatenate([adm_ref[...].astype(f32), jnp.zeros((8, 96), f32)], 1).T
     leaf = jnp.concatenate(
         [jnp.broadcast_to(adm[:T, j : j + 1], (T, 128)) for j in range(J)], 0
@@ -76,19 +79,24 @@
     req_ref[...] = wanted.astype(bf16).reshape(N_PEER, CAP, 128)
 
 
-def index_call(counts, adm, points):
+EDGE_SHAPE = jax.ShapeDtypeStruct((R + 8, HALF), bf16)
+
+
+def index_call(scalars, adm, points, vectors):
     return pl.pallas_call(
         index_kernel,
         out_shape=(
             jax.ShapeDtypeStruct((ENTRIES, 128), i32),
             jax.ShapeDtypeStruct((N_PEER, CAP, 128), bf16),
             jax.ShapeDtypeStruct((T, 8, LEAF), bf16),
+            EDGE_SHAPE,
+            EDGE_SHAPE,
         ),
-        in_specs=[SMEM, VMEM, VMEM],
-        out_specs=(VMEM, VMEM, VMEM),
+        in_specs=[SMEM, VMEM, VMEM, VMEM],
+        out_specs=(VMEM,) * 5,
         name="requests",
         compiler_params=LIMIT,
-    )(counts, adm, points)
+    )(scalars, adm, points, vectors)
 
 
 def coeff_kernel(n_ref, vec_ref, basis_ref, keep_ref, send_ref, rows):
@@ -117,7 +125,12 @@
     )(n, vectors, basis)
 
 
-def pack_kernel(req_ref, table_ref, out_ref):
+def pack_kernel(z_ref, req_ref, *refs):
+    *pieces, out_ref, table_ref = refs
+    for piece, offsets in zip(pieces, OFFSETS):
+        for k, offset in enumerate(offsets):
+            first = pl.multiple_of(((z_ref[0] + offset) & (N_Z - 1)) * T, T)
+            table_ref[pl.ds(first, T), :] = piece[k * T : (k + 1) * T]
     lanes = iota((CAP, 128), 1).astype(f32) + 1.0
     for r in range(0, N_PEER, 4):
         want = [req_ref[r + k].astype(f32) for k in range(4)]
@@ -131,15 +144,16 @@
         out_ref[r : r + 4] = picked.astype(bf16).reshape(4, CAP, RH * A)
 
 
-def pack_call(req, table):
+def pack_call(z, req, pieces):
     return pl.pallas_call(
         pack_kernel,
         out_shape=jax.ShapeDtypeStruct((N_PEER, CAP, RH * A), bf16),
-        in_specs=[VMEM, VMEM],
-        out_specs=VMEM,
+        in_specs=[SMEM] + [VMEM] * (1 + len(pieces)),
+        out_specs=VMEM,
+        scratch_shapes=[pltpu.VMEM((COLUMN, RH * A), bf16)],
         name="pack",
         compiler_params=LIMIT,
-    )(req, table)
+    )(z, req, *pieces)
 
 
 def couple(picked, couple_ref, out_ref):
@@ -202,26 +216,29 @@
     )(picked, couplings)
 
 
-def near_kernel(leaves, scalar_ref, pts_ref, vec_ref, other_ref, left_ref, right_ref, out_ref, *bufs):
-    vals, pts, *kerns = bufs
+def near_kernel(leaves, edges, scalar_ref, pts_ref, vec_ref, other_ref, *refs):
+    edge_refs, out_ref, kerns = refs[: 4 * edges], refs[-5], refs[-4:]
     count, n = scalar_ref[0], scalar_ref[1]
     own = pl.multiple_of(n * HALF, HALF)
     other = pl.multiple_of((1 - n) * HALF, HALF)
-    vals[:T, :, pl.ds(own, HALF)] = vec_ref[...]
-    vals[:T, :, pl.ds(other, HALF)] = other_ref[...]
-    pts[:T] = pts_ref[...]
-    for k, edge in enumerate((left_ref, right_ref)):
-        vals[T + k] = edge[:R]
-        pts[T + k] = edge[R : R + 8]
 
     def sources(t):
-        return jnp.where(t == 0, T, t - 1), t, jnp.where(t == count - 1, T + 1, jnp.minimum(t + 1, T - 1))
+        return (t + T - 1) & (T - 1), t, (t + 1) & (T - 1)
+
+    def taken(t, rows, values):
+        if not edges:
+            return values
+        for k, (u, at) in enumerate(((0, 0), (2, count - 1))):
+            halo = [edge_refs[2 * k + h][rows] for h in range(2)]
+            values[u] = [jnp.where(t == at, a, b) for a, b in zip(halo, values[u])]
+        return values
 
     def fill(t, kern):
-        x = pts[t, :, pl.ds(own, HALF)].astype(f32)
-        x = x.T.astype(bf16)
-        for k, u in enumerate(sources(t)):
-            y = pts[u]
+        x = pts_ref[t, :, pl.ds(own, HALF)].astype(f32).T.astype(bf16)
+        points = [[pts_ref[u, :, pl.ds(h, HALF)] for h in (own, other)] for u in sources(t)]
+        points = taken(t, slice(R, R + 8), points)
+        for k in range(3):
+            y = jnp.concatenate(points[k], 1)
             for p in range(0, HALF, 32):
                 squared = None
                 for i in range(3):
@@ -231,43 +248,50 @@
                 kern[p : p + 32, k * LEAF : (k + 1) * LEAF] = lax.rsqrt(squared)
 
     def product(t, kern):
-        values = jnp.concatenate([vals[u] for u in sources(t)], 1)
-        out_ref[t - leaves[0]] = nt(values, kern[...]) * inverse_four_pi
-
-    first, last = leaves
-    fill(first, kerns[0])
+        values = [[vec_ref[u], other_ref[u]] for u in sources(t)]
+        values = taken(t, slice(0, R), values)
+        values = jnp.concatenate([v for pair in values for v in pair], 1)
+        out_ref[t] = nt(values, kern[...]) * inverse_four_pi
+
+    def leaf(i):
+        if not edges:
+            return leaves[0] + i
+        i = jnp.where(i < leaves[0], i, i + leaves[1] - leaves[0])
+        return jnp.where(i < T, i, count - 1)
+
+    steps = T - leaves[1] + leaves[0] + 1 if edges else leaves[1] - leaves[0]
+    group = 3 if edges else 4
+    fill(leaf(0), kerns[0])
 
     def body(i, _):
-        for s in range(4):
-            t = first + 4 * i + s
-            fill(jnp.minimum(t + 1, last - 1), kerns[(s + 1) % 4])
-            product(t, kerns[s])
+        for s in range(group):
+            fill(leaf(jnp.minimum(group * i + s + 1, steps - 1)), kerns[(s + 1) % group])
+            product(leaf(group * i + s), kerns[s])
         return 0
 
-    lax.fori_loop(0, (last - first) // 4, body, 0)
-
-
-def near_call(leaves, scalars, pts, vectors, other, left, right):
-    size = leaves[1] - leaves[0]
-    return pl.pallas_call(
-        lambda *refs: near_kernel(leaves, *refs),
-        out_shape=jax.ShapeDtypeStruct((size, R, HALF), f32),
-        in_specs=[SMEM] + [VMEM] * 5,
-        out_specs=VMEM,
-        scratch_shapes=[
-            pltpu.VMEM((T + 2, R, LEAF), bf16),
-            pltpu.VMEM((T + 2, 8, LEAF), bf16),
-        ]
-        + [pltpu.VMEM((HALF, 3 * LEAF), bf16)] * 4,
+    lax.fori_loop(0, steps // group, body, 0)
+
+
+def near_call(leaves, args, halos=(), base=None):
+    size = T - leaves[1] + leaves[0] + 1 if halos else leaves[1] - leaves[0]
+    bases = () if base is None else (base,)
+    count = len(args) + len(halos)
+    return pl.pallas_call(
+        lambda *refs: near_kernel(leaves, bool(halos), *refs),
+        out_shape=jax.ShapeDtypeStruct((T, R, HALF), f32),
+        in_specs=[SMEM] + [VMEM] * (count - 1 + len(bases)),
+        out_specs=VMEM,
+        scratch_shapes=[pltpu.VMEM((HALF, 3 * LEAF), bf16)] * 4,
+        input_output_aliases={count: 0} if bases else {},
         cost_estimate=pl.CostEstimate(
             flops=size * 200_000_000, bytes_accessed=2_000_000, transcendentals=0
         ),
         name="near",
         compiler_params=LIMIT,
-    )(scalars, pts, vectors, other, left, right)
-
-
-def final_kernel(scalar_ref, mine_ref, theirs_ref, tgt_ref, near0_ref, near1_ref, out_ref, rows):
+    )(*args, *halos, *bases)
+
+
+def final_kernel(scalar_ref, mine_ref, theirs_ref, tgt_ref, near_ref, out_ref, rows):
     count, n = scalar_ref[0], scalar_ref[1]
     for ref, first in ((mine_ref, n * RH), (theirs_ref, (1 - n) * RH)):
         for r in range(RH):
@@ -279,22 +303,21 @@
         lhs = jnp.where(same, jnp.concatenate([part, part], 1), 0.0).astype(bf16)
         tgt = tgt_ref[4 * g : 4 * g + 4, :, pl.ds(pl.multiple_of(n * HALF, HALF), HALF)]
         far = nn(lhs, tgt.reshape(4 * A, HALF)).reshape(4, R, HALF)
-        near, first = (near0_ref, 4 * g) if 4 * g < CUT else (near1_ref, 4 * g - CUT)
-        total = far + near[first : first + 4]
+        total = far + near_ref[4 * g : 4 * g + 4]
         live = (iota((4, R, HALF), 0) + 4 * g) < count
         out_ref[4 * g : 4 * g + 4] = jnp.where(live, total, 0.0).astype(bf16)
 
 
-def final_call(scalars, mine, theirs, tgt, near0, near1):
+def final_call(scalars, mine, theirs, tgt, near):
     return pl.pallas_call(
         final_kernel,
         out_shape=jax.ShapeDtypeStruct((T, R, HALF), bf16),
-        in_specs=[SMEM] + [VMEM] * 5,
+        in_specs=[SMEM] + [VMEM] * 4,
         out_specs=VMEM,
         scratch_shapes=[pltpu.VMEM((T * R, 128), f32)],
         name="final",
         compiler_params=LIMIT,
-    )(scalars, mine, theirs, tgt, near0, near1)
+    )(scalars, mine, theirs, tgt, near)
 
 
 def shifted(array, axis, by):
@@ -307,46 +330,55 @@
     return lax.all_to_all(copies, axis, split_axis=0, concat_axis=0, tiled=True)
 
 
+def onward(array, by, flip):
+    size = 2 * lax.axis_size(WIDE)
+    return lax.ppermute(
+        array, (*WIDE, "n"), [(i, ((i // 2 * 2 + 2 * by) % size) + (i % 2 ^ flip)) for i in range(size)]
+    )
+
+
 def body(points, vectors, counts, src_basis, tgt_basis, adm_src, couplings):
     n = lax.axis_index("n").astype(i32)
-    count = counts[0]
-    scalars = jnp.stack([count, n])
+    z = lax.axis_index("z").astype(i32)
+    scalars = jnp.stack([counts[0], n])
 
     keep, send = coeff_call(n[None], vectors, src_basis)
     came = shifted(send, "n", 1)
     other = shifted(vectors, "n", 1)
-    sel, req, rows = index_call(counts, adm_src.T, points.transpose(1, 0, 2))
+    sel, req, rows, first, last = index_call(scalars, adm_src.T, points.transpose(1, 0, 2), vectors)
     asked = lax.all_to_all(req, PEERS, split_axis=0, concat_axis=0, tiled=True)
 
     coeffs = (keep + came).astype(bf16)
-    table = to_all(coeffs, "z").reshape(COLUMN, RH * A)
-
-    def edge(slot):
-        halves = [lax.dynamic_index_in_dim(v, slot, 0, keepdims=False) for v in (vectors, other)]
-        row = jnp.where(n == 0, jnp.concatenate(halves, 1), jnp.concatenate(halves[::-1], 1))
-        return jnp.concatenate([row, lax.dynamic_index_in_dim(rows, slot, 0, keepdims=False)], 0)
-
-    last, first = edge(count - 1), edge(0)
-    left = shifted(last, WIDE, 1)
-    right = shifted(first, WIDE, -1)
-    near_args = (scalars, rows, vectors, other, left, right)
-    near1 = near_call((CUT, T), *near_args)
-
-    def some(table):
-        got = lax.all_to_all(pack_call(asked, table), PEERS, split_axis=0, concat_axis=0, tiled=True)
-        return select_call(sel, got, couplings), near_call((0, CUT), *near_args)
-
-    def every(table):
+    up = shifted(coeffs, "z", -2)
+    down = shifted(coeffs, "z", 2)
+    across = shifted(coeffs, "z", 4)
+    odd_up = shifted(jnp.concatenate([coeffs, up]), "z", -1)
+    odd_down = shifted(jnp.concatenate([coeffs, down]), "z", 1)
+    pieces = coeffs, up, down, across, odd_up, odd_down
+
+    halos = tuple(onward(edge, by, flip) for edge, by in ((last, 1), (first, -1)) for flip in range(2))
+    near_args = (scalars, rows, vectors, other)
+    near = near_call((4, 12), near_args)
+    near = near_call((12, 28), near_args, base=near)
+    near = near_call((4, 28), near_args, halos, near)
+
+    got = lax.all_to_all(pack_call(z[None], asked, pieces), PEERS, split_axis=0, concat_axis=0, tiled=True)
+    mine = select_call(sel, got, couplings)
+
+    def every(mine, pieces, couplings):
+        blocks = {o % N_Z: p[k * T : (k + 1) * T] for p, os in zip(pieces, OFFSETS) for k, o in enumerate(os)}
+        twice = jnp.concatenate([blocks[o % N_Z] for o in range(2 * N_Z)])
+        table = lax.dynamic_slice_in_dim(twice, (N_Z - z) % N_Z * T, COLUMN, 0)
         whole = to_all(table, PEERS).reshape(N_PEER * COLUMN, RH * A)
         leaf = adm_src.T.reshape(ENTRIES)
         place = ((leaf >> 11) * 8 + ((leaf >> 5) & 7)) * COLUMN + ((leaf >> 8) & 7) * T + (leaf & (T - 1))
         hot = (place[:, None] == jnp.arange(N_PEER * COLUMN, dtype=i32)[None, :]).astype(bf16)
-        picked = jnp.dot(hot, whole, preferred_element_type=f32)
-        return couple_call(picked, couplings), near_call((0, CUT), *near_args)
-
-    mine, near0 = lax.cond(jnp.min(asked[:, 0, 0]) >= 0, some, every, table)
+        return couple_call(jnp.dot(hot, whole, preferred_element_type=f32), couplings)
+
+    fits = jnp.min(asked[:, 0, 0]) >= 0
+    mine = lax.cond(fits, lambda mine, *_: mine, every, mine, pieces, couplings)
     theirs = shifted(mine, "n", 1)
-    return final_call(scalars, mine, theirs, tgt_basis, near0, near1)
+    return final_call(scalars, mine, theirs, tgt_basis, near)
 
 
 def solution(mesh):

time: 75.7 us -> 84.7 us (1.12)
  starting transfers between devices: 30 us -> 42.6 us
  waiting for transfers between devices: 12.6 us -> 9.32 us
    ppermute x5 -> x8, starting transfers between devices: 7.39 us -> 19.4 us  [shifted(): lax.ppermute(array, axis, [(i, (i + by) % devices) for i in range(devices)])]
    all_to_all x2 -> x1, starting transfers between devices: 15.8 us -> 6.97 us  [body(): lax.all_to_all(pack_call(z[None], asked, pieces), PEERS, split_axis=0, co...]
    ppermute x0 -> x4, starting transfers between devices: none -> 8.75 us  [onward(): lax.ppermute(array, (*WIDE, 'n'), [(i, (i // 2 * 2 + 2 * by) % size + (i...]
    all_to_all x2 -> x1, waiting for transfers between devices: 5.35 us -> 0.01 us  [body(): lax.all_to_all(pack_call(z[None], asked, pieces), PEERS, split_axis=0, co...]
    pallas_call x1, Pallas kernels: 1.3 us -> 3.51 us  [select_call(): pl.pallas_call(select_kernel, out_shape=TC_SHAPE, in_specs=[VMEM, VMEM, V...]
    squeeze x3 -> x0, local copies, waits for them, and re-layouts: 2.16 us -> none  [the longest x2 1.44 us: edge(): lax.dynamic_index_in_dim(v, slot, 0, keepdims=False)]
    ppermute x5 -> x8, waiting for transfers between devices: 7.3 us -> 9.3 us  [shifted(): lax.ppermute(array, axis, [(i, (i + by) % devices) for i in range(devices)])]
    unnamed x6 -> x14, local copies, waits for them, and re-layouts: 2.11 us -> 4.03 us
  transfers between devices with their start and end apart: 8 -> 14, of which waited for: 4 -> 3; matrix products, arithmetic and copies ran while one was open for 4% -> 2% of each run, Pallas kernels for 24% -> 26%
where the time goes in v4:
time: 84.7 us; the launch traced here: 84.2 us
  starting transfers between devices  42.6 us (50%)
  Pallas kernels  25.3 us (30%)
  waiting for transfers between devices  9.32 us (11%)
  local copies, waits for them, and re-layouts  4.79 us (6%)
  between operations  1.44 us (2%)
    ppermute x8, starting transfers between devices, shifted(): lax.ppermute(array, axis, [(i, (i + by) % devices) for i in range(devices)])  19.4 us
    pallas_call x3, Pallas kernels, near_call(): pl.pallas_call(lambda *refs: near_kernel(leaves, bool(halos), *refs), out...  16 us
    ppermute x8, waiting for transfers between devices, shifted(): lax.ppermute(array, axis, [(i, (i + by) % devices) for i in range(devices)])  9.3 us
    ppermute x4, starting transfers between devices, onward(): lax.ppermute(array, (*WIDE, 'n'), [(i, (i // 2 * 2 + 2 * by) % size + (i...  8.75 us
    all_to_all x1, starting transfers between devices, body(): asked = lax.all_to_all(req, PEERS, split_axis=0, concat_axis=0, tiled=True)  7.43 us
    all_to_all x1, starting transfers between devices, body(): lax.all_to_all(pack_call(z[None], asked, pieces), PEERS, split_axis=0, co...  6.97 us
    unnamed x14, local copies, waits for them, and re-layouts  4.03 us
    pallas_call x1, Pallas kernels, select_call(): pl.pallas_call(select_kernel, out_shape=TC_SHAPE, in_specs=[VMEM, VMEM, V...  3.51 us
  transfers between devices with their start and end apart: 14, of which 3 were waited for; matrix products, arithmetic and copies ran while one was open for 2% of the time, Pallas kernels for 26%

profile of v4, /device:TPU:1, one launch (start us, length us, event | category | flops | bytes accessed | tf_op | source)
XLA Modules:
  0.0 84.2 jit_solution(11849834643616517482)
XLA Ops:
  0.0 0.9 %copy-done.1 = bf16[32,16,256]{2,1,0:T(8,128)(2,1)S(1)} copy-done((bf16[32,16,256]{2,1,0:T(8,128)(2,1)S(1)}, bf16[32,16,256]{2,1,0:T(8,128)(2,1)}, u32[]{:S(2)}) %copy-start.1) | copy-done | bytes 262168
  1.0 1.2 %copy-done.4 = bf16[32,64,256]{2,1,0:T(8,128)(2,1)S(1)} copy-done((bf16[32,64,256]{2,1,0:T(8,128)(2,1)S(1)}, bf16[32,64,256]{2,1,0:T(8,128)(2,1)}, u32[]{:S(2)}) %copy-start.4) | copy-done | bytes 1048600
  2.2 0.6 coeffs.1
  2.8 3.8 %collective-permute-start = (f32[32,512]{1,0:T(8,128)S(1)}, f32[32,512]{1,0:T(8,128)S(1)}, u32[]{:S(2)}, u32[]{:S(2)}) collective-permute-start(f32[32,512]{1,0:T(8,128)S(1)} %get-tuple-element.45), channel_id=1, source_target_pairs={{0,1},{1,0},{2,3},{3,2},{4,5},{5,4},{6,7},{7,6},{8,9},{9,8},{10,11... | collective-permute-start | bytes 196616 | tf_op jit(solution)/shard_map/ppermute | solution.py:325
  7.3 1.0 %collective-permute-done = f32[32,512]{1,0:T(8,128)S(1)} collective-permute-done((f32[32,512]{1,0:T(8,128)S(1)}, f32[32,512]{1,0:T(8,128)S(1)}, u32[]{:S(2)}, u32[]{:S(2)}) %collective-permute-start) | collective-permute-done | bytes 65568 | tf_op jit(solution)/shard_map/ppermute | solution.py:325
  8.3 3.1 %collective-permute-start.3 = (bf16[32,512]{1,0:T(8,128)(2,1)S(1)}, bf16[32,512]{1,0:T(8,128)(2,1)S(1)}, u32[]{:S(2)}, u32[]{:S(2)}) collective-permute-start(bf16[32,512]{1,0:T(8,128)(2,1)S(1)} %add_convert_fusion.refs_0_), channel_id=1, source_target_pairs={{0,32},{16,48},{32,64},{48,80},{64,96},{80,112},{96,0},{112,16},{1... | collective-permute-start | bytes 98312 | tf_op jit(solution)/shard_map/ppermute | solution.py:325
  11.4 3.1 %collective-permute-start.1 = (bf16[32,512]{1,0:T(8,128)(2,1)S(1)}, bf16[32,512]{1,0:T(8,128)(2,1)S(1)}, u32[]{:S(2)}, u32[]{:S(2)}) collective-permute-start(bf16[32,512]{1,0:T(8,128)(2,1)S(1)} %add_convert_fusion.refs_0_), channel_id=1, source_target_pairs={{0,96},{16,112},{32,0},{48,16},{64,32},{80,48},{96,64},{112,80},{1... | collective-permute-start | bytes 98312 | tf_op jit(solution)/shard_map/ppermute | solution.py:325
  14.5 0.1 pad_add_fusion.scalar_ref.refs_0_
  14.6 0.9 %copy-done.2 = bf16[32,16,256]{2,1,0:T(8,128)(2,1)S(1)} copy-done((bf16[32,16,256]{2,1,0:T(8,128)(2,1)S(1)}, bf16[32,16,256]{2,1,0:T(8,128)(2,1)}, u32[]{:S(2)}) %copy-start.2) | copy-done | bytes 262168
  15.6 0.9 %copy-done.5 = bf16[32,3,512]{2,0,1:T(8,128)(2,1)S(1)} copy-done((bf16[32,3,512]{2,0,1:T(8,128)(2,1)S(1)}, bf16[32,3,512]{2,0,1:T(8,128)(2,1)}, u32[]{:S(2)}) %copy-start.5) | copy-done | bytes 98328
  16.5 2.2 %requests.1 = (s32[256,128]{1,0:T(8,128)S(1)}, bf16[16,48,128]{2,1,0:T(8,128)(2,1)}, bf16[32,8,512]{2,1,0:T(8,128)(2,1)S(1)}, bf16[24,256]{1,0:T(8,128)(2,1)S(1)}, bf16[24,256]{1,0:T(8,128)(2,1)S(1)}) custom-call(s32[2]{0:T(128)S(1)} %pad_add_fusion.scalar_ref.refs_0_, s32[8,32]{1,0:T(8,128)} %bitcast.9, bf16[3,32,512]{2,1,0:T(8,128)(2,1)S(1)} %bitcast.8, ...), custom_call_target="tpu_custom_call" | custom-call | tf_op jit(solution)/shard_map/requests/pallas_call | solution.py:86
  18.7 7.4 %all-to-all-start.1 = ((bf16[16,48,128]{2,1,0:T(8,128)(2,1)}), bf16[16,48,128]{2,1,0:T(8,128)(2,1)S(1)}, u32[]{:S(2)}, u32[]{:S(2)}) async-start(bf16[16,48,128]{2,1,0:T(8,128)(2,1)} %get-tuple-element.43), calls=%async_computation.1 | async-start | bytes 393216 | tf_op jit(solution)/shard_map/all_to_all | solution.py:349
  26.1 2.2 %collective-permute-start.2 = (bf16[64,512]{1,0:T(8,128)(2,1)S(1)}, bf16[64,512]{1,0:T(8,128)(2,1)S(1)}, u32[]{:S(2)}, u32[]{:S(2)}) collective-permute-start(bf16[64,512]{1,0:T(8,128)(2,1)S(1)} %get-tuple-element.51), channel_id=1, source_target_pairs={{0,112},{16,0},{32,16},{48,32},{64,48},{80,64},{96,80},{112,96},{1... | collective-permute-start | bytes 196616 | tf_op jit(solution)/shard_map/ppermute | solution.py:325
  28.3 4.0 %collective-permute-start.5 = (bf16[32,512]{1,0:T(8,128)(2,1)S(1)}, bf16[32,512]{1,0:T(8,128)(2,1)S(1)}, u32[]{:S(2)}, u32[]{:S(2)}) collective-permute-start(bf16[32,512]{1,0:T(8,128)(2,1)S(1)} %add_convert_fusion.refs_0_), channel_id=1, source_target_pairs={{0,64},{16,80},{32,96},{48,112},{64,0},{80,16},{96,32},{112,48},{1... | collective-permute-start | bytes 98312 | tf_op jit(solution)/shard_map/ppermute | solution.py:325
  32.3 2.8 %collective-permute-done.5.refs_3_ = bf16[32,512]{1,0:T(8,128)(2,1)S(1)} collective-permute-done((bf16[32,512]{1,0:T(8,128)(2,1)S(1)}, bf16[32,512]{1,0:T(8,128)(2,1)S(1)}, u32[]{:S(2)}, u32[]{:S(2)}) %collective-permute-start.5) | collective-permute-done | bytes 32800 | tf_op jit(solution)/shard_map/ppermute | solution.py:325
  35.2 1.3 %pack.1 = bf16[16,48,512]{2,1,0:T(8,128)(2,1)} custom-call(s32[1]{0:T(128)} %bitcast.5.z_ref, bf16[16,48,128]{2,1,0:T(8,128)(2,1)S(1)} %all-to-all-done.1.req_ref, bf16[32,512]{1,0:T(8,128)(2,1)S(1)} %add_convert_fusion.refs_0_, bf16[32,512]{1,0:T(8,128)(2,1)S(1)} %collective-permute-done.1.refs_1_, bf16[32,512]{1,0:T(8,128)(2,1)S(1)} %collective-permute-done.3.refs_2_, ...), custom_call_target="tpu_custom_call" | custom-call | tf_op jit(solution)/shard_map/pack/pallas_call | solution.py:148
  36.5 7.0 %all-to-all-start.2 = ((bf16[16,48,512]{2,1,0:T(8,128)(2,1)}), bf16[16,48,512]{2,1,0:T(8,128)(2,1)S(1)}, u32[]{:S(2)}, u32[]{:S(2)}) async-start(bf16[16,48,512]{2,1,0:T(8,128)(2,1)} %pack.1), calls=%async_computation.2 | async-start | bytes 1572864 | tf_op jit(solution)/shard_map/all_to_all | solution.py:365
  43.5 2.7 %collective-permute-start.7 = (bf16[32,16,256]{2,1,0:T(8,128)(2,1)S(1)}, bf16[32,16,256]{2,1,0:T(8,128)(2,1)S(1)}, u32[]{:S(2)}, u32[]{:S(2)}) collective-permute-start(bf16[32,16,256]{2,1,0:T(8,128)(2,1)S(1)} %copy-done.3), channel_id=1, source_target_pairs={{0,1},{1,0},{2,3},{3,2},{4,5},{5,4},{6,7},{7,6},{8,9},{9,8},{10,11... | collective-permute-start | bytes 786440 | tf_op jit(solution)/shard_map/ppermute | solution.py:325
  46.2 1.9 %collective-permute-start.8 = (bf16[24,256]{1,0:T(8,128)(2,1)S(1)}, bf16[24,256]{1,0:T(8,128)(2,1)S(1)}, u32[]{:S(2)}, u32[]{:S(2)}) collective-permute-start(bf16[24,256]{1,0:T(8,128)(2,1)S(1)} %get-tuple-element.48), channel_id=1, source_target_pairs={{0,2},{1,3},{2,4},{3,5},{4,6},{5,7},{6,8},{7,9},{8,10},{9,11},{10,... | collective-permute-start | bytes 36872 | tf_op jit(solution)/shard_map/ppermute | solution.py:335
  48.1 0.1 collective-permute-start.9
  48.2 0.7 collective-permute-start.10
  48.8 6.1 %collective-permute-start.11 = (bf16[24,256]{1,0:T(8,128)(2,1)S(1)}, bf16[24,256]{1,0:T(8,128)(2,1)S(1)}, u32[]{:S(2)}, u32[]{:S(2)}) collective-permute-start(bf16[24,256]{1,0:T(8,128)(2,1)S(1)} %get-tuple-element.49), channel_id=1, source_target_pairs={{0,255},{1,254},{2,1},{3,0},{4,3},{5,2},{6,5},{7,4},{8,7},{9,6},{1... | collective-permute-start | bytes 36872 | tf_op jit(solution)/shard_map/ppermute | solution.py:335
  54.9 0.6 slice_reduce_fusion
  56.2 5.4 %collective-permute-done.7.refs_3_ = bf16[32,16,256]{2,1,0:T(8,128)(2,1)S(1)} collective-permute-done((bf16[32,16,256]{2,1,0:T(8,128)(2,1)S(1)}, bf16[32,16,256]{2,1,0:T(8,128)(2,1)S(1)}, u32[]{:S(2)}, u32[]{:S(2)}) %collective-permute-start.7) | collective-permute-done | bytes 262176 | tf_op jit(solution)/shard_map/ppermute | solution.py:325
  61.6 4.2 %near.3.refs_4_ = f32[32,16,256]{2,1,0:T(8,128)S(1)} custom-call(s32[2]{0:T(128)S(1)} %pad_add_fusion.scalar_ref.refs_0_, bf16[32,8,512]{2,1,0:T(8,128)(2,1)S(1)} %get-tuple-element.47.refs_1_, bf16[32,16,256]{2,1,0:T(8,128)(2,1)S(1)} %copy-done.3, bf16[32,16,256]{2,1,0:T(8,128)(2,1)S(1)} %collective-permute-done.7.refs_3_), custom_call_target="tpu_custom_call" | custom-call | flops 1600000000 | bytes 2000000 | tf_op jit(solution)/shard_map/near/pallas_call | solution.py:279
  65.8 7.3 %near.4.refs_8_ = f32[32,16,256]{2,1,0:T(8,128)S(1)} custom-call(s32[2]{0:T(128)S(1)} %pad_add_fusion.scalar_ref.refs_0_, bf16[32,8,512]{2,1,0:T(8,128)(2,1)S(1)} %get-tuple-element.47.refs_1_, bf16[32,16,256]{2,1,0:T(8,128)(2,1)S(1)} %copy-done.3, bf16[32,16,256]{2,1,0:T(8,128)(2,1)S(1)} %collective-permute-done.7.refs_3_, ...), custom_call_target="tpu_custom_call", output_to_operand_aliasing={{}: (4, {})} | custom-call | flops 3200000000 | bytes 2000000 | tf_op jit(solution)/shard_map/near/pallas_call | solution.py:279
  73.1 3.5 %select.3 = bf16[4,32,128]{2,1,0:T(8,128)(2,1)} custom-call(s32[256,128]{1,0:T(8,128)S(1)} %get-tuple-element.46.sel_ref, bf16[16,48,512]{2,1,0:T(8,128)(2,1)S(1)} %all-to-all-done.2.got_ref, bf16[32,64,512]{2,1,0:T(8,128)(2,1)} %couple_ref.1), custom_call_target="tpu_custom_call" | custom-call | tf_op jit(solution)/shard_map/select/pallas_call | solution.py:194
  76.6 0.8 conditional.1
  76.6 0.8 copy.26
  77.4 0.5 collective-permute-start.6
  77.9 4.5 %near.5.near_ref = f32[32,16,256]{2,1,0:T(8,128)S(1)} custom-call(s32[2]{0:T(128)S(1)} %pad_add_fusion.scalar_ref.refs_0_, bf16[32,8,512]{2,1,0:T(8,128)(2,1)S(1)} %get-tuple-element.47.refs_1_, bf16[32,16,256]{2,1,0:T(8,128)(2,1)S(1)} %copy-done.3, bf16[32,16,256]{2,1,0:T(8,128)(2,1)S(1)} %collective-permute-done.7.refs_3_, ...), custom_call_target="tpu_custom_call", output_to_operand_aliasing={{}: (8, {})} | custom-call | flops 1800000000 | bytes 2000000 | tf_op jit(solution)/shard_map/near/pallas_call | solution.py:279
  82.5 1.7 %final.1 = bf16[32,16,256]{2,1,0:T(8,128)(2,1)} custom-call(s32[2]{0:T(128)S(1)} %pad_add_fusion.scalar_ref.refs_0_, bf16[4,32,128]{2,1,0:T(8,128)(2,1)S(1)} %get-tuple-element.52.mine_ref, bf16[4,32,128]{2,1,0:T(8,128)(2,1)S(1)} %collective-permute-done.6.theirs_ref, bf16[32,64,512]{2,1,0:T(8,128)(2,1)S(1)} %copy-done, f32[32,16,256]{2,1,0:T(8,128)S(1)} %near.5.near_ref), custom_call_target="tpu_custom_call" | custom-call | tf_op jit(solution)/shard_map/final/pallas_call | solution.py:312
  (24 shorter events, 0.1 us)
Async XLA Ops:
  0.0 0.9 %copy-start.1 = (bf16[32,16,256]{2,1,0:T(8,128)(2,1)S(1)}, bf16[32,16,256]{2,1,0:T(8,128)(2,1)}, u32[]{:S(2)}) copy-start(bf16[32,16,256]{2,1,0:T(8,128)(2,1)} %refs_2_.5) | copy-start | bytes 786436
  1.0 1.2 %copy-start.4 = (bf16[32,64,256]{2,1,0:T(8,128)(2,1)S(1)}, bf16[32,64,256]{2,1,0:T(8,128)(2,1)}, u32[]{:S(2)}) copy-start(bf16[32,64,256]{2,1,0:T(8,128)(2,1)} %basis_ref.1) | copy-start | bytes 3145732
  2.2 41.3 %copy-start.3 = (bf16[32,16,256]{2,1,0:T(8,128)(2,1)S(1)}, bf16[32,16,256]{2,1,0:T(8,128)(2,1)}, u32[]{:S(2)}) copy-start(bf16[32,16,256]{2,1,0:T(8,128)(2,1)} %refs_2_.5) | copy-start | bytes 786436
  2.8 5.5 %collective-permute-start = (f32[32,512]{1,0:T(8,128)S(1)}, f32[32,512]{1,0:T(8,128)S(1)}, u32[]{:S(2)}, u32[]{:S(2)}) collective-permute-start(f32[32,512]{1,0:T(8,128)S(1)} %get-tuple-element.45), channel_id=1, source_target_pairs={{0,1},{1,0},{2,3},{3,2},{4,5},{5,4},{6,7},{7,6},{8,9},{9,8},{10,11... | collective-permute-start | bytes 196616 | tf_op jit(solution)/shard_map/ppermute | solution.py:325
  8.3 17.8 %collective-permute-start.3 = (bf16[32,512]{1,0:T(8,128)(2,1)S(1)}, bf16[32,512]{1,0:T(8,128)(2,1)S(1)}, u32[]{:S(2)}, u32[]{:S(2)}) collective-permute-start(bf16[32,512]{1,0:T(8,128)(2,1)S(1)} %add_convert_fusion.refs_0_), channel_id=1, source_target_pairs={{0,32},{16,48},{32,64},{48,80},{64,96},{80,112},{96,0},{112,16},{1... | collective-permute-start | bytes 98312 | tf_op jit(solution)/shard_map/ppermute | solution.py:325
  11.4 14.7 %collective-permute-start.1 = (bf16[32,512]{1,0:T(8,128)(2,1)S(1)}, bf16[32,512]{1,0:T(8,128)(2,1)S(1)}, u32[]{:S(2)}, u32[]{:S(2)}) collective-permute-start(bf16[32,512]{1,0:T(8,128)(2,1)S(1)} %add_convert_fusion.refs_0_), channel_id=1, source_target_pairs={{0,96},{16,112},{32,0},{48,16},{64,32},{80,48},{96,64},{112,80},{1... | collective-permute-start | bytes 98312 | tf_op jit(solution)/shard_map/ppermute | solution.py:325
  14.6 0.9 %copy-start.2 = (bf16[32,16,256]{2,1,0:T(8,128)(2,1)S(1)}, bf16[32,16,256]{2,1,0:T(8,128)(2,1)}, u32[]{:S(2)}) copy-start(bf16[32,16,256]{2,1,0:T(8,128)(2,1)} %refs_2_.5) | copy-start | bytes 786436
  15.6 0.9 %copy-start.5 = (bf16[32,3,512]{2,0,1:T(8,128)(2,1)S(1)}, bf16[32,3,512]{2,0,1:T(8,128)(2,1)}, u32[]{:S(2)}) copy-start(bf16[32,3,512]{2,0,1:T(8,128)(2,1)} %param.9) | copy-start | bytes 294916
  18.7 16.5 %all-to-all-start.1 = ((bf16[16,48,128]{2,1,0:T(8,128)(2,1)}), bf16[16,48,128]{2,1,0:T(8,128)(2,1)S(1)}, u32[]{:S(2)}, u32[]{:S(2)}) async-start(bf16[16,48,128]{2,1,0:T(8,128)(2,1)} %get-tuple-element.43), calls=%async_computation.1 | async-start | bytes 393216 | tf_op jit(solution)/shard_map/all_to_all | solution.py:349
  26.1 9.1 %collective-permute-start.2 = (bf16[64,512]{1,0:T(8,128)(2,1)S(1)}, bf16[64,512]{1,0:T(8,128)(2,1)S(1)}, u32[]{:S(2)}, u32[]{:S(2)}) collective-permute-start(bf16[64,512]{1,0:T(8,128)(2,1)S(1)} %get-tuple-element.51), channel_id=1, source_target_pairs={{0,112},{16,0},{32,16},{48,32},{64,48},{80,64},{96,80},{112,96},{1... | collective-permute-start | bytes 196616 | tf_op jit(solution)/shard_map/ppermute | solution.py:325
  28.3 6.9 %collective-permute-start.4 = (bf16[64,512]{1,0:T(8,128)(2,1)S(1)}, bf16[64,512]{1,0:T(8,128)(2,1)S(1)}, u32[]{:S(2)}, u32[]{:S(2)}) collective-permute-start(bf16[64,512]{1,0:T(8,128)(2,1)S(1)} %get-tuple-element.50), channel_id=1, source_target_pairs={{0,16},{16,32},{32,48},{48,64},{64,80},{80,96},{96,112},{112,0},{1... | collective-permute-start | bytes 196616 | tf_op jit(solution)/shard_map/ppermute | solution.py:325
  28.3 6.9 %collective-permute-start.5 = (bf16[32,512]{1,0:T(8,128)(2,1)S(1)}, bf16[32,512]{1,0:T(8,128)(2,1)S(1)}, u32[]{:S(2)}, u32[]{:S(2)}) collective-permute-start(bf16[32,512]{1,0:T(8,128)(2,1)S(1)} %add_convert_fusion.refs_0_), channel_id=1, source_target_pairs={{0,64},{16,80},{32,96},{48,112},{64,0},{80,16},{96,32},{112,48},{1... | collective-permute-start | bytes 98312 | tf_op jit(solution)/shard_map/ppermute | solution.py:325
  36.5 36.6 %all-to-all-start.2 = ((bf16[16,48,512]{2,1,0:T(8,128)(2,1)}), bf16[16,48,512]{2,1,0:T(8,128)(2,1)S(1)}, u32[]{:S(2)}, u32[]{:S(2)}) async-start(bf16[16,48,512]{2,1,0:T(8,128)(2,1)} %pack.1), calls=%async_computation.2 | async-start | bytes 1572864 | tf_op jit(solution)/shard_map/all_to_all | solution.py:365
  43.5 18.2 %collective-permute-start.7 = (bf16[32,16,256]{2,1,0:T(8,128)(2,1)S(1)}, bf16[32,16,256]{2,1,0:T(8,128)(2,1)S(1)}, u32[]{:S(2)}, u32[]{:S(2)}) collective-permute-start(bf16[32,16,256]{2,1,0:T(8,128)(2,1)S(1)} %copy-done.3), channel_id=1, source_target_pairs={{0,1},{1,0},{2,3},{3,2},{4,5},{5,4},{6,7},{7,6},{8,9},{9,8},{10,11... | collective-permute-start | bytes 786440 | tf_op jit(solution)/shard_map/ppermute | solution.py:325
  46.2 31.7 %collective-permute-start.8 = (bf16[24,256]{1,0:T(8,128)(2,1)S(1)}, bf16[24,256]{1,0:T(8,128)(2,1)S(1)}, u32[]{:S(2)}, u32[]{:S(2)}) collective-permute-start(bf16[24,256]{1,0:T(8,128)(2,1)S(1)} %get-tuple-element.48), channel_id=1, source_target_pairs={{0,2},{1,3},{2,4},{3,5},{4,6},{5,7},{6,8},{7,9},{8,10},{9,11},{10,... | collective-permute-start | bytes 36872 | tf_op jit(solution)/shard_map/ppermute | solution.py:335
  48.1 29.8 %collective-permute-start.9 = (bf16[24,256]{1,0:T(8,128)(2,1)S(1)}, bf16[24,256]{1,0:T(8,128)(2,1)S(1)}, u32[]{:S(2)}, u32[]{:S(2)}) collective-permute-start(bf16[24,256]{1,0:T(8,128)(2,1)S(1)} %get-tuple-element.48), channel_id=1, source_target_pairs={{0,3},{1,2},{2,5},{3,4},{4,7},{5,6},{6,9},{7,8},{8,11},{9,10},{10,... | collective-permute-start | bytes 36872 | tf_op jit(solution)/shard_map/ppermute | solution.py:335
  48.2 29.7 %collective-permute-start.10 = (bf16[24,256]{1,0:T(8,128)(2,1)S(1)}, bf16[24,256]{1,0:T(8,128)(2,1)S(1)}, u32[]{:S(2)}, u32[]{:S(2)}) collective-permute-start(bf16[24,256]{1,0:T(8,128)(2,1)S(1)} %get-tuple-element.49), channel_id=1, source_target_pairs={{0,254},{1,255},{2,0},{3,1},{4,2},{5,3},{6,4},{7,5},{8,6},{9,7},{1... | collective-permute-start | bytes 36872 | tf_op jit(solution)/shard_map/ppermute | solution.py:335
  48.8 29.1 %collective-permute-start.11 = (bf16[24,256]{1,0:T(8,128)(2,1)S(1)}, bf16[24,256]{1,0:T(8,128)(2,1)S(1)}, u32[]{:S(2)}, u32[]{:S(2)}) collective-permute-start(bf16[24,256]{1,0:T(8,128)(2,1)S(1)} %get-tuple-element.49), channel_id=1, source_target_pairs={{0,255},{1,254},{2,1},{3,0},{4,3},{5,2},{6,5},{7,4},{8,7},{9,6},{1... | collective-permute-start | bytes 36872 | tf_op jit(solution)/shard_map/ppermute | solution.py:335
  65.8 7.3 %copy-start.7 = (s32[32,8]{0,1:T(8,128)S(1)}, s32[32,8]{0,1:T(8,128)}, u32[]{:S(2)}) copy-start(s32[32,8]{0,1:T(8,128)} %param.14) | copy-start | bytes 3076
  77.4 5.1 %copy-start = (bf16[32,64,512]{2,1,0:T(8,128)(2,1)S(1)}, bf16[32,64,512]{2,1,0:T(8,128)(2,1)}, u32[]{:S(2)}) copy-start(bf16[32,64,512]{2,1,0:T(8,128)(2,1)} %tgt_ref.1) | copy-start | bytes 6291460
  77.4 5.0 %collective-permute-start.6 = (bf16[4,32,128]{2,1,0:T(8,128)(2,1)S(1)}, bf16[4,32,128]{2,1,0:T(8,128)(2,1)S(1)}, u32[]{:S(2)}, u32[]{:S(2)}) collective-permute-start(bf16[4,32,128]{2,1,0:T(8,128)(2,1)S(1)} %get-tuple-element.52.mine_ref), channel_id=1, source_target_pairs={{0,1},{1,0},{2,3},{3,2},{4,5},{5,4},{6,7},{7,6},{8,9},{9,8},{10,11... | collective-permute-start | bytes 98312 | tf_op jit(solution)/shard_map/ppermute | solution.py:325

commit v5 on v4

--- a/solution.py
+++ b/solution.py
@@ -26,6 +26,7 @@
 
 VMEM = pl.BlockSpec(memory_space=pltpu.VMEM)
 SMEM = pl.BlockSpec(memory_space=pltpu.SMEM)
+HBM = pl.BlockSpec(memory_space=pltpu.HBM)
 LIMIT = pltpu.CompilerParams(vmem_limit_bytes=20 * 2**20)
 
 
@@ -46,15 +47,22 @@
     return two[:, :64] + two[:, 64:]
 
 
-def index_kernel(scalar_ref, adm_ref, pts_ref, vec_ref, sel_ref, req_ref, rows_ref, first_ref, last_ref):
+def chunks(source, target, sems, size):
+    copies = [
+        pltpu.make_async_copy(source.at[pl.ds(k, size)], target.at[pl.ds(k, size)], sems.at[k // size])
+        for k in range(0, T, size)
+    ]
+    for copy in copies:
+        copy.start()
+    return copies
+
+
+def index_kernel(scalar_ref, adm_ref, pts_ref, sel_ref, req_ref, rows_ref):
     pts = pts_ref[...].astype(f32)
     blank = jnp.zeros((5, LEAF), f32)
     for t in range(T):
         rows_ref[t] = jnp.concatenate([pts[i, t : t + 1] for i in range(3)] + [blank], 0).astype(bf16)
-    count, own = scalar_ref[0], pl.multiple_of(scalar_ref[1] * HALF, HALF)
-    for ref, t in ((first_ref, 0), (last_ref, count - 1)):
-        ref[:R] = vec_ref[t]
-        ref[R:] = rows_ref[t, :, pl.ds(own, HALF)]
+    count = scalar_ref[0]
     adm = jnp.concatenate([adm_ref[...].astype(f32), jnp.zeros((8, 96), f32)], 1).T
     leaf = jnp.concatenate(
         [jnp.broadcast_to(adm[:T, j : j + 1], (T, 128)) for j in range(J)], 0
@@ -79,30 +87,30 @@
     req_ref[...] = wanted.astype(bf16).reshape(N_PEER, CAP, 128)
 
 
-EDGE_SHAPE = jax.ShapeDtypeStruct((R + 8, HALF), bf16)
-
-
-def index_call(scalars, adm, points, vectors):
+def index_call(scalars, adm, points):
     return pl.pallas_call(
         index_kernel,
         out_shape=(
             jax.ShapeDtypeStruct((ENTRIES, 128), i32),
             jax.ShapeDtypeStruct((N_PEER, CAP, 128), bf16),
             jax.ShapeDtypeStruct((T, 8, LEAF), bf16),
-            EDGE_SHAPE,
-            EDGE_SHAPE,
         ),
-        in_specs=[SMEM, VMEM, VMEM, VMEM],
-        out_specs=(VMEM,) * 5,
+        in_specs=[SMEM, VMEM, VMEM],
+        out_specs=(VMEM,) * 3,
         name="requests",
         compiler_params=LIMIT,
-    )(scalars, adm, points, vectors)
-
-
-def coeff_kernel(n_ref, vec_ref, basis_ref, keep_ref, send_ref, rows):
+    )(scalars, adm, points)
+
+
+def coeff_kernel(n_ref, vec_hbm, basis_hbm, keep_ref, send_ref, rows, vec_ref, basis_ref, sems):
+    vec_copies = chunks(vec_hbm, vec_ref, sems.at[0], 8)
+    basis_copies = chunks(basis_hbm, basis_ref, sems.at[1], 8)
     n = n_ref[0]
     same = (iota((64, 256), 0) >> 4) == (iota((64, 256), 1) >> 6)
     for g in range(T // 4):
+        if g % 2 == 0:
+            vec_copies[g // 2].wait()
+            basis_copies[g // 2].wait()
         lhs = vec_ref[4 * g : 4 * g + 4].reshape(64, HALF)
         rhs = basis_ref[4 * g : 4 * g + 4].reshape(4 * A, HALF)
         rows[64 * g : 64 * g + 64, :64] = folded(jnp.where(same, nt(lhs, rhs), 0.0))
@@ -117,16 +125,23 @@
     return pl.pallas_call(
         coeff_kernel,
         out_shape=(shape, shape),
-        in_specs=[SMEM, VMEM, VMEM],
+        in_specs=[SMEM, HBM, HBM],
         out_specs=(VMEM, VMEM),
-        scratch_shapes=[pltpu.VMEM((T * R, 128), f32)],
+        scratch_shapes=[
+            pltpu.VMEM((T * R, 128), f32),
+            pltpu.VMEM((T, R, HALF), bf16),
+            pltpu.VMEM((T, A, HALF), bf16),
+            pltpu.SemaphoreType.DMA((2, 4)),
+        ],
         name="coeffs",
         compiler_params=LIMIT,
     )(n, vectors, basis)
 
 
 def pack_kernel(z_ref, req_ref, *refs):
-    *pieces, out_ref, table_ref = refs
+    *pieces, out_ref, fits_ref, table_ref = refs
+    refused = jnp.min(req_ref[:, :8].astype(f32)) < 0.0
+    fits_ref[0] = jnp.where(refused, 0, 1)
     for piece, offsets in zip(pieces, OFFSETS):
         for k, offset in enumerate(offsets):
             first = pl.multiple_of(((z_ref[0] + offset) & (N_Z - 1)) * T, T)
@@ -147,16 +162,19 @@
 def pack_call(z, req, pieces):
     return pl.pallas_call(
         pack_kernel,
-        out_shape=jax.ShapeDtypeStruct((N_PEER, CAP, RH * A), bf16),
+        out_shape=(
+            jax.ShapeDtypeStruct((N_PEER, CAP, RH * A), bf16),
+            jax.ShapeDtypeStruct((1,), i32),
+        ),
         in_specs=[SMEM] + [VMEM] * (1 + len(pieces)),
-        out_specs=VMEM,
+        out_specs=(VMEM, SMEM),
         scratch_shapes=[pltpu.VMEM((COLUMN, RH * A), bf16)],
         name="pack",
         compiler_params=LIMIT,
     )(z, req, *pieces)
 
 
-def couple(picked, couple_ref, out_ref):
+def couple(picked, couple_ref, out_ref, copies=()):
     lows = [picked[j * T : (j + 1) * T] for j in range(J)]
     by_rhs = []
     for r in range(RH):
@@ -169,6 +187,8 @@
         total = jnp.zeros((16 * RH, A), f32)
         for g in range(4):
             first = 16 * h + 4 * g
+            if copies and first % 8 == 0:
+                copies[first // 8].wait()
             rhs = couple_ref[first : first + 4].reshape(4 * A, J * A)
             total = total + folded(jnp.where(row_t == col_t + 4 * g, nt(lhs, rhs), 0.0))
         total = total.reshape(RH, 16, A)
@@ -177,14 +197,16 @@
             out_ref[r // 2, 16 * h : 16 * h + 16, :] = pair.astype(bf16)
 
 
-def select_kernel(sel_ref, got_ref, couple_ref, out_ref):
+def select_kernel(sel_ref, got_ref, couple_hbm, out_ref, couple_ref, sems):
+    copies = chunks(couple_hbm, couple_ref, sems, 8)
     slots = N_PEER * CAP
     sel = sel_ref[...]
     lanes = iota((ENTRIES, 128), 1)
     hot = jnp.concatenate(
         [jnp.where(sel == lanes + 128 * k, 1.0, 0.0) for k in range(slots // 128)], 1
     )
-    couple(nn(hot.astype(bf16), got_ref[...].reshape(slots, RH * A)), couple_ref, out_ref)
+    picked = nn(hot.astype(bf16), got_ref[...].reshape(slots, RH * A))
+    couple(picked, couple_ref, out_ref, copies)
 
 
 TC_SHAPE = jax.ShapeDtypeStruct((RH // 2, T, 2 * A), bf16)
@@ -194,8 +216,9 @@
     return pl.pallas_call(
         select_kernel,
         out_shape=TC_SHAPE,
-        in_specs=[VMEM, VMEM, VMEM],
+        in_specs=[VMEM, VMEM, HBM],
         out_specs=VMEM,
+        scratch_shapes=[pltpu.VMEM((T, A, J * A), bf16), pltpu.SemaphoreType.DMA((4,))],
         name="select",
         compiler_params=LIMIT,
     )(sel, got, couplings)
@@ -216,11 +239,18 @@
     )(picked, couplings)
 
 
-def near_kernel(leaves, edges, scalar_ref, pts_ref, vec_ref, other_ref, *refs):
-    edge_refs, out_ref, kerns = refs[: 4 * edges], refs[-5], refs[-4:]
+def near_kernel(leaves, edges, group, scalar_ref, pts_ref, vec_ref, other_ref, *refs):
+    edge_refs, kerns, outs = refs[: 2 * edges], refs[-group:], refs[:-group]
+    send_refs = () if edges or len(outs) < 3 else outs[-2:]
+    out_ref = outs[-3] if send_refs else outs[-1]
     count, n = scalar_ref[0], scalar_ref[1]
     own = pl.multiple_of(n * HALF, HALF)
     other = pl.multiple_of((1 - n) * HALF, HALF)
+
+    for ref, t in zip(send_refs, (0, count - 1)):
+        ref[:R, pl.ds(own, HALF)] = vec_ref[t]
+        ref[:R, pl.ds(other, HALF)] = other_ref[t]
+        ref[R:] = pts_ref[t]
 
     def sources(t):
         return (t + T - 1) & (T - 1), t, (t + 1) & (T - 1)
@@ -229,7 +259,7 @@
         if not edges:
             return values
         for k, (u, at) in enumerate(((0, 0), (2, count - 1))):
-            halo = [edge_refs[2 * k + h][rows] for h in range(2)]
+            halo = [edge_refs[k][rows, pl.ds(h, HALF)] for h in (own, other)]
             values[u] = [jnp.where(t == at, a, b) for a, b in zip(halo, values[u])]
         return values
 
@@ -260,7 +290,6 @@
         return jnp.where(i < T, i, count - 1)
 
     steps = T - leaves[1] + leaves[0] + 1 if edges else leaves[1] - leaves[0]
-    group = 3 if edges else 4
     fill(leaf(0), kerns[0])
 
     def body(i, _):
@@ -276,12 +305,15 @@
     size = T - leaves[1] + leaves[0] + 1 if halos else leaves[1] - leaves[0]
     bases = () if base is None else (base,)
     count = len(args) + len(halos)
-    return pl.pallas_call(
-        lambda *refs: near_kernel(leaves, bool(halos), *refs),
-        out_shape=jax.ShapeDtypeStruct((T, R, HALF), f32),
+    group = size if halos else 8
+    field = jax.ShapeDtypeStruct((T, R, HALF), f32)
+    edge = jax.ShapeDtypeStruct((R + 8, LEAF), bf16)
+    return pl.pallas_call(
+        lambda *refs: near_kernel(leaves, bool(halos), group, *refs),
+        out_shape=field if bases else (field, edge, edge),
         in_specs=[SMEM] + [VMEM] * (count - 1 + len(bases)),
-        out_specs=VMEM,
-        scratch_shapes=[pltpu.VMEM((HALF, 3 * LEAF), bf16)] * 4,
+        out_specs=VMEM if bases else (VMEM,) * 3,
+        scratch_shapes=[pltpu.VMEM((HALF, 3 * LEAF), bf16)] * group,
         input_output_aliases={count: 0} if bases else {},
         cost_estimate=pl.CostEstimate(
             flops=size * 200_000_000, bytes_accessed=2_000_000, transcendentals=0
@@ -330,13 +362,6 @@
     return lax.all_to_all(copies, axis, split_axis=0, concat_axis=0, tiled=True)
 
 
-def onward(array, by, flip):
-    size = 2 * lax.axis_size(WIDE)
-    return lax.ppermute(
-        array, (*WIDE, "n"), [(i, ((i // 2 * 2 + 2 * by) % size) + (i % 2 ^ flip)) for i in range(size)]
-    )
-
-
 def body(points, vectors, counts, src_basis, tgt_basis, adm_src, couplings):
     n = lax.axis_index("n").astype(i32)
     z = lax.axis_index("z").astype(i32)
@@ -345,7 +370,7 @@
     keep, send = coeff_call(n[None], vectors, src_basis)
     came = shifted(send, "n", 1)
     other = shifted(vectors, "n", 1)
-    sel, req, rows, first, last = index_call(scalars, adm_src.T, points.transpose(1, 0, 2), vectors)
+    sel, req, rows = index_call(scalars, adm_src.T, points.transpose(1, 0, 2))
     asked = lax.all_to_all(req, PEERS, split_axis=0, concat_axis=0, tiled=True)
 
     coeffs = (keep + came).astype(bf16)
@@ -356,13 +381,14 @@
     odd_down = shifted(jnp.concatenate([coeffs, down]), "z", 1)
     pieces = coeffs, up, down, across, odd_up, odd_down
 
-    halos = tuple(onward(edge, by, flip) for edge, by in ((last, 1), (first, -1)) for flip in range(2))
     near_args = (scalars, rows, vectors, other)
-    near = near_call((4, 12), near_args)
+    near, first, last = near_call((4, 12), near_args)
+    halos = shifted(last, WIDE, 1), shifted(first, WIDE, -1)
     near = near_call((12, 28), near_args, base=near)
     near = near_call((4, 28), near_args, halos, near)
 
-    got = lax.all_to_all(pack_call(z[None], asked, pieces), PEERS, split_axis=0, concat_axis=0, tiled=True)
+    packed, fits = pack_call(z[None], asked, pieces)
+    got = lax.all_to_all(packed, PEERS, split_axis=0, concat_axis=0, tiled=True)
     mine = select_call(sel, got, couplings)
 
     def every(mine, pieces, couplings):
@@ -375,8 +401,7 @@
         hot = (place[:, None] == jnp.arange(N_PEER * COLUMN, dtype=i32)[None, :]).astype(bf16)
         return couple_call(jnp.dot(hot, whole, preferred_element_type=f32), couplings)
 
-    fits = jnp.min(asked[:, 0, 0]) >= 0
-    mine = lax.cond(fits, lambda mine, *_: mine, every, mine, pieces, couplings)
+    mine = lax.cond(fits[0] != 0, lambda mine, *_: mine, every, mine, pieces, couplings)
     theirs = shifted(mine, "n", 1)
     return final_call(scalars, mine, theirs, tgt_basis, near)
 

time: 84.7 us -> 88.9 us (1.050)
  the two profiles are of different devices: /device:TPU:1 before, /device:TPU:8 now
where the time goes in v5:
time: 88.9 us; the launch traced here: 88.4 us
  starting transfers between devices  35.8 us (40%)
  Pallas kernels  23.7 us (27%)
  waiting for transfers between devices  23.6 us (27%)
  local copies, waits for them, and re-layouts  3.84 us (4%)
  between operations  1.41 us (2%)
    ppermute x10, starting transfers between devices, shifted(): lax.ppermute(array, axis, [(i, (i + by) % devices) for i in range(devices)])  24.3 us
    ppermute x10, waiting for transfers between devices, shifted(): lax.ppermute(array, axis, [(i, (i + by) % devices) for i in range(devices)])  23.6 us
    pallas_call x3, Pallas kernels, near_call(): pl.pallas_call(lambda *refs: near_kernel(leaves, bool(halos), group, *ref...  13.3 us
    all_to_all x1, starting transfers between devices, body(): asked = lax.all_to_all(req, PEERS, split_axis=0, concat_axis=0, tiled=True)  5.77 us
    all_to_all x1, starting transfers between devices, body(): got = lax.all_to_all(packed, PEERS, split_axis=0, concat_axis=0, tiled=True)  5.73 us
    pallas_call x1, Pallas kernels, select_call(): pl.pallas_call(select_kernel, out_shape=TC_SHAPE, in_specs=[VMEM, VMEM, H...  3.46 us
    unnamed x12, local copies, waits for them, and re-layouts  3.08 us
    pallas_call x1, Pallas kernels, index_call(): pl.pallas_call(index_kernel, out_shape=(jax.ShapeDtypeStruct((ENTRIES, 12...  2.21 us
  transfers between devices with their start and end apart: 12, of which 4 were waited for; matrix products, arithmetic and copies ran while one was open for 1% of the time, Pallas kernels for 22%

profile of v5, /device:TPU:8, one launch (start us, length us, event | category | flops | bytes accessed | tf_op | source)
XLA Modules:
  0.0 88.4 jit_solution(11922925776913358889)
XLA Ops:
  0.0 1.2 %copy-done.1 = bf16[32,64,256]{2,1,0:T(8,128)(2,1)S(1)} copy-done((bf16[32,64,256]{2,1,0:T(8,128)(2,1)S(1)}, bf16[32,64,256]{2,1,0:T(8,128)(2,1)}, u32[]{:S(2)}) %copy-start.1) | copy-done | bytes 1048600
  1.2 0.9 %copy-done.2 = bf16[32,16,256]{2,1,0:T(8,128)(2,1)S(1)} copy-done((bf16[32,16,256]{2,1,0:T(8,128)(2,1)S(1)}, bf16[32,16,256]{2,1,0:T(8,128)(2,1)}, u32[]{:S(2)}) %copy-start.2) | copy-done | bytes 262168
  2.2 1.7 %coeffs.1 = (f32[32,512]{1,0:T(8,128)S(1)}, f32[32,512]{1,0:T(8,128)S(1)}) custom-call(s32[1]{0:T(128)} %bitcast.2.n_ref, bf16[32,16,256]{2,1,0:T(8,128)(2,1)S(1)} %copy-done.2, bf16[32,64,256]{2,1,0:T(8,128)(2,1)S(1)} %copy-done.1), custom_call_target="tpu_custom_call" | custom-call | tf_op jit(solution)/shard_map/coeffs/pallas_call | solution.py:125
  3.9 2.4 %collective-permute-start = (f32[32,512]{1,0:T(8,128)S(1)}, f32[32,512]{1,0:T(8,128)S(1)}, u32[]{:S(2)}, u32[]{:S(2)}) collective-permute-start(f32[32,512]{1,0:T(8,128)S(1)} %get-tuple-element.48), channel_id=1, source_target_pairs={{0,1},{1,0},{2,3},{3,2},{4,5},{5,4},{6,7},{7,6},{8,9},{9,8},{10,11... | collective-permute-start | bytes 196616 | tf_op jit(solution)/shard_map/ppermute | solution.py:357
  6.9 2.8 %collective-permute-done = f32[32,512]{1,0:T(8,128)S(1)} collective-permute-done((f32[32,512]{1,0:T(8,128)S(1)}, f32[32,512]{1,0:T(8,128)S(1)}, u32[]{:S(2)}, u32[]{:S(2)}) %collective-permute-start) | collective-permute-done | bytes 65568 | tf_op jit(solution)/shard_map/ppermute | solution.py:357
  9.8 6.4 %collective-permute-start.1 = (bf16[32,512]{1,0:T(8,128)(2,1)S(1)}, bf16[32,512]{1,0:T(8,128)(2,1)S(1)}, u32[]{:S(2)}, u32[]{:S(2)}) collective-permute-start(bf16[32,512]{1,0:T(8,128)(2,1)S(1)} %add_convert_fusion.refs_0_), channel_id=1, source_target_pairs={{0,96},{16,112},{32,0},{48,16},{64,32},{80,48},{96,64},{112,80},{1... | collective-permute-start | bytes 98312 | tf_op jit(solution)/shard_map/ppermute | solution.py:357
  16.1 0.0 collective-permute-start.2
  16.1 0.1 pad_add_fusion.scalar_ref.refs_0_
  16.2 0.9 %copy-done.4 = bf16[32,3,512]{2,0,1:T(8,128)(2,1)S(1)} copy-done((bf16[32,3,512]{2,0,1:T(8,128)(2,1)S(1)}, bf16[32,3,512]{2,0,1:T(8,128)(2,1)}, u32[]{:S(2)}) %copy-start.4) | copy-done | bytes 98328
  17.1 2.2 %requests.1 = (s32[256,128]{1,0:T(8,128)S(1)}, bf16[16,48,128]{2,1,0:T(8,128)(2,1)}, bf16[32,8,512]{2,1,0:T(8,128)(2,1)S(1)}) custom-call(s32[2]{0:T(128)S(1)} %pad_add_fusion.scalar_ref.refs_0_, s32[8,32]{1,0:T(8,128)} %bitcast.10, bf16[3,32,512]{2,1,0:T(8,128)(2,1)S(1)} %bitcast.9), custom_call_target="tpu_custom_call" | custom-call | tf_op jit(solution)/shard_map/requests/pallas_call | solution.py:91
  19.3 5.8 %all-to-all-start.1 = ((bf16[16,48,128]{2,1,0:T(8,128)(2,1)}), bf16[16,48,128]{2,1,0:T(8,128)(2,1)S(1)}, u32[]{:S(2)}, u32[]{:S(2)}) async-start(bf16[16,48,128]{2,1,0:T(8,128)(2,1)} %get-tuple-element.46), calls=%async_computation.1 | async-start | bytes 393216 | tf_op jit(solution)/shard_map/all_to_all | solution.py:374
  25.1 0.0 collective-permute-done.1.refs_1_
  25.1 3.8 %collective-permute-start.4 = (bf16[64,512]{1,0:T(8,128)(2,1)S(1)}, bf16[64,512]{1,0:T(8,128)(2,1)S(1)}, u32[]{:S(2)}, u32[]{:S(2)}) collective-permute-start(bf16[64,512]{1,0:T(8,128)(2,1)S(1)} %get-tuple-element.57), channel_id=1, source_target_pairs={{0,112},{16,0},{32,16},{48,32},{64,48},{80,64},{96,80},{112,96},{1... | collective-permute-start | bytes 196616 | tf_op jit(solution)/shard_map/ppermute | solution.py:357
  28.9 2.1 %collective-permute-start.3 = (bf16[32,512]{1,0:T(8,128)(2,1)S(1)}, bf16[32,512]{1,0:T(8,128)(2,1)S(1)}, u32[]{:S(2)}, u32[]{:S(2)}) collective-permute-start(bf16[32,512]{1,0:T(8,128)(2,1)S(1)} %add_convert_fusion.refs_0_), channel_id=1, source_target_pairs={{0,64},{16,80},{32,96},{48,112},{64,0},{80,16},{96,32},{112,48},{1... | collective-permute-start | bytes 98312 | tf_op jit(solution)/shard_map/ppermute | solution.py:357
  31.0 5.7 %collective-permute-done.3.refs_3_ = bf16[32,512]{1,0:T(8,128)(2,1)S(1)} collective-permute-done((bf16[32,512]{1,0:T(8,128)(2,1)S(1)}, bf16[32,512]{1,0:T(8,128)(2,1)S(1)}, u32[]{:S(2)}, u32[]{:S(2)}) %collective-permute-start.3) | collective-permute-done | bytes 32800 | tf_op jit(solution)/shard_map/ppermute | solution.py:357
  36.7 0.0 collective-permute-done.4.refs_4_
  36.7 0.0 collective-permute-done.5.refs_5_
  36.7 0.0 all-to-all-done.1.req_ref
  36.7 1.3 %pack.1 = (bf16[16,48,512]{2,1,0:T(8,128)(2,1)}, s32[1]{0:T(128)}) custom-call(s32[1]{0:T(128)} %bitcast.3.z_ref, bf16[16,48,128]{2,1,0:T(8,128)(2,1)S(1)} %all-to-all-done.1.req_ref, bf16[32,512]{1,0:T(8,128)(2,1)S(1)} %add_convert_fusion.refs_0_, bf16[32,512]{1,0:T(8,128)(2,1)S(1)} %collective-permute-done.1.refs_1_, ...), custom_call_target="tpu_custom_call" | custom-call | tf_op jit(solution)/shard_map/pack/pallas_call | solution.py:163
  38.0 5.7 %all-to-all-start.2 = ((bf16[16,48,512]{2,1,0:T(8,128)(2,1)}), bf16[16,48,512]{2,1,0:T(8,128)(2,1)S(1)}, u32[]{:S(2)}, u32[]{:S(2)}) async-start(bf16[16,48,512]{2,1,0:T(8,128)(2,1)} %get-tuple-element.51), calls=%async_computation.2 | async-start | bytes 1572864 | tf_op jit(solution)/shard_map/all_to_all | solution.py:391
  43.8 2.4 %collective-permute-start.7 = (bf16[32,16,256]{2,1,0:T(8,128)(2,1)S(1)}, bf16[32,16,256]{2,1,0:T(8,128)(2,1)S(1)}, u32[]{:S(2)}, u32[]{:S(2)}) collective-permute-start(bf16[32,16,256]{2,1,0:T(8,128)(2,1)S(1)} %copy-done.3), channel_id=1, source_target_pairs={{0,1},{1,0},{2,3},{3,2},{4,5},{5,4},{6,7},{7,6},{8,9},{9,8},{10,11... | collective-permute-start | bytes 786440 | tf_op jit(solution)/shard_map/ppermute | solution.py:357
  46.8 14.5 %collective-permute-done.7.refs_3_ = bf16[32,16,256]{2,1,0:T(8,128)(2,1)S(1)} collective-permute-done((bf16[32,16,256]{2,1,0:T(8,128)(2,1)S(1)}, bf16[32,16,256]{2,1,0:T(8,128)(2,1)S(1)}, u32[]{:S(2)}, u32[]{:S(2)}) %collective-permute-start.7) | collective-permute-done | bytes 262176 | tf_op jit(solution)/shard_map/ppermute | solution.py:357
  61.3 3.2 %near.3 = (f32[32,16,256]{2,1,0:T(8,128)S(1)}, bf16[24,512]{1,0:T(8,128)(2,1)S(1)}, bf16[24,512]{1,0:T(8,128)(2,1)S(1)}) custom-call(s32[2]{0:T(128)S(1)} %pad_add_fusion.scalar_ref.refs_0_, bf16[32,8,512]{2,1,0:T(8,128)(2,1)S(1)} %get-tuple-element.52.refs_1_, bf16[32,16,256]{2,1,0:T(8,128)(2,1)S(1)} %copy-done.3, ...), custom_call_target="tpu_custom_call" | custom-call | flops 1600000000 | bytes 2000000 | tf_op jit(solution)/shard_map/near/pallas_call | solution.py:311
  64.5 6.0 %collective-permute-start.9 = (bf16[24,512]{1,0:T(8,128)(2,1)S(1)}, bf16[24,512]{1,0:T(8,128)(2,1)S(1)}, u32[]{:S(2)}, u32[]{:S(2)}) collective-permute-start(bf16[24,512]{1,0:T(8,128)(2,1)S(1)} %get-tuple-element.54), channel_id=1, source_target_pairs={{0,254},{2,0},{4,2},{6,4},{8,6},{10,8},{12,10},{14,12},{16,14},{18... | collective-permute-start | bytes 73736 | tf_op jit(solution)/shard_map/ppermute | solution.py:357
  70.5 6.5 %near.4.refs_6_ = f32[32,16,256]{2,1,0:T(8,128)S(1)} custom-call(s32[2]{0:T(128)S(1)} %pad_add_fusion.scalar_ref.refs_0_, bf16[32,8,512]{2,1,0:T(8,128)(2,1)S(1)} %get-tuple-element.52.refs_1_, bf16[32,16,256]{2,1,0:T(8,128)(2,1)S(1)} %copy-done.3, bf16[32,16,256]{2,1,0:T(8,128)(2,1)S(1)} %collective-permute-done.7.refs_3_, ...), custom_call_target="tpu_custom_call", output_to_operand_aliasing={{}: (4, {})} | custom-call | flops 3200000000 | bytes 2000000 | tf_op jit(solution)/shard_map/near/pallas_call | solution.py:311
  77.1 3.5 %select.3 = bf16[4,32,128]{2,1,0:T(8,128)(2,1)} custom-call(s32[256,128]{1,0:T(8,128)S(1)} %get-tuple-element.50.sel_ref, bf16[16,48,512]{2,1,0:T(8,128)(2,1)S(1)} %all-to-all-done.2.got_ref, bf16[32,64,512]{2,1,0:T(8,128)(2,1)} %couple_hbm.1), custom_call_target="tpu_custom_call" | custom-call | tf_op jit(solution)/shard_map/select/pallas_call | solution.py:216
  80.5 0.8 conditional.1
  80.6 0.8 copy.26
  81.3 1.2 %collective-permute-start.6 = (bf16[4,32,128]{2,1,0:T(8,128)(2,1)S(1)}, bf16[4,32,128]{2,1,0:T(8,128)(2,1)S(1)}, u32[]{:S(2)}, u32[]{:S(2)}) collective-permute-start(bf16[4,32,128]{2,1,0:T(8,128)(2,1)S(1)} %get-tuple-element.58.mine_ref), channel_id=1, source_target_pairs={{0,1},{1,0},{2,3},{3,2},{4,5},{5,4},{6,7},{7,6},{8,9},{9,8},{10,11... | collective-permute-start | bytes 98312 | tf_op jit(solution)/shard_map/ppermute | solution.py:357
  82.6 3.6 %near.5.near_ref = f32[32,16,256]{2,1,0:T(8,128)S(1)} custom-call(s32[2]{0:T(128)S(1)} %pad_add_fusion.scalar_ref.refs_0_, bf16[32,8,512]{2,1,0:T(8,128)(2,1)S(1)} %get-tuple-element.52.refs_1_, bf16[32,16,256]{2,1,0:T(8,128)(2,1)S(1)} %copy-done.3, bf16[32,16,256]{2,1,0:T(8,128)(2,1)S(1)} %collective-permute-done.7.refs_3_, ...), custom_call_target="tpu_custom_call", output_to_operand_aliasing={{}: (6, {})} | custom-call | flops 1800000000 | bytes 2000000 | tf_op jit(solution)/shard_map/near/pallas_call | solution.py:311
  86.1 0.6 collective-permute-done.6.theirs_ref
  86.8 1.7 %final.1 = bf16[32,16,256]{2,1,0:T(8,128)(2,1)} custom-call(s32[2]{0:T(128)S(1)} %pad_add_fusion.scalar_ref.refs_0_, bf16[4,32,128]{2,1,0:T(8,128)(2,1)S(1)} %get-tuple-element.58.mine_ref, bf16[4,32,128]{2,1,0:T(8,128)(2,1)S(1)} %collective-permute-done.6.theirs_ref, bf16[32,64,512]{2,1,0:T(8,128)(2,1)S(1)} %copy-done, f32[32,16,256]{2,1,0:T(8,128)S(1)} %near.5.near_ref), custom_call_target="tpu_custom_call" | custom-call | tf_op jit(solution)/shard_map/final/pallas_call | solution.py:344
  (17 shorter events, 0.1 us)
Async XLA Ops:
  0.0 1.2 %copy-start.1 = (bf16[32,64,256]{2,1,0:T(8,128)(2,1)S(1)}, bf16[32,64,256]{2,1,0:T(8,128)(2,1)}, u32[]{:S(2)}) copy-start(bf16[32,64,256]{2,1,0:T(8,128)(2,1)} %basis_hbm.1) | copy-start | bytes 3145732
  1.2 0.9 %copy-start.2 = (bf16[32,16,256]{2,1,0:T(8,128)(2,1)S(1)}, bf16[32,16,256]{2,1,0:T(8,128)(2,1)}, u32[]{:S(2)}) copy-start(bf16[32,16,256]{2,1,0:T(8,128)(2,1)} %refs_2_.5) | copy-start | bytes 786436
  2.2 41.6 %copy-start.3 = (bf16[32,16,256]{2,1,0:T(8,128)(2,1)S(1)}, bf16[32,16,256]{2,1,0:T(8,128)(2,1)}, u32[]{:S(2)}) copy-start(bf16[32,16,256]{2,1,0:T(8,128)(2,1)} %refs_2_.5) | copy-start | bytes 786436
  3.9 5.9 %collective-permute-start = (f32[32,512]{1,0:T(8,128)S(1)}, f32[32,512]{1,0:T(8,128)S(1)}, u32[]{:S(2)}, u32[]{:S(2)}) collective-permute-start(f32[32,512]{1,0:T(8,128)S(1)} %get-tuple-element.48), channel_id=1, source_target_pairs={{0,1},{1,0},{2,3},{3,2},{4,5},{5,4},{6,7},{7,6},{8,9},{9,8},{10,11... | collective-permute-start | bytes 196616 | tf_op jit(solution)/shard_map/ppermute | solution.py:357
  9.8 15.3 %collective-permute-start.1 = (bf16[32,512]{1,0:T(8,128)(2,1)S(1)}, bf16[32,512]{1,0:T(8,128)(2,1)S(1)}, u32[]{:S(2)}, u32[]{:S(2)}) collective-permute-start(bf16[32,512]{1,0:T(8,128)(2,1)S(1)} %add_convert_fusion.refs_0_), channel_id=1, source_target_pairs={{0,96},{16,112},{32,0},{48,16},{64,32},{80,48},{96,64},{112,80},{1... | collective-permute-start | bytes 98312 | tf_op jit(solution)/shard_map/ppermute | solution.py:357
  16.1 9.0 %collective-permute-start.2 = (bf16[32,512]{1,0:T(8,128)(2,1)S(1)}, bf16[32,512]{1,0:T(8,128)(2,1)S(1)}, u32[]{:S(2)}, u32[]{:S(2)}) collective-permute-start(bf16[32,512]{1,0:T(8,128)(2,1)S(1)} %add_convert_fusion.refs_0_), channel_id=1, source_target_pairs={{0,32},{16,48},{32,64},{48,80},{64,96},{80,112},{96,0},{112,16},{1... | collective-permute-start | bytes 98312 | tf_op jit(solution)/shard_map/ppermute | solution.py:357
  16.2 0.9 %copy-start.4 = (bf16[32,3,512]{2,0,1:T(8,128)(2,1)S(1)}, bf16[32,3,512]{2,0,1:T(8,128)(2,1)}, u32[]{:S(2)}) copy-start(bf16[32,3,512]{2,0,1:T(8,128)(2,1)} %param.9) | copy-start | bytes 294916
  19.3 17.4 %all-to-all-start.1 = ((bf16[16,48,128]{2,1,0:T(8,128)(2,1)}), bf16[16,48,128]{2,1,0:T(8,128)(2,1)S(1)}, u32[]{:S(2)}, u32[]{:S(2)}) async-start(bf16[16,48,128]{2,1,0:T(8,128)(2,1)} %get-tuple-element.46), calls=%async_computation.1 | async-start | bytes 393216 | tf_op jit(solution)/shard_map/all_to_all | solution.py:374
  25.1 11.6 %collective-permute-start.4 = (bf16[64,512]{1,0:T(8,128)(2,1)S(1)}, bf16[64,512]{1,0:T(8,128)(2,1)S(1)}, u32[]{:S(2)}, u32[]{:S(2)}) collective-permute-start(bf16[64,512]{1,0:T(8,128)(2,1)S(1)} %get-tuple-element.57), channel_id=1, source_target_pairs={{0,112},{16,0},{32,16},{48,32},{64,48},{80,64},{96,80},{112,96},{1... | collective-permute-start | bytes 196616 | tf_op jit(solution)/shard_map/ppermute | solution.py:357
  28.9 7.8 %collective-permute-start.5 = (bf16[64,512]{1,0:T(8,128)(2,1)S(1)}, bf16[64,512]{1,0:T(8,128)(2,1)S(1)}, u32[]{:S(2)}, u32[]{:S(2)}) collective-permute-start(bf16[64,512]{1,0:T(8,128)(2,1)S(1)} %get-tuple-element.56), channel_id=1, source_target_pairs={{0,16},{16,32},{32,48},{48,64},{64,80},{80,96},{96,112},{112,0},{1... | collective-permute-start | bytes 196616 | tf_op jit(solution)/shard_map/ppermute | solution.py:357
  28.9 7.8 %collective-permute-start.3 = (bf16[32,512]{1,0:T(8,128)(2,1)S(1)}, bf16[32,512]{1,0:T(8,128)(2,1)S(1)}, u32[]{:S(2)}, u32[]{:S(2)}) collective-permute-start(bf16[32,512]{1,0:T(8,128)(2,1)S(1)} %add_convert_fusion.refs_0_), channel_id=1, source_target_pairs={{0,64},{16,80},{32,96},{48,112},{64,0},{80,16},{96,32},{112,48},{1... | collective-permute-start | bytes 98312 | tf_op jit(solution)/shard_map/ppermute | solution.py:357
  38.0 39.0 %all-to-all-start.2 = ((bf16[16,48,512]{2,1,0:T(8,128)(2,1)}), bf16[16,48,512]{2,1,0:T(8,128)(2,1)S(1)}, u32[]{:S(2)}, u32[]{:S(2)}) async-start(bf16[16,48,512]{2,1,0:T(8,128)(2,1)} %get-tuple-element.51), calls=%async_computation.2 | async-start | bytes 1572864 | tf_op jit(solution)/shard_map/all_to_all | solution.py:391
  43.8 17.5 %collective-permute-start.7 = (bf16[32,16,256]{2,1,0:T(8,128)(2,1)S(1)}, bf16[32,16,256]{2,1,0:T(8,128)(2,1)S(1)}, u32[]{:S(2)}, u32[]{:S(2)}) collective-permute-start(bf16[32,16,256]{2,1,0:T(8,128)(2,1)S(1)} %copy-done.3), channel_id=1, source_target_pairs={{0,1},{1,0},{2,3},{3,2},{4,5},{5,4},{6,7},{7,6},{8,9},{9,8},{10,11... | collective-permute-start | bytes 786440 | tf_op jit(solution)/shard_map/ppermute | solution.py:357
  64.5 18.0 %collective-permute-start.8 = (bf16[24,512]{1,0:T(8,128)(2,1)S(1)}, bf16[24,512]{1,0:T(8,128)(2,1)S(1)}, u32[]{:S(2)}, u32[]{:S(2)}) collective-permute-start(bf16[24,512]{1,0:T(8,128)(2,1)S(1)} %get-tuple-element.53), channel_id=1, source_target_pairs={{0,2},{2,4},{4,6},{6,8},{8,10},{10,12},{12,14},{14,16},{16,18},{18... | collective-permute-start | bytes 73736 | tf_op jit(solution)/shard_map/ppermute | solution.py:357
  64.5 18.0 %collective-permute-start.9 = (bf16[24,512]{1,0:T(8,128)(2,1)S(1)}, bf16[24,512]{1,0:T(8,128)(2,1)S(1)}, u32[]{:S(2)}, u32[]{:S(2)}) collective-permute-start(bf16[24,512]{1,0:T(8,128)(2,1)S(1)} %get-tuple-element.54), channel_id=1, source_target_pairs={{0,254},{2,0},{4,2},{6,4},{8,6},{10,8},{12,10},{14,12},{16,14},{18... | collective-permute-start | bytes 73736 | tf_op jit(solution)/shard_map/ppermute | solution.py:357
  70.5 10.0 %copy-start.6 = (s32[32,8]{0,1:T(8,128)S(1)}, s32[32,8]{0,1:T(8,128)}, u32[]{:S(2)}) copy-start(s32[32,8]{0,1:T(8,128)} %param.14) | copy-start | bytes 3076
  81.3 5.4 %copy-start = (bf16[32,64,512]{2,1,0:T(8,128)(2,1)S(1)}, bf16[32,64,512]{2,1,0:T(8,128)(2,1)}, u32[]{:S(2)}) copy-start(bf16[32,64,512]{2,1,0:T(8,128)(2,1)} %tgt_ref.1) | copy-start | bytes 6291460
  81.3 5.4 %collective-permute-start.6 = (bf16[4,32,128]{2,1,0:T(8,128)(2,1)S(1)}, bf16[4,32,128]{2,1,0:T(8,128)(2,1)S(1)}, u32[]{:S(2)}, u32[]{:S(2)}) collective-permute-start(bf16[4,32,128]{2,1,0:T(8,128)(2,1)S(1)} %get-tuple-element.58.mine_ref), channel_id=1, source_target_pairs={{0,1},{1,0},{2,3},{3,2},{4,5},{5,4},{6,7},{7,6},{8,9},{9,8},{10,11... | collective-permute-start | bytes 98312 | tf_op jit(solution)/shard_map/ppermute | solution.py:357

commit v6 on v5

--- a/solution.py
+++ b/solution.py
@@ -20,7 +20,8 @@
 N_Z, N_PEER = 8, 16
 CAP = 48
 ENTRIES = T * J
-OFFSETS = (0,), (2,), (-2,), (4,), (1, 3), (-1, -3)
+OFFSETS = (0,), (-1,), (1,), (2, 3, 4), (-2, -3)
+SENT = T * R + 4 * T
 COLUMN = N_Z * T
 bf16, f32, i32 = jnp.bfloat16, jnp.float32, jnp.int32
 
@@ -102,37 +103,39 @@
     )(scalars, adm, points)
 
 
-def coeff_kernel(n_ref, vec_hbm, basis_hbm, keep_ref, send_ref, rows, vec_ref, basis_ref, sems):
-    vec_copies = chunks(vec_hbm, vec_ref, sems.at[0], 8)
-    basis_copies = chunks(basis_hbm, basis_ref, sems.at[1], 8)
+def coeff_kernel(n_ref, vec_ref, basis_ref, keep_ref, send_ref, rows):
     n = n_ref[0]
     same = (iota((64, 256), 0) >> 4) == (iota((64, 256), 1) >> 6)
     for g in range(T // 4):
-        if g % 2 == 0:
-            vec_copies[g // 2].wait()
-            basis_copies[g // 2].wait()
         lhs = vec_ref[4 * g : 4 * g + 4].reshape(64, HALF)
+        send_ref[64 * g : 64 * g + 64] = lhs
         rhs = basis_ref[4 * g : 4 * g + 4].reshape(4 * A, HALF)
         rows[64 * g : 64 * g + 64, :64] = folded(jnp.where(same, nt(lhs, rhs), 0.0))
-    for out, first in ((send_ref, (1 - n) * RH), (keep_ref, n * RH)):
+    for mine, first in ((False, (1 - n) * RH), (True, n * RH)):
         for r in range(0, RH, 2):
             pair = [rows[pl.ds(first + r + k, T, stride=R), :][:, :64] for k in range(2)]
-            out[:, r * A : (r + 2) * A] = jnp.concatenate(pair, 1)
+            value = jnp.concatenate(pair, 1)
+            row, lane = r * A // HALF * T, r * A % HALF
+            if mine:
+                keep_ref[row : row + T, lane : lane + 2 * A] = value
+            else:
+                high = value.astype(bf16)
+                row += T * R
+                send_ref[row : row + T, lane : lane + 2 * A] = high
+                row += 2 * T
+                send_ref[row : row + T, lane : lane + 2 * A] = (value - high.astype(f32)).astype(bf16)
 
 
 def coeff_call(n, vectors, basis):
-    shape = jax.ShapeDtypeStruct((T, RH * A), f32)
     return pl.pallas_call(
         coeff_kernel,
-        out_shape=(shape, shape),
-        in_specs=[SMEM, HBM, HBM],
+        out_shape=(
+            jax.ShapeDtypeStruct((2 * T, HALF), f32),
+            jax.ShapeDtypeStruct((SENT, HALF), bf16),
+        ),
+        in_specs=[SMEM, VMEM, VMEM],
         out_specs=(VMEM, VMEM),
-        scratch_shapes=[
-            pltpu.VMEM((T * R, 128), f32),
-            pltpu.VMEM((T, R, HALF), bf16),
-            pltpu.VMEM((T, A, HALF), bf16),
-            pltpu.SemaphoreType.DMA((2, 4)),
-        ],
+        scratch_shapes=[pltpu.VMEM((T * R, 128), f32)],
         name="coeffs",
         compiler_params=LIMIT,
     )(n, vectors, basis)
@@ -145,7 +148,9 @@
     for piece, offsets in zip(pieces, OFFSETS):
         for k, offset in enumerate(offsets):
             first = pl.multiple_of(((z_ref[0] + offset) & (N_Z - 1)) * T, T)
-            table_ref[pl.ds(first, T), :] = piece[k * T : (k + 1) * T]
+            for h in range(2):
+                row = (2 * k + h) * T
+                table_ref[pl.ds(first, T), h * HALF : (h + 1) * HALF] = piece[row : row + T]
     lanes = iota((CAP, 128), 1).astype(f32) + 1.0
     for r in range(0, N_PEER, 4):
         want = [req_ref[r + k].astype(f32) for k in range(4)]
@@ -239,17 +244,23 @@
     )(picked, couplings)
 
 
-def near_kernel(leaves, edges, group, scalar_ref, pts_ref, vec_ref, other_ref, *refs):
-    edge_refs, kerns, outs = refs[: 2 * edges], refs[-group:], refs[:-group]
-    send_refs = () if edges or len(outs) < 3 else outs[-2:]
-    out_ref = outs[-3] if send_refs else outs[-1]
+def near_kernel(kind, leaves, group, scalar_ref, pts_ref, vec_ref, other_ref, *refs):
+    edges, send_refs = (), ()
+    refs, kerns = refs[:-group], refs[-group:]
+    if kind == "early":
+        out_ref, *send_refs = refs
+    else:
+        *edges, _, out_ref = refs
     count, n = scalar_ref[0], scalar_ref[1]
     own = pl.multiple_of(n * HALF, HALF)
     other = pl.multiple_of((1 - n) * HALF, HALF)
 
+    def other_values(t):
+        return other_ref[pl.ds(pl.multiple_of(t * R, R), R)]
+
     for ref, t in zip(send_refs, (0, count - 1)):
         ref[:R, pl.ds(own, HALF)] = vec_ref[t]
-        ref[:R, pl.ds(other, HALF)] = other_ref[t]
+        ref[:R, pl.ds(other, HALF)] = other_values(t)
         ref[R:] = pts_ref[t]
 
     def sources(t):
@@ -259,7 +270,7 @@
         if not edges:
             return values
         for k, (u, at) in enumerate(((0, 0), (2, count - 1))):
-            halo = [edge_refs[k][rows, pl.ds(h, HALF)] for h in (own, other)]
+            halo = [edges[k][rows, pl.ds(h, HALF)] for h in (own, other)]
             values[u] = [jnp.where(t == at, a, b) for a, b in zip(halo, values[u])]
         return values
 
@@ -278,7 +289,7 @@
                 kern[p : p + 32, k * LEAF : (k + 1) * LEAF] = lax.rsqrt(squared)
 
     def product(t, kern):
-        values = [[vec_ref[u], other_ref[u]] for u in sources(t)]
+        values = [[vec_ref[u], other_values(u)] for u in sources(t)]
         values = taken(t, slice(0, R), values)
         values = jnp.concatenate([v for pair in values for v in pair], 1)
         out_ref[t] = nt(values, kern[...]) * inverse_four_pi
@@ -289,7 +300,7 @@
         i = jnp.where(i < leaves[0], i, i + leaves[1] - leaves[0])
         return jnp.where(i < T, i, count - 1)
 
-    steps = T - leaves[1] + leaves[0] + 1 if edges else leaves[1] - leaves[0]
+    steps, group = near_steps(kind, leaves), len(kerns)
     fill(leaf(0), kerns[0])
 
     def body(i, _):
@@ -301,26 +312,27 @@
     lax.fori_loop(0, steps // group, body, 0)
 
 
-def near_call(leaves, args, halos=(), base=None):
-    size = T - leaves[1] + leaves[0] + 1 if halos else leaves[1] - leaves[0]
-    bases = () if base is None else (base,)
-    count = len(args) + len(halos)
-    group = size if halos else 8
+def near_steps(kind, leaves):
+    return T - leaves[1] + leaves[0] + 1 if kind == "rest" else leaves[1] - leaves[0]
+
+
+def near_call(kind, leaves, group, args, more=()):
     field = jax.ShapeDtypeStruct((T, R, HALF), f32)
     edge = jax.ShapeDtypeStruct((R + 8, LEAF), bf16)
-    return pl.pallas_call(
-        lambda *refs: near_kernel(leaves, bool(halos), group, *refs),
-        out_shape=field if bases else (field, edge, edge),
-        in_specs=[SMEM] + [VMEM] * (count - 1 + len(bases)),
-        out_specs=VMEM if bases else (VMEM,) * 3,
+    outs = (field, edge, edge) if kind == "early" else (field,)
+    return pl.pallas_call(
+        lambda *refs: near_kernel(kind, leaves, group, *refs),
+        out_shape=outs,
+        in_specs=[SMEM] + [VMEM] * (len(args) - 1 + len(more)),
+        out_specs=(VMEM,) * len(outs),
         scratch_shapes=[pltpu.VMEM((HALF, 3 * LEAF), bf16)] * group,
-        input_output_aliases={count: 0} if bases else {},
+        input_output_aliases={} if kind == "early" else {len(args) + len(more) - 1: 0},
         cost_estimate=pl.CostEstimate(
-            flops=size * 200_000_000, bytes_accessed=2_000_000, transcendentals=0
+            flops=near_steps(kind, leaves) * 200_000_000, bytes_accessed=2_000_000, transcendentals=0
         ),
         name="near",
         compiler_params=LIMIT,
-    )(*args, *halos, *bases)
+    )(*args, *more)
 
 
 def final_kernel(scalar_ref, mine_ref, theirs_ref, tgt_ref, near_ref, out_ref, rows):
@@ -369,30 +381,33 @@
 
     keep, send = coeff_call(n[None], vectors, src_basis)
     came = shifted(send, "n", 1)
-    other = shifted(vectors, "n", 1)
     sel, req, rows = index_call(scalars, adm_src.T, points.transpose(1, 0, 2))
     asked = lax.all_to_all(req, PEERS, split_axis=0, concat_axis=0, tiled=True)
 
-    coeffs = (keep + came).astype(bf16)
-    up = shifted(coeffs, "z", -2)
-    down = shifted(coeffs, "z", 2)
-    across = shifted(coeffs, "z", 4)
-    odd_up = shifted(jnp.concatenate([coeffs, up]), "z", -1)
-    odd_down = shifted(jnp.concatenate([coeffs, down]), "z", 1)
-    pieces = coeffs, up, down, across, odd_up, odd_down
-
-    near_args = (scalars, rows, vectors, other)
-    near, first, last = near_call((4, 12), near_args)
+    high, low = came[T * R : T * R + 2 * T], came[T * R + 2 * T :]
+    coeffs = (keep + high.astype(f32) + low.astype(f32)).astype(bf16)
+    below = shifted(coeffs, "z", 1)
+    above = shifted(coeffs, "z", -1)
+    up = shifted(jnp.concatenate([below, coeffs, above]), "z", -3)
+    down = shifted(jnp.concatenate([above, coeffs]), "z", 3)
+    pieces = coeffs, below, above, up, down
+
+    near_args = (scalars, rows, vectors, came)
+    near, first, last = near_call("early", (2, 10), 8, near_args)
     halos = shifted(last, WIDE, 1), shifted(first, WIDE, -1)
-    near = near_call((12, 28), near_args, base=near)
-    near = near_call((4, 28), near_args, halos, near)
+    (near,) = near_call("inner", (10, 30), 10, near_args, (near,))
+    (near,) = near_call("rest", (2, 30), 5, near_args, (*halos, near))
 
     packed, fits = pack_call(z[None], asked, pieces)
     got = lax.all_to_all(packed, PEERS, split_axis=0, concat_axis=0, tiled=True)
     mine = select_call(sel, got, couplings)
 
     def every(mine, pieces, couplings):
-        blocks = {o % N_Z: p[k * T : (k + 1) * T] for p, os in zip(pieces, OFFSETS) for k, o in enumerate(os)}
+        blocks = {
+            o % N_Z: jnp.concatenate([p[2 * k * T :][:T], p[(2 * k + 1) * T :][:T]], 1)
+            for p, os in zip(pieces, OFFSETS)
+            for k, o in enumerate(os)
+        }
         twice = jnp.concatenate([blocks[o % N_Z] for o in range(2 * N_Z)])
         table = lax.dynamic_slice_in_dim(twice, (N_Z - z) % N_Z * T, COLUMN, 0)
         whole = to_all(table, PEERS).reshape(N_PEER * COLUMN, RH * A)

time: 88.9 us -> 78.9 us (0.89)
  the two profiles are of different devices: /device:TPU:8 before, /device:TPU:24 now
where the time goes in v6:
time: 78.9 us; the launch traced here: 78.3 us
  starting transfers between devices  29.9 us (38%)
  Pallas kernels  23.3 us (30%)
  waiting for transfers between devices  19.2 us (24%)
  local copies, waits for them, and re-layouts  4.44 us (6%)
  between operations  1.39 us (2%)
    ppermute x8, starting transfers between devices, shifted(): lax.ppermute(array, axis, [(i, (i + by) % devices) for i in range(devices)])  18.4 us
    ppermute x8, waiting for transfers between devices, shifted(): lax.ppermute(array, axis, [(i, (i + by) % devices) for i in range(devices)])  17.4 us
    pallas_call x3, Pallas kernels, near_call(): pl.pallas_call(lambda *refs: near_kernel(kind, leaves, group, *refs), out...  13.8 us
    all_to_all x1, starting transfers between devices, body(): asked = lax.all_to_all(req, PEERS, split_axis=0, concat_axis=0, tiled=True)  5.78 us
    all_to_all x1, starting transfers between devices, body(): got = lax.all_to_all(packed, PEERS, split_axis=0, concat_axis=0, tiled=True)  5.73 us
    pallas_call x1, Pallas kernels, select_call(): pl.pallas_call(select_kernel, out_shape=TC_SHAPE, in_specs=[VMEM, VMEM, H...  3.46 us
    unnamed x12, local copies, waits for them, and re-layouts  3.08 us
    pallas_call x1, Pallas kernels, index_call(): pl.pallas_call(index_kernel, out_shape=(jax.ShapeDtypeStruct((ENTRIES, 12...  2.21 us
  transfers between devices with their start and end apart: 10, of which 4 were waited for; matrix products, arithmetic and copies ran while one was open for 2% of the time, Pallas kernels for 25%

profile of v6, /device:TPU:24, one launch (start us, length us, event | category | flops | bytes accessed | tf_op | source)
XLA Modules:
  0.0 78.3 jit_solution(10747347486311770073)
XLA Ops:
  0.0 1.2 %copy-done.1 = bf16[32,64,256]{2,1,0:T(8,128)(2,1)S(1)} copy-done((bf16[32,64,256]{2,1,0:T(8,128)(2,1)S(1)}, bf16[32,64,256]{2,1,0:T(8,128)(2,1)}, u32[]{:S(2)}) %copy-start.1) | copy-done | bytes 1048600
  1.2 0.9 %copy-done.2 = bf16[32,16,256]{2,1,0:T(8,128)(2,1)S(1)} copy-done((bf16[32,16,256]{2,1,0:T(8,128)(2,1)S(1)}, bf16[32,16,256]{2,1,0:T(8,128)(2,1)}, u32[]{:S(2)}) %copy-start.2) | copy-done | bytes 262168
  2.2 0.6 coeffs.1
  2.8 1.3 %collective-permute-start = (bf16[640,256]{1,0:T(8,128)(2,1)S(1)}, bf16[640,256]{1,0:T(8,128)(2,1)S(1)}, u32[]{:S(2)}, u32[]{:S(2)}) collective-permute-start(bf16[640,256]{1,0:T(8,128)(2,1)S(1)} %get-tuple-element.45), channel_id=1, source_target_pairs={{0,1},{1,0},{2,3},{3,2},{4,5},{5,4},{6,7},{7,6},{8,9},{9,8},{10,11... | collective-permute-start | bytes 983048 | tf_op jit(solution)/shard_map/ppermute | solution.py:369
  4.8 9.1 %collective-permute-done.refs_3_ = bf16[640,256]{1,0:T(8,128)(2,1)S(1)} collective-permute-done((bf16[640,256]{1,0:T(8,128)(2,1)S(1)}, bf16[640,256]{1,0:T(8,128)(2,1)S(1)}, u32[]{:S(2)}, u32[]{:S(2)}) %collective-permute-start) | collective-permute-done | bytes 327712 | tf_op jit(solution)/shard_map/ppermute | solution.py:369
  13.9 5.9 %collective-permute-start.2 = (bf16[64,256]{1,0:T(8,128)(2,1)S(1)}, bf16[64,256]{1,0:T(8,128)(2,1)S(1)}, u32[]{:S(2)}, u32[]{:S(2)}) collective-permute-start(bf16[64,256]{1,0:T(8,128)(2,1)S(1)} %add_convert_fusion.refs_0_), channel_id=1, source_target_pairs={{0,112},{16,0},{32,16},{48,32},{64,48},{80,64},{96,80},{112,96},{1... | collective-permute-start | bytes 98312 | tf_op jit(solution)/shard_map/ppermute | solution.py:369
  19.8 0.1 pad_add_fusion.scalar_ref.refs_0_
  19.9 0.9 %copy-done.4 = bf16[32,3,512]{2,0,1:T(8,128)(2,1)S(1)} copy-done((bf16[32,3,512]{2,0,1:T(8,128)(2,1)S(1)}, bf16[32,3,512]{2,0,1:T(8,128)(2,1)}, u32[]{:S(2)}) %copy-start.4) | copy-done | bytes 98328
  20.8 2.2 %requests.1 = (s32[256,128]{1,0:T(8,128)S(1)}, bf16[16,48,128]{2,1,0:T(8,128)(2,1)}, bf16[32,8,512]{2,1,0:T(8,128)(2,1)S(1)}) custom-call(s32[2]{0:T(128)S(1)} %pad_add_fusion.scalar_ref.refs_0_, s32[8,32]{1,0:T(8,128)} %bitcast.10, bf16[3,32,512]{2,1,0:T(8,128)(2,1)S(1)} %bitcast.9), custom_call_target="tpu_custom_call" | custom-call | tf_op jit(solution)/shard_map/requests/pallas_call | solution.py:92
  23.0 5.8 %all-to-all-start.1 = ((bf16[16,48,128]{2,1,0:T(8,128)(2,1)}), bf16[16,48,128]{2,1,0:T(8,128)(2,1)S(1)}, u32[]{:S(2)}, u32[]{:S(2)}) async-start(bf16[16,48,128]{2,1,0:T(8,128)(2,1)} %get-tuple-element.43), calls=%async_computation.1 | async-start | bytes 393216 | tf_op jit(solution)/shard_map/all_to_all | solution.py:385
  28.8 0.0 collective-permute-done.2.refs_2_
  28.8 3.0 %collective-permute-start.3 = (bf16[192,256]{1,0:T(8,128)(2,1)S(1)}, bf16[192,256]{1,0:T(8,128)(2,1)S(1)}, u32[]{:S(2)}, u32[]{:S(2)}) collective-permute-start(bf16[192,256]{1,0:T(8,128)(2,1)S(1)} %pad_maximum_fusion.8), channel_id=1, source_target_pairs={{0,80},{16,96},{32,112},{48,0},{64,16},{80,32},{96,48},{112,64},{1... | collective-permute-start | bytes 294920 | tf_op jit(solution)/shard_map/ppermute | solution.py:369
  31.8 0.9 %collective-permute-start.4 = (bf16[128,256]{1,0:T(8,128)(2,1)S(1)}, bf16[128,256]{1,0:T(8,128)(2,1)S(1)}, u32[]{:S(2)}, u32[]{:S(2)}) collective-permute-start(bf16[128,256]{1,0:T(8,128)(2,1)S(1)} %pad_maximum_fusion.9), channel_id=1, source_target_pairs={{0,48},{16,64},{32,80},{48,96},{64,112},{80,0},{96,16},{112,32},{1... | collective-permute-start | bytes 196616 | tf_op jit(solution)/shard_map/ppermute | solution.py:369
  32.7 1.7 %all-to-all-done.1.req_ref = bf16[16,48,128]{2,1,0:T(8,128)(2,1)S(1)} async-done(((bf16[16,48,128]{2,1,0:T(8,128)(2,1)}), bf16[16,48,128]{2,1,0:T(8,128)(2,1)S(1)}, u32[]{:S(2)}, u32[]{:S(2)}) %all-to-all-start.1) | async-done | bytes 196640 | tf_op jit(solution)/shard_map/all_to_all | solution.py:385
  34.4 6.3 %collective-permute-done.4.refs_4_ = bf16[128,256]{1,0:T(8,128)(2,1)S(1)} collective-permute-done((bf16[128,256]{1,0:T(8,128)(2,1)S(1)}, bf16[128,256]{1,0:T(8,128)(2,1)S(1)}, u32[]{:S(2)}, u32[]{:S(2)}) %collective-permute-start.4) | collective-permute-done | bytes 65568 | tf_op jit(solution)/shard_map/ppermute | solution.py:369
  40.7 0.0 collective-permute-done.3.refs_3_
  40.7 1.3 %pack.1 = (bf16[16,48,512]{2,1,0:T(8,128)(2,1)}, s32[1]{0:T(128)}) custom-call(s32[1]{0:T(128)} %bitcast.3.z_ref, bf16[16,48,128]{2,1,0:T(8,128)(2,1)S(1)} %all-to-all-done.1.req_ref, bf16[64,256]{1,0:T(8,128)(2,1)S(1)} %add_convert_fusion.refs_0_, bf16[64,256]{1,0:T(8,128)(2,1)S(1)} %collective-permute-done.1.refs_1_, ...), custom_call_target="tpu_custom_call" | custom-call | tf_op jit(solution)/shard_map/pack/pallas_call | solution.py:168
  42.1 5.7 %all-to-all-start.2 = ((bf16[16,48,512]{2,1,0:T(8,128)(2,1)}), bf16[16,48,512]{2,1,0:T(8,128)(2,1)S(1)}, u32[]{:S(2)}, u32[]{:S(2)}) async-start(bf16[16,48,512]{2,1,0:T(8,128)(2,1)} %get-tuple-element.48), calls=%async_computation.2 | async-start | bytes 1572864 | tf_op jit(solution)/shard_map/all_to_all | solution.py:402
  47.8 3.7 %near.3 = (f32[32,16,256]{2,1,0:T(8,128)S(1)}, bf16[24,512]{1,0:T(8,128)(2,1)S(1)}, bf16[24,512]{1,0:T(8,128)(2,1)}) custom-call(s32[2]{0:T(128)S(1)} %pad_add_fusion.scalar_ref.refs_0_, bf16[32,8,512]{2,1,0:T(8,128)(2,1)S(1)} %get-tuple-element.49.refs_1_, bf16[32,16,256]{2,1,0:T(8,128)(2,1)S(1)} %copy-done.3, bf16[640,256]{1,0:T(8,128)(2,1)S(1)} %collective-permute-done.refs_3_), custom_call_target="tpu_custom_call" | custom-call | flops 1600000000 | bytes 2000000 | tf_op jit(solution)/shard_map/near/pallas_call | solution.py:323
  51.5 0.1 collective-permute-start.6
  51.6 5.8 %collective-permute-start.7 = (bf16[24,512]{1,0:T(8,128)(2,1)S(1)}, bf16[24,512]{1,0:T(8,128)(2,1)S(1)}, u32[]{:S(2)}, u32[]{:S(2)}) collective-permute-start(bf16[24,512]{1,0:T(8,128)(2,1)S(1)} %get-tuple-element.51), channel_id=1, source_target_pairs={{0,254},{2,0},{4,2},{6,4},{8,6},{10,8},{12,10},{14,12},{16,14},{18... | collective-permute-start | bytes 73736 | tf_op jit(solution)/shard_map/ppermute | solution.py:369
  57.5 7.8 %near.4.refs_6_ = f32[32,16,256]{2,1,0:T(8,128)S(1)} custom-call(s32[2]{0:T(128)S(1)} %pad_add_fusion.scalar_ref.refs_0_, bf16[32,8,512]{2,1,0:T(8,128)(2,1)S(1)} %get-tuple-element.49.refs_1_, bf16[32,16,256]{2,1,0:T(8,128)(2,1)S(1)} %copy-done.3, bf16[640,256]{1,0:T(8,128)(2,1)S(1)} %collective-permute-done.refs_3_, ...), custom_call_target="tpu_custom_call", output_to_operand_aliasing={{}: (4, {})} | custom-call | flops 4000000000 | bytes 2000000 | tf_op jit(solution)/shard_map/near/pallas_call | solution.py:323
  65.9 0.0 all-to-all-done.2.got_ref
  65.9 3.5 %select.3 = bf16[4,32,128]{2,1,0:T(8,128)(2,1)} custom-call(s32[256,128]{1,0:T(8,128)S(1)} %get-tuple-element.47.sel_ref, bf16[16,48,512]{2,1,0:T(8,128)(2,1)S(1)} %all-to-all-done.2.got_ref, bf16[32,64,512]{2,1,0:T(8,128)(2,1)} %couple_hbm.1), custom_call_target="tpu_custom_call" | custom-call | tf_op jit(solution)/shard_map/select/pallas_call | solution.py:221
  69.4 1.4 %conditional.1 = (bf16[4,32,128]{2,1,0:T(8,128)(2,1)}) conditional(s32[]{:T(128)} %bitcast.6, (s32[32,8]{0,1:T(8,128)S(1)}, bf16[64,256]{1,0:T(8,128)(2,1)S(1)}, bf16[64,256]{1,0:T(8,128)(2,1)S(1)}, bf16[192,256]{1,0:T(8,128)(2,1)S(1)}, bf16[128,256]{1,0:T(8,128)(2,1)S(1)}, /*index=5*/bf16[64,256]{1,0:T(8,128)(2,1)S(1)}, s32[]{:T(128)}, ...), branch_computations={%region_0.1_spmd, %region_1.2_spmd} | conditional | flops 1075842048 | bytes 32249072 | solution.py:419
  69.4 1.4 %copy.26 = bf16[4,32,128]{2,1,0:T(8,128)(2,1)} copy(bf16[4,32,128]{2,1,0:T(8,128)(2,1)} %param.1) | data formatting | bytes 65536 | tf_op jit(solution)/shard_map/cond
  70.8 1.2 %collective-permute-start.5 = (bf16[4,32,128]{2,1,0:T(8,128)(2,1)}, bf16[4,32,128]{2,1,0:T(8,128)(2,1)S(1)}, u32[]{:S(2)}, u32[]{:S(2)}) collective-permute-start(bf16[4,32,128]{2,1,0:T(8,128)(2,1)} %get-tuple-element.75.mine_ref), channel_id=1, source_target_pairs={{0,1},{1,0},{2,3},{3,2},{4,5},{5,4},{6,7},{7,6},{8,9},{9,8},{10,11... | collective-permute-start | bytes 98312 | tf_op jit(solution)/shard_map/ppermute | solution.py:369
  72.0 0.0 collective-permute-done.6.refs_4_
  72.0 0.0 collective-permute-done.7.refs_5_
  72.0 2.4 %near.5.near_ref = f32[32,16,256]{2,1,0:T(8,128)S(1)} custom-call(s32[2]{0:T(128)S(1)} %pad_add_fusion.scalar_ref.refs_0_, bf16[32,8,512]{2,1,0:T(8,128)(2,1)S(1)} %get-tuple-element.49.refs_1_, bf16[32,16,256]{2,1,0:T(8,128)(2,1)S(1)} %copy-done.3, bf16[640,256]{1,0:T(8,128)(2,1)S(1)} %collective-permute-done.refs_3_, ...), custom_call_target="tpu_custom_call", output_to_operand_aliasing={{}: (6, {})} | custom-call | flops 1000000000 | bytes 2000000 | tf_op jit(solution)/shard_map/near/pallas_call | solution.py:323
  74.4 2.0 %collective-permute-done.5.theirs_ref = bf16[4,32,128]{2,1,0:T(8,128)(2,1)S(1)} collective-permute-done((bf16[4,32,128]{2,1,0:T(8,128)(2,1)}, bf16[4,32,128]{2,1,0:T(8,128)(2,1)S(1)}, u32[]{:S(2)}, u32[]{:S(2)}) %collective-permute-start.5) | collective-permute-done | bytes 32800 | tf_op jit(solution)/shard_map/ppermute | solution.py:369
  76.4 1.9 %final.1 = bf16[32,16,256]{2,1,0:T(8,128)(2,1)} custom-call(s32[2]{0:T(128)S(1)} %pad_add_fusion.scalar_ref.refs_0_, bf16[4,32,128]{2,1,0:T(8,128)(2,1)} %get-tuple-element.75.mine_ref, bf16[4,32,128]{2,1,0:T(8,128)(2,1)S(1)} %collective-permute-done.5.theirs_ref, bf16[32,64,512]{2,1,0:T(8,128)(2,1)S(1)} %copy-done, f32[32,16,256]{2,1,0:T(8,128)S(1)} %near.5.near_ref), custom_call_target="tpu_custom_call" | custom-call | tf_op jit(solution)/shard_map/final/pallas_call | solution.py:356
  (14 shorter events, 0.0 us)
Async XLA Ops:
  0.0 1.2 %copy-start.1 = (bf16[32,64,256]{2,1,0:T(8,128)(2,1)S(1)}, bf16[32,64,256]{2,1,0:T(8,128)(2,1)}, u32[]{:S(2)}) copy-start(bf16[32,64,256]{2,1,0:T(8,128)(2,1)} %basis_ref.1) | copy-start | bytes 3145732
  1.2 0.9 %copy-start.2 = (bf16[32,16,256]{2,1,0:T(8,128)(2,1)S(1)}, bf16[32,16,256]{2,1,0:T(8,128)(2,1)}, u32[]{:S(2)}) copy-start(bf16[32,16,256]{2,1,0:T(8,128)(2,1)} %refs_2_.5) | copy-start | bytes 786436
  2.2 45.6 %copy-start.3 = (bf16[32,16,256]{2,1,0:T(8,128)(2,1)S(1)}, bf16[32,16,256]{2,1,0:T(8,128)(2,1)}, u32[]{:S(2)}) copy-start(bf16[32,16,256]{2,1,0:T(8,128)(2,1)} %refs_2_.5) | copy-start | bytes 786436
  2.8 11.0 %collective-permute-start = (bf16[640,256]{1,0:T(8,128)(2,1)S(1)}, bf16[640,256]{1,0:T(8,128)(2,1)S(1)}, u32[]{:S(2)}, u32[]{:S(2)}) collective-permute-start(bf16[640,256]{1,0:T(8,128)(2,1)S(1)} %get-tuple-element.45), channel_id=1, source_target_pairs={{0,1},{1,0},{2,3},{3,2},{4,5},{5,4},{6,7},{7,6},{8,9},{9,8},{10,11... | collective-permute-start | bytes 983048 | tf_op jit(solution)/shard_map/ppermute | solution.py:369
  13.9 14.9 %collective-permute-start.2 = (bf16[64,256]{1,0:T(8,128)(2,1)S(1)}, bf16[64,256]{1,0:T(8,128)(2,1)S(1)}, u32[]{:S(2)}, u32[]{:S(2)}) collective-permute-start(bf16[64,256]{1,0:T(8,128)(2,1)S(1)} %add_convert_fusion.refs_0_), channel_id=1, source_target_pairs={{0,112},{16,0},{32,16},{48,32},{64,48},{80,64},{96,80},{112,96},{1... | collective-permute-start | bytes 98312 | tf_op jit(solution)/shard_map/ppermute | solution.py:369
  19.8 9.0 %collective-permute-start.1 = (bf16[64,256]{1,0:T(8,128)(2,1)S(1)}, bf16[64,256]{1,0:T(8,128)(2,1)S(1)}, u32[]{:S(2)}, u32[]{:S(2)}) collective-permute-start(bf16[64,256]{1,0:T(8,128)(2,1)S(1)} %add_convert_fusion.refs_0_), channel_id=1, source_target_pairs={{0,16},{16,32},{32,48},{48,64},{64,80},{80,96},{96,112},{112,0},{1... | collective-permute-start | bytes 98312 | tf_op jit(solution)/shard_map/ppermute | solution.py:369
  19.9 0.9 %copy-start.4 = (bf16[32,3,512]{2,0,1:T(8,128)(2,1)S(1)}, bf16[32,3,512]{2,0,1:T(8,128)(2,1)}, u32[]{:S(2)}) copy-start(bf16[32,3,512]{2,0,1:T(8,128)(2,1)} %param.9) | copy-start | bytes 294916
  23.0 11.5 %all-to-all-start.1 = ((bf16[16,48,128]{2,1,0:T(8,128)(2,1)}), bf16[16,48,128]{2,1,0:T(8,128)(2,1)S(1)}, u32[]{:S(2)}, u32[]{:S(2)}) async-start(bf16[16,48,128]{2,1,0:T(8,128)(2,1)} %get-tuple-element.43), calls=%async_computation.1 | async-start | bytes 393216 | tf_op jit(solution)/shard_map/all_to_all | solution.py:385
  28.8 12.0 %collective-permute-start.3 = (bf16[192,256]{1,0:T(8,128)(2,1)S(1)}, bf16[192,256]{1,0:T(8,128)(2,1)S(1)}, u32[]{:S(2)}, u32[]{:S(2)}) collective-permute-start(bf16[192,256]{1,0:T(8,128)(2,1)S(1)} %pad_maximum_fusion.8), channel_id=1, source_target_pairs={{0,80},{16,96},{32,112},{48,0},{64,16},{80,32},{96,48},{112,64},{1... | collective-permute-start | bytes 294920 | tf_op jit(solution)/shard_map/ppermute | solution.py:369
  31.8 9.0 %collective-permute-start.4 = (bf16[128,256]{1,0:T(8,128)(2,1)S(1)}, bf16[128,256]{1,0:T(8,128)(2,1)S(1)}, u32[]{:S(2)}, u32[]{:S(2)}) collective-permute-start(bf16[128,256]{1,0:T(8,128)(2,1)S(1)} %pad_maximum_fusion.9), channel_id=1, source_target_pairs={{0,48},{16,64},{32,80},{48,96},{64,112},{80,0},{96,16},{112,32},{1... | collective-permute-start | bytes 196616 | tf_op jit(solution)/shard_map/ppermute | solution.py:369
  42.1 23.8 %all-to-all-start.2 = ((bf16[16,48,512]{2,1,0:T(8,128)(2,1)}), bf16[16,48,512]{2,1,0:T(8,128)(2,1)S(1)}, u32[]{:S(2)}, u32[]{:S(2)}) async-start(bf16[16,48,512]{2,1,0:T(8,128)(2,1)} %get-tuple-element.48), calls=%async_computation.2 | async-start | bytes 1572864 | tf_op jit(solution)/shard_map/all_to_all | solution.py:402
  51.5 20.5 %collective-permute-start.6 = (bf16[24,512]{1,0:T(8,128)(2,1)}, bf16[24,512]{1,0:T(8,128)(2,1)S(1)}, u32[]{:S(2)}, u32[]{:S(2)}) collective-permute-start(bf16[24,512]{1,0:T(8,128)(2,1)} %get-tuple-element.50), channel_id=1, source_target_pairs={{0,2},{2,4},{4,6},{6,8},{8,10},{10,12},{12,14},{14,16},{16,18},{18... | collective-permute-start | bytes 73736 | tf_op jit(solution)/shard_map/ppermute | solution.py:369
  51.6 20.4 %collective-permute-start.7 = (bf16[24,512]{1,0:T(8,128)(2,1)S(1)}, bf16[24,512]{1,0:T(8,128)(2,1)S(1)}, u32[]{:S(2)}, u32[]{:S(2)}) collective-permute-start(bf16[24,512]{1,0:T(8,128)(2,1)S(1)} %get-tuple-element.51), channel_id=1, source_target_pairs={{0,254},{2,0},{4,2},{6,4},{8,6},{10,8},{12,10},{14,12},{16,14},{18... | collective-permute-start | bytes 73736 | tf_op jit(solution)/shard_map/ppermute | solution.py:369
  57.5 11.9 %copy-start.6 = (s32[32,8]{0,1:T(8,128)S(1)}, s32[32,8]{0,1:T(8,128)}, u32[]{:S(2)}) copy-start(s32[32,8]{0,1:T(8,128)} %param.14) | copy-start | bytes 3076
  70.8 5.6 %copy-start = (bf16[32,64,512]{2,1,0:T(8,128)(2,1)S(1)}, bf16[32,64,512]{2,1,0:T(8,128)(2,1)}, u32[]{:S(2)}) copy-start(bf16[32,64,512]{2,1,0:T(8,128)(2,1)} %tgt_ref.1) | copy-start | bytes 6291460
  70.8 5.6 %collective-permute-start.5 = (bf16[4,32,128]{2,1,0:T(8,128)(2,1)}, bf16[4,32,128]{2,1,0:T(8,128)(2,1)S(1)}, u32[]{:S(2)}, u32[]{:S(2)}) collective-permute-start(bf16[4,32,128]{2,1,0:T(8,128)(2,1)} %get-tuple-element.75.mine_ref), channel_id=1, source_target_pairs={{0,1},{1,0},{2,3},{3,2},{4,5},{5,4},{6,7},{7,6},{8,9},{9,8},{10,11... | collective-permute-start | bytes 98312 | tf_op jit(solution)/shard_map/ppermute | solution.py:369

commit v7 on v6

--- a/solution.py
+++ b/solution.py
@@ -18,7 +18,7 @@
 T, R, A, J, HALF, LEAF = 32, 16, 64, 8, 256, 512
 RH = R // 2
 N_Z, N_PEER = 8, 16
-CAP = 48
+CAP = 40
 ENTRIES = T * J
 OFFSETS = (0,), (-1,), (1,), (2, 3, 4), (-2, -3)
 SENT = T * R + 4 * T
@@ -27,7 +27,6 @@
 
 VMEM = pl.BlockSpec(memory_space=pltpu.VMEM)
 SMEM = pl.BlockSpec(memory_space=pltpu.SMEM)
-HBM = pl.BlockSpec(memory_space=pltpu.HBM)
 LIMIT = pltpu.CompilerParams(vmem_limit_bytes=20 * 2**20)
 
 
@@ -46,16 +45,6 @@
 def folded(wide):
     two = wide[:, :128] + wide[:, 128:]
     return two[:, :64] + two[:, 64:]
-
-
-def chunks(source, target, sems, size):
-    copies = [
-        pltpu.make_async_copy(source.at[pl.ds(k, size)], target.at[pl.ds(k, size)], sems.at[k // size])
-        for k in range(0, T, size)
-    ]
-    for copy in copies:
-        copy.start()
-    return copies
 
 
 def index_kernel(scalar_ref, adm_ref, pts_ref, sel_ref, req_ref, rows_ref):
@@ -179,7 +168,7 @@
     )(z, req, *pieces)
 
 
-def couple(picked, couple_ref, out_ref, copies=()):
+def couple(picked, couple_ref, out_ref):
     lows = [picked[j * T : (j + 1) * T] for j in range(J)]
     by_rhs = []
     for r in range(RH):
@@ -192,8 +181,6 @@
         total = jnp.zeros((16 * RH, A), f32)
         for g in range(4):
             first = 16 * h + 4 * g
-            if copies and first % 8 == 0:
-                copies[first // 8].wait()
             rhs = couple_ref[first : first + 4].reshape(4 * A, J * A)
             total = total + folded(jnp.where(row_t == col_t + 4 * g, nt(lhs, rhs), 0.0))
         total = total.reshape(RH, 16, A)
@@ -202,8 +189,7 @@
             out_ref[r // 2, 16 * h : 16 * h + 16, :] = pair.astype(bf16)
 
 
-def select_kernel(sel_ref, got_ref, couple_hbm, out_ref, couple_ref, sems):
-    copies = chunks(couple_hbm, couple_ref, sems, 8)
+def select_kernel(sel_ref, got_ref, couple_ref, out_ref):
     slots = N_PEER * CAP
     sel = sel_ref[...]
     lanes = iota((ENTRIES, 128), 1)
@@ -211,7 +197,7 @@
         [jnp.where(sel == lanes + 128 * k, 1.0, 0.0) for k in range(slots // 128)], 1
     )
     picked = nn(hot.astype(bf16), got_ref[...].reshape(slots, RH * A))
-    couple(picked, couple_ref, out_ref, copies)
+    couple(picked, couple_ref, out_ref)
 
 
 TC_SHAPE = jax.ShapeDtypeStruct((RH // 2, T, 2 * A), bf16)
@@ -221,9 +207,8 @@
     return pl.pallas_call(
         select_kernel,
         out_shape=TC_SHAPE,
-        in_specs=[VMEM, VMEM, HBM],
+        in_specs=[VMEM, VMEM, VMEM],
         out_specs=VMEM,
-        scratch_shapes=[pltpu.VMEM((T, A, J * A), bf16), pltpu.SemaphoreType.DMA((4,))],
         name="select",
         compiler_params=LIMIT,
     )(sel, got, couplings)
@@ -255,12 +240,12 @@
     own = pl.multiple_of(n * HALF, HALF)
     other = pl.multiple_of((1 - n) * HALF, HALF)
 
-    def other_values(t):
-        return other_ref[pl.ds(pl.multiple_of(t * R, R), R)]
+    def values_of(ref, t):
+        return ref[pl.ds(pl.multiple_of(t * R, R), R)]
 
     for ref, t in zip(send_refs, (0, count - 1)):
-        ref[:R, pl.ds(own, HALF)] = vec_ref[t]
-        ref[:R, pl.ds(other, HALF)] = other_values(t)
+        ref[:R, pl.ds(own, HALF)] = values_of(vec_ref, t)
+        ref[:R, pl.ds(other, HALF)] = values_of(other_ref, t)
         ref[R:] = pts_ref[t]
 
     def sources(t):
@@ -289,7 +274,7 @@
                 kern[p : p + 32, k * LEAF : (k + 1) * LEAF] = lax.rsqrt(squared)
 
     def product(t, kern):
-        values = [[vec_ref[u], other_values(u)] for u in sources(t)]
+        values = [[values_of(vec_ref, u), values_of(other_ref, u)] for u in sources(t)]
         values = taken(t, slice(0, R), values)
         values = jnp.concatenate([v for pair in values for v in pair], 1)
         out_ref[t] = nt(values, kern[...]) * inverse_four_pi
@@ -392,7 +377,7 @@
     down = shifted(jnp.concatenate([above, coeffs]), "z", 3)
     pieces = coeffs, below, above, up, down
 
-    near_args = (scalars, rows, vectors, came)
+    near_args = (scalars, rows, send, came)
     near, first, last = near_call("early", (2, 10), 8, near_args)
     halos = shifted(last, WIDE, 1), shifted(first, WIDE, -1)
     (near,) = near_call("inner", (10, 30), 10, near_args, (near,))
@@ -400,9 +385,8 @@
 
     packed, fits = pack_call(z[None], asked, pieces)
     got = lax.all_to_all(packed, PEERS, split_axis=0, concat_axis=0, tiled=True)
-    mine = select_call(sel, got, couplings)
-
-    def every(mine, pieces, couplings):
+
+    def every(sel, got, pieces, couplings):
         blocks = {
             o % N_Z: jnp.concatenate([p[2 * k * T :][:T], p[(2 * k + 1) * T :][:T]], 1)
             for p, os in zip(pieces, OFFSETS)
@@ -416,7 +400,10 @@
         hot = (place[:, None] == jnp.arange(N_PEER * COLUMN, dtype=i32)[None, :]).astype(bf16)
         return couple_call(jnp.dot(hot, whole, preferred_element_type=f32), couplings)
 
-    mine = lax.cond(fits[0] != 0, lambda mine, *_: mine, every, mine, pieces, couplings)
+    def some(sel, got, pieces, couplings):
+        return select_call(sel, got, couplings)
+
+    mine = lax.cond(fits[0] != 0, some, every, sel, got, pieces, couplings)
     theirs = shifted(mine, "n", 1)
     return final_call(scalars, mine, theirs, tgt_basis, near)
 

time: 78.9 us -> 77.1 us (0.977)
  local copies, waits for them, and re-layouts: 4.44 us -> 3.1 us
    cond x1 -> x0, local copies, waits for them, and re-layouts: 1.36 us -> none
    unnamed x12 -> x22, local copies, waits for them, and re-layouts: 3.08 us -> 3.1 us
  transfers between devices with their start and end apart: 10 -> 10, of which waited for: 4 -> 4; matrix products, arithmetic and copies ran while one was open for 2% -> 0% of each run, Pallas kernels for 25% -> 25%
where the time goes in v7:
time: 77.1 us; the launch traced here: 76.5 us
  starting transfers between devices  29.9 us (39%)
  Pallas kernels  23.1 us (30%)
  waiting for transfers between devices  18.9 us (25%)
  local copies, waits for them, and re-layouts  3.1 us (4%)
  between operations  1.43 us (2%)
    ppermute x8, starting transfers between devices, shifted(): lax.ppermute(array, axis, [(i, (i + by) % devices) for i in range(devices)])  18.3 us
    ppermute x8, waiting for transfers between devices, shifted(): lax.ppermute(array, axis, [(i, (i + by) % devices) for i in range(devices)])  17.5 us
    pallas_call x3, Pallas kernels, near_call(): pl.pallas_call(lambda *refs: near_kernel(kind, leaves, group, *refs), out...  14.1 us
    all_to_all x1, starting transfers between devices, body(): asked = lax.all_to_all(req, PEERS, split_axis=0, concat_axis=0, tiled=True)  5.78 us
    all_to_all x1, starting transfers between devices, body(): got = lax.all_to_all(packed, PEERS, split_axis=0, concat_axis=0, tiled=True)  5.73 us
    pallas_call x1, Pallas kernels, select_call(): pl.pallas_call(select_kernel, out_shape=TC_SHAPE, in_specs=[VMEM, VMEM, V...  3.11 us
    unnamed x22, local copies, waits for them, and re-layouts  3.1 us
    pallas_call x1, Pallas kernels, index_call(): pl.pallas_call(index_kernel, out_shape=(jax.ShapeDtypeStruct((ENTRIES, 12...  2.18 us
  transfers between devices with their start and end apart: 10, of which 4 were waited for; matrix products, arithmetic and copies ran while one was open for 0% of the time, Pallas kernels for 25%

profile of v7, /device:TPU:24, one launch (start us, length us, event | category | flops | bytes accessed | tf_op | source)
XLA Modules:
  0.0 76.5 jit_solution(2198537717309032620)
XLA Ops:
  0.0 1.2 %copy-done.1 = bf16[32,64,256]{2,1,0:T(8,128)(2,1)S(1)} copy-done((bf16[32,64,256]{2,1,0:T(8,128)(2,1)S(1)}, bf16[32,64,256]{2,1,0:T(8,128)(2,1)}, u32[]{:S(2)}) %copy-start.1) | copy-done | bytes 1048600
  1.2 0.9 %copy-done.2 = bf16[32,16,256]{2,1,0:T(8,128)(2,1)S(1)} copy-done((bf16[32,16,256]{2,1,0:T(8,128)(2,1)S(1)}, bf16[32,16,256]{2,1,0:T(8,128)(2,1)}, u32[]{:S(2)}) %copy-start.2) | copy-done | bytes 262168
  2.2 0.6 coeffs.1
  2.8 1.3 %collective-permute-start = (bf16[640,256]{1,0:T(8,128)(2,1)S(1)}, bf16[640,256]{1,0:T(8,128)(2,1)S(1)}, u32[]{:S(2)}, u32[]{:S(2)}) collective-permute-start(bf16[640,256]{1,0:T(8,128)(2,1)S(1)} %get-tuple-element.53.refs_2_), channel_id=1, source_target_pairs={{0,1},{1,0},{2,3},{3,2},{4,5},{5,4},{6,7},{7,6},{8,9},{9,8},{10,11... | collective-permute-start | bytes 983048 | tf_op jit(solution)/shard_map/ppermute | solution.py:354
  4.8 9.1 %collective-permute-done.refs_3_ = bf16[640,256]{1,0:T(8,128)(2,1)S(1)} collective-permute-done((bf16[640,256]{1,0:T(8,128)(2,1)S(1)}, bf16[640,256]{1,0:T(8,128)(2,1)S(1)}, u32[]{:S(2)}, u32[]{:S(2)}) %collective-permute-start) | collective-permute-done | bytes 327712 | tf_op jit(solution)/shard_map/ppermute | solution.py:354
  13.9 5.9 %collective-permute-start.2 = (bf16[64,256]{1,0:T(8,128)(2,1)S(1)}, bf16[64,256]{1,0:T(8,128)(2,1)S(1)}, u32[]{:S(2)}, u32[]{:S(2)}) collective-permute-start(bf16[64,256]{1,0:T(8,128)(2,1)S(1)} %add_convert_fusion.refs_0_), channel_id=1, source_target_pairs={{0,112},{16,0},{32,16},{48,32},{64,48},{80,64},{96,80},{112,96},{1... | collective-permute-start | bytes 98312 | tf_op jit(solution)/shard_map/ppermute | solution.py:354
  19.8 0.0 collective-permute-start.1
  19.8 0.1 pad_add_fusion.scalar_ref.refs_0_
  19.9 0.9 %copy-done.3 = bf16[32,3,512]{2,0,1:T(8,128)(2,1)S(1)} copy-done((bf16[32,3,512]{2,0,1:T(8,128)(2,1)S(1)}, bf16[32,3,512]{2,0,1:T(8,128)(2,1)}, u32[]{:S(2)}) %copy-start.3) | copy-done | bytes 98328
  20.8 2.2 %requests.1 = (s32[256,128]{1,0:T(8,128)}, bf16[16,40,128]{2,1,0:T(8,128)(2,1)}, bf16[32,8,512]{2,1,0:T(8,128)(2,1)S(1)}) custom-call(s32[2]{0:T(128)S(1)} %pad_add_fusion.scalar_ref.refs_0_, s32[8,32]{1,0:T(8,128)} %bitcast.10, bf16[3,32,512]{2,1,0:T(8,128)(2,1)S(1)} %bitcast.9), custom_call_target="tpu_custom_call" | custom-call | tf_op jit(solution)/shard_map/requests/pallas_call | solution.py:81
  23.0 5.8 %all-to-all-start.1 = ((bf16[16,40,128]{2,1,0:T(8,128)(2,1)}), bf16[16,40,128]{2,1,0:T(8,128)(2,1)S(1)}, u32[]{:S(2)}, u32[]{:S(2)}) async-start(bf16[16,40,128]{2,1,0:T(8,128)(2,1)} %get-tuple-element.51), calls=%async_computation.1 | async-start | bytes 327680 | tf_op jit(solution)/shard_map/all_to_all | solution.py:370
  28.7 0.0 collective-permute-done.2.refs_2_
  28.8 0.0 collective-permute-done.1.refs_1_
  28.8 3.0 %collective-permute-start.3 = (bf16[192,256]{1,0:T(8,128)(2,1)S(1)}, bf16[192,256]{1,0:T(8,128)(2,1)S(1)}, u32[]{:S(2)}, u32[]{:S(2)}) collective-permute-start(bf16[192,256]{1,0:T(8,128)(2,1)S(1)} %pad_maximum_fusion.8), channel_id=1, source_target_pairs={{0,80},{16,96},{32,112},{48,0},{64,16},{80,32},{96,48},{112,64},{1... | collective-permute-start | bytes 294920 | tf_op jit(solution)/shard_map/ppermute | solution.py:354
  31.8 0.9 %collective-permute-start.4 = (bf16[128,256]{1,0:T(8,128)(2,1)S(1)}, bf16[128,256]{1,0:T(8,128)(2,1)S(1)}, u32[]{:S(2)}, u32[]{:S(2)}) collective-permute-start(bf16[128,256]{1,0:T(8,128)(2,1)S(1)} %pad_maximum_fusion.9), channel_id=1, source_target_pairs={{0,48},{16,64},{32,80},{48,96},{64,112},{80,0},{96,16},{112,32},{1... | collective-permute-start | bytes 196616 | tf_op jit(solution)/shard_map/ppermute | solution.py:354
  32.7 1.4 %all-to-all-done.1.req_ref = bf16[16,40,128]{2,1,0:T(8,128)(2,1)S(1)} async-done(((bf16[16,40,128]{2,1,0:T(8,128)(2,1)}), bf16[16,40,128]{2,1,0:T(8,128)(2,1)S(1)}, u32[]{:S(2)}, u32[]{:S(2)}) %all-to-all-start.1) | async-done | bytes 163872 | tf_op jit(solution)/shard_map/all_to_all | solution.py:370
  34.1 6.6 %collective-permute-done.4.refs_4_ = bf16[128,256]{1,0:T(8,128)(2,1)S(1)} collective-permute-done((bf16[128,256]{1,0:T(8,128)(2,1)S(1)}, bf16[128,256]{1,0:T(8,128)(2,1)S(1)}, u32[]{:S(2)}, u32[]{:S(2)}) %collective-permute-start.4) | collective-permute-done | bytes 65568 | tf_op jit(solution)/shard_map/ppermute | solution.py:354
  40.7 1.2 %pack.1 = (bf16[16,40,512]{2,1,0:T(8,128)(2,1)}, s32[1]{0:T(128)}) custom-call(s32[1]{0:T(128)} %bitcast.3.z_ref, bf16[16,40,128]{2,1,0:T(8,128)(2,1)S(1)} %all-to-all-done.1.req_ref, bf16[64,256]{1,0:T(8,128)(2,1)S(1)} %add_convert_fusion.refs_0_, bf16[64,256]{1,0:T(8,128)(2,1)S(1)} %collective-permute-done.1.refs_1_, ...), custom_call_target="tpu_custom_call" | custom-call | tf_op jit(solution)/shard_map/pack/pallas_call | solution.py:157
  41.9 5.7 %all-to-all-start.2 = ((bf16[16,40,512]{2,1,0:T(8,128)(2,1)}), bf16[16,40,512]{2,1,0:T(8,128)(2,1)}, u32[]{:S(2)}, u32[]{:S(2)}) async-start(bf16[16,40,512]{2,1,0:T(8,128)(2,1)} %get-tuple-element.56), calls=%async_computation.2 | async-start | bytes 1310720 | tf_op jit(solution)/shard_map/all_to_all | solution.py:387
  47.7 3.7 %near.3 = (f32[32,16,256]{2,1,0:T(8,128)S(1)}, bf16[24,512]{1,0:T(8,128)(2,1)}, bf16[24,512]{1,0:T(8,128)(2,1)}) custom-call(s32[2]{0:T(128)S(1)} %pad_add_fusion.scalar_ref.refs_0_, bf16[32,8,512]{2,1,0:T(8,128)(2,1)S(1)} %get-tuple-element.57.refs_1_, bf16[640,256]{1,0:T(8,128)(2,1)S(1)} %get-tuple-element.53.refs_2_, ...), custom_call_target="tpu_custom_call" | custom-call | flops 1600000000 | bytes 2000000 | tf_op jit(solution)/shard_map/near/pallas_call | solution.py:308
  51.4 0.1 collective-permute-start.6
  51.6 5.8 %collective-permute-start.7 = (bf16[24,512]{1,0:T(8,128)(2,1)}, bf16[24,512]{1,0:T(8,128)(2,1)}, u32[]{:S(2)}, u32[]{:S(2)}) collective-permute-start(bf16[24,512]{1,0:T(8,128)(2,1)} %get-tuple-element.59), channel_id=1, source_target_pairs={{0,254},{2,0},{4,2},{6,4},{8,6},{10,8},{12,10},{14,12},{16,14},{18... | collective-permute-start | bytes 73736 | tf_op jit(solution)/shard_map/ppermute | solution.py:354
  57.4 7.8 %near.4.refs_6_ = f32[32,16,256]{2,1,0:T(8,128)S(1)} custom-call(s32[2]{0:T(128)S(1)} %pad_add_fusion.scalar_ref.refs_0_, bf16[32,8,512]{2,1,0:T(8,128)(2,1)S(1)} %get-tuple-element.57.refs_1_, bf16[640,256]{1,0:T(8,128)(2,1)S(1)} %get-tuple-element.53.refs_2_, bf16[640,256]{1,0:T(8,128)(2,1)S(1)} %collective-permute-done.refs_3_, ...), custom_call_target="tpu_custom_call", output_to_operand_aliasing={{}: (4, {})} | custom-call | flops 4000000000 | bytes 2000000 | tf_op jit(solution)/shard_map/near/pallas_call | solution.py:308
  65.8 0.0 all-to-all-done.2
  65.8 3.1 %conditional.1 = (bf16[4,32,128]{2,1,0:T(8,128)(2,1)}) conditional(s32[]{:T(128)} %bitcast.6, (s32[32,8]{0,1:T(8,128)S(1)}, bf16[64,256]{1,0:T(8,128)(2,1)}, bf16[64,256]{1,0:T(8,128)(2,1)}, bf16[192,256]{1,0:T(8,128)(2,1)}, bf16[128,256]{1,0:T(8,128)(2,1)}, /*index=5*/bf16[64,256]{1,0:T(8,128)(2,1)}, s32[]{:T(128)}, ...), branch_computations={%region_0.1_spmd, %region_1.2_spmd} | conditional | flops 1075842048 | bytes 23860436 | solution.py:406
  65.9 3.1 %select.3 = bf16[4,32,128]{2,1,0:T(8,128)(2,1)} custom-call(s32[256,128]{1,0:T(8,128)} %get-tuple-element.38.sel_ref, bf16[16,40,512]{2,1,0:T(8,128)(2,1)} %get-tuple-element.39.got_ref, bf16[32,64,512]{2,1,0:T(8,128)(2,1)S(1)} %get-tuple-element.40.couple_ref), custom_call_target="tpu_custom_call" | custom-call | tf_op jit(solution)/shard_map/cond/branch_1_fun/select/pallas_call | solution.py:207
  69.0 1.2 %collective-permute-start.5 = (bf16[4,32,128]{2,1,0:T(8,128)(2,1)}, bf16[4,32,128]{2,1,0:T(8,128)(2,1)S(1)}, u32[]{:S(2)}, u32[]{:S(2)}) collective-permute-start(bf16[4,32,128]{2,1,0:T(8,128)(2,1)} %get-tuple-element.83.mine_ref), channel_id=1, source_target_pairs={{0,1},{1,0},{2,3},{3,2},{4,5},{5,4},{6,7},{7,6},{8,9},{9,8},{10,11... | collective-permute-start | bytes 98312 | tf_op jit(solution)/shard_map/ppermute | solution.py:354
  70.2 0.0 collective-permute-done.6.refs_4_
  70.2 0.0 collective-permute-done.7.refs_5_
  70.2 2.6 %near.5.near_ref = f32[32,16,256]{2,1,0:T(8,128)S(1)} custom-call(s32[2]{0:T(128)S(1)} %pad_add_fusion.scalar_ref.refs_0_, bf16[32,8,512]{2,1,0:T(8,128)(2,1)S(1)} %get-tuple-element.57.refs_1_, bf16[640,256]{1,0:T(8,128)(2,1)S(1)} %get-tuple-element.53.refs_2_, bf16[640,256]{1,0:T(8,128)(2,1)S(1)} %collective-permute-done.refs_3_, ...), custom_call_target="tpu_custom_call", output_to_operand_aliasing={{}: (6, {})} | custom-call | flops 1000000000 | bytes 2000000 | tf_op jit(solution)/shard_map/near/pallas_call | solution.py:308
  72.8 1.8 %collective-permute-done.5.theirs_ref = bf16[4,32,128]{2,1,0:T(8,128)(2,1)S(1)} collective-permute-done((bf16[4,32,128]{2,1,0:T(8,128)(2,1)}, bf16[4,32,128]{2,1,0:T(8,128)(2,1)S(1)}, u32[]{:S(2)}, u32[]{:S(2)}) %collective-permute-start.5) | collective-permute-done | bytes 32800 | tf_op jit(solution)/shard_map/ppermute | solution.py:354
  74.6 1.9 %final.1 = bf16[32,16,256]{2,1,0:T(8,128)(2,1)} custom-call(s32[2]{0:T(128)S(1)} %pad_add_fusion.scalar_ref.refs_0_, bf16[4,32,128]{2,1,0:T(8,128)(2,1)} %get-tuple-element.83.mine_ref, bf16[4,32,128]{2,1,0:T(8,128)(2,1)S(1)} %collective-permute-done.5.theirs_ref, bf16[32,64,512]{2,1,0:T(8,128)(2,1)S(1)} %copy-done, f32[32,16,256]{2,1,0:T(8,128)S(1)} %near.5.near_ref), custom_call_target="tpu_custom_call" | custom-call | tf_op jit(solution)/shard_map/final/pallas_call | solution.py:341
  (23 shorter events, 0.1 us)
Async XLA Ops:
  0.0 1.2 %copy-start.1 = (bf16[32,64,256]{2,1,0:T(8,128)(2,1)S(1)}, bf16[32,64,256]{2,1,0:T(8,128)(2,1)}, u32[]{:S(2)}) copy-start(bf16[32,64,256]{2,1,0:T(8,128)(2,1)} %basis_ref.1) | copy-start | bytes 3145732
  1.2 0.9 %copy-start.2 = (bf16[32,16,256]{2,1,0:T(8,128)(2,1)S(1)}, bf16[32,16,256]{2,1,0:T(8,128)(2,1)}, u32[]{:S(2)}) copy-start(bf16[32,16,256]{2,1,0:T(8,128)(2,1)} %vec_ref.1) | copy-start | bytes 786436
  2.8 11.0 %collective-permute-start = (bf16[640,256]{1,0:T(8,128)(2,1)S(1)}, bf16[640,256]{1,0:T(8,128)(2,1)S(1)}, u32[]{:S(2)}, u32[]{:S(2)}) collective-permute-start(bf16[640,256]{1,0:T(8,128)(2,1)S(1)} %get-tuple-element.53.refs_2_), channel_id=1, source_target_pairs={{0,1},{1,0},{2,3},{3,2},{4,5},{5,4},{6,7},{7,6},{8,9},{9,8},{10,11... | collective-permute-start | bytes 983048 | tf_op jit(solution)/shard_map/ppermute | solution.py:354
  13.9 37.6 %copy-start.5 = (bf16[64,256]{1,0:T(8,128)(2,1)}, bf16[64,256]{1,0:T(8,128)(2,1)S(1)}, u32[]{:S(2)}) copy-start(bf16[64,256]{1,0:T(8,128)(2,1)S(1)} %add_convert_fusion.refs_0_) | copy-start | bytes 98308
  13.9 14.9 %collective-permute-start.2 = (bf16[64,256]{1,0:T(8,128)(2,1)S(1)}, bf16[64,256]{1,0:T(8,128)(2,1)S(1)}, u32[]{:S(2)}, u32[]{:S(2)}) collective-permute-start(bf16[64,256]{1,0:T(8,128)(2,1)S(1)} %add_convert_fusion.refs_0_), channel_id=1, source_target_pairs={{0,112},{16,0},{32,16},{48,32},{64,48},{80,64},{96,80},{112,96},{1... | collective-permute-start | bytes 98312 | tf_op jit(solution)/shard_map/ppermute | solution.py:354
  19.8 8.9 %collective-permute-start.1 = (bf16[64,256]{1,0:T(8,128)(2,1)S(1)}, bf16[64,256]{1,0:T(8,128)(2,1)S(1)}, u32[]{:S(2)}, u32[]{:S(2)}) collective-permute-start(bf16[64,256]{1,0:T(8,128)(2,1)S(1)} %add_convert_fusion.refs_0_), channel_id=1, source_target_pairs={{0,16},{16,32},{32,48},{48,64},{64,80},{80,96},{96,112},{112,0},{1... | collective-permute-start | bytes 98312 | tf_op jit(solution)/shard_map/ppermute | solution.py:354
  19.9 0.9 %copy-start.3 = (bf16[32,3,512]{2,0,1:T(8,128)(2,1)S(1)}, bf16[32,3,512]{2,0,1:T(8,128)(2,1)}, u32[]{:S(2)}) copy-start(bf16[32,3,512]{2,0,1:T(8,128)(2,1)} %param.9) | copy-start | bytes 294916
  23.0 11.2 %all-to-all-start.1 = ((bf16[16,40,128]{2,1,0:T(8,128)(2,1)}), bf16[16,40,128]{2,1,0:T(8,128)(2,1)S(1)}, u32[]{:S(2)}, u32[]{:S(2)}) async-start(bf16[16,40,128]{2,1,0:T(8,128)(2,1)} %get-tuple-element.51), calls=%async_computation.1 | async-start | bytes 327680 | tf_op jit(solution)/shard_map/all_to_all | solution.py:370
  28.7 18.9 %copy-start.6 = (bf16[64,256]{1,0:T(8,128)(2,1)}, bf16[64,256]{1,0:T(8,128)(2,1)S(1)}, u32[]{:S(2)}) copy-start(bf16[64,256]{1,0:T(8,128)(2,1)S(1)} %collective-permute-done.2.refs_2_) | copy-start | bytes 98308
  28.8 18.9 %copy-start.8 = (bf16[64,256]{1,0:T(8,128)(2,1)}, bf16[64,256]{1,0:T(8,128)(2,1)S(1)}, u32[]{:S(2)}) copy-start(bf16[64,256]{1,0:T(8,128)(2,1)S(1)} %collective-permute-done.1.refs_1_) | copy-start | bytes 98308
  28.8 11.9 %collective-permute-start.3 = (bf16[192,256]{1,0:T(8,128)(2,1)S(1)}, bf16[192,256]{1,0:T(8,128)(2,1)S(1)}, u32[]{:S(2)}, u32[]{:S(2)}) collective-permute-start(bf16[192,256]{1,0:T(8,128)(2,1)S(1)} %pad_maximum_fusion.8), channel_id=1, source_target_pairs={{0,80},{16,96},{32,112},{48,0},{64,16},{80,32},{96,48},{112,64},{1... | collective-permute-start | bytes 294920 | tf_op jit(solution)/shard_map/ppermute | solution.py:354
  31.8 8.9 %collective-permute-start.4 = (bf16[128,256]{1,0:T(8,128)(2,1)S(1)}, bf16[128,256]{1,0:T(8,128)(2,1)S(1)}, u32[]{:S(2)}, u32[]{:S(2)}) collective-permute-start(bf16[128,256]{1,0:T(8,128)(2,1)S(1)} %pad_maximum_fusion.9), channel_id=1, source_target_pairs={{0,48},{16,64},{32,80},{48,96},{64,112},{80,0},{96,16},{112,32},{1... | collective-permute-start | bytes 196616 | tf_op jit(solution)/shard_map/ppermute | solution.py:354
  40.7 7.0 %copy-start.9 = (bf16[128,256]{1,0:T(8,128)(2,1)}, bf16[128,256]{1,0:T(8,128)(2,1)S(1)}, u32[]{:S(2)}) copy-start(bf16[128,256]{1,0:T(8,128)(2,1)S(1)} %collective-permute-done.4.refs_4_) | copy-start | bytes 196612
  40.7 7.0 %copy-start.7 = (bf16[192,256]{1,0:T(8,128)(2,1)}, bf16[192,256]{1,0:T(8,128)(2,1)S(1)}, u32[]{:S(2)}) copy-start(bf16[192,256]{1,0:T(8,128)(2,1)S(1)} %collective-permute-done.3.refs_3_) | copy-start | bytes 294916
  41.9 23.9 %all-to-all-start.2 = ((bf16[16,40,512]{2,1,0:T(8,128)(2,1)}), bf16[16,40,512]{2,1,0:T(8,128)(2,1)}, u32[]{:S(2)}, u32[]{:S(2)}) async-start(bf16[16,40,512]{2,1,0:T(8,128)(2,1)} %get-tuple-element.56), calls=%async_computation.2 | async-start | bytes 1310720 | tf_op jit(solution)/shard_map/all_to_all | solution.py:387
  51.4 18.8 %collective-permute-start.6 = (bf16[24,512]{1,0:T(8,128)(2,1)}, bf16[24,512]{1,0:T(8,128)(2,1)}, u32[]{:S(2)}, u32[]{:S(2)}) collective-permute-start(bf16[24,512]{1,0:T(8,128)(2,1)} %get-tuple-element.58), channel_id=1, source_target_pairs={{0,2},{2,4},{4,6},{6,8},{8,10},{10,12},{12,14},{14,16},{16,18},{18... | collective-permute-start | bytes 73736 | tf_op jit(solution)/shard_map/ppermute | solution.py:354
  51.6 18.7 %collective-permute-start.7 = (bf16[24,512]{1,0:T(8,128)(2,1)}, bf16[24,512]{1,0:T(8,128)(2,1)}, u32[]{:S(2)}, u32[]{:S(2)}) collective-permute-start(bf16[24,512]{1,0:T(8,128)(2,1)} %get-tuple-element.59), channel_id=1, source_target_pairs={{0,254},{2,0},{4,2},{6,4},{8,6},{10,8},{12,10},{14,12},{16,14},{18... | collective-permute-start | bytes 73736 | tf_op jit(solution)/shard_map/ppermute | solution.py:354
  57.4 8.4 %copy-start.4 = (bf16[32,64,512]{2,1,0:T(8,128)(2,1)S(1)}, bf16[32,64,512]{2,1,0:T(8,128)(2,1)}, u32[]{:S(2)}) copy-start(bf16[32,64,512]{2,1,0:T(8,128)(2,1)} %param.15) | copy-start | bytes 6291460
  57.4 8.4 %copy-start.10 = (s32[32,8]{0,1:T(8,128)S(1)}, s32[32,8]{0,1:T(8,128)}, u32[]{:S(2)}) copy-start(s32[32,8]{0,1:T(8,128)} %param.14) | copy-start | bytes 3076
  69.0 5.6 %copy-start = (bf16[32,64,512]{2,1,0:T(8,128)(2,1)S(1)}, bf16[32,64,512]{2,1,0:T(8,128)(2,1)}, u32[]{:S(2)}) copy-start(bf16[32,64,512]{2,1,0:T(8,128)(2,1)} %tgt_ref.1) | copy-start | bytes 6291460
  69.0 5.6 %collective-permute-start.5 = (bf16[4,32,128]{2,1,0:T(8,128)(2,1)}, bf16[4,32,128]{2,1,0:T(8,128)(2,1)S(1)}, u32[]{:S(2)}, u32[]{:S(2)}) collective-permute-start(bf16[4,32,128]{2,1,0:T(8,128)(2,1)} %get-tuple-element.83.mine_ref), channel_id=1, source_target_pairs={{0,1},{1,0},{2,3},{3,2},{4,5},{5,4},{6,7},{7,6},{8,9},{9,8},{10,11... | collective-permute-start | bytes 98312 | tf_op jit(solution)/shard_map/ppermute | solution.py:354

commit v8 on v7

--- a/solution.py
+++ b/solution.py
@@ -21,7 +21,6 @@
 CAP = 40
 ENTRIES = T * J
 OFFSETS = (0,), (-1,), (1,), (2, 3, 4), (-2, -3)
-SENT = T * R + 4 * T
 COLUMN = N_Z * T
 bf16, f32, i32 = jnp.bfloat16, jnp.float32, jnp.int32
 
@@ -92,27 +91,19 @@
     )(scalars, adm, points)
 
 
-def coeff_kernel(n_ref, vec_ref, basis_ref, keep_ref, send_ref, rows):
+def coeff_kernel(n_ref, vec_ref, basis_ref, keep_ref, send_ref, held_ref, rows):
     n = n_ref[0]
     same = (iota((64, 256), 0) >> 4) == (iota((64, 256), 1) >> 6)
     for g in range(T // 4):
         lhs = vec_ref[4 * g : 4 * g + 4].reshape(64, HALF)
-        send_ref[64 * g : 64 * g + 64] = lhs
+        held_ref[64 * g : 64 * g + 64] = lhs
         rhs = basis_ref[4 * g : 4 * g + 4].reshape(4 * A, HALF)
         rows[64 * g : 64 * g + 64, :64] = folded(jnp.where(same, nt(lhs, rhs), 0.0))
-    for mine, first in ((False, (1 - n) * RH), (True, n * RH)):
+    for out, first in ((send_ref, (1 - n) * RH), (keep_ref, n * RH)):
         for r in range(0, RH, 2):
             pair = [rows[pl.ds(first + r + k, T, stride=R), :][:, :64] for k in range(2)]
-            value = jnp.concatenate(pair, 1)
             row, lane = r * A // HALF * T, r * A % HALF
-            if mine:
-                keep_ref[row : row + T, lane : lane + 2 * A] = value
-            else:
-                high = value.astype(bf16)
-                row += T * R
-                send_ref[row : row + T, lane : lane + 2 * A] = high
-                row += 2 * T
-                send_ref[row : row + T, lane : lane + 2 * A] = (value - high.astype(f32)).astype(bf16)
+            out[row : row + T, lane : lane + 2 * A] = jnp.concatenate(pair, 1)
 
 
 def coeff_call(n, vectors, basis):
@@ -120,10 +111,11 @@
         coeff_kernel,
         out_shape=(
             jax.ShapeDtypeStruct((2 * T, HALF), f32),
-            jax.ShapeDtypeStruct((SENT, HALF), bf16),
+            jax.ShapeDtypeStruct((2 * T, HALF), f32),
+            jax.ShapeDtypeStruct((T * R, HALF), bf16),
         ),
         in_specs=[SMEM, VMEM, VMEM],
-        out_specs=(VMEM, VMEM),
+        out_specs=(VMEM, VMEM, VMEM),
         scratch_shapes=[pltpu.VMEM((T * R, 128), f32)],
         name="coeffs",
         compiler_params=LIMIT,
@@ -364,20 +356,20 @@
     z = lax.axis_index("z").astype(i32)
     scalars = jnp.stack([counts[0], n])
 
-    keep, send = coeff_call(n[None], vectors, src_basis)
+    keep, send, held = coeff_call(n[None], vectors, src_basis)
     came = shifted(send, "n", 1)
+    other = shifted(held, "n", 1)
     sel, req, rows = index_call(scalars, adm_src.T, points.transpose(1, 0, 2))
     asked = lax.all_to_all(req, PEERS, split_axis=0, concat_axis=0, tiled=True)
 
-    high, low = came[T * R : T * R + 2 * T], came[T * R + 2 * T :]
-    coeffs = (keep + high.astype(f32) + low.astype(f32)).astype(bf16)
+    coeffs = (keep + came).astype(bf16)
     below = shifted(coeffs, "z", 1)
     above = shifted(coeffs, "z", -1)
     up = shifted(jnp.concatenate([below, coeffs, above]), "z", -3)
     down = shifted(jnp.concatenate([above, coeffs]), "z", 3)
     pieces = coeffs, below, above, up, down
 
-    near_args = (scalars, rows, send, came)
+    near_args = (scalars, rows, held, other)
     near, first, last = near_call("early", (2, 10), 8, near_args)
     halos = shifted(last, WIDE, 1), shifted(first, WIDE, -1)
     (near,) = near_call("inner", (10, 30), 10, near_args, (near,))

time: 77.1 us -> 71 us (0.921)
  waiting for transfers between devices: 18.9 us -> 12.8 us
  starting transfers between devices: 29.9 us -> 31.6 us
  Pallas kernels: 23.1 us -> 21.5 us
    ppermute x8 -> x9, waiting for transfers between devices: 17.5 us -> 11.4 us  [shifted(): lax.ppermute(array, axis, [(i, (i + by) % devices) for i in range(devices)])]
    ppermute x8 -> x9, starting transfers between devices: 18.3 us -> 20.1 us  [shifted(): lax.ppermute(array, axis, [(i, (i + by) % devices) for i in range(devices)])]
    unnamed x22 -> x20, local copies, waits for them, and re-layouts: 3.1 us -> 3.09 us
  transfers between devices with their start and end apart: 10 -> 11, of which waited for: 4 -> 4; matrix products, arithmetic and copies ran while one was open for 0% -> 0% of each run, Pallas kernels for 25% -> 27%
where the time goes in v8:
time: 71 us; the launch traced here: 70.6 us
  starting transfers between devices  31.6 us (45%)
  Pallas kernels  21.5 us (30%)
  waiting for transfers between devices  12.8 us (18%)
  local copies, waits for them, and re-layouts  3.09 us (4%)
  between operations  1.43 us (2%)
    ppermute x9, starting transfers between devices, shifted(): lax.ppermute(array, axis, [(i, (i + by) % devices) for i in range(devices)])  20.1 us
    pallas_call x3, Pallas kernels, near_call(): pl.pallas_call(lambda *refs: near_kernel(kind, leaves, group, *refs), out...  13.3 us
    ppermute x9, waiting for transfers between devices, shifted(): lax.ppermute(array, axis, [(i, (i + by) % devices) for i in range(devices)])  11.4 us
    all_to_all x1, starting transfers between devices, body(): asked = lax.all_to_all(req, PEERS, split_axis=0, concat_axis=0, tiled=True)  5.78 us
    all_to_all x1, starting transfers between devices, body(): got = lax.all_to_all(packed, PEERS, split_axis=0, concat_axis=0, tiled=True)  5.73 us
    unnamed x20, local copies, waits for them, and re-layouts  3.09 us
    pallas_call x1, Pallas kernels, select_call(): pl.pallas_call(select_kernel, out_shape=TC_SHAPE, in_specs=[VMEM, VMEM, V...  2.49 us
    pallas_call x1, Pallas kernels, index_call(): pl.pallas_call(index_kernel, out_shape=(jax.ShapeDtypeStruct((ENTRIES, 12...  2.18 us
  transfers between devices with their start and end apart: 11, of which 4 were waited for; matrix products, arithmetic and copies ran while one was open for 0% of the time, Pallas kernels for 27%

profile of v8, /device:TPU:24, one launch (start us, length us, event | category | flops | bytes accessed | tf_op | source)
XLA Modules:
  0.0 70.6 jit_solution(14612284966876339121)
XLA Ops:
  0.0 1.2 %copy-done.1 = bf16[32,64,256]{2,1,0:T(8,128)(2,1)S(1)} copy-done((bf16[32,64,256]{2,1,0:T(8,128)(2,1)S(1)}, bf16[32,64,256]{2,1,0:T(8,128)(2,1)}, u32[]{:S(2)}) %copy-start.1) | copy-done | bytes 1048600
  1.2 0.9 %copy-done.2 = bf16[32,16,256]{2,1,0:T(8,128)(2,1)S(1)} copy-done((bf16[32,16,256]{2,1,0:T(8,128)(2,1)S(1)}, bf16[32,16,256]{2,1,0:T(8,128)(2,1)}, u32[]{:S(2)}) %copy-start.2) | copy-done | bytes 262168
  2.2 0.6 coeffs.1
  2.8 1.3 %collective-permute-start = (f32[64,256]{1,0:T(8,128)S(1)}, f32[64,256]{1,0:T(8,128)S(1)}, u32[]{:S(2)}, u32[]{:S(2)}) collective-permute-start(f32[64,256]{1,0:T(8,128)S(1)} %get-tuple-element.54), channel_id=1, source_target_pairs={{0,1},{1,0},{2,3},{3,2},{4,5},{5,4},{6,7},{7,6},{8,9},{9,8},{10,11... | collective-permute-start | bytes 196616 | tf_op jit(solution)/shard_map/ppermute | solution.py:346
  4.1 2.3 %collective-permute-start.6 = (bf16[512,256]{1,0:T(8,128)(2,1)S(1)}, bf16[512,256]{1,0:T(8,128)(2,1)S(1)}, u32[]{:S(2)}, u32[]{:S(2)}) collective-permute-start(bf16[512,256]{1,0:T(8,128)(2,1)S(1)} %get-tuple-element.59.refs_2_), channel_id=1, source_target_pairs={{0,1},{1,0},{2,3},{3,2},{4,5},{5,4},{6,7},{7,6},{8,9},{9,8},{10,11... | collective-permute-start | bytes 786440 | tf_op jit(solution)/shard_map/ppermute | solution.py:346
  7.1 2.3 %collective-permute-done = f32[64,256]{1,0:T(8,128)S(1)} collective-permute-done((f32[64,256]{1,0:T(8,128)S(1)}, f32[64,256]{1,0:T(8,128)S(1)}, u32[]{:S(2)}, u32[]{:S(2)}) %collective-permute-start) | collective-permute-done | bytes 65568 | tf_op jit(solution)/shard_map/ppermute | solution.py:346
  9.4 5.9 %collective-permute-start.2 = (bf16[64,256]{1,0:T(8,128)(2,1)S(1)}, bf16[64,256]{1,0:T(8,128)(2,1)S(1)}, u32[]{:S(2)}, u32[]{:S(2)}) collective-permute-start(bf16[64,256]{1,0:T(8,128)(2,1)S(1)} %add_convert_fusion.refs_0_), channel_id=1, source_target_pairs={{0,112},{16,0},{32,16},{48,32},{64,48},{80,64},{96,80},{112,96},{1... | collective-permute-start | bytes 98312 | tf_op jit(solution)/shard_map/ppermute | solution.py:346
  15.3 0.1 pad_add_fusion.scalar_ref.refs_0_
  15.4 0.9 %copy-done.3 = bf16[32,3,512]{2,0,1:T(8,128)(2,1)S(1)} copy-done((bf16[32,3,512]{2,0,1:T(8,128)(2,1)S(1)}, bf16[32,3,512]{2,0,1:T(8,128)(2,1)}, u32[]{:S(2)}) %copy-start.3) | copy-done | bytes 98328
  16.3 2.2 %requests.1 = (s32[256,128]{1,0:T(8,128)}, bf16[16,40,128]{2,1,0:T(8,128)(2,1)}, bf16[32,8,512]{2,1,0:T(8,128)(2,1)S(1)}) custom-call(s32[2]{0:T(128)S(1)} %pad_add_fusion.scalar_ref.refs_0_, s32[8,32]{1,0:T(8,128)} %bitcast.10, bf16[3,32,512]{2,1,0:T(8,128)(2,1)S(1)} %bitcast.9), custom_call_target="tpu_custom_call" | custom-call | tf_op jit(solution)/shard_map/requests/pallas_call | solution.py:80
  18.4 5.8 %all-to-all-start.1 = ((bf16[16,40,128]{2,1,0:T(8,128)(2,1)}), bf16[16,40,128]{2,1,0:T(8,128)(2,1)S(1)}, u32[]{:S(2)}, u32[]{:S(2)}) async-start(bf16[16,40,128]{2,1,0:T(8,128)(2,1)} %get-tuple-element.52), calls=%async_computation.1 | async-start | bytes 327680 | tf_op jit(solution)/shard_map/all_to_all | solution.py:363
  24.2 0.0 collective-permute-done.2.refs_2_
  24.3 3.0 %collective-permute-start.3 = (bf16[192,256]{1,0:T(8,128)(2,1)S(1)}, bf16[192,256]{1,0:T(8,128)(2,1)S(1)}, u32[]{:S(2)}, u32[]{:S(2)}) collective-permute-start(bf16[192,256]{1,0:T(8,128)(2,1)S(1)} %pad_maximum_fusion.8), channel_id=1, source_target_pairs={{0,80},{16,96},{32,112},{48,0},{64,16},{80,32},{96,48},{112,64},{1... | collective-permute-start | bytes 294920 | tf_op jit(solution)/shard_map/ppermute | solution.py:346
  27.3 0.9 %collective-permute-start.4 = (bf16[128,256]{1,0:T(8,128)(2,1)S(1)}, bf16[128,256]{1,0:T(8,128)(2,1)S(1)}, u32[]{:S(2)}, u32[]{:S(2)}) collective-permute-start(bf16[128,256]{1,0:T(8,128)(2,1)S(1)} %pad_maximum_fusion.9), channel_id=1, source_target_pairs={{0,48},{16,64},{32,80},{48,96},{64,112},{80,0},{96,16},{112,32},{1... | collective-permute-start | bytes 196616 | tf_op jit(solution)/shard_map/ppermute | solution.py:346
  28.2 1.4 %all-to-all-done.1.req_ref = bf16[16,40,128]{2,1,0:T(8,128)(2,1)S(1)} async-done(((bf16[16,40,128]{2,1,0:T(8,128)(2,1)}), bf16[16,40,128]{2,1,0:T(8,128)(2,1)S(1)}, u32[]{:S(2)}, u32[]{:S(2)}) %all-to-all-start.1) | async-done | bytes 163872 | tf_op jit(solution)/shard_map/all_to_all | solution.py:363
  29.6 6.6 %collective-permute-done.4.refs_4_ = bf16[128,256]{1,0:T(8,128)(2,1)S(1)} collective-permute-done((bf16[128,256]{1,0:T(8,128)(2,1)S(1)}, bf16[128,256]{1,0:T(8,128)(2,1)S(1)}, u32[]{:S(2)}, u32[]{:S(2)}) %collective-permute-start.4) | collective-permute-done | bytes 65568 | tf_op jit(solution)/shard_map/ppermute | solution.py:346
  36.2 1.2 %pack.1 = (bf16[16,40,512]{2,1,0:T(8,128)(2,1)}, s32[1]{0:T(128)}) custom-call(s32[1]{0:T(128)} %bitcast.3.z_ref, bf16[16,40,128]{2,1,0:T(8,128)(2,1)S(1)} %all-to-all-done.1.req_ref, bf16[64,256]{1,0:T(8,128)(2,1)S(1)} %add_convert_fusion.refs_0_, bf16[64,256]{1,0:T(8,128)(2,1)S(1)} %collective-permute-done.1.refs_1_, ...), custom_call_target="tpu_custom_call" | custom-call | tf_op jit(solution)/shard_map/pack/pallas_call | solution.py:149
  37.4 5.7 %all-to-all-start.2 = ((bf16[16,40,512]{2,1,0:T(8,128)(2,1)}), bf16[16,40,512]{2,1,0:T(8,128)(2,1)}, u32[]{:S(2)}, u32[]{:S(2)}) async-start(bf16[16,40,512]{2,1,0:T(8,128)(2,1)} %get-tuple-element.57), calls=%async_computation.2 | async-start | bytes 1310720 | tf_op jit(solution)/shard_map/all_to_all | solution.py:379
  43.8 0.0 collective-permute-done.6.refs_3_
  43.9 3.2 %near.3 = (f32[32,16,256]{2,1,0:T(8,128)S(1)}, bf16[24,512]{1,0:T(8,128)(2,1)S(1)}, bf16[24,512]{1,0:T(8,128)(2,1)S(1)}) custom-call(s32[2]{0:T(128)S(1)} %pad_add_fusion.scalar_ref.refs_0_, bf16[32,8,512]{2,1,0:T(8,128)(2,1)S(1)} %get-tuple-element.58.refs_1_, bf16[512,256]{1,0:T(8,128)(2,1)S(1)} %get-tuple-element.59.refs_2_, ...), custom_call_target="tpu_custom_call" | custom-call | flops 1600000000 | bytes 2000000 | tf_op jit(solution)/shard_map/near/pallas_call | solution.py:300
  47.1 0.1 collective-permute-start.7
  47.2 5.8 %collective-permute-start.8 = (bf16[24,512]{1,0:T(8,128)(2,1)S(1)}, bf16[24,512]{1,0:T(8,128)(2,1)S(1)}, u32[]{:S(2)}, u32[]{:S(2)}) collective-permute-start(bf16[24,512]{1,0:T(8,128)(2,1)S(1)} %get-tuple-element.61), channel_id=1, source_target_pairs={{0,254},{2,0},{4,2},{6,4},{8,6},{10,8},{12,10},{14,12},{16,14},{18... | collective-permute-start | bytes 73736 | tf_op jit(solution)/shard_map/ppermute | solution.py:346
  53.1 7.8 %near.4.refs_6_ = f32[32,16,256]{2,1,0:T(8,128)S(1)} custom-call(s32[2]{0:T(128)S(1)} %pad_add_fusion.scalar_ref.refs_0_, bf16[32,8,512]{2,1,0:T(8,128)(2,1)S(1)} %get-tuple-element.58.refs_1_, bf16[512,256]{1,0:T(8,128)(2,1)S(1)} %get-tuple-element.59.refs_2_, bf16[512,256]{1,0:T(8,128)(2,1)S(1)} %collective-permute-done.6.refs_3_, ...), custom_call_target="tpu_custom_call", output_to_operand_aliasing={{}: (4, {})} | custom-call | flops 4000000000 | bytes 2000000 | tf_op jit(solution)/shard_map/near/pallas_call | solution.py:300
  60.8 0.0 all-to-all-done.2
  60.9 2.5 %conditional.1 = (bf16[4,32,128]{2,1,0:T(8,128)(2,1)S(1)}) conditional(s32[]{:T(128)} %bitcast.6, (s32[32,8]{0,1:T(8,128)S(1)}, bf16[64,256]{1,0:T(8,128)(2,1)S(1)}, bf16[64,256]{1,0:T(8,128)(2,1)}, bf16[192,256]{1,0:T(8,128)(2,1)}, bf16[128,256]{1,0:T(8,128)(2,1)}, /*index=5*/bf16[64,256]{1,0:T(8,128)(2,1)}, s32[]{:T(128)}, ...), branch_computations={%region_0.1_spmd, %region_1.2_spmd} | conditional | flops 1075842048 | bytes 23860436 | solution.py:398
  60.9 2.5 %select.3 = bf16[4,32,128]{2,1,0:T(8,128)(2,1)S(1)} custom-call(s32[256,128]{1,0:T(8,128)} %get-tuple-element.38.sel_ref, bf16[16,40,512]{2,1,0:T(8,128)(2,1)} %get-tuple-element.39.got_ref, bf16[32,64,512]{2,1,0:T(8,128)(2,1)S(1)} %get-tuple-element.40.couple_ref), custom_call_target="tpu_custom_call" | custom-call | tf_op jit(solution)/shard_map/cond/branch_1_fun/select/pallas_call | solution.py:199
  63.4 0.6 collective-permute-start.5
  64.0 0.0 collective-permute-done.7.refs_4_
  64.0 0.0 collective-permute-done.8.refs_5_
  64.0 2.4 %near.5.near_ref = f32[32,16,256]{2,1,0:T(8,128)S(1)} custom-call(s32[2]{0:T(128)S(1)} %pad_add_fusion.scalar_ref.refs_0_, bf16[32,8,512]{2,1,0:T(8,128)(2,1)S(1)} %get-tuple-element.58.refs_1_, bf16[512,256]{1,0:T(8,128)(2,1)S(1)} %get-tuple-element.59.refs_2_, bf16[512,256]{1,0:T(8,128)(2,1)S(1)} %collective-permute-done.6.refs_3_, ...), custom_call_target="tpu_custom_call", output_to_operand_aliasing={{}: (6, {})} | custom-call | flops 1000000000 | bytes 2000000 | tf_op jit(solution)/shard_map/near/pallas_call | solution.py:300
  66.4 2.5 %collective-permute-done.5.theirs_ref = bf16[4,32,128]{2,1,0:T(8,128)(2,1)S(1)} collective-permute-done((bf16[4,32,128]{2,1,0:T(8,128)(2,1)S(1)}, bf16[4,32,128]{2,1,0:T(8,128)(2,1)S(1)}, u32[]{:S(2)}, u32[]{:S(2)}) %collective-permute-start.5) | collective-permute-done | bytes 32800 | tf_op jit(solution)/shard_map/ppermute | solution.py:346
  68.9 1.7 %final.1 = bf16[32,16,256]{2,1,0:T(8,128)(2,1)} custom-call(s32[2]{0:T(128)S(1)} %pad_add_fusion.scalar_ref.refs_0_, bf16[4,32,128]{2,1,0:T(8,128)(2,1)S(1)} %get-tuple-element.85.mine_ref, bf16[4,32,128]{2,1,0:T(8,128)(2,1)S(1)} %collective-permute-done.5.theirs_ref, bf16[32,64,512]{2,1,0:T(8,128)(2,1)S(1)} %copy-done, f32[32,16,256]{2,1,0:T(8,128)S(1)} %near.5.near_ref), custom_call_target="tpu_custom_call" | custom-call | tf_op jit(solution)/shard_map/final/pallas_call | solution.py:333
  (23 shorter events, 0.1 us)
Async XLA Ops:
  0.0 1.2 %copy-start.1 = (bf16[32,64,256]{2,1,0:T(8,128)(2,1)S(1)}, bf16[32,64,256]{2,1,0:T(8,128)(2,1)}, u32[]{:S(2)}) copy-start(bf16[32,64,256]{2,1,0:T(8,128)(2,1)} %basis_ref.1) | copy-start | bytes 3145732
  1.2 0.9 %copy-start.2 = (bf16[32,16,256]{2,1,0:T(8,128)(2,1)S(1)}, bf16[32,16,256]{2,1,0:T(8,128)(2,1)}, u32[]{:S(2)}) copy-start(bf16[32,16,256]{2,1,0:T(8,128)(2,1)} %vec_ref.1) | copy-start | bytes 786436
  2.8 6.6 %collective-permute-start = (f32[64,256]{1,0:T(8,128)S(1)}, f32[64,256]{1,0:T(8,128)S(1)}, u32[]{:S(2)}, u32[]{:S(2)}) collective-permute-start(f32[64,256]{1,0:T(8,128)S(1)} %get-tuple-element.54), channel_id=1, source_target_pairs={{0,1},{1,0},{2,3},{3,2},{4,5},{5,4},{6,7},{7,6},{8,9},{9,8},{10,11... | collective-permute-start | bytes 196616 | tf_op jit(solution)/shard_map/ppermute | solution.py:346
  4.1 39.7 %collective-permute-start.6 = (bf16[512,256]{1,0:T(8,128)(2,1)S(1)}, bf16[512,256]{1,0:T(8,128)(2,1)S(1)}, u32[]{:S(2)}, u32[]{:S(2)}) collective-permute-start(bf16[512,256]{1,0:T(8,128)(2,1)S(1)} %get-tuple-element.59.refs_2_), channel_id=1, source_target_pairs={{0,1},{1,0},{2,3},{3,2},{4,5},{5,4},{6,7},{7,6},{8,9},{9,8},{10,11... | collective-permute-start | bytes 786440 | tf_op jit(solution)/shard_map/ppermute | solution.py:346
  9.4 14.9 %collective-permute-start.2 = (bf16[64,256]{1,0:T(8,128)(2,1)S(1)}, bf16[64,256]{1,0:T(8,128)(2,1)S(1)}, u32[]{:S(2)}, u32[]{:S(2)}) collective-permute-start(bf16[64,256]{1,0:T(8,128)(2,1)S(1)} %add_convert_fusion.refs_0_), channel_id=1, source_target_pairs={{0,112},{16,0},{32,16},{48,32},{64,48},{80,64},{96,80},{112,96},{1... | collective-permute-start | bytes 98312 | tf_op jit(solution)/shard_map/ppermute | solution.py:346
  15.3 9.0 %collective-permute-start.1 = (bf16[64,256]{1,0:T(8,128)(2,1)S(1)}, bf16[64,256]{1,0:T(8,128)(2,1)S(1)}, u32[]{:S(2)}, u32[]{:S(2)}) collective-permute-start(bf16[64,256]{1,0:T(8,128)(2,1)S(1)} %add_convert_fusion.refs_0_), channel_id=1, source_target_pairs={{0,16},{16,32},{32,48},{48,64},{64,80},{80,96},{96,112},{112,0},{1... | collective-permute-start | bytes 98312 | tf_op jit(solution)/shard_map/ppermute | solution.py:346
  15.4 0.9 %copy-start.3 = (bf16[32,3,512]{2,0,1:T(8,128)(2,1)S(1)}, bf16[32,3,512]{2,0,1:T(8,128)(2,1)}, u32[]{:S(2)}) copy-start(bf16[32,3,512]{2,0,1:T(8,128)(2,1)} %param.9) | copy-start | bytes 294916
  18.4 11.2 %all-to-all-start.1 = ((bf16[16,40,128]{2,1,0:T(8,128)(2,1)}), bf16[16,40,128]{2,1,0:T(8,128)(2,1)S(1)}, u32[]{:S(2)}, u32[]{:S(2)}) async-start(bf16[16,40,128]{2,1,0:T(8,128)(2,1)} %get-tuple-element.52), calls=%async_computation.1 | async-start | bytes 327680 | tf_op jit(solution)/shard_map/all_to_all | solution.py:363
  24.2 28.8 %copy-start.5 = (bf16[64,256]{1,0:T(8,128)(2,1)}, bf16[64,256]{1,0:T(8,128)(2,1)S(1)}, u32[]{:S(2)}) copy-start(bf16[64,256]{1,0:T(8,128)(2,1)S(1)} %collective-permute-done.2.refs_2_) | copy-start | bytes 98308
  24.3 19.6 %copy-start.7 = (bf16[64,256]{1,0:T(8,128)(2,1)}, bf16[64,256]{1,0:T(8,128)(2,1)S(1)}, u32[]{:S(2)}) copy-start(bf16[64,256]{1,0:T(8,128)(2,1)S(1)} %collective-permute-done.1.refs_1_) | copy-start | bytes 98308
  24.3 11.9 %collective-permute-start.3 = (bf16[192,256]{1,0:T(8,128)(2,1)S(1)}, bf16[192,256]{1,0:T(8,128)(2,1)S(1)}, u32[]{:S(2)}, u32[]{:S(2)}) collective-permute-start(bf16[192,256]{1,0:T(8,128)(2,1)S(1)} %pad_maximum_fusion.8), channel_id=1, source_target_pairs={{0,80},{16,96},{32,112},{48,0},{64,16},{80,32},{96,48},{112,64},{1... | collective-permute-start | bytes 294920 | tf_op jit(solution)/shard_map/ppermute | solution.py:346
  27.3 8.9 %collective-permute-start.4 = (bf16[128,256]{1,0:T(8,128)(2,1)S(1)}, bf16[128,256]{1,0:T(8,128)(2,1)S(1)}, u32[]{:S(2)}, u32[]{:S(2)}) collective-permute-start(bf16[128,256]{1,0:T(8,128)(2,1)S(1)} %pad_maximum_fusion.9), channel_id=1, source_target_pairs={{0,48},{16,64},{32,80},{48,96},{64,112},{80,0},{96,16},{112,32},{1... | collective-permute-start | bytes 196616 | tf_op jit(solution)/shard_map/ppermute | solution.py:346
  36.2 7.6 %copy-start.8 = (bf16[128,256]{1,0:T(8,128)(2,1)}, bf16[128,256]{1,0:T(8,128)(2,1)S(1)}, u32[]{:S(2)}) copy-start(bf16[128,256]{1,0:T(8,128)(2,1)S(1)} %collective-permute-done.4.refs_4_) | copy-start | bytes 196612
  36.2 7.6 %copy-start.6 = (bf16[192,256]{1,0:T(8,128)(2,1)}, bf16[192,256]{1,0:T(8,128)(2,1)S(1)}, u32[]{:S(2)}) copy-start(bf16[192,256]{1,0:T(8,128)(2,1)S(1)} %collective-permute-done.3.refs_3_) | copy-start | bytes 294916
  37.4 23.4 %all-to-all-start.2 = ((bf16[16,40,512]{2,1,0:T(8,128)(2,1)}), bf16[16,40,512]{2,1,0:T(8,128)(2,1)}, u32[]{:S(2)}, u32[]{:S(2)}) async-start(bf16[16,40,512]{2,1,0:T(8,128)(2,1)} %get-tuple-element.57), calls=%async_computation.2 | async-start | bytes 1310720 | tf_op jit(solution)/shard_map/all_to_all | solution.py:379
  47.1 16.9 %collective-permute-start.7 = (bf16[24,512]{1,0:T(8,128)(2,1)S(1)}, bf16[24,512]{1,0:T(8,128)(2,1)S(1)}, u32[]{:S(2)}, u32[]{:S(2)}) collective-permute-start(bf16[24,512]{1,0:T(8,128)(2,1)S(1)} %get-tuple-element.60), channel_id=1, source_target_pairs={{0,2},{2,4},{4,6},{6,8},{8,10},{10,12},{12,14},{14,16},{16,18},{18... | collective-permute-start | bytes 73736 | tf_op jit(solution)/shard_map/ppermute | solution.py:346
  47.2 16.8 %collective-permute-start.8 = (bf16[24,512]{1,0:T(8,128)(2,1)S(1)}, bf16[24,512]{1,0:T(8,128)(2,1)S(1)}, u32[]{:S(2)}, u32[]{:S(2)}) collective-permute-start(bf16[24,512]{1,0:T(8,128)(2,1)S(1)} %get-tuple-element.61), channel_id=1, source_target_pairs={{0,254},{2,0},{4,2},{6,4},{8,6},{10,8},{12,10},{14,12},{16,14},{18... | collective-permute-start | bytes 73736 | tf_op jit(solution)/shard_map/ppermute | solution.py:346
  53.1 7.8 %copy-start.4 = (bf16[32,64,512]{2,1,0:T(8,128)(2,1)S(1)}, bf16[32,64,512]{2,1,0:T(8,128)(2,1)}, u32[]{:S(2)}) copy-start(bf16[32,64,512]{2,1,0:T(8,128)(2,1)} %param.15) | copy-start | bytes 6291460
  53.1 7.8 %copy-start.9 = (s32[32,8]{0,1:T(8,128)S(1)}, s32[32,8]{0,1:T(8,128)}, u32[]{:S(2)}) copy-start(s32[32,8]{0,1:T(8,128)} %param.14) | copy-start | bytes 3076
  63.4 5.5 %copy-start = (bf16[32,64,512]{2,1,0:T(8,128)(2,1)S(1)}, bf16[32,64,512]{2,1,0:T(8,128)(2,1)}, u32[]{:S(2)}) copy-start(bf16[32,64,512]{2,1,0:T(8,128)(2,1)} %tgt_ref.1) | copy-start | bytes 6291460
  63.4 5.5 %collective-permute-start.5 = (bf16[4,32,128]{2,1,0:T(8,128)(2,1)S(1)}, bf16[4,32,128]{2,1,0:T(8,128)(2,1)S(1)}, u32[]{:S(2)}, u32[]{:S(2)}) collective-permute-start(bf16[4,32,128]{2,1,0:T(8,128)(2,1)S(1)} %get-tuple-element.85.mine_ref), channel_id=1, source_target_pairs={{0,1},{1,0},{2,3},{3,2},{4,5},{5,4},{6,7},{7,6},{8,9},{9,8},{10,11... | collective-permute-start | bytes 98312 | tf_op jit(solution)/shard_map/ppermute | solution.py:346

commit v9 on v8

--- a/solution.py
+++ b/solution.py
@@ -20,7 +20,7 @@
 N_Z, N_PEER = 8, 16
 CAP = 40
 ENTRIES = T * J
-OFFSETS = (0,), (-1,), (1,), (2, 3, 4), (-2, -3)
+OFFSETS = (0,), (2,), (-2,), (4,), (1, 3), (-1, -3)
 COLUMN = N_Z * T
 bf16, f32, i32 = jnp.bfloat16, jnp.float32, jnp.int32
 
@@ -363,11 +363,12 @@
     asked = lax.all_to_all(req, PEERS, split_axis=0, concat_axis=0, tiled=True)
 
     coeffs = (keep + came).astype(bf16)
-    below = shifted(coeffs, "z", 1)
-    above = shifted(coeffs, "z", -1)
-    up = shifted(jnp.concatenate([below, coeffs, above]), "z", -3)
-    down = shifted(jnp.concatenate([above, coeffs]), "z", 3)
-    pieces = coeffs, below, above, up, down
+    up = shifted(coeffs, "z", -2)
+    down = shifted(coeffs, "z", 2)
+    across = shifted(coeffs, "z", 4)
+    odd_up = shifted(jnp.concatenate([coeffs, up]), "z", -1)
+    odd_down = shifted(jnp.concatenate([coeffs, down]), "z", 1)
+    pieces = coeffs, up, down, across, odd_up, odd_down
 
     near_args = (scalars, rows, held, other)
     near, first, last = near_call("early", (2, 10), 8, near_args)

time: 71 us -> 71.2 us (level)
  the two profiles are of different devices: /device:TPU:24 before, /device:TPU:16 now
where the time goes in v9:
time: 71.2 us; the launch traced here: 70.8 us
  starting transfers between devices  33.5 us (47%)
  Pallas kernels  21.6 us (30%)
  waiting for transfers between devices  11 us (15%)
  local copies, waits for them, and re-layouts  3.1 us (4%)
  between operations  1.43 us (2%)
    ppermute x10, starting transfers between devices, shifted(): lax.ppermute(array, axis, [(i, (i + by) % devices) for i in range(devices)])  22.7 us
    pallas_call x3, Pallas kernels, near_call(): pl.pallas_call(lambda *refs: near_kernel(kind, leaves, group, *refs), out...  13.3 us
    ppermute x10, waiting for transfers between devices, shifted(): lax.ppermute(array, axis, [(i, (i + by) % devices) for i in range(devices)])  11 us
    all_to_all x1, starting transfers between devices, body(): got = lax.all_to_all(packed, PEERS, split_axis=0, concat_axis=0, tiled=True)  5.75 us
    all_to_all x1, starting transfers between devices, body(): asked = lax.all_to_all(req, PEERS, split_axis=0, concat_axis=0, tiled=True)  5.12 us
    unnamed x22, local copies, waits for them, and re-layouts  3.1 us
    pallas_call x1, Pallas kernels, select_call(): pl.pallas_call(select_kernel, out_shape=TC_SHAPE, in_specs=[VMEM, VMEM, V...  2.49 us
    pallas_call x1, Pallas kernels, index_call(): pl.pallas_call(index_kernel, out_shape=(jax.ShapeDtypeStruct((ENTRIES, 12...  2.18 us
  transfers between devices with their start and end apart: 12, of which 3 were waited for; matrix products, arithmetic and copies ran while one was open for 0% of the time, Pallas kernels for 27%

profile of v9, /device:TPU:16, one launch (start us, length us, event | category | flops | bytes accessed | tf_op | source)
XLA Modules:
  0.0 70.8 jit_solution(11720036486665802676)
XLA Ops:
  0.0 1.2 %copy-done.1 = bf16[32,64,256]{2,1,0:T(8,128)(2,1)S(1)} copy-done((bf16[32,64,256]{2,1,0:T(8,128)(2,1)S(1)}, bf16[32,64,256]{2,1,0:T(8,128)(2,1)}, u32[]{:S(2)}) %copy-start.1) | copy-done | bytes 1048600
  1.2 0.9 %copy-done.2 = bf16[32,16,256]{2,1,0:T(8,128)(2,1)S(1)} copy-done((bf16[32,16,256]{2,1,0:T(8,128)(2,1)S(1)}, bf16[32,16,256]{2,1,0:T(8,128)(2,1)}, u32[]{:S(2)}) %copy-start.2) | copy-done | bytes 262168
  2.2 0.6 coeffs.1
  2.8 2.1 %collective-permute-start = (f32[64,256]{1,0:T(8,128)S(1)}, f32[64,256]{1,0:T(8,128)S(1)}, u32[]{:S(2)}, u32[]{:S(2)}) collective-permute-start(f32[64,256]{1,0:T(8,128)S(1)} %get-tuple-element.57), channel_id=1, source_target_pairs={{0,1},{1,0},{2,3},{3,2},{4,5},{5,4},{6,7},{7,6},{8,9},{9,8},{10,11... | collective-permute-start | bytes 196616 | tf_op jit(solution)/shard_map/ppermute | solution.py:346
  4.9 1.5 %collective-permute-start.7 = (bf16[512,256]{1,0:T(8,128)(2,1)S(1)}, bf16[512,256]{1,0:T(8,128)(2,1)S(1)}, u32[]{:S(2)}, u32[]{:S(2)}) collective-permute-start(bf16[512,256]{1,0:T(8,128)(2,1)S(1)} %get-tuple-element.62.refs_2_), channel_id=1, source_target_pairs={{0,1},{1,0},{2,3},{3,2},{4,5},{5,4},{6,7},{7,6},{8,9},{9,8},{10,11... | collective-permute-start | bytes 786440 | tf_op jit(solution)/shard_map/ppermute | solution.py:346
  7.1 2.3 %collective-permute-done = f32[64,256]{1,0:T(8,128)S(1)} collective-permute-done((f32[64,256]{1,0:T(8,128)S(1)}, f32[64,256]{1,0:T(8,128)S(1)}, u32[]{:S(2)}, u32[]{:S(2)}) %collective-permute-start) | collective-permute-done | bytes 65568 | tf_op jit(solution)/shard_map/ppermute | solution.py:346
  9.4 6.4 %collective-permute-start.1 = (bf16[64,256]{1,0:T(8,128)(2,1)S(1)}, bf16[64,256]{1,0:T(8,128)(2,1)S(1)}, u32[]{:S(2)}, u32[]{:S(2)}) collective-permute-start(bf16[64,256]{1,0:T(8,128)(2,1)S(1)} %add_convert_fusion.refs_0_), channel_id=1, source_target_pairs={{0,96},{16,112},{32,0},{48,16},{64,32},{80,48},{96,64},{112,80},{1... | collective-permute-start | bytes 98312 | tf_op jit(solution)/shard_map/ppermute | solution.py:346
  15.7 0.0 collective-permute-start.2
  15.8 0.1 pad_add_fusion.scalar_ref.refs_0_
  15.8 0.9 %copy-done.3 = bf16[32,3,512]{2,0,1:T(8,128)(2,1)S(1)} copy-done((bf16[32,3,512]{2,0,1:T(8,128)(2,1)S(1)}, bf16[32,3,512]{2,0,1:T(8,128)(2,1)}, u32[]{:S(2)}) %copy-start.3) | copy-done | bytes 98328
  16.7 2.2 %requests.1 = (s32[256,128]{1,0:T(8,128)}, bf16[16,40,128]{2,1,0:T(8,128)(2,1)}, bf16[32,8,512]{2,1,0:T(8,128)(2,1)S(1)}) custom-call(s32[2]{0:T(128)S(1)} %pad_add_fusion.scalar_ref.refs_0_, s32[8,32]{1,0:T(8,128)} %bitcast.10, bf16[3,32,512]{2,1,0:T(8,128)(2,1)S(1)} %bitcast.9), custom_call_target="tpu_custom_call" | custom-call | tf_op jit(solution)/shard_map/requests/pallas_call | solution.py:80
  18.9 5.1 %all-to-all-start.1 = ((bf16[16,40,128]{2,1,0:T(8,128)(2,1)}), bf16[16,40,128]{2,1,0:T(8,128)(2,1)S(1)}, u32[]{:S(2)}, u32[]{:S(2)}) async-start(bf16[16,40,128]{2,1,0:T(8,128)(2,1)} %get-tuple-element.55), calls=%async_computation.1 | async-start | bytes 327680 | tf_op jit(solution)/shard_map/all_to_all | solution.py:363
  24.1 3.8 %collective-permute-start.4 = (bf16[128,256]{1,0:T(8,128)(2,1)S(1)}, bf16[128,256]{1,0:T(8,128)(2,1)S(1)}, u32[]{:S(2)}, u32[]{:S(2)}) collective-permute-start(bf16[128,256]{1,0:T(8,128)(2,1)S(1)} %get-tuple-element.91), channel_id=1, source_target_pairs={{0,112},{16,0},{32,16},{48,32},{64,48},{80,64},{96,80},{112,96},{1... | collective-permute-start | bytes 196616 | tf_op jit(solution)/shard_map/ppermute | solution.py:346
  27.9 0.0 collective-permute-start.5
  27.9 2.1 %collective-permute-start.3 = (bf16[64,256]{1,0:T(8,128)(2,1)S(1)}, bf16[64,256]{1,0:T(8,128)(2,1)S(1)}, u32[]{:S(2)}, u32[]{:S(2)}) collective-permute-start(bf16[64,256]{1,0:T(8,128)(2,1)S(1)} %add_convert_fusion.refs_0_), channel_id=1, source_target_pairs={{0,64},{16,80},{32,96},{48,112},{64,0},{80,16},{96,32},{112,48},{1... | collective-permute-start | bytes 98312 | tf_op jit(solution)/shard_map/ppermute | solution.py:346
  30.0 5.7 %collective-permute-done.3.refs_3_ = bf16[64,256]{1,0:T(8,128)(2,1)S(1)} collective-permute-done((bf16[64,256]{1,0:T(8,128)(2,1)S(1)}, bf16[64,256]{1,0:T(8,128)(2,1)S(1)}, u32[]{:S(2)}, u32[]{:S(2)}) %collective-permute-start.3) | collective-permute-done | bytes 32800 | tf_op jit(solution)/shard_map/ppermute | solution.py:346
  35.7 0.0 all-to-all-done.1.req_ref
  35.7 0.0 collective-permute-done.4.refs_4_
  35.7 0.0 copy-start.7
  35.7 1.2 %pack.1 = (bf16[16,40,512]{2,1,0:T(8,128)(2,1)}, s32[1]{0:T(128)}) custom-call(s32[1]{0:T(128)} %bitcast.3.z_ref, bf16[16,40,128]{2,1,0:T(8,128)(2,1)S(1)} %all-to-all-done.1.req_ref, bf16[64,256]{1,0:T(8,128)(2,1)S(1)} %add_convert_fusion.refs_0_, bf16[64,256]{1,0:T(8,128)(2,1)S(1)} %collective-permute-done.1.refs_1_, ...), custom_call_target="tpu_custom_call" | custom-call | tf_op jit(solution)/shard_map/pack/pallas_call | solution.py:149
  37.0 5.8 %all-to-all-start.2 = ((bf16[16,40,512]{2,1,0:T(8,128)(2,1)}), bf16[16,40,512]{2,1,0:T(8,128)(2,1)}, u32[]{:S(2)}, u32[]{:S(2)}) async-start(bf16[16,40,512]{2,1,0:T(8,128)(2,1)} %get-tuple-element.60), calls=%async_computation.2 | async-start | bytes 1310720 | tf_op jit(solution)/shard_map/all_to_all | solution.py:380
  43.3 3.2 %near.3 = (f32[32,16,256]{2,1,0:T(8,128)S(1)}, bf16[24,512]{1,0:T(8,128)(2,1)S(1)}, bf16[24,512]{1,0:T(8,128)(2,1)S(1)}) custom-call(s32[2]{0:T(128)S(1)} %pad_add_fusion.scalar_ref.refs_0_, bf16[32,8,512]{2,1,0:T(8,128)(2,1)S(1)} %get-tuple-element.61.refs_1_, bf16[512,256]{1,0:T(8,128)(2,1)S(1)} %get-tuple-element.62.refs_2_, ...), custom_call_target="tpu_custom_call" | custom-call | flops 1600000000 | bytes 2000000 | tf_op jit(solution)/shard_map/near/pallas_call | solution.py:300
  46.6 0.4 collective-permute-start.8
  47.0 6.3 %collective-permute-start.9 = (bf16[24,512]{1,0:T(8,128)(2,1)S(1)}, bf16[24,512]{1,0:T(8,128)(2,1)S(1)}, u32[]{:S(2)}, u32[]{:S(2)}) collective-permute-start(bf16[24,512]{1,0:T(8,128)(2,1)S(1)} %get-tuple-element.64), channel_id=1, source_target_pairs={{0,254},{2,0},{4,2},{6,4},{8,6},{10,8},{12,10},{14,12},{16,14},{18... | collective-permute-start | bytes 73736 | tf_op jit(solution)/shard_map/ppermute | solution.py:346
  53.2 7.8 %near.4.refs_6_ = f32[32,16,256]{2,1,0:T(8,128)S(1)} custom-call(s32[2]{0:T(128)S(1)} %pad_add_fusion.scalar_ref.refs_0_, bf16[32,8,512]{2,1,0:T(8,128)(2,1)S(1)} %get-tuple-element.61.refs_1_, bf16[512,256]{1,0:T(8,128)(2,1)S(1)} %get-tuple-element.62.refs_2_, bf16[512,256]{1,0:T(8,128)(2,1)S(1)} %collective-permute-done.7.refs_3_, ...), custom_call_target="tpu_custom_call", output_to_operand_aliasing={{}: (4, {})} | custom-call | flops 4000000000 | bytes 2000000 | tf_op jit(solution)/shard_map/near/pallas_call | solution.py:300
  61.0 0.0 all-to-all-done.2
  61.0 2.5 %conditional.1 = (bf16[4,32,128]{2,1,0:T(8,128)(2,1)S(1)}) conditional(s32[]{:T(128)} %bitcast.6, (s32[32,8]{0,1:T(8,128)S(1)}, bf16[64,256]{1,0:T(8,128)(2,1)S(1)}, bf16[128,256]{1,0:T(8,128)(2,1)}, bf16[64,256]{1,0:T(8,128)(2,1)}, bf16[64,256]{1,0:T(8,128)(2,1)}, /*index=5*/bf16[128,256]{1,0:T(8,128)(2,1)}, bf16[64,256]{1,0:T(8,128)(2,1)}, ...), branch_computations={%region_0.1_spmd, %region_1.2_spmd} | conditional | flops 1075842048 | bytes 23860436 | solution.py:399
  61.1 2.5 %select.3 = bf16[4,32,128]{2,1,0:T(8,128)(2,1)S(1)} custom-call(s32[256,128]{1,0:T(8,128)} %get-tuple-element.41.sel_ref, bf16[16,40,512]{2,1,0:T(8,128)(2,1)} %get-tuple-element.42.got_ref, bf16[32,64,512]{2,1,0:T(8,128)(2,1)S(1)} %get-tuple-element.43.couple_ref), custom_call_target="tpu_custom_call" | custom-call | tf_op jit(solution)/shard_map/cond/branch_1_fun/select/pallas_call | solution.py:199
  63.6 0.1 collective-permute-start.6
  63.7 2.4 %near.5.near_ref = f32[32,16,256]{2,1,0:T(8,128)S(1)} custom-call(s32[2]{0:T(128)S(1)} %pad_add_fusion.scalar_ref.refs_0_, bf16[32,8,512]{2,1,0:T(8,128)(2,1)S(1)} %get-tuple-element.61.refs_1_, bf16[512,256]{1,0:T(8,128)(2,1)S(1)} %get-tuple-element.62.refs_2_, bf16[512,256]{1,0:T(8,128)(2,1)S(1)} %collective-permute-done.7.refs_3_, ...), custom_call_target="tpu_custom_call", output_to_operand_aliasing={{}: (6, {})} | custom-call | flops 1000000000 | bytes 2000000 | tf_op jit(solution)/shard_map/near/pallas_call | solution.py:300
  66.0 3.0 %collective-permute-done.6.theirs_ref = bf16[4,32,128]{2,1,0:T(8,128)(2,1)S(1)} collective-permute-done((bf16[4,32,128]{2,1,0:T(8,128)(2,1)S(1)}, bf16[4,32,128]{2,1,0:T(8,128)(2,1)S(1)}, u32[]{:S(2)}, u32[]{:S(2)}) %collective-permute-start.6) | collective-permute-done | bytes 32800 | tf_op jit(solution)/shard_map/ppermute | solution.py:346
  69.1 1.7 %final.1 = bf16[32,16,256]{2,1,0:T(8,128)(2,1)} custom-call(s32[2]{0:T(128)S(1)} %pad_add_fusion.scalar_ref.refs_0_, bf16[4,32,128]{2,1,0:T(8,128)(2,1)S(1)} %get-tuple-element.92.mine_ref, bf16[4,32,128]{2,1,0:T(8,128)(2,1)S(1)} %collective-permute-done.6.theirs_ref, bf16[32,64,512]{2,1,0:T(8,128)(2,1)S(1)} %copy-done, f32[32,16,256]{2,1,0:T(8,128)S(1)} %near.5.near_ref), custom_call_target="tpu_custom_call" | custom-call | tf_op jit(solution)/shard_map/final/pallas_call | solution.py:333
  (26 shorter events, 0.1 us)
Async XLA Ops:
  0.0 1.2 %copy-start.1 = (bf16[32,64,256]{2,1,0:T(8,128)(2,1)S(1)}, bf16[32,64,256]{2,1,0:T(8,128)(2,1)}, u32[]{:S(2)}) copy-start(bf16[32,64,256]{2,1,0:T(8,128)(2,1)} %basis_ref.1) | copy-start | bytes 3145732
  1.2 0.9 %copy-start.2 = (bf16[32,16,256]{2,1,0:T(8,128)(2,1)S(1)}, bf16[32,16,256]{2,1,0:T(8,128)(2,1)}, u32[]{:S(2)}) copy-start(bf16[32,16,256]{2,1,0:T(8,128)(2,1)} %vec_ref.1) | copy-start | bytes 786436
  2.8 6.6 %collective-permute-start = (f32[64,256]{1,0:T(8,128)S(1)}, f32[64,256]{1,0:T(8,128)S(1)}, u32[]{:S(2)}, u32[]{:S(2)}) collective-permute-start(f32[64,256]{1,0:T(8,128)S(1)} %get-tuple-element.57), channel_id=1, source_target_pairs={{0,1},{1,0},{2,3},{3,2},{4,5},{5,4},{6,7},{7,6},{8,9},{9,8},{10,11... | collective-permute-start | bytes 196616 | tf_op jit(solution)/shard_map/ppermute | solution.py:346
  4.9 38.4 %collective-permute-start.7 = (bf16[512,256]{1,0:T(8,128)(2,1)S(1)}, bf16[512,256]{1,0:T(8,128)(2,1)S(1)}, u32[]{:S(2)}, u32[]{:S(2)}) collective-permute-start(bf16[512,256]{1,0:T(8,128)(2,1)S(1)} %get-tuple-element.62.refs_2_), channel_id=1, source_target_pairs={{0,1},{1,0},{2,3},{3,2},{4,5},{5,4},{6,7},{7,6},{8,9},{9,8},{10,11... | collective-permute-start | bytes 786440 | tf_op jit(solution)/shard_map/ppermute | solution.py:346
  9.4 14.7 %collective-permute-start.1 = (bf16[64,256]{1,0:T(8,128)(2,1)S(1)}, bf16[64,256]{1,0:T(8,128)(2,1)S(1)}, u32[]{:S(2)}, u32[]{:S(2)}) collective-permute-start(bf16[64,256]{1,0:T(8,128)(2,1)S(1)} %add_convert_fusion.refs_0_), channel_id=1, source_target_pairs={{0,96},{16,112},{32,0},{48,16},{64,32},{80,48},{96,64},{112,80},{1... | collective-permute-start | bytes 98312 | tf_op jit(solution)/shard_map/ppermute | solution.py:346
  15.7 8.3 %collective-permute-start.2 = (bf16[64,256]{1,0:T(8,128)(2,1)S(1)}, bf16[64,256]{1,0:T(8,128)(2,1)S(1)}, u32[]{:S(2)}, u32[]{:S(2)}) collective-permute-start(bf16[64,256]{1,0:T(8,128)(2,1)S(1)} %add_convert_fusion.refs_0_), channel_id=1, source_target_pairs={{0,32},{16,48},{32,64},{48,80},{64,96},{80,112},{96,0},{112,16},{1... | collective-permute-start | bytes 98312 | tf_op jit(solution)/shard_map/ppermute | solution.py:346
  15.8 0.9 %copy-start.3 = (bf16[32,3,512]{2,0,1:T(8,128)(2,1)S(1)}, bf16[32,3,512]{2,0,1:T(8,128)(2,1)}, u32[]{:S(2)}) copy-start(bf16[32,3,512]{2,0,1:T(8,128)(2,1)} %param.9) | copy-start | bytes 294916
  18.9 16.8 %all-to-all-start.1 = ((bf16[16,40,128]{2,1,0:T(8,128)(2,1)}), bf16[16,40,128]{2,1,0:T(8,128)(2,1)S(1)}, u32[]{:S(2)}, u32[]{:S(2)}) async-start(bf16[16,40,128]{2,1,0:T(8,128)(2,1)} %get-tuple-element.55), calls=%async_computation.1 | async-start | bytes 327680 | tf_op jit(solution)/shard_map/all_to_all | solution.py:363
  24.0 29.2 %copy-start.5 = (bf16[64,256]{1,0:T(8,128)(2,1)}, bf16[64,256]{1,0:T(8,128)(2,1)S(1)}, u32[]{:S(2)}) copy-start(bf16[64,256]{1,0:T(8,128)(2,1)S(1)} %collective-permute-done.1.refs_1_) | copy-start | bytes 98308
  24.1 19.2 %copy-start.6 = (bf16[64,256]{1,0:T(8,128)(2,1)}, bf16[64,256]{1,0:T(8,128)(2,1)S(1)}, u32[]{:S(2)}) copy-start(bf16[64,256]{1,0:T(8,128)(2,1)S(1)} %collective-permute-done.2.refs_2_) | copy-start | bytes 98308
  24.1 11.6 %collective-permute-start.4 = (bf16[128,256]{1,0:T(8,128)(2,1)S(1)}, bf16[128,256]{1,0:T(8,128)(2,1)S(1)}, u32[]{:S(2)}, u32[]{:S(2)}) collective-permute-start(bf16[128,256]{1,0:T(8,128)(2,1)S(1)} %get-tuple-element.91), channel_id=1, source_target_pairs={{0,112},{16,0},{32,16},{48,32},{64,48},{80,64},{96,80},{112,96},{1... | collective-permute-start | bytes 196616 | tf_op jit(solution)/shard_map/ppermute | solution.py:346
  27.9 7.9 %collective-permute-start.5 = (bf16[128,256]{1,0:T(8,128)(2,1)S(1)}, bf16[128,256]{1,0:T(8,128)(2,1)S(1)}, u32[]{:S(2)}, u32[]{:S(2)}) collective-permute-start(bf16[128,256]{1,0:T(8,128)(2,1)S(1)} %get-tuple-element.90), channel_id=1, source_target_pairs={{0,16},{16,32},{32,48},{48,64},{64,80},{80,96},{96,112},{112,0},{1... | collective-permute-start | bytes 196616 | tf_op jit(solution)/shard_map/ppermute | solution.py:346
  27.9 7.8 %collective-permute-start.3 = (bf16[64,256]{1,0:T(8,128)(2,1)S(1)}, bf16[64,256]{1,0:T(8,128)(2,1)S(1)}, u32[]{:S(2)}, u32[]{:S(2)}) collective-permute-start(bf16[64,256]{1,0:T(8,128)(2,1)S(1)} %add_convert_fusion.refs_0_), channel_id=1, source_target_pairs={{0,64},{16,80},{32,96},{48,112},{64,0},{80,16},{96,32},{112,48},{1... | collective-permute-start | bytes 98312 | tf_op jit(solution)/shard_map/ppermute | solution.py:346
  35.7 7.6 %copy-start.9 = (bf16[64,256]{1,0:T(8,128)(2,1)}, bf16[64,256]{1,0:T(8,128)(2,1)S(1)}, u32[]{:S(2)}) copy-start(bf16[64,256]{1,0:T(8,128)(2,1)S(1)} %collective-permute-done.3.refs_3_) | copy-start | bytes 98308
  35.7 7.6 %copy-start.7 = (bf16[128,256]{1,0:T(8,128)(2,1)}, bf16[128,256]{1,0:T(8,128)(2,1)S(1)}, u32[]{:S(2)}) copy-start(bf16[128,256]{1,0:T(8,128)(2,1)S(1)} %collective-permute-done.4.refs_4_) | copy-start | bytes 196612
  35.7 7.6 %copy-start.8 = (bf16[128,256]{1,0:T(8,128)(2,1)}, bf16[128,256]{1,0:T(8,128)(2,1)S(1)}, u32[]{:S(2)}) copy-start(bf16[128,256]{1,0:T(8,128)(2,1)S(1)} %collective-permute-done.5.refs_5_) | copy-start | bytes 196612
  37.0 24.0 %all-to-all-start.2 = ((bf16[16,40,512]{2,1,0:T(8,128)(2,1)}), bf16[16,40,512]{2,1,0:T(8,128)(2,1)}, u32[]{:S(2)}, u32[]{:S(2)}) async-start(bf16[16,40,512]{2,1,0:T(8,128)(2,1)} %get-tuple-element.60), calls=%async_computation.2 | async-start | bytes 1310720 | tf_op jit(solution)/shard_map/all_to_all | solution.py:380
  46.6 17.1 %collective-permute-start.8 = (bf16[24,512]{1,0:T(8,128)(2,1)S(1)}, bf16[24,512]{1,0:T(8,128)(2,1)S(1)}, u32[]{:S(2)}, u32[]{:S(2)}) collective-permute-start(bf16[24,512]{1,0:T(8,128)(2,1)S(1)} %get-tuple-element.63), channel_id=1, source_target_pairs={{0,2},{2,4},{4,6},{6,8},{8,10},{10,12},{12,14},{14,16},{16,18},{18... | collective-permute-start | bytes 73736 | tf_op jit(solution)/shard_map/ppermute | solution.py:346
  47.0 16.7 %collective-permute-start.9 = (bf16[24,512]{1,0:T(8,128)(2,1)S(1)}, bf16[24,512]{1,0:T(8,128)(2,1)S(1)}, u32[]{:S(2)}, u32[]{:S(2)}) collective-permute-start(bf16[24,512]{1,0:T(8,128)(2,1)S(1)} %get-tuple-element.64), channel_id=1, source_target_pairs={{0,254},{2,0},{4,2},{6,4},{8,6},{10,8},{12,10},{14,12},{16,14},{18... | collective-permute-start | bytes 73736 | tf_op jit(solution)/shard_map/ppermute | solution.py:346
  53.2 7.8 %copy-start.4 = (bf16[32,64,512]{2,1,0:T(8,128)(2,1)S(1)}, bf16[32,64,512]{2,1,0:T(8,128)(2,1)}, u32[]{:S(2)}) copy-start(bf16[32,64,512]{2,1,0:T(8,128)(2,1)} %param.15) | copy-start | bytes 6291460
  53.2 7.8 %copy-start.10 = (s32[32,8]{0,1:T(8,128)S(1)}, s32[32,8]{0,1:T(8,128)}, u32[]{:S(2)}) copy-start(s32[32,8]{0,1:T(8,128)} %param.14) | copy-start | bytes 3076
  63.5 5.5 %copy-start = (bf16[32,64,512]{2,1,0:T(8,128)(2,1)S(1)}, bf16[32,64,512]{2,1,0:T(8,128)(2,1)}, u32[]{:S(2)}) copy-start(bf16[32,64,512]{2,1,0:T(8,128)(2,1)} %tgt_ref.1) | copy-start | bytes 6291460
  63.6 5.5 %collective-permute-start.6 = (bf16[4,32,128]{2,1,0:T(8,128)(2,1)S(1)}, bf16[4,32,128]{2,1,0:T(8,128)(2,1)S(1)}, u32[]{:S(2)}, u32[]{:S(2)}) collective-permute-start(bf16[4,32,128]{2,1,0:T(8,128)(2,1)S(1)} %get-tuple-element.92.mine_ref), channel_id=1, source_target_pairs={{0,1},{1,0},{2,3},{3,2},{4,5},{5,4},{6,7},{7,6},{8,9},{9,8},{10,11... | collective-permute-start | bytes 98312 | tf_op jit(solution)/shard_map/ppermute | solution.py:346

commit v10 on v9

--- a/solution.py
+++ b/solution.py
@@ -280,13 +280,17 @@
     steps, group = near_steps(kind, leaves), len(kerns)
     fill(leaf(0), kerns[0])
 
-    def body(i, _):
+    def body(i, ends):
         for s in range(group):
-            fill(leaf(jnp.minimum(group * i + s + 1, steps - 1)), kerns[(s + 1) % group])
+            if not ends or s < group - 1:
+                fill(leaf(group * i + s + 1), kerns[(s + 1) % group])
             product(leaf(group * i + s), kerns[s])
         return 0
 
-    lax.fori_loop(0, steps // group, body, 0)
+    whole = steps // group - 1
+    if whole:
+        lax.fori_loop(0, whole, lambda i, _: body(i, False), 0)
+    lax.fori_loop(whole, whole + 1, lambda i, _: body(i, True), 0)
 
 
 def near_steps(kind, leaves):
@@ -371,10 +375,10 @@
     pieces = coeffs, up, down, across, odd_up, odd_down
 
     near_args = (scalars, rows, held, other)
-    near, first, last = near_call("early", (2, 10), 8, near_args)
+    near, first, last = near_call("early", (3, 11), 8, near_args)
     halos = shifted(last, WIDE, 1), shifted(first, WIDE, -1)
-    (near,) = near_call("inner", (10, 30), 10, near_args, (near,))
-    (near,) = near_call("rest", (2, 30), 5, near_args, (*halos, near))
+    (near,) = near_call("inner", (11, 29), 9, near_args, (near,))
+    (near,) = near_call("rest", (3, 29), 7, near_args, (*halos, near))
 
     packed, fits = pack_call(z[None], asked, pieces)
     got = lax.all_to_all(packed, PEERS, split_axis=0, concat_axis=0, tiled=True)

time: 71.2 us -> 69.8 us (0.980)
  Pallas kernels: 21.6 us -> 20.7 us
    pallas_call x3, Pallas kernels: 13.3 us -> 12.5 us  [near_call(): pl.pallas_call(lambda *refs: near_kernel(kind, leaves, group, *refs), out...]
where the time goes in v10:
time: 69.8 us; the launch traced here: 69.3 us
  starting transfers between devices  33.5 us (48%)
  Pallas kernels  20.7 us (30%)
  waiting for transfers between devices  10.4 us (15%)
  local copies, waits for them, and re-layouts  3.1 us (4%)
  between operations  1.42 us (2%)
    ppermute x10, starting transfers between devices, shifted(): lax.ppermute(array, axis, [(i, (i + by) % devices) for i in range(devices)])  22.7 us
    pallas_call x3, Pallas kernels, near_call(): pl.pallas_call(lambda *refs: near_kernel(kind, leaves, group, *refs), out...  12.5 us
    ppermute x10, waiting for transfers between devices, shifted(): lax.ppermute(array, axis, [(i, (i + by) % devices) for i in range(devices)])  10.4 us
    all_to_all x1, starting transfers between devices, body(): got = lax.all_to_all(packed, PEERS, split_axis=0, concat_axis=0, tiled=True)  5.75 us
    all_to_all x1, starting transfers between devices, body(): asked = lax.all_to_all(req, PEERS, split_axis=0, concat_axis=0, tiled=True)  5.12 us
    unnamed x22, local copies, waits for them, and re-layouts  3.1 us
    pallas_call x1, Pallas kernels, select_call(): pl.pallas_call(select_kernel, out_shape=TC_SHAPE, in_specs=[VMEM, VMEM, V...  2.49 us
    pallas_call x1, Pallas kernels, index_call(): pl.pallas_call(index_kernel, out_shape=(jax.ShapeDtypeStruct((ENTRIES, 12...  2.18 us
  transfers between devices with their start and end apart: 12, of which 3 were waited for; matrix products, arithmetic and copies ran while one was open for 0% of the time, Pallas kernels for 27%

profile of v10, /device:TPU:16, one launch (start us, length us, event | category | flops | bytes accessed | tf_op | source)
XLA Modules:
  0.0 69.3 jit_solution(17139829024062835337)
XLA Ops:
  0.0 1.2 %copy-done.1 = bf16[32,64,256]{2,1,0:T(8,128)(2,1)S(1)} copy-done((bf16[32,64,256]{2,1,0:T(8,128)(2,1)S(1)}, bf16[32,64,256]{2,1,0:T(8,128)(2,1)}, u32[]{:S(2)}) %copy-start.1) | copy-done | bytes 1048600
  1.2 0.9 %copy-done.2 = bf16[32,16,256]{2,1,0:T(8,128)(2,1)S(1)} copy-done((bf16[32,16,256]{2,1,0:T(8,128)(2,1)S(1)}, bf16[32,16,256]{2,1,0:T(8,128)(2,1)}, u32[]{:S(2)}) %copy-start.2) | copy-done | bytes 262168
  2.2 0.6 coeffs.1
  2.8 2.1 %collective-permute-start = (f32[64,256]{1,0:T(8,128)S(1)}, f32[64,256]{1,0:T(8,128)S(1)}, u32[]{:S(2)}, u32[]{:S(2)}) collective-permute-start(f32[64,256]{1,0:T(8,128)S(1)} %get-tuple-element.57), channel_id=1, source_target_pairs={{0,1},{1,0},{2,3},{3,2},{4,5},{5,4},{6,7},{7,6},{8,9},{9,8},{10,11... | collective-permute-start | bytes 196616 | tf_op jit(solution)/shard_map/ppermute | solution.py:350
  4.9 1.5 %collective-permute-start.7 = (bf16[512,256]{1,0:T(8,128)(2,1)S(1)}, bf16[512,256]{1,0:T(8,128)(2,1)S(1)}, u32[]{:S(2)}, u32[]{:S(2)}) collective-permute-start(bf16[512,256]{1,0:T(8,128)(2,1)S(1)} %get-tuple-element.62.refs_2_), channel_id=1, source_target_pairs={{0,1},{1,0},{2,3},{3,2},{4,5},{5,4},{6,7},{7,6},{8,9},{9,8},{10,11... | collective-permute-start | bytes 786440 | tf_op jit(solution)/shard_map/ppermute | solution.py:350
  7.1 2.3 %collective-permute-done = f32[64,256]{1,0:T(8,128)S(1)} collective-permute-done((f32[64,256]{1,0:T(8,128)S(1)}, f32[64,256]{1,0:T(8,128)S(1)}, u32[]{:S(2)}, u32[]{:S(2)}) %collective-permute-start) | collective-permute-done | bytes 65568 | tf_op jit(solution)/shard_map/ppermute | solution.py:350
  9.4 6.4 %collective-permute-start.1 = (bf16[64,256]{1,0:T(8,128)(2,1)S(1)}, bf16[64,256]{1,0:T(8,128)(2,1)S(1)}, u32[]{:S(2)}, u32[]{:S(2)}) collective-permute-start(bf16[64,256]{1,0:T(8,128)(2,1)S(1)} %add_convert_fusion.refs_0_), channel_id=1, source_target_pairs={{0,96},{16,112},{32,0},{48,16},{64,32},{80,48},{96,64},{112,80},{1... | collective-permute-start | bytes 98312 | tf_op jit(solution)/shard_map/ppermute | solution.py:350
  15.7 0.0 collective-permute-start.2
  15.8 0.1 pad_add_fusion.scalar_ref.refs_0_
  15.8 0.9 %copy-done.3 = bf16[32,3,512]{2,0,1:T(8,128)(2,1)S(1)} copy-done((bf16[32,3,512]{2,0,1:T(8,128)(2,1)S(1)}, bf16[32,3,512]{2,0,1:T(8,128)(2,1)}, u32[]{:S(2)}) %copy-start.3) | copy-done | bytes 98328
  16.7 2.2 %requests.1 = (s32[256,128]{1,0:T(8,128)}, bf16[16,40,128]{2,1,0:T(8,128)(2,1)}, bf16[32,8,512]{2,1,0:T(8,128)(2,1)S(1)}) custom-call(s32[2]{0:T(128)S(1)} %pad_add_fusion.scalar_ref.refs_0_, s32[8,32]{1,0:T(8,128)} %bitcast.10, bf16[3,32,512]{2,1,0:T(8,128)(2,1)S(1)} %bitcast.9), custom_call_target="tpu_custom_call" | custom-call | tf_op jit(solution)/shard_map/requests/pallas_call | solution.py:80
  18.9 5.1 %all-to-all-start.1 = ((bf16[16,40,128]{2,1,0:T(8,128)(2,1)}), bf16[16,40,128]{2,1,0:T(8,128)(2,1)S(1)}, u32[]{:S(2)}, u32[]{:S(2)}) async-start(bf16[16,40,128]{2,1,0:T(8,128)(2,1)} %get-tuple-element.55), calls=%async_computation.1 | async-start | bytes 327680 | tf_op jit(solution)/shard_map/all_to_all | solution.py:367
  24.1 3.8 %collective-permute-start.4 = (bf16[128,256]{1,0:T(8,128)(2,1)S(1)}, bf16[128,256]{1,0:T(8,128)(2,1)S(1)}, u32[]{:S(2)}, u32[]{:S(2)}) collective-permute-start(bf16[128,256]{1,0:T(8,128)(2,1)S(1)} %get-tuple-element.91), channel_id=1, source_target_pairs={{0,112},{16,0},{32,16},{48,32},{64,48},{80,64},{96,80},{112,96},{1... | collective-permute-start | bytes 196616 | tf_op jit(solution)/shard_map/ppermute | solution.py:350
  27.9 0.0 collective-permute-start.5
  27.9 2.1 %collective-permute-start.3 = (bf16[64,256]{1,0:T(8,128)(2,1)S(1)}, bf16[64,256]{1,0:T(8,128)(2,1)S(1)}, u32[]{:S(2)}, u32[]{:S(2)}) collective-permute-start(bf16[64,256]{1,0:T(8,128)(2,1)S(1)} %add_convert_fusion.refs_0_), channel_id=1, source_target_pairs={{0,64},{16,80},{32,96},{48,112},{64,0},{80,16},{96,32},{112,48},{1... | collective-permute-start | bytes 98312 | tf_op jit(solution)/shard_map/ppermute | solution.py:350
  30.0 5.7 %collective-permute-done.3.refs_3_ = bf16[64,256]{1,0:T(8,128)(2,1)S(1)} collective-permute-done((bf16[64,256]{1,0:T(8,128)(2,1)S(1)}, bf16[64,256]{1,0:T(8,128)(2,1)S(1)}, u32[]{:S(2)}, u32[]{:S(2)}) %collective-permute-start.3) | collective-permute-done | bytes 32800 | tf_op jit(solution)/shard_map/ppermute | solution.py:350
  35.7 0.0 all-to-all-done.1.req_ref
  35.7 0.0 collective-permute-done.4.refs_4_
  35.7 0.0 copy-start.7
  35.7 1.2 %pack.1 = (bf16[16,40,512]{2,1,0:T(8,128)(2,1)}, s32[1]{0:T(128)}) custom-call(s32[1]{0:T(128)} %bitcast.3.z_ref, bf16[16,40,128]{2,1,0:T(8,128)(2,1)S(1)} %all-to-all-done.1.req_ref, bf16[64,256]{1,0:T(8,128)(2,1)S(1)} %add_convert_fusion.refs_0_, bf16[64,256]{1,0:T(8,128)(2,1)S(1)} %collective-permute-done.1.refs_1_, ...), custom_call_target="tpu_custom_call" | custom-call | tf_op jit(solution)/shard_map/pack/pallas_call | solution.py:149
  37.0 5.8 %all-to-all-start.2 = ((bf16[16,40,512]{2,1,0:T(8,128)(2,1)}), bf16[16,40,512]{2,1,0:T(8,128)(2,1)}, u32[]{:S(2)}, u32[]{:S(2)}) async-start(bf16[16,40,512]{2,1,0:T(8,128)(2,1)} %get-tuple-element.60), calls=%async_computation.2 | async-start | bytes 1310720 | tf_op jit(solution)/shard_map/all_to_all | solution.py:384
  43.3 3.2 %near.3 = (f32[32,16,256]{2,1,0:T(8,128)S(1)}, bf16[24,512]{1,0:T(8,128)(2,1)S(1)}, bf16[24,512]{1,0:T(8,128)(2,1)S(1)}) custom-call(s32[2]{0:T(128)S(1)} %pad_add_fusion.scalar_ref.refs_0_, bf16[32,8,512]{2,1,0:T(8,128)(2,1)S(1)} %get-tuple-element.61.refs_1_, bf16[512,256]{1,0:T(8,128)(2,1)S(1)} %get-tuple-element.62.refs_2_, ...), custom_call_target="tpu_custom_call" | custom-call | flops 1600000000 | bytes 2000000 | tf_op jit(solution)/shard_map/near/pallas_call | solution.py:304
  46.6 0.4 collective-permute-start.8
  47.0 6.3 %collective-permute-start.9 = (bf16[24,512]{1,0:T(8,128)(2,1)S(1)}, bf16[24,512]{1,0:T(8,128)(2,1)S(1)}, u32[]{:S(2)}, u32[]{:S(2)}) collective-permute-start(bf16[24,512]{1,0:T(8,128)(2,1)S(1)} %get-tuple-element.64), channel_id=1, source_target_pairs={{0,254},{2,0},{4,2},{6,4},{8,6},{10,8},{12,10},{14,12},{16,14},{18... | collective-permute-start | bytes 73736 | tf_op jit(solution)/shard_map/ppermute | solution.py:350
  53.2 6.3 %near.4.refs_6_ = f32[32,16,256]{2,1,0:T(8,128)S(1)} custom-call(s32[2]{0:T(128)S(1)} %pad_add_fusion.scalar_ref.refs_0_, bf16[32,8,512]{2,1,0:T(8,128)(2,1)S(1)} %get-tuple-element.61.refs_1_, bf16[512,256]{1,0:T(8,128)(2,1)S(1)} %get-tuple-element.62.refs_2_, bf16[512,256]{1,0:T(8,128)(2,1)S(1)} %collective-permute-done.7.refs_3_, ...), custom_call_target="tpu_custom_call", output_to_operand_aliasing={{}: (4, {})} | custom-call | flops 3600000000 | bytes 2000000 | tf_op jit(solution)/shard_map/near/pallas_call | solution.py:304
  59.6 0.0 copy-done.4
  59.6 2.5 %conditional.1 = (bf16[4,32,128]{2,1,0:T(8,128)(2,1)S(1)}) conditional(s32[]{:T(128)} %bitcast.6, (s32[32,8]{0,1:T(8,128)S(1)}, bf16[64,256]{1,0:T(8,128)(2,1)S(1)}, bf16[128,256]{1,0:T(8,128)(2,1)}, bf16[64,256]{1,0:T(8,128)(2,1)}, bf16[64,256]{1,0:T(8,128)(2,1)}, /*index=5*/bf16[128,256]{1,0:T(8,128)(2,1)}, bf16[64,256]{1,0:T(8,128)(2,1)}, ...), branch_computations={%region_0.1_spmd, %region_1.2_spmd} | conditional | flops 1075842048 | bytes 23860436 | solution.py:403
  59.6 2.5 %select.3 = bf16[4,32,128]{2,1,0:T(8,128)(2,1)S(1)} custom-call(s32[256,128]{1,0:T(8,128)} %get-tuple-element.41.sel_ref, bf16[16,40,512]{2,1,0:T(8,128)(2,1)} %get-tuple-element.42.got_ref, bf16[32,64,512]{2,1,0:T(8,128)(2,1)S(1)} %get-tuple-element.43.couple_ref), custom_call_target="tpu_custom_call" | custom-call | tf_op jit(solution)/shard_map/cond/branch_1_fun/select/pallas_call | solution.py:199
  62.1 0.1 collective-permute-start.6
  62.2 3.0 %near.5.near_ref = f32[32,16,256]{2,1,0:T(8,128)S(1)} custom-call(s32[2]{0:T(128)S(1)} %pad_add_fusion.scalar_ref.refs_0_, bf16[32,8,512]{2,1,0:T(8,128)(2,1)S(1)} %get-tuple-element.61.refs_1_, bf16[512,256]{1,0:T(8,128)(2,1)S(1)} %get-tuple-element.62.refs_2_, bf16[512,256]{1,0:T(8,128)(2,1)S(1)} %collective-permute-done.7.refs_3_, ...), custom_call_target="tpu_custom_call", output_to_operand_aliasing={{}: (6, {})} | custom-call | flops 1400000000 | bytes 2000000 | tf_op jit(solution)/shard_map/near/pallas_call | solution.py:304
  65.2 2.4 %collective-permute-done.6.theirs_ref = bf16[4,32,128]{2,1,0:T(8,128)(2,1)S(1)} collective-permute-done((bf16[4,32,128]{2,1,0:T(8,128)(2,1)S(1)}, bf16[4,32,128]{2,1,0:T(8,128)(2,1)S(1)}, u32[]{:S(2)}, u32[]{:S(2)}) %collective-permute-start.6) | collective-permute-done | bytes 32800 | tf_op jit(solution)/shard_map/ppermute | solution.py:350
  67.6 1.7 %final.1 = bf16[32,16,256]{2,1,0:T(8,128)(2,1)} custom-call(s32[2]{0:T(128)S(1)} %pad_add_fusion.scalar_ref.refs_0_, bf16[4,32,128]{2,1,0:T(8,128)(2,1)S(1)} %get-tuple-element.92.mine_ref, bf16[4,32,128]{2,1,0:T(8,128)(2,1)S(1)} %collective-permute-done.6.theirs_ref, bf16[32,64,512]{2,1,0:T(8,128)(2,1)S(1)} %copy-done, f32[32,16,256]{2,1,0:T(8,128)S(1)} %near.5.near_ref), custom_call_target="tpu_custom_call" | custom-call | tf_op jit(solution)/shard_map/final/pallas_call | solution.py:337
  (26 shorter events, 0.1 us)
Async XLA Ops:
  0.0 1.2 %copy-start.1 = (bf16[32,64,256]{2,1,0:T(8,128)(2,1)S(1)}, bf16[32,64,256]{2,1,0:T(8,128)(2,1)}, u32[]{:S(2)}) copy-start(bf16[32,64,256]{2,1,0:T(8,128)(2,1)} %basis_ref.1) | copy-start | bytes 3145732
  1.2 0.9 %copy-start.2 = (bf16[32,16,256]{2,1,0:T(8,128)(2,1)S(1)}, bf16[32,16,256]{2,1,0:T(8,128)(2,1)}, u32[]{:S(2)}) copy-start(bf16[32,16,256]{2,1,0:T(8,128)(2,1)} %vec_ref.1) | copy-start | bytes 786436
  2.8 6.6 %collective-permute-start = (f32[64,256]{1,0:T(8,128)S(1)}, f32[64,256]{1,0:T(8,128)S(1)}, u32[]{:S(2)}, u32[]{:S(2)}) collective-permute-start(f32[64,256]{1,0:T(8,128)S(1)} %get-tuple-element.57), channel_id=1, source_target_pairs={{0,1},{1,0},{2,3},{3,2},{4,5},{5,4},{6,7},{7,6},{8,9},{9,8},{10,11... | collective-permute-start | bytes 196616 | tf_op jit(solution)/shard_map/ppermute | solution.py:350
  4.9 38.4 %collective-permute-start.7 = (bf16[512,256]{1,0:T(8,128)(2,1)S(1)}, bf16[512,256]{1,0:T(8,128)(2,1)S(1)}, u32[]{:S(2)}, u32[]{:S(2)}) collective-permute-start(bf16[512,256]{1,0:T(8,128)(2,1)S(1)} %get-tuple-element.62.refs_2_), channel_id=1, source_target_pairs={{0,1},{1,0},{2,3},{3,2},{4,5},{5,4},{6,7},{7,6},{8,9},{9,8},{10,11... | collective-permute-start | bytes 786440 | tf_op jit(solution)/shard_map/ppermute | solution.py:350
  9.4 14.7 %collective-permute-start.1 = (bf16[64,256]{1,0:T(8,128)(2,1)S(1)}, bf16[64,256]{1,0:T(8,128)(2,1)S(1)}, u32[]{:S(2)}, u32[]{:S(2)}) collective-permute-start(bf16[64,256]{1,0:T(8,128)(2,1)S(1)} %add_convert_fusion.refs_0_), channel_id=1, source_target_pairs={{0,96},{16,112},{32,0},{48,16},{64,32},{80,48},{96,64},{112,80},{1... | collective-permute-start | bytes 98312 | tf_op jit(solution)/shard_map/ppermute | solution.py:350
  15.7 8.3 %collective-permute-start.2 = (bf16[64,256]{1,0:T(8,128)(2,1)S(1)}, bf16[64,256]{1,0:T(8,128)(2,1)S(1)}, u32[]{:S(2)}, u32[]{:S(2)}) collective-permute-start(bf16[64,256]{1,0:T(8,128)(2,1)S(1)} %add_convert_fusion.refs_0_), channel_id=1, source_target_pairs={{0,32},{16,48},{32,64},{48,80},{64,96},{80,112},{96,0},{112,16},{1... | collective-permute-start | bytes 98312 | tf_op jit(solution)/shard_map/ppermute | solution.py:350
  15.8 0.9 %copy-start.3 = (bf16[32,3,512]{2,0,1:T(8,128)(2,1)S(1)}, bf16[32,3,512]{2,0,1:T(8,128)(2,1)}, u32[]{:S(2)}) copy-start(bf16[32,3,512]{2,0,1:T(8,128)(2,1)} %param.9) | copy-start | bytes 294916
  18.9 16.8 %all-to-all-start.1 = ((bf16[16,40,128]{2,1,0:T(8,128)(2,1)}), bf16[16,40,128]{2,1,0:T(8,128)(2,1)S(1)}, u32[]{:S(2)}, u32[]{:S(2)}) async-start(bf16[16,40,128]{2,1,0:T(8,128)(2,1)} %get-tuple-element.55), calls=%async_computation.1 | async-start | bytes 327680 | tf_op jit(solution)/shard_map/all_to_all | solution.py:367
  24.0 29.2 %copy-start.5 = (bf16[64,256]{1,0:T(8,128)(2,1)}, bf16[64,256]{1,0:T(8,128)(2,1)S(1)}, u32[]{:S(2)}) copy-start(bf16[64,256]{1,0:T(8,128)(2,1)S(1)} %collective-permute-done.1.refs_1_) | copy-start | bytes 98308
  24.1 19.2 %copy-start.6 = (bf16[64,256]{1,0:T(8,128)(2,1)}, bf16[64,256]{1,0:T(8,128)(2,1)S(1)}, u32[]{:S(2)}) copy-start(bf16[64,256]{1,0:T(8,128)(2,1)S(1)} %collective-permute-done.2.refs_2_) | copy-start | bytes 98308
  24.1 11.6 %collective-permute-start.4 = (bf16[128,256]{1,0:T(8,128)(2,1)S(1)}, bf16[128,256]{1,0:T(8,128)(2,1)S(1)}, u32[]{:S(2)}, u32[]{:S(2)}) collective-permute-start(bf16[128,256]{1,0:T(8,128)(2,1)S(1)} %get-tuple-element.91), channel_id=1, source_target_pairs={{0,112},{16,0},{32,16},{48,32},{64,48},{80,64},{96,80},{112,96},{1... | collective-permute-start | bytes 196616 | tf_op jit(solution)/shard_map/ppermute | solution.py:350
  27.9 7.9 %collective-permute-start.5 = (bf16[128,256]{1,0:T(8,128)(2,1)S(1)}, bf16[128,256]{1,0:T(8,128)(2,1)S(1)}, u32[]{:S(2)}, u32[]{:S(2)}) collective-permute-start(bf16[128,256]{1,0:T(8,128)(2,1)S(1)} %get-tuple-element.90), channel_id=1, source_target_pairs={{0,16},{16,32},{32,48},{48,64},{64,80},{80,96},{96,112},{112,0},{1... | collective-permute-start | bytes 196616 | tf_op jit(solution)/shard_map/ppermute | solution.py:350
  27.9 7.8 %collective-permute-start.3 = (bf16[64,256]{1,0:T(8,128)(2,1)S(1)}, bf16[64,256]{1,0:T(8,128)(2,1)S(1)}, u32[]{:S(2)}, u32[]{:S(2)}) collective-permute-start(bf16[64,256]{1,0:T(8,128)(2,1)S(1)} %add_convert_fusion.refs_0_), channel_id=1, source_target_pairs={{0,64},{16,80},{32,96},{48,112},{64,0},{80,16},{96,32},{112,48},{1... | collective-permute-start | bytes 98312 | tf_op jit(solution)/shard_map/ppermute | solution.py:350
  35.7 7.6 %copy-start.9 = (bf16[64,256]{1,0:T(8,128)(2,1)}, bf16[64,256]{1,0:T(8,128)(2,1)S(1)}, u32[]{:S(2)}) copy-start(bf16[64,256]{1,0:T(8,128)(2,1)S(1)} %collective-permute-done.3.refs_3_) | copy-start | bytes 98308
  35.7 7.6 %copy-start.7 = (bf16[128,256]{1,0:T(8,128)(2,1)}, bf16[128,256]{1,0:T(8,128)(2,1)S(1)}, u32[]{:S(2)}) copy-start(bf16[128,256]{1,0:T(8,128)(2,1)S(1)} %collective-permute-done.4.refs_4_) | copy-start | bytes 196612
  35.7 7.6 %copy-start.8 = (bf16[128,256]{1,0:T(8,128)(2,1)}, bf16[128,256]{1,0:T(8,128)(2,1)S(1)}, u32[]{:S(2)}) copy-start(bf16[128,256]{1,0:T(8,128)(2,1)S(1)} %collective-permute-done.5.refs_5_) | copy-start | bytes 196612
  37.0 22.6 %all-to-all-start.2 = ((bf16[16,40,512]{2,1,0:T(8,128)(2,1)}), bf16[16,40,512]{2,1,0:T(8,128)(2,1)}, u32[]{:S(2)}, u32[]{:S(2)}) async-start(bf16[16,40,512]{2,1,0:T(8,128)(2,1)} %get-tuple-element.60), calls=%async_computation.2 | async-start | bytes 1310720 | tf_op jit(solution)/shard_map/all_to_all | solution.py:384
  46.6 15.7 %collective-permute-start.8 = (bf16[24,512]{1,0:T(8,128)(2,1)S(1)}, bf16[24,512]{1,0:T(8,128)(2,1)S(1)}, u32[]{:S(2)}, u32[]{:S(2)}) collective-permute-start(bf16[24,512]{1,0:T(8,128)(2,1)S(1)} %get-tuple-element.63), channel_id=1, source_target_pairs={{0,2},{2,4},{4,6},{6,8},{8,10},{10,12},{12,14},{14,16},{16,18},{18... | collective-permute-start | bytes 73736 | tf_op jit(solution)/shard_map/ppermute | solution.py:350
  47.0 15.3 %collective-permute-start.9 = (bf16[24,512]{1,0:T(8,128)(2,1)S(1)}, bf16[24,512]{1,0:T(8,128)(2,1)S(1)}, u32[]{:S(2)}, u32[]{:S(2)}) collective-permute-start(bf16[24,512]{1,0:T(8,128)(2,1)S(1)} %get-tuple-element.64), channel_id=1, source_target_pairs={{0,254},{2,0},{4,2},{6,4},{8,6},{10,8},{12,10},{14,12},{16,14},{18... | collective-permute-start | bytes 73736 | tf_op jit(solution)/shard_map/ppermute | solution.py:350
  53.2 6.4 %copy-start.4 = (bf16[32,64,512]{2,1,0:T(8,128)(2,1)S(1)}, bf16[32,64,512]{2,1,0:T(8,128)(2,1)}, u32[]{:S(2)}) copy-start(bf16[32,64,512]{2,1,0:T(8,128)(2,1)} %param.15) | copy-start | bytes 6291460
  53.2 6.4 %copy-start.10 = (s32[32,8]{0,1:T(8,128)S(1)}, s32[32,8]{0,1:T(8,128)}, u32[]{:S(2)}) copy-start(s32[32,8]{0,1:T(8,128)} %param.14) | copy-start | bytes 3076
  62.1 5.5 %copy-start = (bf16[32,64,512]{2,1,0:T(8,128)(2,1)S(1)}, bf16[32,64,512]{2,1,0:T(8,128)(2,1)}, u32[]{:S(2)}) copy-start(bf16[32,64,512]{2,1,0:T(8,128)(2,1)} %tgt_ref.1) | copy-start | bytes 6291460
  62.1 5.5 %collective-permute-start.6 = (bf16[4,32,128]{2,1,0:T(8,128)(2,1)S(1)}, bf16[4,32,128]{2,1,0:T(8,128)(2,1)S(1)}, u32[]{:S(2)}, u32[]{:S(2)}) collective-permute-start(bf16[4,32,128]{2,1,0:T(8,128)(2,1)S(1)} %get-tuple-element.92.mine_ref), channel_id=1, source_target_pairs={{0,1},{1,0},{2,3},{3,2},{4,5},{5,4},{6,7},{7,6},{8,9},{9,8},{10,11... | collective-permute-start | bytes 98312 | tf_op jit(solution)/shard_map/ppermute | solution.py:350

commit v11 on v10

--- a/solution.py
+++ b/solution.py
@@ -256,14 +256,15 @@
         points = [[pts_ref[u, :, pl.ds(h, HALF)] for h in (own, other)] for u in sources(t)]
         points = taken(t, slice(R, R + 8), points)
         for k in range(3):
-            y = jnp.concatenate(points[k], 1)
             for p in range(0, HALF, 32):
-                squared = None
-                for i in range(3):
-                    differ = x[p : p + 32, i : i + 1] - y[i : i + 1, :]
-                    differ = differ * differ
-                    squared = differ + bf16(soften_sq) if squared is None else squared + differ
-                kern[p : p + 32, k * LEAF : (k + 1) * LEAF] = lax.rsqrt(squared)
+                for h, y in enumerate(points[k]):
+                    squared = None
+                    for i in range(3):
+                        differ = x[p : p + 32, i : i + 1] - y[i : i + 1, :]
+                        differ = differ * differ
+                        squared = differ + bf16(soften_sq) if squared is None else squared + differ
+                    lane = k * LEAF + h * HALF
+                    kern[p : p + 32, lane : lane + HALF] = lax.rsqrt(squared)
 
     def product(t, kern):
         values = [[values_of(vec_ref, u), values_of(other_ref, u)] for u in sources(t)]
@@ -377,7 +378,7 @@
     near_args = (scalars, rows, held, other)
     near, first, last = near_call("early", (3, 11), 8, near_args)
     halos = shifted(last, WIDE, 1), shifted(first, WIDE, -1)
-    (near,) = near_call("inner", (11, 29), 9, near_args, (near,))
+    (near,) = near_call("inner", (11, 29), 18, near_args, (near,))
     (near,) = near_call("rest", (3, 29), 7, near_args, (*halos, near))
 
     packed, fits = pack_call(z[None], asked, pieces)

time: 69.8 us -> 69.7 us (level)
  no operation moved by 1% of the time
where the time goes in v11:
time: 69.7 us; the launch traced here: 69.3 us
  starting transfers between devices  33.5 us (48%)
  Pallas kernels  20.7 us (30%)
  waiting for transfers between devices  10.4 us (15%)
  local copies, waits for them, and re-layouts  3.1 us (4%)
  between operations  1.42 us (2%)
    ppermute x10, starting transfers between devices, shifted(): lax.ppermute(array, axis, [(i, (i + by) % devices) for i in range(devices)])  22.7 us
    pallas_call x3, Pallas kernels, near_call(): pl.pallas_call(lambda *refs: near_kernel(kind, leaves, group, *refs), out...  12.5 us
    ppermute x10, waiting for transfers between devices, shifted(): lax.ppermute(array, axis, [(i, (i + by) % devices) for i in range(devices)])  10.4 us
    all_to_all x1, starting transfers between devices, body(): got = lax.all_to_all(packed, PEERS, split_axis=0, concat_axis=0, tiled=True)  5.75 us
    all_to_all x1, starting transfers between devices, body(): asked = lax.all_to_all(req, PEERS, split_axis=0, concat_axis=0, tiled=True)  5.12 us
    unnamed x22, local copies, waits for them, and re-layouts  3.1 us
    pallas_call x1, Pallas kernels, select_call(): pl.pallas_call(select_kernel, out_shape=TC_SHAPE, in_specs=[VMEM, VMEM, V...  2.49 us
    pallas_call x1, Pallas kernels, index_call(): pl.pallas_call(index_kernel, out_shape=(jax.ShapeDtypeStruct((ENTRIES, 12...  2.18 us
  transfers between devices with their start and end apart: 12, of which 3 were waited for; matrix products, arithmetic and copies ran while one was open for 0% of the time, Pallas kernels for 27%

profile of v11, /device:TPU:16, one launch (start us, length us, event | category | flops | bytes accessed | tf_op | source)
XLA Modules:
  0.0 69.3 jit_solution(6337470015961327560)
XLA Ops:
  0.0 1.2 %copy-done.1 = bf16[32,64,256]{2,1,0:T(8,128)(2,1)S(1)} copy-done((bf16[32,64,256]{2,1,0:T(8,128)(2,1)S(1)}, bf16[32,64,256]{2,1,0:T(8,128)(2,1)}, u32[]{:S(2)}) %copy-start.1) | copy-done | bytes 1048600
  1.2 0.9 %copy-done.2 = bf16[32,16,256]{2,1,0:T(8,128)(2,1)S(1)} copy-done((bf16[32,16,256]{2,1,0:T(8,128)(2,1)S(1)}, bf16[32,16,256]{2,1,0:T(8,128)(2,1)}, u32[]{:S(2)}) %copy-start.2) | copy-done | bytes 262168
  2.2 0.6 coeffs.1
  2.8 2.1 %collective-permute-start = (f32[64,256]{1,0:T(8,128)S(1)}, f32[64,256]{1,0:T(8,128)S(1)}, u32[]{:S(2)}, u32[]{:S(2)}) collective-permute-start(f32[64,256]{1,0:T(8,128)S(1)} %get-tuple-element.57), channel_id=1, source_target_pairs={{0,1},{1,0},{2,3},{3,2},{4,5},{5,4},{6,7},{7,6},{8,9},{9,8},{10,11... | collective-permute-start | bytes 196616 | tf_op jit(solution)/shard_map/ppermute | solution.py:351
  4.9 1.5 %collective-permute-start.7 = (bf16[512,256]{1,0:T(8,128)(2,1)S(1)}, bf16[512,256]{1,0:T(8,128)(2,1)S(1)}, u32[]{:S(2)}, u32[]{:S(2)}) collective-permute-start(bf16[512,256]{1,0:T(8,128)(2,1)S(1)} %get-tuple-element.62.refs_2_), channel_id=1, source_target_pairs={{0,1},{1,0},{2,3},{3,2},{4,5},{5,4},{6,7},{7,6},{8,9},{9,8},{10,11... | collective-permute-start | bytes 786440 | tf_op jit(solution)/shard_map/ppermute | solution.py:351
  7.1 2.3 %collective-permute-done = f32[64,256]{1,0:T(8,128)S(1)} collective-permute-done((f32[64,256]{1,0:T(8,128)S(1)}, f32[64,256]{1,0:T(8,128)S(1)}, u32[]{:S(2)}, u32[]{:S(2)}) %collective-permute-start) | collective-permute-done | bytes 65568 | tf_op jit(solution)/shard_map/ppermute | solution.py:351
  9.4 6.4 %collective-permute-start.1 = (bf16[64,256]{1,0:T(8,128)(2,1)S(1)}, bf16[64,256]{1,0:T(8,128)(2,1)S(1)}, u32[]{:S(2)}, u32[]{:S(2)}) collective-permute-start(bf16[64,256]{1,0:T(8,128)(2,1)S(1)} %add_convert_fusion.refs_0_), channel_id=1, source_target_pairs={{0,96},{16,112},{32,0},{48,16},{64,32},{80,48},{96,64},{112,80},{1... | collective-permute-start | bytes 98312 | tf_op jit(solution)/shard_map/ppermute | solution.py:351
  15.7 0.0 collective-permute-start.2
  15.8 0.1 pad_add_fusion.scalar_ref.refs_0_
  15.8 0.9 %copy-done.3 = bf16[32,3,512]{2,0,1:T(8,128)(2,1)S(1)} copy-done((bf16[32,3,512]{2,0,1:T(8,128)(2,1)S(1)}, bf16[32,3,512]{2,0,1:T(8,128)(2,1)}, u32[]{:S(2)}) %copy-start.3) | copy-done | bytes 98328
  16.7 2.2 %requests.1 = (s32[256,128]{1,0:T(8,128)}, bf16[16,40,128]{2,1,0:T(8,128)(2,1)}, bf16[32,8,512]{2,1,0:T(8,128)(2,1)S(1)}) custom-call(s32[2]{0:T(128)S(1)} %pad_add_fusion.scalar_ref.refs_0_, s32[8,32]{1,0:T(8,128)} %bitcast.10, bf16[3,32,512]{2,1,0:T(8,128)(2,1)S(1)} %bitcast.9), custom_call_target="tpu_custom_call" | custom-call | tf_op jit(solution)/shard_map/requests/pallas_call | solution.py:80
  18.9 5.1 %all-to-all-start.1 = ((bf16[16,40,128]{2,1,0:T(8,128)(2,1)}), bf16[16,40,128]{2,1,0:T(8,128)(2,1)S(1)}, u32[]{:S(2)}, u32[]{:S(2)}) async-start(bf16[16,40,128]{2,1,0:T(8,128)(2,1)} %get-tuple-element.55), calls=%async_computation.1 | async-start | bytes 327680 | tf_op jit(solution)/shard_map/all_to_all | solution.py:368
  24.1 3.8 %collective-permute-start.4 = (bf16[128,256]{1,0:T(8,128)(2,1)S(1)}, bf16[128,256]{1,0:T(8,128)(2,1)S(1)}, u32[]{:S(2)}, u32[]{:S(2)}) collective-permute-start(bf16[128,256]{1,0:T(8,128)(2,1)S(1)} %get-tuple-element.91), channel_id=1, source_target_pairs={{0,112},{16,0},{32,16},{48,32},{64,48},{80,64},{96,80},{112,96},{1... | collective-permute-start | bytes 196616 | tf_op jit(solution)/shard_map/ppermute | solution.py:351
  27.9 0.0 collective-permute-start.5
  27.9 2.1 %collective-permute-start.3 = (bf16[64,256]{1,0:T(8,128)(2,1)S(1)}, bf16[64,256]{1,0:T(8,128)(2,1)S(1)}, u32[]{:S(2)}, u32[]{:S(2)}) collective-permute-start(bf16[64,256]{1,0:T(8,128)(2,1)S(1)} %add_convert_fusion.refs_0_), channel_id=1, source_target_pairs={{0,64},{16,80},{32,96},{48,112},{64,0},{80,16},{96,32},{112,48},{1... | collective-permute-start | bytes 98312 | tf_op jit(solution)/shard_map/ppermute | solution.py:351
  30.0 5.7 %collective-permute-done.3.refs_3_ = bf16[64,256]{1,0:T(8,128)(2,1)S(1)} collective-permute-done((bf16[64,256]{1,0:T(8,128)(2,1)S(1)}, bf16[64,256]{1,0:T(8,128)(2,1)S(1)}, u32[]{:S(2)}, u32[]{:S(2)}) %collective-permute-start.3) | collective-permute-done | bytes 32800 | tf_op jit(solution)/shard_map/ppermute | solution.py:351
  35.7 0.0 all-to-all-done.1.req_ref
  35.7 0.0 collective-permute-done.4.refs_4_
  35.7 0.0 copy-start.7
  35.7 1.2 %pack.1 = (bf16[16,40,512]{2,1,0:T(8,128)(2,1)}, s32[1]{0:T(128)}) custom-call(s32[1]{0:T(128)} %bitcast.3.z_ref, bf16[16,40,128]{2,1,0:T(8,128)(2,1)S(1)} %all-to-all-done.1.req_ref, bf16[64,256]{1,0:T(8,128)(2,1)S(1)} %add_convert_fusion.refs_0_, bf16[64,256]{1,0:T(8,128)(2,1)S(1)} %collective-permute-done.1.refs_1_, ...), custom_call_target="tpu_custom_call" | custom-call | tf_op jit(solution)/shard_map/pack/pallas_call | solution.py:149
  37.0 5.8 %all-to-all-start.2 = ((bf16[16,40,512]{2,1,0:T(8,128)(2,1)}), bf16[16,40,512]{2,1,0:T(8,128)(2,1)}, u32[]{:S(2)}, u32[]{:S(2)}) async-start(bf16[16,40,512]{2,1,0:T(8,128)(2,1)} %get-tuple-element.60), calls=%async_computation.2 | async-start | bytes 1310720 | tf_op jit(solution)/shard_map/all_to_all | solution.py:385
  43.3 3.2 %near.3 = (f32[32,16,256]{2,1,0:T(8,128)S(1)}, bf16[24,512]{1,0:T(8,128)(2,1)S(1)}, bf16[24,512]{1,0:T(8,128)(2,1)S(1)}) custom-call(s32[2]{0:T(128)S(1)} %pad_add_fusion.scalar_ref.refs_0_, bf16[32,8,512]{2,1,0:T(8,128)(2,1)S(1)} %get-tuple-element.61.refs_1_, bf16[512,256]{1,0:T(8,128)(2,1)S(1)} %get-tuple-element.62.refs_2_, ...), custom_call_target="tpu_custom_call" | custom-call | flops 1600000000 | bytes 2000000 | tf_op jit(solution)/shard_map/near/pallas_call | solution.py:305
  46.6 0.4 collective-permute-start.8
  47.0 6.3 %collective-permute-start.9 = (bf16[24,512]{1,0:T(8,128)(2,1)S(1)}, bf16[24,512]{1,0:T(8,128)(2,1)S(1)}, u32[]{:S(2)}, u32[]{:S(2)}) collective-permute-start(bf16[24,512]{1,0:T(8,128)(2,1)S(1)} %get-tuple-element.64), channel_id=1, source_target_pairs={{0,254},{2,0},{4,2},{6,4},{8,6},{10,8},{12,10},{14,12},{16,14},{18... | collective-permute-start | bytes 73736 | tf_op jit(solution)/shard_map/ppermute | solution.py:351
  53.2 6.3 %near.4.refs_6_ = f32[32,16,256]{2,1,0:T(8,128)S(1)} custom-call(s32[2]{0:T(128)S(1)} %pad_add_fusion.scalar_ref.refs_0_, bf16[32,8,512]{2,1,0:T(8,128)(2,1)S(1)} %get-tuple-element.61.refs_1_, bf16[512,256]{1,0:T(8,128)(2,1)S(1)} %get-tuple-element.62.refs_2_, bf16[512,256]{1,0:T(8,128)(2,1)S(1)} %collective-permute-done.7.refs_3_, ...), custom_call_target="tpu_custom_call", output_to_operand_aliasing={{}: (4, {})} | custom-call | flops 3600000000 | bytes 2000000 | tf_op jit(solution)/shard_map/near/pallas_call | solution.py:305
  59.5 0.0 copy-done.4
  59.6 2.5 %conditional.1 = (bf16[4,32,128]{2,1,0:T(8,128)(2,1)S(1)}) conditional(s32[]{:T(128)} %bitcast.6, (s32[32,8]{0,1:T(8,128)S(1)}, bf16[64,256]{1,0:T(8,128)(2,1)S(1)}, bf16[128,256]{1,0:T(8,128)(2,1)}, bf16[64,256]{1,0:T(8,128)(2,1)}, bf16[64,256]{1,0:T(8,128)(2,1)}, /*index=5*/bf16[128,256]{1,0:T(8,128)(2,1)}, bf16[64,256]{1,0:T(8,128)(2,1)}, ...), branch_computations={%region_0.1_spmd, %region_1.2_spmd} | conditional | flops 1075842048 | bytes 23860436 | solution.py:404
  59.6 2.5 %select.3 = bf16[4,32,128]{2,1,0:T(8,128)(2,1)S(1)} custom-call(s32[256,128]{1,0:T(8,128)} %get-tuple-element.41.sel_ref, bf16[16,40,512]{2,1,0:T(8,128)(2,1)} %get-tuple-element.42.got_ref, bf16[32,64,512]{2,1,0:T(8,128)(2,1)S(1)} %get-tuple-element.43.couple_ref), custom_call_target="tpu_custom_call" | custom-call | tf_op jit(solution)/shard_map/cond/branch_1_fun/select/pallas_call | solution.py:199
  62.1 0.1 collective-permute-start.6
  62.2 3.0 %near.5.near_ref = f32[32,16,256]{2,1,0:T(8,128)S(1)} custom-call(s32[2]{0:T(128)S(1)} %pad_add_fusion.scalar_ref.refs_0_, bf16[32,8,512]{2,1,0:T(8,128)(2,1)S(1)} %get-tuple-element.61.refs_1_, bf16[512,256]{1,0:T(8,128)(2,1)S(1)} %get-tuple-element.62.refs_2_, bf16[512,256]{1,0:T(8,128)(2,1)S(1)} %collective-permute-done.7.refs_3_, ...), custom_call_target="tpu_custom_call", output_to_operand_aliasing={{}: (6, {})} | custom-call | flops 1400000000 | bytes 2000000 | tf_op jit(solution)/shard_map/near/pallas_call | solution.py:305
  65.2 2.4 %collective-permute-done.6.theirs_ref = bf16[4,32,128]{2,1,0:T(8,128)(2,1)S(1)} collective-permute-done((bf16[4,32,128]{2,1,0:T(8,128)(2,1)S(1)}, bf16[4,32,128]{2,1,0:T(8,128)(2,1)S(1)}, u32[]{:S(2)}, u32[]{:S(2)}) %collective-permute-start.6) | collective-permute-done | bytes 32800 | tf_op jit(solution)/shard_map/ppermute | solution.py:351
  67.6 1.7 %final.1 = bf16[32,16,256]{2,1,0:T(8,128)(2,1)} custom-call(s32[2]{0:T(128)S(1)} %pad_add_fusion.scalar_ref.refs_0_, bf16[4,32,128]{2,1,0:T(8,128)(2,1)S(1)} %get-tuple-element.92.mine_ref, bf16[4,32,128]{2,1,0:T(8,128)(2,1)S(1)} %collective-permute-done.6.theirs_ref, bf16[32,64,512]{2,1,0:T(8,128)(2,1)S(1)} %copy-done, f32[32,16,256]{2,1,0:T(8,128)S(1)} %near.5.near_ref), custom_call_target="tpu_custom_call" | custom-call | tf_op jit(solution)/shard_map/final/pallas_call | solution.py:338
  (26 shorter events, 0.1 us)
Async XLA Ops:
  0.0 1.2 %copy-start.1 = (bf16[32,64,256]{2,1,0:T(8,128)(2,1)S(1)}, bf16[32,64,256]{2,1,0:T(8,128)(2,1)}, u32[]{:S(2)}) copy-start(bf16[32,64,256]{2,1,0:T(8,128)(2,1)} %basis_ref.1) | copy-start | bytes 3145732
  1.2 0.9 %copy-start.2 = (bf16[32,16,256]{2,1,0:T(8,128)(2,1)S(1)}, bf16[32,16,256]{2,1,0:T(8,128)(2,1)}, u32[]{:S(2)}) copy-start(bf16[32,16,256]{2,1,0:T(8,128)(2,1)} %vec_ref.1) | copy-start | bytes 786436
  2.8 6.6 %collective-permute-start = (f32[64,256]{1,0:T(8,128)S(1)}, f32[64,256]{1,0:T(8,128)S(1)}, u32[]{:S(2)}, u32[]{:S(2)}) collective-permute-start(f32[64,256]{1,0:T(8,128)S(1)} %get-tuple-element.57), channel_id=1, source_target_pairs={{0,1},{1,0},{2,3},{3,2},{4,5},{5,4},{6,7},{7,6},{8,9},{9,8},{10,11... | collective-permute-start | bytes 196616 | tf_op jit(solution)/shard_map/ppermute | solution.py:351
  4.9 38.4 %collective-permute-start.7 = (bf16[512,256]{1,0:T(8,128)(2,1)S(1)}, bf16[512,256]{1,0:T(8,128)(2,1)S(1)}, u32[]{:S(2)}, u32[]{:S(2)}) collective-permute-start(bf16[512,256]{1,0:T(8,128)(2,1)S(1)} %get-tuple-element.62.refs_2_), channel_id=1, source_target_pairs={{0,1},{1,0},{2,3},{3,2},{4,5},{5,4},{6,7},{7,6},{8,9},{9,8},{10,11... | collective-permute-start | bytes 786440 | tf_op jit(solution)/shard_map/ppermute | solution.py:351
  9.4 14.7 %collective-permute-start.1 = (bf16[64,256]{1,0:T(8,128)(2,1)S(1)}, bf16[64,256]{1,0:T(8,128)(2,1)S(1)}, u32[]{:S(2)}, u32[]{:S(2)}) collective-permute-start(bf16[64,256]{1,0:T(8,128)(2,1)S(1)} %add_convert_fusion.refs_0_), channel_id=1, source_target_pairs={{0,96},{16,112},{32,0},{48,16},{64,32},{80,48},{96,64},{112,80},{1... | collective-permute-start | bytes 98312 | tf_op jit(solution)/shard_map/ppermute | solution.py:351
  15.7 8.3 %collective-permute-start.2 = (bf16[64,256]{1,0:T(8,128)(2,1)S(1)}, bf16[64,256]{1,0:T(8,128)(2,1)S(1)}, u32[]{:S(2)}, u32[]{:S(2)}) collective-permute-start(bf16[64,256]{1,0:T(8,128)(2,1)S(1)} %add_convert_fusion.refs_0_), channel_id=1, source_target_pairs={{0,32},{16,48},{32,64},{48,80},{64,96},{80,112},{96,0},{112,16},{1... | collective-permute-start | bytes 98312 | tf_op jit(solution)/shard_map/ppermute | solution.py:351
  15.8 0.9 %copy-start.3 = (bf16[32,3,512]{2,0,1:T(8,128)(2,1)S(1)}, bf16[32,3,512]{2,0,1:T(8,128)(2,1)}, u32[]{:S(2)}) copy-start(bf16[32,3,512]{2,0,1:T(8,128)(2,1)} %param.9) | copy-start | bytes 294916
  18.9 16.8 %all-to-all-start.1 = ((bf16[16,40,128]{2,1,0:T(8,128)(2,1)}), bf16[16,40,128]{2,1,0:T(8,128)(2,1)S(1)}, u32[]{:S(2)}, u32[]{:S(2)}) async-start(bf16[16,40,128]{2,1,0:T(8,128)(2,1)} %get-tuple-element.55), calls=%async_computation.1 | async-start | bytes 327680 | tf_op jit(solution)/shard_map/all_to_all | solution.py:368
  24.0 29.2 %copy-start.5 = (bf16[64,256]{1,0:T(8,128)(2,1)}, bf16[64,256]{1,0:T(8,128)(2,1)S(1)}, u32[]{:S(2)}) copy-start(bf16[64,256]{1,0:T(8,128)(2,1)S(1)} %collective-permute-done.1.refs_1_) | copy-start | bytes 98308
  24.1 19.2 %copy-start.6 = (bf16[64,256]{1,0:T(8,128)(2,1)}, bf16[64,256]{1,0:T(8,128)(2,1)S(1)}, u32[]{:S(2)}) copy-start(bf16[64,256]{1,0:T(8,128)(2,1)S(1)} %collective-permute-done.2.refs_2_) | copy-start | bytes 98308
  24.1 11.6 %collective-permute-start.4 = (bf16[128,256]{1,0:T(8,128)(2,1)S(1)}, bf16[128,256]{1,0:T(8,128)(2,1)S(1)}, u32[]{:S(2)}, u32[]{:S(2)}) collective-permute-start(bf16[128,256]{1,0:T(8,128)(2,1)S(1)} %get-tuple-element.91), channel_id=1, source_target_pairs={{0,112},{16,0},{32,16},{48,32},{64,48},{80,64},{96,80},{112,96},{1... | collective-permute-start | bytes 196616 | tf_op jit(solution)/shard_map/ppermute | solution.py:351
  27.9 7.9 %collective-permute-start.5 = (bf16[128,256]{1,0:T(8,128)(2,1)S(1)}, bf16[128,256]{1,0:T(8,128)(2,1)S(1)}, u32[]{:S(2)}, u32[]{:S(2)}) collective-permute-start(bf16[128,256]{1,0:T(8,128)(2,1)S(1)} %get-tuple-element.90), channel_id=1, source_target_pairs={{0,16},{16,32},{32,48},{48,64},{64,80},{80,96},{96,112},{112,0},{1... | collective-permute-start | bytes 196616 | tf_op jit(solution)/shard_map/ppermute | solution.py:351
  27.9 7.8 %collective-permute-start.3 = (bf16[64,256]{1,0:T(8,128)(2,1)S(1)}, bf16[64,256]{1,0:T(8,128)(2,1)S(1)}, u32[]{:S(2)}, u32[]{:S(2)}) collective-permute-start(bf16[64,256]{1,0:T(8,128)(2,1)S(1)} %add_convert_fusion.refs_0_), channel_id=1, source_target_pairs={{0,64},{16,80},{32,96},{48,112},{64,0},{80,16},{96,32},{112,48},{1... | collective-permute-start | bytes 98312 | tf_op jit(solution)/shard_map/ppermute | solution.py:351
  35.7 7.6 %copy-start.9 = (bf16[64,256]{1,0:T(8,128)(2,1)}, bf16[64,256]{1,0:T(8,128)(2,1)S(1)}, u32[]{:S(2)}) copy-start(bf16[64,256]{1,0:T(8,128)(2,1)S(1)} %collective-permute-done.3.refs_3_) | copy-start | bytes 98308
  35.7 7.6 %copy-start.7 = (bf16[128,256]{1,0:T(8,128)(2,1)}, bf16[128,256]{1,0:T(8,128)(2,1)S(1)}, u32[]{:S(2)}) copy-start(bf16[128,256]{1,0:T(8,128)(2,1)S(1)} %collective-permute-done.4.refs_4_) | copy-start | bytes 196612
  35.7 7.6 %copy-start.8 = (bf16[128,256]{1,0:T(8,128)(2,1)}, bf16[128,256]{1,0:T(8,128)(2,1)S(1)}, u32[]{:S(2)}) copy-start(bf16[128,256]{1,0:T(8,128)(2,1)S(1)} %collective-permute-done.5.refs_5_) | copy-start | bytes 196612
  37.0 22.6 %all-to-all-start.2 = ((bf16[16,40,512]{2,1,0:T(8,128)(2,1)}), bf16[16,40,512]{2,1,0:T(8,128)(2,1)}, u32[]{:S(2)}, u32[]{:S(2)}) async-start(bf16[16,40,512]{2,1,0:T(8,128)(2,1)} %get-tuple-element.60), calls=%async_computation.2 | async-start | bytes 1310720 | tf_op jit(solution)/shard_map/all_to_all | solution.py:385
  46.6 15.6 %collective-permute-start.8 = (bf16[24,512]{1,0:T(8,128)(2,1)S(1)}, bf16[24,512]{1,0:T(8,128)(2,1)S(1)}, u32[]{:S(2)}, u32[]{:S(2)}) collective-permute-start(bf16[24,512]{1,0:T(8,128)(2,1)S(1)} %get-tuple-element.63), channel_id=1, source_target_pairs={{0,2},{2,4},{4,6},{6,8},{8,10},{10,12},{12,14},{14,16},{16,18},{18... | collective-permute-start | bytes 73736 | tf_op jit(solution)/shard_map/ppermute | solution.py:351
  47.0 15.2 %collective-permute-start.9 = (bf16[24,512]{1,0:T(8,128)(2,1)S(1)}, bf16[24,512]{1,0:T(8,128)(2,1)S(1)}, u32[]{:S(2)}, u32[]{:S(2)}) collective-permute-start(bf16[24,512]{1,0:T(8,128)(2,1)S(1)} %get-tuple-element.64), channel_id=1, source_target_pairs={{0,254},{2,0},{4,2},{6,4},{8,6},{10,8},{12,10},{14,12},{16,14},{18... | collective-permute-start | bytes 73736 | tf_op jit(solution)/shard_map/ppermute | solution.py:351
  53.2 6.3 %copy-start.4 = (bf16[32,64,512]{2,1,0:T(8,128)(2,1)S(1)}, bf16[32,64,512]{2,1,0:T(8,128)(2,1)}, u32[]{:S(2)}) copy-start(bf16[32,64,512]{2,1,0:T(8,128)(2,1)} %param.15) | copy-start | bytes 6291460
  53.2 6.3 %copy-start.10 = (s32[32,8]{0,1:T(8,128)S(1)}, s32[32,8]{0,1:T(8,128)}, u32[]{:S(2)}) copy-start(s32[32,8]{0,1:T(8,128)} %param.14) | copy-start | bytes 3076
  62.1 5.5 %copy-start = (bf16[32,64,512]{2,1,0:T(8,128)(2,1)S(1)}, bf16[32,64,512]{2,1,0:T(8,128)(2,1)}, u32[]{:S(2)}) copy-start(bf16[32,64,512]{2,1,0:T(8,128)(2,1)} %tgt_ref.1) | copy-start | bytes 6291460
  62.1 5.5 %collective-permute-start.6 = (bf16[4,32,128]{2,1,0:T(8,128)(2,1)S(1)}, bf16[4,32,128]{2,1,0:T(8,128)(2,1)S(1)}, u32[]{:S(2)}, u32[]{:S(2)}) collective-permute-start(bf16[4,32,128]{2,1,0:T(8,128)(2,1)S(1)} %get-tuple-element.92.mine_ref), channel_id=1, source_target_pairs={{0,1},{1,0},{2,3},{3,2},{4,5},{5,4},{6,7},{7,6},{8,9},{9,8},{10,11... | collective-permute-start | bytes 98312 | tf_op jit(solution)/shard_map/ppermute | solution.py:351
